TPU v7x, 32 devices: a whole 2x2x4 slice. The times are simulated.
32 devices in a mesh: section: 2 (over core), dp: 4 (over z), tensor: 4 (over y, x).
Axes of the slice: x: 2, y: 2, z: 4, core: 2. Of those that a mesh axis runs over, the one named last changes fastest.
Arguments:
- inputs: bfloat16 [2, 512, 4096], P(None, 'dp', 'tensor'), may hold values from -6 to 6
- adapter_down: bfloat16 [2, 4096, 128], P('section', 'tensor'), may hold values from -0.09375 to 0.09375
- adapter_up: bfloat16 [2, 128, 4096], P('section', None, 'tensor'), may hold values from -0.5 to 0.5
- gains: bfloat16 [2, 4096], P('section', 'tensor'), may hold values from 0.25 to 1.75
- head: bfloat16 [4096, 128], P('tensor'), may hold values from -0.375 to 0.375
- labels: int32 [2, 512], P(None, 'dp'), may hold values from 0 to 127
- valid: int32 [2, 512], P(None, 'dp'), may hold values from 0 to 1, as said below
Outputs:
- grads_down: float32 [2, 4096, 128], P('section', 'tensor', 'dp')
- grads_up: float32 [2, 128, 4096], P('section', 'dp', 'tensor')
- grads_gain: float32 [2, 4096], P('section', 'tensor')
Inputs may be any that keep to these rules, and one draw needn't show every extreme that they name: In each microbatch the first of every 128 consecutive tokens is valid.
All inputs are finite; a program needn't handle non-finite values.
Results may differ from a plain program's by a relative error of at most 0.015.
Values may be sent and summed in bfloat16 or wider, within the bound.
No kernel may reach another device: no remote copies, remote signals or barrier semaphores. Data moves between devices by JAX's collectives and lax.ppermute only.
A program may use at most 64 MiB of HBM per device.

v0:
```python
import jax
import jax.numpy as jnp
from jax import lax
from jax.sharding import PartitionSpec as P

D = 4096


epsilon = 1e-05


def passed_along(value, axis, by):
    size = lax.axis_size(axis)
    pairs = [(i, i + by) for i in range(size) if 0 <= i + by < size]
    return lax.ppermute(value, axis, pairs)


def store_slot(store, item, slot, active):
    previous = lax.dynamic_index_in_dim(store, slot, 0, keepdims=False)
    return lax.dynamic_update_index_in_dim(store, jnp.where(active, item, previous), slot, 0)


def layer_forward(inbound, gain_row, down_weight, up_weight):
    values = inbound.astype(jnp.float32)
    squares = jnp.sum(values * values, axis=1)
    scaled = (values * gain_row).astype(jnp.bfloat16)
    partial_proj = jnp.dot(scaled, down_weight, preferred_element_type=jnp.float32)
    share_squares, projected = (
        lax.psum_scatter(squares, "tensor", scatter_dimension=0, tiled=True),
        lax.psum_scatter(partial_proj, "tensor", scatter_dimension=0, tiled=True),
    )
    inverse = lax.rsqrt(share_squares / D + epsilon)
    hidden_share = jax.nn.silu(inverse[:, None] * projected).astype(jnp.bfloat16)
    hidden = lax.all_gather(hidden_share, "tensor", axis=0, tiled=True)
    outbound = (values + jnp.dot(hidden, up_weight, preferred_element_type=jnp.float32)).astype(
        jnp.bfloat16
    )
    return (outbound, projected, inverse, hidden)


def head_backward(final_state, head, label_row, valid_row):
    values = final_state.astype(jnp.float32)
    squares = jnp.sum(values * values, axis=1)
    partial_logit = jnp.dot(final_state, head, preferred_element_type=jnp.float32)
    squares, logit_base = lax.psum((squares, partial_logit), "tensor")
    inverse = lax.rsqrt(squares / D + epsilon)
    logits = inverse[:, None] * logit_base
    shifted = logits - jnp.max(logits, axis=1, keepdims=True)
    expo_terms = jnp.exp(shifted)
    softmax_prob = expo_terms / jnp.sum(expo_terms, axis=1, keepdims=True)
    classes = lax.broadcasted_iota(jnp.int32, logits.shape, 1)
    onehot = (classes == label_row[:, None]).astype(jnp.float32)
    cotangent = (softmax_prob - onehot) * valid_row[:, None].astype(jnp.float32)
    radial = jnp.sum(cotangent * logit_base, axis=1)
    weighted = (inverse[:, None] * cotangent).astype(jnp.bfloat16)
    back_term = lax.dot_general(
        weighted, head, (((1,), (1,)), ((), ())), preferred_element_type=jnp.float32
    )
    result = back_term - (inverse**3 / D * radial)[:, None] * values
    return result.astype(jnp.bfloat16)


def bottleneck_grad(hidden_grad, projected, inverse):
    pre_act = inverse[:, None] * projected
    sigmoid_val = jax.nn.sigmoid(pre_act)
    act_grad = hidden_grad * sigmoid_val * (1.0 + pre_act * (1.0 - sigmoid_val))
    radial = jnp.sum(act_grad * projected, axis=1)
    weighted = (inverse[:, None] * act_grad).astype(jnp.bfloat16)
    factor_row = inverse**3 / D * radial
    return (weighted, factor_row)


def layer_backward(
    cotangent, inbound, projected, inverse, hidden, gain_row, down_weight, up_weight
):
    partial_back = lax.dot_general(
        cotangent, up_weight, (((1,), (1,)), ((), ())), preferred_element_type=jnp.float32
    )
    grad_share = lax.psum_scatter(partial_back, "tensor", scatter_dimension=0, tiled=True)
    weighted_share, factor_share = bottleneck_grad(grad_share, projected, inverse)
    weighted = lax.all_gather(weighted_share, "tensor", axis=0, tiled=True)
    factor_row = lax.all_gather(factor_share, "tensor", axis=0, tiled=True)
    scaled_grad = lax.dot_general(
        weighted, down_weight, (((1,), (1,)), ((), ())), preferred_element_type=jnp.float32
    )
    values = inbound.astype(jnp.float32)
    outbound = (
        cotangent.astype(jnp.float32) + gain_row * scaled_grad - factor_row[:, None] * values
    ).astype(jnp.bfloat16)
    scaled = (values * gain_row).astype(jnp.bfloat16)
    down_grad = lax.dot_general(
        scaled, weighted, (((0,), (0,)), ((), ())), preferred_element_type=jnp.float32
    )
    up_grad = lax.dot_general(
        hidden, cotangent, (((0,), (0,)), ((), ())), preferred_element_type=jnp.float32
    )
    gain_grad = jnp.sum(scaled_grad * values, axis=0)
    return (outbound, down_grad, up_grad, gain_grad)


def local(inputs, adapter_down, adapter_up, gains, head, labels, valid):
    section_count = lax.axis_size("section")
    section_id = lax.axis_index("section")
    micro_count = inputs.shape[0]
    tick_count = micro_count + section_count - 1
    down_weight = adapter_down[0]
    up_weight = adapter_up[0]
    gain_row = gains[0].astype(jnp.float32)
    token_rows = inputs.shape[1]
    rank_width = down_weight.shape[1]
    saved_rows = token_rows // lax.axis_size("tensor")
    local_count = jnp.sum(valid.astype(jnp.float32))
    pre_scale = 1.0
    inbound_store = jnp.zeros_like(inputs)
    outbound_store = jnp.zeros_like(inputs)
    proj_store = jnp.zeros((micro_count, saved_rows, rank_width), jnp.float32)
    inverse_store = jnp.zeros((micro_count, saved_rows), jnp.float32)
    hidden_store = jnp.zeros((micro_count, token_rows, rank_width), jnp.bfloat16)
    received = jnp.zeros_like(inputs[0])
    for step_index in range(tick_count):
        micro_index = step_index - section_id
        active = (micro_index >= 0) & (micro_index < micro_count)
        clipped = jnp.clip(micro_index, 0, micro_count - 1)
        first_input = lax.dynamic_index_in_dim(inputs, clipped, 0, keepdims=False)
        inbound = jnp.where(section_id == 0, first_input, received)
        outbound, projected, inverse, hidden = layer_forward(
            inbound, gain_row, down_weight, up_weight
        )
        inbound_store = store_slot(inbound_store, inbound, clipped, active)
        outbound_store = store_slot(outbound_store, outbound, clipped, active)
        proj_store = store_slot(proj_store, projected, clipped, active)
        inverse_store = store_slot(inverse_store, inverse, clipped, active)
        hidden_store = store_slot(hidden_store, hidden, clipped, active)
        if step_index + 1 < tick_count:
            received = passed_along(outbound, "section", 1)
    down_total = jnp.zeros(down_weight.shape, jnp.float32)
    up_total = jnp.zeros(up_weight.shape, jnp.float32)
    gain_total = jnp.zeros(gain_row.shape, jnp.float32)
    back_received = jnp.zeros_like(inputs[0])
    is_last = section_id == section_count - 1
    for step_index in range(tick_count):
        micro_index = step_index - (section_count - 1 - section_id)
        active = (micro_index >= 0) & (micro_index < micro_count)
        clipped = jnp.clip(micro_index, 0, micro_count - 1)
        final_state = lax.dynamic_index_in_dim(outbound_store, clipped, 0, keepdims=False)
        label_row = lax.dynamic_index_in_dim(labels, clipped, 0, keepdims=False)
        valid_row = lax.dynamic_index_in_dim(valid, clipped, 0, keepdims=False)
        head_grad = head_backward(final_state, head, label_row, valid_row)
        cotangent = jnp.where(is_last & active, head_grad, back_received)
        saved_in = lax.dynamic_index_in_dim(inbound_store, clipped, 0, keepdims=False)
        saved_proj = lax.dynamic_index_in_dim(proj_store, clipped, 0, keepdims=False)
        saved_inverse = lax.dynamic_index_in_dim(inverse_store, clipped, 0, keepdims=False)
        saved_hidden = lax.dynamic_index_in_dim(hidden_store, clipped, 0, keepdims=False)
        outbound, down_grad, up_grad, gain_grad = layer_backward(
            cotangent,
            saved_in,
            saved_proj,
            saved_inverse,
            saved_hidden,
            gain_row,
            down_weight,
            up_weight,
        )
        factor = active.astype(jnp.float32)
        down_total = down_total + down_grad * factor
        up_total = up_total + up_grad * factor
        gain_total = gain_total + gain_grad * factor
        if step_index + 1 < tick_count:
            back_received = passed_along(outbound, "section", -1)
    down_piece, up_piece = (
        lax.psum_scatter(
            (down_total * pre_scale).astype(jnp.bfloat16), "dp", scatter_dimension=1, tiled=True
        ).astype(jnp.float32),
        lax.psum_scatter(
            (up_total * pre_scale).astype(jnp.bfloat16), "dp", scatter_dimension=0, tiled=True
        ).astype(jnp.float32),
    )
    gain_summed, count_summed = lax.psum((gain_total, local_count), "dp")
    post_scale = 1.0 / count_summed
    gain_final = gain_summed * post_scale
    return ((down_piece * post_scale)[None], (up_piece * post_scale)[None], gain_final[None])


def solution(mesh):
    return jax.shard_map(
        local,
        mesh=mesh,
        in_specs=(
            P(None, "dp", "tensor"),
            P("section", "tensor", None),
            P("section", None, "tensor"),
            P("section", "tensor"),
            P("tensor", None),
            P(None, "dp"),
            P(None, "dp"),
        ),
        out_specs=(
            P("section", "tensor", "dp"),
            P("section", "dp", "tensor"),
            P("section", "tensor"),
        ),
        check_vma=False,
    )
```

profile of v0, /device:TPU:0, one launch (start us, length us, event | category | flops | bytes accessed | tf_op | source)
XLA Modules:
  0.0 359.1 jit_solution(9906430966281404676)
XLA Ops:
  8.0 1.9 fusion.46
  10.2 11.4 %all-reduce.2 = f32[128]{0:T(128)S(1)} all-reduce(f32[128]{0:T(128)S(1)} %fusion.23), channel_id=2, replica_groups=mesh['section'=2,'dp'=4,'tensor'=4] {'tensor'}, use_global_device_ids=true, to_apply=%region_1.2.clone | all-reduce | flops 128 | bytes 1024
  26.9 11.2 %reduce-scatter.9.cloned.1.call-done = f32[32,128]{1,0:T(8,128)} async-done(((f32[128,128]{1,0:T(8,128)}), f32[32,128]{1,0:T(8,128)}) %reduce-scatter.9.cloned.1.call-update) | async-done | bytes 16400 | tf_op jit(solution)/shard_map/reduce_scatter | solution.py:30
  38.9 8.2 %all_gather.24 = bf16[128,128]{1,0:T(8,128)(2,1)S(1)} all-gather(bf16[32,128]{1,0:T(8,128)(2,1)S(1)} %multiply_convert_fusion.11), channel_id=1, replica_groups=mesh['section'=2,'dp'=4,'tensor'=4] {'tensor'}, dimensions={0}, use_global_device_ids=true | all-gather | bytes 40960 | tf_op jit(solution)/shard_map/all_gather | solution.py:34
  51.5 8.9 %all-reduce.3 = f32[128]{0:T(128)S(1)} all-reduce(f32[128]{0:T(128)S(1)} %fusion.26), channel_id=4, replica_groups=mesh['section'=2,'dp'=4,'tensor'=4] {'tensor'}, use_global_device_ids=true, to_apply=%region_4.5.clone | all-reduce | flops 128 | bytes 1024
  60.6 15.1 %reduce-scatter.11.cloned.1.call-done = f32[32,128]{1,0:T(8,128)} async-done(((f32[128,128]{1,0:T(8,128)}), f32[32,128]{1,0:T(8,128)}) %reduce-scatter.11.cloned.1.call-update) | async-done | bytes 16400 | tf_op jit(solution)/shard_map/reduce_scatter | solution.py:30
  76.5 8.1 %all_gather.25 = bf16[128,128]{1,0:T(8,128)(2,1)S(1)} all-gather(bf16[32,128]{1,0:T(8,128)(2,1)S(1)} %multiply_convert_fusion.10), channel_id=1, replica_groups=mesh['section'=2,'dp'=4,'tensor'=4] {'tensor'}, dimensions={0}, use_global_device_ids=true | all-gather | bytes 40960 | tf_op jit(solution)/shard_map/all_gather | solution.py:34
  88.5 8.9 %all-reduce.4 = f32[128]{0:T(128)S(1)} all-reduce(f32[128]{0:T(128)S(1)} %fusion.28), channel_id=6, replica_groups=mesh['section'=2,'dp'=4,'tensor'=4] {'tensor'}, use_global_device_ids=true, to_apply=%region_7.8.clone | all-reduce | flops 128 | bytes 1024
  97.6 23.1 %reduce-scatter.13.cloned.1.call-done = f32[32,128]{1,0:T(8,128)} async-done(((f32[128,128]{1,0:T(8,128)}), f32[32,128]{1,0:T(8,128)}) %reduce-scatter.13.cloned.1.call-update) | async-done | bytes 16400 | tf_op jit(solution)/shard_map/reduce_scatter | solution.py:30
  121.5 8.1 %all_gather.26 = bf16[128,128]{1,0:T(8,128)(2,1)S(1)} all-gather(bf16[32,128]{1,0:T(8,128)(2,1)S(1)} %multiply_convert_fusion.9), channel_id=1, replica_groups=mesh['section'=2,'dp'=4,'tensor'=4] {'tensor'}, dimensions={0}, use_global_device_ids=true | all-gather | bytes 40960 | tf_op jit(solution)/shard_map/all_gather | solution.py:34
  133.8 8.9 %psum.56 = f32[128]{0:T(128)S(1)} all-reduce(f32[128]{0:T(128)S(1)} %get-tuple-element.7), channel_id=1, replica_groups=mesh['section'=2,'dp'=4,'tensor'=4] {'tensor'}, use_global_device_ids=true, to_apply=%region_10.11 | all-reduce | flops 128 | bytes 1024 | tf_op jit(solution)/shard_map/psum | solution.py:45
  142.8 42.3 %all-reduce.11.cloned.1.call-done = (f32[128,128]{1,0:T(8,128)}, f32[128,128]{1,0:T(8,128)}, f32[128,128]{1,0:T(8,128)}) async-done(((f32[128,128]{1,0:T(8,128)}, f32[128,128]{1,0:T(8,128)}, f32[128,128]{1,0:T(8,128)}), (f32[128,128]{1,0:T(8,128)}, f32[128,128]{1,0:T(8,128)}, f32[128,128]{1,0:T(8,128)})) %all-reduce.11.cloned.1.call-update) | async-done | bytes 196624 | tf_op jit(solution)/shard_map/psum | solution.py:45
  188.6 23.8 %reduce-scatter.15.cloned.1.call-done = f32[32,128]{1,0:T(8,128)} async-done(((f32[128,128]{1,0:T(8,128)}), f32[32,128]{1,0:T(8,128)}) %reduce-scatter.15.cloned.1.call-update) | async-done | bytes 16400 | tf_op jit(solution)/shard_map/reduce_scatter | solution.py:79
  213.5 8.9 %all-reduce.6 = (f32[128]{0:T(128)S(1)}, f32[128]{0:T(128)S(1)}) all-reduce(f32[128]{0:T(128)S(1)} %fusion.128, f32[128]{0:T(128)S(1)} %get-tuple-element.6), channel_id=1, replica_groups=mesh['section'=2,'dp'=4,'tensor'=4] {'tensor'}, use_global_device_ids=true, to_apply=%add | all-reduce | flops 256 | bytes 2048
  222.8 8.1 %all_gather.27 = bf16[128,128]{1,0:T(8,128)(2,1)S(1)} all-gather(bf16[32,128]{1,0:T(8,128)(2,1)S(1)} %multiply_convert_fusion.8), channel_id=1, replica_groups=mesh['section'=2,'dp'=4,'tensor'=4] {'tensor'}, dimensions={0}, use_global_device_ids=true | all-gather | bytes 40960 | tf_op jit(solution)/shard_map/all_gather | solution.py:81
  236.5 23.9 %reduce-scatter.17.cloned.1.call-done = f32[32,128]{1,0:T(8,128)} async-done(((f32[128,128]{1,0:T(8,128)}), f32[32,128]{1,0:T(8,128)}) %reduce-scatter.17.cloned.1.call-update) | async-done | bytes 16400 | tf_op jit(solution)/shard_map/reduce_scatter | solution.py:79
  261.5 9.0 %all-reduce.5 = (f32[128]{0:T(128)S(1)}, f32[128]{0:T(128)S(1)}) all-reduce(f32[128]{0:T(128)S(1)} %fusion.133, f32[128]{0:T(128)} %get-tuple-element.5), channel_id=1, replica_groups=mesh['section'=2,'dp'=4,'tensor'=4] {'tensor'}, use_global_device_ids=true, to_apply=%add.1 | all-reduce | flops 256 | bytes 2048
  271.0 8.1 %all_gather.29 = bf16[128,128]{1,0:T(8,128)(2,1)S(1)} all-gather(bf16[32,128]{1,0:T(8,128)(2,1)S(1)} %multiply_convert_fusion.7), channel_id=1, replica_groups=mesh['section'=2,'dp'=4,'tensor'=4] {'tensor'}, dimensions={0}, use_global_device_ids=true | all-gather | bytes 40960 | tf_op jit(solution)/shard_map/all_gather | solution.py:81
  285.5 22.9 %reduce-scatter.19.cloned.1.call-done = f32[32,128]{1,0:T(8,128)} async-done(((f32[128,128]{1,0:T(8,128)}), f32[32,128]{1,0:T(8,128)}) %reduce-scatter.19.cloned.1.call-update) | async-done | bytes 16400 | tf_op jit(solution)/shard_map/reduce_scatter | solution.py:79
  309.2 8.1 %all_gather.31 = bf16[128,128]{1,0:T(8,128)(2,1)S(1)} all-gather(bf16[32,128]{1,0:T(8,128)(2,1)S(1)} %multiply_convert_fusion.6), channel_id=1, replica_groups=mesh['section'=2,'dp'=4,'tensor'=4] {'tensor'}, dimensions={0}, use_global_device_ids=true | all-gather | bytes 40960 | tf_op jit(solution)/shard_map/all_gather | solution.py:81
  319.3 12.4 %all-reduce.8 = (f32[]{:T(128)}, f32[1024]{0:T(1024)S(1)}) all-reduce(f32[]{:T(128)} %convert_reduce_fusion, f32[1024]{0:T(1024)S(1)} %multiply_add_fusion), channel_id=1, replica_groups=mesh['section'=2,'dp'=4,'tensor'=4] {'dp'}, use_global_device_ids=true, to_apply=%region_34.35 | all-reduce | flops 1025 | bytes 8200 | tf_op jit(solution)/shard_map/psum | solution.py:178
  333.0 1.5 multiply_bitcast_fusion
  334.6 16.5 %reduce-scatter.21.cloned.1.call-done = bf16[1024,32]{0,1:T(8,128)(2,1)} async-done(((bf16[1024,128]{0,1:T(8,128)(2,1)}), bf16[1024,32]{0,1:T(8,128)(2,1)}) %reduce-scatter.21.cloned.1.call-update) | async-done | bytes 65552 | tf_op jit(solution)/shard_map/reduce_scatter | solution.py:171
  351.1 1.5 multiply_bitcast_fusion.1
  (158 shorter events, 41.6 us)
Async XLA Ops:
  7.2 40.0 %copy-start = (bf16[1,128,1024]{2,1,0:T(8,128)(2,1)S(1)}, bf16[1,128,1024]{2,1,0:T(8,128)(2,1)}, u32[]{:S(2)}) copy-start(bf16[1,128,1024]{2,1,0:T(8,128)(2,1)} %param.9) | copy-start | bytes 786436
  7.2 2.8 copy-start.3
  7.2 30.9 %reduce-scatter.9.cloned.1.call-start = ((), (), s32[]{:S(2)}) async-start(), calls=%async_computation.8 | async-start | bytes 81920 | tf_op jit(solution)/shard_map/reduce_scatter | solution.py:30
  9.9 65.8 %reduce-scatter.11.cloned.1.call-start = ((), (), s32[]{:S(2)}) async-start(), calls=%async_computation.9 | async-start | bytes 81920 | tf_op jit(solution)/shard_map/reduce_scatter | solution.py:30
  47.4 2.4 collective-permute-start
  49.5 1.0 copy-start.1
  51.5 69.2 %reduce-scatter.13.cloned.1.call-start = ((), (), s32[]{:S(2)}) async-start(), calls=%async_computation.10 | async-start | bytes 81920 | tf_op jit(solution)/shard_map/reduce_scatter | solution.py:30
  84.9 1.4 copy-start.12
  84.9 2.4 collective-permute-start.1
  97.4 87.8 %all-reduce.11.cloned.1.call-start = ((), (), s32[]{:S(2)}) async-start(), calls=%async_computation.16 | async-start | bytes 393216 | tf_op jit(solution)/shard_map/psum | solution.py:45
  129.7 1.0 copy-start.2
  142.8 69.7 %reduce-scatter.15.cloned.1.call-start = ((), (), s32[]{:S(2)}) async-start(), calls=%async_computation.11 | async-start | bytes 81920 | tf_op jit(solution)/shard_map/reduce_scatter | solution.py:79
  185.2 1.1 copy-start.6
  187.9 34.4 %copy-start.5 = (f32[128,128]{1,0:T(8,128)S(1)}, f32[128,128]{1,0:T(8,128)}, u32[]{:S(2)}) copy-start(f32[128,128]{1,0:T(8,128)} %get-tuple-element.13) | copy-start | bytes 196612
  188.0 72.5 %reduce-scatter.17.cloned.1.call-start = ((), (), s32[]{:S(2)}) async-start(), calls=%async_computation.12 | async-start | bytes 81920 | tf_op jit(solution)/shard_map/reduce_scatter | solution.py:79
  188.6 34.1 %copy-start.7 = (f32[2,32,128]{2,1,0:T(8,128)}, f32[2,32,128]{2,1,0:T(8,128)S(1)}, u32[]{:S(2)}) copy-start(f32[2,32,128]{2,1,0:T(8,128)S(1)} %bitcast_dynamic-update-slice_fusion.7) | copy-start | bytes 98308
  231.6 3.4 collective-permute-start.2
  236.2 72.1 %reduce-scatter.19.cloned.1.call-start = ((), (), s32[]{:S(2)}) async-start(), calls=%async_computation.13 | async-start | bytes 81920 | tf_op jit(solution)/shard_map/reduce_scatter | solution.py:79
  236.5 34.0 %copy-start.4 = (f32[128,128]{1,0:T(8,128)S(1)}, f32[128,128]{1,0:T(8,128)}, u32[]{:S(2)}) copy-start(f32[128,128]{1,0:T(8,128)} %get-tuple-element.14) | copy-start | bytes 196612
  279.5 3.4 collective-permute-start.3
  284.1 48.9 %reduce-scatter.23.cloned.1.call-start = ((), (), s32[]{:S(2)}) async-start(), calls=%async_computation.15 | async-start | bytes 327680 | tf_op jit(solution)/shard_map/reduce_scatter | solution.py:174
  285.4 23.0 %copy-start.8 = (f32[2,32,128]{2,1,0:T(8,128)S(1)}, f32[2,32,128]{2,1,0:T(8,128)}, u32[]{:S(2)}) copy-start(f32[2,32,128]{2,1,0:T(8,128)} %copy-done.7) | copy-start | bytes 98308
  285.4 65.7 %reduce-scatter.21.cloned.1.call-start = ((), (), s32[]{:S(2)}) async-start(), calls=%async_computation.14 | async-start | bytes 327680 | tf_op jit(solution)/shard_map/reduce_scatter | solution.py:171
  317.6 0.8 copy-start.10
  (10 other events, 6.7 us)
Sparse Core Ops, SparseCore 0:
  11.3 26.7 reduce-scatter.8
  51.6 24.0 reduce-scatter.10
  97.5 23.1 reduce-scatter.12
  142.9 42.2 all-reduce.10
  188.3 24.0 reduce-scatter.14
  236.3 24.0 reduce-scatter.16
  284.2 24.0 reduce-scatter.18
  310.6 20.0 reduce-scatter.22
  333.0 18.0 reduce-scatter.20
where the time goes:
time: 360 us; the launch traced here: 359 us
  waiting for transfers between devices  183 us (51%)
  blocking collectives  117 us (32%)
  between operations  16.4 us (5%)
  other arithmetic  15.5 us (4%)
  matrix products  14.2 us (4%)
  local copies, waits for them, and re-layouts  7.62 us (2%)
  starting transfers between devices  5.56 us (2%)
    reduce_scatter x3, waiting for transfers between devices, layer_backward(): lax.psum_scatter(partial_back, 'tensor', scatter_dimension=0, tiled=True)  70.6 us
    reduce_scatter x3, waiting for transfers between devices, layer_forward(): lax.psum_scatter(partial_proj, 'tensor', scatter_dimension=0, tiled=True)  49.5 us
    unnamed x5, blocking collectives  47.1 us
    psum x1, waiting for transfers between devices, head_backward(): squares, logit_base = lax.psum((squares, partial_logit), 'tensor')  42.3 us
    all_gather x3, blocking collectives, layer_forward(): hidden = lax.all_gather(hidden_share, 'tensor', axis=0, tiled=True)  24.4 us
    all_gather x3, blocking collectives, layer_backward(): weighted = lax.all_gather(weighted_share, 'tensor', axis=0, tiled=True)  24.4 us
    reduce_scatter x1, waiting for transfers between devices, local(): lax.psum_scatter((down_total * pre_scale).astype(jnp.bfloat16), 'dp', sca...  16.5 us
    psum x1, blocking collectives, local(): gain_summed, count_summed = lax.psum((gain_total, local_count), 'dp')  12.4 us
  transfers between devices with their start and end apart: 13, of which 12 were waited for; matrix products, arithmetic and copies ran while one was open for 3% of the time, Pallas kernels for 0%

commit v1 on v0

v1 whole, which is shorter than its diff:
```python
import jax
import jax.numpy as jnp
from jax import lax
from jax.sharding import PartitionSpec as P

epsilon = 1e-05
F32 = jnp.float32
BF16 = jnp.bfloat16


def dot(a, b):
    return jnp.dot(a, b, preferred_element_type=F32)


def dot_nt(a, b):
    return lax.dot_general(a, b, (((1,), (1,)), ((), ())), preferred_element_type=F32)


def dot_tn(a, b):
    return lax.dot_general(a, b, (((0,), (0,)), ((), ())), preferred_element_type=F32)


def partner_pairs(axis, step):
    size = lax.axis_size(axis)
    if size & (size - 1) == 0:
        return [(i, i ^ step) for i in range(size)]
    return [(i, (i + step) % size) for i in range(size)]


def from_all(value, axis):
    return [
        lax.ppermute(value, axis, partner_pairs(axis, step))
        for step in range(1, lax.axis_size(axis))
    ]


def high_low(value):
    high = value.astype(BF16)
    return high, (value - high.astype(F32)).astype(BF16)


def chain(width, squares, proj0, proj1, cross0, cross1, base, grams, labels, valid):
    m01, b0h, b0b0, b1h, b1b1, b0b1 = grams
    inv0 = lax.rsqrt(squares / width + epsilon)
    pre0 = inv0 * proj0
    sig0 = jax.nn.sigmoid(pre0)
    hidden0 = (pre0 * sig0).astype(BF16)
    hid0 = hidden0.astype(F32)
    one_b0 = cross0 + dot(hidden0, b0b0)
    squares1 = squares + jnp.sum(hid0 * (cross0 + one_b0), axis=1, keepdims=True)
    inv1 = lax.rsqrt(squares1 / width + epsilon)
    proj1 = proj1 + dot(hidden0, m01)
    pre1 = inv1 * proj1
    sig1 = jax.nn.sigmoid(pre1)
    hidden1 = (pre1 * sig1).astype(BF16)
    hid1 = hidden1.astype(F32)
    one_b1 = cross1 + dot(hidden0, b0b1)
    two_b0 = one_b0 + dot_nt(hidden1, b0b1)
    two_b1 = one_b1 + dot(hidden1, b1b1)
    squares2 = squares1 + jnp.sum(hid1 * (one_b1 + two_b1), axis=1, keepdims=True)
    inv2 = lax.rsqrt(squares2 / width + epsilon)
    base = base + dot(hidden0, b0h) + dot(hidden1, b1h)
    logits = inv2 * base
    expo = jnp.exp(logits - jnp.max(logits, axis=1, keepdims=True))
    prob = expo / jnp.sum(expo, axis=1, keepdims=True)
    classes = lax.broadcasted_iota(jnp.int32, logits.shape, 1)
    onehot = (classes == labels).astype(F32)
    cot = (prob - onehot) * valid.astype(F32)
    factor2 = inv2**3 / width * jnp.sum(cot * base, axis=1, keepdims=True)
    weighted2 = (inv2 * cot).astype(BF16)
    grad1 = dot_nt(weighted2, b1h) - factor2 * two_b1
    act1 = grad1 * sig1 * (1.0 + pre1 * (1.0 - sig1))
    factor1 = inv1**3 / width * jnp.sum(act1 * proj1, axis=1, keepdims=True)
    weighted1 = (inv1 * act1).astype(BF16)
    grad0 = dot_nt(weighted2, b0h) - factor2 * two_b0 + dot_nt(weighted1, m01) - factor1 * one_b0
    act0 = grad0 * sig0 * (1.0 + pre0 * (1.0 - sig0))
    weighted0 = (inv0 * act0).astype(BF16)
    scaled0 = ((factor2 + factor1) * hid0).astype(BF16)
    scaled1 = (factor2 * hid1).astype(BF16)
    return hidden0, hidden1, weighted0, weighted1, weighted2, scaled0, scaled1


def local(inputs, adapter_down, adapter_up, gains, head, labels, valid):
    sections, tensors, dps = (lax.axis_size(a) for a in ("section", "tensor", "dp"))
    first = lax.axis_index("section") == 0
    features = inputs.shape[2]
    width = features * tensors
    rank = adapter_down.shape[2]
    states = inputs.reshape(-1, features)
    rows = states.shape[0]
    half = rows // sections
    offset = lax.axis_index("section") * half
    gain = gains.astype(F32)
    down_t = adapter_down[0].T
    scaled_down = (down_t.astype(F32) * gain).astype(BF16)
    up = adapter_up[0]
    swap = partner_pairs("section", 1)

    own = jnp.concatenate([scaled_down, up], axis=0)
    other = lax.ppermute(own, "section", swap)
    third = jnp.where(first, other[:rank], other[rank:])
    mine = lax.dynamic_slice_in_dim(states, offset, half, 0)
    mine32 = mine.astype(F32)
    squares = jnp.sum(mine32 * mine32, axis=1)
    both = dot_nt(states, own)
    logit = dot(mine, head)
    gram = jnp.concatenate([dot_nt(up, third), dot(up, head), dot_nt(up, up)], axis=1)
    square_parts = jnp.stack(high_low(squares), axis=1)
    packed = jnp.concatenate(
        [
            both[:, :rank],
            both[:, rank:],
            logit,
            gram[:, :rank],
            gram[:, rank : 2 * rank],
            gram[:, 2 * rank :],
        ],
        axis=0,
    ).astype(BF16)
    wide = from_all(packed, "tensor")
    small = from_all(square_parts, "tensor")
    total = packed.astype(F32) + sum(w.astype(F32) for w in wide)
    squares = squares + sum(jnp.sum(s.astype(F32), axis=1) for s in small)
    proj, cross = total[:rows], total[rows : 2 * rows]
    logit = total[2 * rows : 2 * rows + half]
    gram = total[2 * rows + half :].astype(BF16)
    away = half - offset
    sent = jnp.concatenate(
        [
            lax.dynamic_slice_in_dim(proj, away, half, 0).astype(BF16),
            lax.dynamic_slice_in_dim(cross, away, half, 0).astype(BF16),
            gram,
        ],
        axis=0,
    )
    got = lax.ppermute(sent, "section", swap)
    own_proj = lax.dynamic_slice_in_dim(proj, offset, half, 0)
    own_cross = lax.dynamic_slice_in_dim(cross, offset, half, 0)
    got_proj, got_cross = got[:half].astype(F32), got[half : 2 * half].astype(F32)
    got_gram = got[2 * half :]

    def ordered(a, b):
        return jnp.where(first, a, b), jnp.where(first, b, a)

    proj0, proj1 = ordered(own_proj, got_proj)
    cross0, cross1 = ordered(own_cross, got_cross)
    gram0, gram1 = ordered(gram, got_gram)
    m01, b0h, b0b0 = jnp.split(gram0, 3, axis=0)
    b1b0, b1h, b1b1 = jnp.split(gram1, 3, axis=0)
    label_rows = lax.dynamic_slice_in_dim(labels.reshape(-1, 1), offset, half, 0)
    valid_rows = lax.dynamic_slice_in_dim(valid.reshape(-1, 1), offset, half, 0)
    hidden0, hidden1, weighted0, weighted1, weighted2, scaled0, scaled1 = chain(
        width,
        squares[:, None],
        proj0,
        proj1,
        cross0,
        cross1,
        logit,
        (m01, b0h, b0b0, b1h, b1b1, b1b0.T),
        label_rows,
        valid_rows,
    )
    made = jnp.stack([hidden0, hidden1, weighted0, weighted1, weighted2, scaled0, scaled1])
    met = lax.ppermute(made, "section", swap)
    front, back = ordered(made, met)
    hidden0, hidden1, weighted0, weighted1, weighted2, scaled0, scaled1 = jnp.concatenate(
        [front, back], axis=1
    )
    own_hidden = jnp.where(first, hidden0, hidden1)
    own_weighted = jnp.where(first, weighted0, weighted1)
    own_scaled = jnp.where(first, scaled0, scaled1)
    up0 = jnp.where(first, up, other[rank:])
    up1 = jnp.where(first, other[rank:], up)
    zero = jnp.zeros((rank, rank), BF16)
    mix_down = jnp.where(first, zero, dot_tn(weighted1, hidden0).astype(BF16))
    down_grad = dot_tn(own_weighted, states) + dot(mix_down, up0)
    gain_grad = jnp.sum(down_grad * down_t.astype(F32), axis=0)
    mix_head = dot_tn(own_hidden, weighted2).astype(BF16)
    mix_up0 = dot_tn(own_scaled, hidden0).astype(BF16)
    mix_up1 = jnp.where(first, dot_tn(hidden0, scaled1), dot_tn(scaled1, hidden1)).astype(BF16)
    mix_down1 = jnp.where(first, dot_tn(hidden0, weighted1).astype(BF16), zero)
    up_grad = (
        dot_nt(mix_head, head)
        - dot_tn(own_scaled, states)
        - dot(mix_up0, up0)
        - dot(mix_up1, up1)
        + dot(mix_down1, other[:rank])
    )
    down_grad = down_grad * gain
    count = jnp.sum(valid.astype(F32))
    slim = rank // dps
    tail = jnp.stack([*high_low(gain_grad), *high_low(jnp.broadcast_to(count, gain_grad.shape))])
    index = lax.axis_index("dp")
    parts = jnp.concatenate(
        [down_grad.reshape(dps, slim, features), up_grad.reshape(dps, slim, features)], axis=1
    )
    summed = lax.dynamic_index_in_dim(parts, index, 0, keepdims=False)
    parts = parts.astype(BF16)
    gain_sum, count_sum = gain_grad, count
    for step in range(1, dps):
        pairs = partner_pairs("dp", step)
        target = jnp.array([t for _, t in sorted(pairs)])[index]
        part = lax.dynamic_index_in_dim(parts, target, 0, keepdims=False)
        got = lax.ppermute(jnp.concatenate([part, tail], axis=0), "dp", pairs).astype(F32)
        summed = summed + got[: 2 * slim]
        gain_sum = gain_sum + got[2 * slim] + got[2 * slim + 1]
        count_sum = count_sum + got[2 * slim + 2, 0] + got[2 * slim + 3, 0]
    scale = 1.0 / count_sum
    summed = summed * scale
    return summed[:slim].T[None], summed[slim:][None], (gain_sum * scale)[None]


def solution(mesh):
    return jax.shard_map(
        local,
        mesh=mesh,
        in_specs=(
            P(None, "dp", "tensor"),
            P("section", "tensor", None),
            P("section", None, "tensor"),
            P("section", "tensor"),
            P("tensor", None),
            P(None, "dp"),
            P(None, "dp"),
        ),
        out_specs=(
            P("section", "tensor", "dp"),
            P("section", "dp", "tensor"),
            P("section", "tensor"),
        ),
        check_vma=False,
    )
```

time: 360 us -> 69.5 us (0.19)
  waiting for transfers between devices: 183 us -> 21.6 us
  blocking collectives: 117 us -> 0 us
  other arithmetic: 15.5 us -> 4.07 us
  starting transfers between devices: 5.56 us -> 13.1 us
  matrix products: 14.2 us -> 9.68 us
    reduce_scatter x8 -> x0, waiting for transfers between devices: 137 us -> none  [the longest x3 70.6 us: layer_backward(): lax.psum_scatter(partial_back, 'tensor', scatter_dimension=0, tiled=True)]
    all_gather x6 -> x0, blocking collectives: 48.8 us -> none  [the longest x3 24.4 us: layer_forward(): hidden = lax.all_gather(hidden_share, 'tensor', axis=0, tiled=True)]
    unnamed x5 -> x0, blocking collectives: 47.1 us -> none
    psum x1 -> x0, waiting for transfers between devices: 42.3 us -> none  [head_backward(): squares, logit_base = lax.psum((squares, partial_logit), 'tensor')]
    psum x2 -> x0, blocking collectives: 21.3 us -> none  [the longest x1 12.4 us: local(): gain_summed, count_summed = lax.psum((gain_total, local_count), 'dp')]
    ppermute x4 -> x12, waiting for transfers between devices: 3.43 us -> 21.6 us  [the longest x6 11.7 us: from_all(): lax.ppermute(value, axis, partner_pairs(axis, step))]
    ppermute x4 -> x12, starting transfers between devices: 5.18 us -> 13.1 us  [the longest x6 8.18 us: from_all(): lax.ppermute(value, axis, partner_pairs(axis, step))]
    dot_general x24 -> x23, matrix products: 14.2 us -> 9.68 us  [the longest x12 5.97 us: dot(): return jnp.dot(a, b, preferred_element_type=F32)]
  transfers between devices with their start and end apart: 13 -> 12, of which waited for: 12 -> 5; matrix products, arithmetic and copies ran while one was open for 3% -> 7% of each run, Pallas kernels for 0% -> 0%
where the time goes in v1:
time: 69.5 us; the launch traced here: 69.1 us
  waiting for transfers between devices  21.6 us (31%)
  starting transfers between devices  13.1 us (19%)
  between operations  13 us (19%)
  matrix products  9.68 us (14%)
  local copies, waits for them, and re-layouts  7.62 us (11%)
  other arithmetic  4.07 us (6%)
    ppermute x6, waiting for transfers between devices, from_all(): lax.ppermute(value, axis, partner_pairs(axis, step))  11.7 us
    ppermute x3, waiting for transfers between devices, local(): lax.ppermute(jnp.concatenate([part, tail], axis=0), 'dp', pairs).astype(F32)  8.57 us
    ppermute x6, starting transfers between devices, from_all(): lax.ppermute(value, axis, partner_pairs(axis, step))  8.18 us
    dot_general x12, matrix products, dot(): return jnp.dot(a, b, preferred_element_type=F32)  5.97 us
    ppermute x3, starting transfers between devices, local(): lax.ppermute(jnp.concatenate([part, tail], axis=0), 'dp', pairs).astype(F32)  4.58 us
    unnamed x25, local copies, waits for them, and re-layouts  3.35 us
    dot_general x8, matrix products, dot_nt(): lax.dot_general(a, b, (((1,), (1,)), ((), ())), preferred_element_type=F32)  3.01 us
    dynamic_slice x3, local copies, waits for them, and re-layouts, local(): target = jnp.array([t for _, t in sorted(pairs)])[index]  1.76 us
  transfers between devices with their start and end apart: 12, of which 5 were waited for; matrix products, arithmetic and copies ran while one was open for 7% of the time, Pallas kernels for 0%

profile of v1, /device:TPU:0, one launch (start us, length us, event | category | flops | bytes accessed | tf_op | source)
XLA Modules:
  0.0 69.1 jit_solution(8801101898481379107)
XLA Ops:
  0.7 1.1 %multiply_reduce_fusion = f32[128]{0:T(128)S(1)} fusion(bf16[256,1024]{1,0:T(8,128)(2,1)} %bitcast.175, s32[]{:T(128)S(6)} %select_n.130), kind=kLoop, calls=%fused_computation.65 | loop fusion | flops 393088 | bytes 262660 | tf_op jit(solution)/shard_map/reduce_sum | solution.py:104
  1.8 4.0 %collective-permute-start.2 = (bf16[128,2]{0,1:T(2,128)(2,1)S(1)}, bf16[128,2]{0,1:T(2,128)(2,1)S(1)}, u32[]{:S(2)}, u32[]{:S(2)}) collective-permute-start(bf16[128,2]{0,1:T(2,128)(2,1)S(1)} %pad_maximum_fusion.4), channel_id=1, source_target_pairs={{0,3},{1,2},{2,1},{3,0},{4,7},{5,6},{6,5},{7,4},{8,11},{9,10},{10,... | collective-permute-start | bytes 1544 | tf_op jit(solution)/shard_map/ppermute | solution.py:32
  6.7 0.9 %copy-done.1 = bf16[1,128,1024]{2,1,0:T(8,128)(2,1)S(1)} copy-done((bf16[1,128,1024]{2,1,0:T(8,128)(2,1)S(1)}, bf16[1,128,1024]{2,1,0:T(8,128)(2,1)}, u32[]{:S(2)}) %copy-start.1) | copy-done | bytes 262168
  7.7 0.9 %copy-done.2 = bf16[2,128,1024]{2,1,0:T(8,128)(2,1)S(1)} copy-done((bf16[2,128,1024]{2,1,0:T(8,128)(2,1)S(1)}, bf16[2,128,1024]{2,1,0:T(8,128)(2,1)}, u32[]{:S(2)}) %copy-start.2) | copy-done | bytes 524312
  9.0 0.6 copy-done.7
  10.7 1.9 %collective-permute-start.4 = (bf16[1024,128]{1,0:T(8,128)(2,1)S(1)}, bf16[1024,128]{1,0:T(8,128)(2,1)S(1)}, u32[]{:S(2)}, u32[]{:S(2)}) collective-permute-start(bf16[1024,128]{1,0:T(8,128)(2,1)S(1)} %fusion.13), channel_id=1, source_target_pairs={{0,1},{1,0},{2,3},{3,2},{4,5},{5,4},{6,7},{7,6},{8,9},{9,8},{10,11... | collective-permute-start | bytes 786440 | tf_op jit(solution)/shard_map/ppermute | solution.py:32
  12.7 1.5 %collective-permute-start.5 = (bf16[1024,128]{1,0:T(8,128)(2,1)S(1)}, bf16[1024,128]{1,0:T(8,128)(2,1)S(1)}, u32[]{:S(2)}, u32[]{:S(2)}) collective-permute-start(bf16[1024,128]{1,0:T(8,128)(2,1)S(1)} %fusion.13), channel_id=1, source_target_pairs={{0,2},{1,3},{2,0},{3,1},{4,6},{5,7},{6,4},{7,5},{8,10},{9,11},{10,... | collective-permute-start | bytes 786440 | tf_op jit(solution)/shard_map/ppermute | solution.py:32
  14.4 5.6 %collective-permute-done.4 = bf16[1024,128]{1,0:T(8,128)(2,1)S(1)} collective-permute-done((bf16[1024,128]{1,0:T(8,128)(2,1)S(1)}, bf16[1024,128]{1,0:T(8,128)(2,1)S(1)}, u32[]{:S(2)}, u32[]{:S(2)}) %collective-permute-start.4) | collective-permute-done | bytes 262176 | tf_op jit(solution)/shard_map/ppermute | solution.py:32
  20.0 6.0 %collective-permute-done.5 = bf16[1024,128]{1,0:T(8,128)(2,1)S(1)} collective-permute-done((bf16[1024,128]{1,0:T(8,128)(2,1)S(1)}, bf16[1024,128]{1,0:T(8,128)(2,1)S(1)}, u32[]{:S(2)}, u32[]{:S(2)}) %collective-permute-start.5) | collective-permute-done | bytes 262176 | tf_op jit(solution)/shard_map/ppermute | solution.py:32
  26.3 1.4 %collective-permute-done.7 = bf16[640,128]{1,0:T(8,128)(2,1)S(1)} collective-permute-done((bf16[640,128]{1,0:T(8,128)(2,1)S(1)}, bf16[640,128]{1,0:T(8,128)(2,1)S(1)}, u32[]{:S(2)}, u32[]{:S(2)}) %collective-permute-start.7) | collective-permute-done | bytes 163872 | tf_op jit(solution)/shard_map/ppermute | solution.py:136
  31.2 0.7 copy-done.10
  33.8 0.6 dynamic_slice.54
  35.7 0.6 dynamic_slice.56
  37.6 0.7 convert_reduce_fusion
  42.8 1.2 %convolution_subtract_fusion.1 = f32[128,1024]{1,0:T(8,128)} fusion(f32[128,1024]{1,0:T(8,128)S(1)} %fusion.67, bf16[1024,128]{1,0:T(8,128)(2,1)S(1)} %copy-done, bf16[1,256,128]{2,1,0:T(8,128)(2,1)S(1)} %get-tuple-element.21, bf16[7,128,128]{2,1,0:T(8,128)(2,1)S(1)} %get-tuple-element.23, bf16[7,128,128]{2,1,0:T(8,128)(2,1)S(1)} %get-tuple-element.22, ...), kind=kOutput, calls=%fused_computation.4 | convolution fusion | flops 42385408 | bytes 2293761 | tf_op jit(solution)/shard_map/dot_general | solution.py:16
  44.0 1.2 %fusion.18 = f32[128,1024]{1,0:T(8,128)} fusion(bf16[256,1024]{1,0:T(8,128)(2,1)S(1)} %collective-permute-done.3, bf16[1,256,128]{2,1,0:T(8,128)(2,1)S(1)} %get-tuple-element.21, pred[]{:T(512)S(6)} %eq.13, bf16[7,128,128]{2,1,0:T(8,128)(2,1)S(1)} %get-tuple-element.23, bf16[7,128,128]{2,1,0:T(8,128)(2,1)S(1)} %get-tuple-element.22), kind=kOutput, calls=%fused_computation.39 | convolution fusion | flops 42106880 | bytes 1310721 | tf_op jit(solution)/shard_map/dot_general | solution.py:12
  45.2 1.2 %fusion.19 = f32[128,1024]{1,0:T(8,128)} fusion(bf16[128,128]{1,0:T(8,128)(2,1)S(1)} %fusion.60, pred[]{:T(512)S(6)} %eq.13, bf16[256,1024]{1,0:T(8,128)(2,1)S(1)} %collective-permute-done.3, bf16[1,256,128]{2,1,0:T(8,128)(2,1)S(1)} %get-tuple-element.20, bf16[1,256,128]{2,1,0:T(8,128)(2,1)S(1)} %get-tuple-element.21, bf16[1,128,1024]{2,1,0:T(8,128)(2,1)S(1)} %copy-done.1), kind=kOutput, calls=%fused_computation.40 | convolution fusion | flops 42090496 | bytes 1213440 | tf_op jit(solution)/shard_map/dot_general | solution.py:12
  46.3 1.6 %fusion.1 = f32[128,1024]{1,0:T(8,128)S(1)} fusion(f32[128,1024]{1,0:T(8,128)} %fusion.18, f32[128,1024]{1,0:T(8,128)} %fusion.19, f32[128,1024]{1,0:T(8,128)S(1)} %copy-done.3, pred[]{:T(512)S(6)} %eq.13, bf16[256,1024]{1,0:T(8,128)(2,1)S(1)} %collective-permute-done.3, bf16[1,256,128]{2,1,0:T(8,128)(2,1)S(1)} %get-tuple-element.21, ...), kind=kOutput, calls=%fused_computation.7 | convolution fusion | flops 42647552 | bytes 3212288 | tf_op jit(solution)/shard_map/dot_general | solution.py:12
  48.1 1.6 %collective-permute-start.9 = (bf16[68,1024]{1,0:T(8,128)(2,1)S(1)}, bf16[68,1024]{1,0:T(8,128)(2,1)S(1)}, u32[]{:S(2)}, u32[]{:S(2)}) collective-permute-start(bf16[68,1024]{1,0:T(8,128)(2,1)S(1)} %concatenate.33), channel_id=1, source_target_pairs={{0,4},{4,0},{8,12},{12,8},{1,5},{5,1},{9,13},{13,9},{2,6},{6,2},{1... | collective-permute-start | bytes 417800 | tf_op jit(solution)/shard_map/ppermute | solution.py:205
  49.8 2.7 %collective-permute-start.10 = (bf16[68,1024]{1,0:T(8,128)(2,1)S(1)}, bf16[68,1024]{1,0:T(8,128)(2,1)S(1)}, u32[]{:S(2)}, u32[]{:S(2)}) collective-permute-start(bf16[68,1024]{1,0:T(8,128)(2,1)S(1)} %concatenate.34), channel_id=1, source_target_pairs={{0,8},{4,12},{8,0},{12,4},{1,9},{5,13},{9,1},{13,5},{2,10},{6,14},... | collective-permute-start | bytes 417800 | tf_op jit(solution)/shard_map/ppermute | solution.py:205
  52.8 4.0 %collective-permute-done.9 = bf16[68,1024]{1,0:T(8,128)(2,1)S(1)} collective-permute-done((bf16[68,1024]{1,0:T(8,128)(2,1)S(1)}, bf16[68,1024]{1,0:T(8,128)(2,1)S(1)}, u32[]{:S(2)}, u32[]{:S(2)}) %collective-permute-start.9) | collective-permute-done | bytes 139296 | tf_op jit(solution)/shard_map/ppermute | solution.py:205
  59.3 4.5 %collective-permute-done.10 = bf16[68,1024]{1,0:T(8,128)(2,1)S(1)} collective-permute-done((bf16[68,1024]{1,0:T(8,128)(2,1)S(1)}, bf16[68,1024]{1,0:T(8,128)(2,1)S(1)}, u32[]{:S(2)}, u32[]{:S(2)}) %collective-permute-start.10) | collective-permute-done | bytes 139296 | tf_op jit(solution)/shard_map/ppermute | solution.py:205
  67.6 0.6 fusion.125
  68.3 0.7 %slice_bitcast_fusion = (f32[1,32,1024]{2,1,0:T(8,128)}, f32[1,1024,32]{1,2,0:T(8,128)}) fusion(f32[64,1024]{1,0:T(8,128)S(1)} %fusion.34), kind=kLoop, calls=%fused_computation.87 | loop fusion | bytes 524288 | tf_op jit(solution)/shard_map/broadcast_in_dim | solution.py:211
  (101 shorter events, 10.2 us)
Async XLA Ops:
  0.6 9.1 %copy-start = (bf16[1024,128]{1,0:T(8,128)(2,1)S(1)}, bf16[1024,128]{1,0:T(8,128)(2,1)}, u32[]{:S(2)}) copy-start(bf16[1024,128]{1,0:T(8,128)(2,1)} %param.14) | copy-start | bytes 786436
  0.6 5.8 %copy-start.4 = (bf16[1,1024,128]{2,1,0:T(8,128)(2,1)S(1)}, bf16[1,1024,128]{2,1,0:T(8,128)(2,1)}, u32[]{:S(2)}) copy-start(bf16[1,1024,128]{2,1,0:T(8,128)(2,1)} %param.11) | copy-start | bytes 786436
  1.8 4.8 %copy-start.5 = (bf16[1,1024]{1,0:T(2,128)(2,1)S(1)}, bf16[1,1024]{1,0:T(2,128)(2,1)}, u32[]{:S(2)}) copy-start(bf16[1,1024]{1,0:T(2,128)(2,1)} %param.13) | copy-start | bytes 6148
  1.8 12.4 %collective-permute-start.2 = (bf16[128,2]{0,1:T(2,128)(2,1)S(1)}, bf16[128,2]{0,1:T(2,128)(2,1)S(1)}, u32[]{:S(2)}, u32[]{:S(2)}) collective-permute-start(bf16[128,2]{0,1:T(2,128)(2,1)S(1)} %pad_maximum_fusion.4), channel_id=1, source_target_pairs={{0,3},{1,2},{2,1},{3,0},{4,7},{5,6},{6,5},{7,4},{8,11},{9,10},{10,... | collective-permute-start | bytes 1544 | tf_op jit(solution)/shard_map/ppermute | solution.py:32
  5.8 8.5 %collective-permute-start.1 = (bf16[128,2]{0,1:T(2,128)(2,1)S(1)}, bf16[128,2]{0,1:T(2,128)(2,1)S(1)}, u32[]{:S(2)}, u32[]{:S(2)}) collective-permute-start(bf16[128,2]{0,1:T(2,128)(2,1)S(1)} %pad_maximum_fusion.4), channel_id=1, source_target_pairs={{0,2},{1,3},{2,0},{3,1},{4,6},{5,7},{6,4},{7,5},{8,10},{9,11},{10,... | collective-permute-start | bytes 1544 | tf_op jit(solution)/shard_map/ppermute | solution.py:32
  6.3 8.0 %collective-permute-start = (bf16[128,2]{0,1:T(2,128)(2,1)S(1)}, bf16[128,2]{0,1:T(2,128)(2,1)S(1)}, u32[]{:S(2)}, u32[]{:S(2)}) collective-permute-start(bf16[128,2]{0,1:T(2,128)(2,1)S(1)} %pad_maximum_fusion.4), channel_id=1, source_target_pairs={{0,1},{1,0},{2,3},{3,2},{4,5},{5,4},{6,7},{7,6},{8,9},{9,8},{10,11... | collective-permute-start | bytes 1544 | tf_op jit(solution)/shard_map/ppermute | solution.py:32
  6.7 1.0 %copy-start.1 = (bf16[1,128,1024]{2,1,0:T(8,128)(2,1)S(1)}, bf16[1,128,1024]{2,1,0:T(8,128)(2,1)}, u32[]{:S(2)}) copy-start(bf16[1,128,1024]{2,1,0:T(8,128)(2,1)} %param.12) | copy-start | bytes 786436
  7.6 1.0 %copy-start.2 = (bf16[2,128,1024]{2,1,0:T(8,128)(2,1)S(1)}, bf16[2,128,1024]{2,1,0:T(8,128)(2,1)}, u32[]{:S(2)}) copy-start(bf16[2,128,1024]{2,1,0:T(8,128)(2,1)} %param.10) | copy-start | bytes 1572868
  7.6 2.3 %collective-permute-start.3 = (bf16[256,1024]{1,0:T(8,128)(2,1)S(1)}, bf16[256,1024]{1,0:T(8,128)(2,1)S(1)}, u32[]{:S(2)}, u32[]{:S(2)}) collective-permute-start(bf16[256,1024]{1,0:T(8,128)(2,1)S(1)} %pad_maximum_fusion.1), channel_id=1, source_target_pairs={{0,16},{16,0},{1,17},{17,1},{2,18},{18,2},{3,19},{19,3},{4,20},{20... | collective-permute-start | bytes 1572872 | tf_op jit(solution)/shard_map/ppermute | solution.py:100
  9.0 0.7 copy-start.7
  9.0 0.7 copy-start.6
  10.7 9.2 %collective-permute-start.4 = (bf16[1024,128]{1,0:T(8,128)(2,1)S(1)}, bf16[1024,128]{1,0:T(8,128)(2,1)S(1)}, u32[]{:S(2)}, u32[]{:S(2)}) collective-permute-start(bf16[1024,128]{1,0:T(8,128)(2,1)S(1)} %fusion.13), channel_id=1, source_target_pairs={{0,1},{1,0},{2,3},{3,2},{4,5},{5,4},{6,7},{7,6},{8,9},{9,8},{10,11... | collective-permute-start | bytes 786440 | tf_op jit(solution)/shard_map/ppermute | solution.py:32
  12.7 13.3 %collective-permute-start.5 = (bf16[1024,128]{1,0:T(8,128)(2,1)S(1)}, bf16[1024,128]{1,0:T(8,128)(2,1)S(1)}, u32[]{:S(2)}, u32[]{:S(2)}) collective-permute-start(bf16[1024,128]{1,0:T(8,128)(2,1)S(1)} %fusion.13), channel_id=1, source_target_pairs={{0,2},{1,3},{2,0},{3,1},{4,6},{5,7},{6,4},{7,5},{8,10},{9,11},{10,... | collective-permute-start | bytes 786440 | tf_op jit(solution)/shard_map/ppermute | solution.py:32
  14.2 11.8 %collective-permute-start.6 = (bf16[1024,128]{1,0:T(8,128)(2,1)S(1)}, bf16[1024,128]{1,0:T(8,128)(2,1)S(1)}, u32[]{:S(2)}, u32[]{:S(2)}) collective-permute-start(bf16[1024,128]{1,0:T(8,128)(2,1)S(1)} %fusion.13), channel_id=1, source_target_pairs={{0,3},{1,2},{2,1},{3,0},{4,7},{5,6},{6,5},{7,4},{8,11},{9,10},{10,... | collective-permute-start | bytes 786440 | tf_op jit(solution)/shard_map/ppermute | solution.py:32
  26.2 1.5 %collective-permute-start.7 = (bf16[640,128]{1,0:T(8,128)(2,1)S(1)}, bf16[640,128]{1,0:T(8,128)(2,1)S(1)}, u32[]{:S(2)}, u32[]{:S(2)}) collective-permute-start(bf16[640,128]{1,0:T(8,128)(2,1)S(1)} %pad_maximum_fusion.2), channel_id=1, source_target_pairs={{0,16},{16,0},{1,17},{17,1},{2,18},{18,2},{3,19},{19,3},{4,20},{20... | collective-permute-start | bytes 491528 | tf_op jit(solution)/shard_map/ppermute | solution.py:136
  31.0 10.6 %collective-permute-start.8 = (bf16[7,128,128]{2,1,0:T(8,128)(2,1)S(1)}, bf16[7,128,128]{2,1,0:T(8,128)(2,1)S(1)}, u32[]{:S(2)}, u32[]{:S(2)}) collective-permute-start(bf16[7,128,128]{2,1,0:T(8,128)(2,1)S(1)} %fusion.96), channel_id=1, source_target_pairs={{0,16},{16,0},{1,17},{17,1},{2,18},{18,2},{3,19},{19,3},{4,20},{20... | collective-permute-start | bytes 688136 | tf_op jit(solution)/shard_map/ppermute | solution.py:165
  31.2 0.7 copy-start.10
  33.1 0.7 copy-start.9
  35.0 0.7 copy-start.8
  45.2 1.2 %copy-start.3 = (f32[128,1024]{1,0:T(8,128)S(1)}, f32[128,1024]{1,0:T(8,128)}, u32[]{:S(2)}) copy-start(f32[128,1024]{1,0:T(8,128)} %convolution_subtract_fusion.1) | copy-start | bytes 1572868
  48.1 8.7 %collective-permute-start.9 = (bf16[68,1024]{1,0:T(8,128)(2,1)S(1)}, bf16[68,1024]{1,0:T(8,128)(2,1)S(1)}, u32[]{:S(2)}, u32[]{:S(2)}) collective-permute-start(bf16[68,1024]{1,0:T(8,128)(2,1)S(1)} %concatenate.33), channel_id=1, source_target_pairs={{0,4},{4,0},{8,12},{12,8},{1,5},{5,1},{9,13},{13,9},{2,6},{6,2},{1... | collective-permute-start | bytes 417800 | tf_op jit(solution)/shard_map/ppermute | solution.py:205
  49.8 14.0 %collective-permute-start.10 = (bf16[68,1024]{1,0:T(8,128)(2,1)S(1)}, bf16[68,1024]{1,0:T(8,128)(2,1)S(1)}, u32[]{:S(2)}, u32[]{:S(2)}) collective-permute-start(bf16[68,1024]{1,0:T(8,128)(2,1)S(1)} %concatenate.34), channel_id=1, source_target_pairs={{0,8},{4,12},{8,0},{12,4},{1,9},{5,13},{9,1},{13,5},{2,10},{6,14},... | collective-permute-start | bytes 417800 | tf_op jit(solution)/shard_map/ppermute | solution.py:205
  52.5 13.2 %collective-permute-start.11 = (bf16[68,1024]{1,0:T(8,128)(2,1)S(1)}, bf16[68,1024]{1,0:T(8,128)(2,1)S(1)}, u32[]{:S(2)}, u32[]{:S(2)}) collective-permute-start(bf16[68,1024]{1,0:T(8,128)(2,1)S(1)} %concatenate.35), channel_id=1, source_target_pairs={{0,12},{4,8},{8,4},{12,0},{1,13},{5,9},{9,5},{13,1},{2,14},{6,10},... | collective-permute-start | bytes 417800 | tf_op jit(solution)/shard_map/ppermute | solution.py:205

commit v2 on v1

v2 whole, which is shorter than its diff:
```python
import functools

import jax
import jax.numpy as jnp
from jax import lax
from jax.experimental import pallas as pl
from jax.experimental.pallas import tpu as pltpu
from jax.sharding import PartitionSpec as P

epsilon = 1e-05
F32 = jnp.float32
BF16 = jnp.bfloat16
PACK = 16


def dot(a, b):
    return jnp.dot(a, b, preferred_element_type=F32)


def dot_nt(a, b):
    return lax.dot_general(a, b, (((1,), (1,)), ((), ())), preferred_element_type=F32)


def dot_tn(a, b):
    return lax.dot_general(a, b, (((0,), (0,)), ((), ())), preferred_element_type=F32)


def rows_of(start, count):
    return pl.ds(pl.multiple_of(start, count), count)


def transposed(value):
    return value.astype(F32).T.astype(value.dtype)


def partner(index, step, size):
    if size & (size - 1) == 0:
        return index ^ step
    return (index + step) % size


def from_partner(value, axis, step):
    size = lax.axis_size(axis)
    return lax.ppermute(value, axis, [(i, partner(i, step, size)) for i in range(size)])


def high_low(value):
    high = value.astype(BF16).astype(F32)
    return jnp.concatenate([high, value - high], axis=0).astype(BF16)


def call(kernel, out, flops, *args):
    moved = sum(a.size * a.dtype.itemsize for a in args)
    return pl.pallas_call(
        kernel,
        out_shape=out,
        cost_estimate=pl.CostEstimate(flops=flops, bytes_accessed=moved, transcendentals=0),
        compiler_params=pltpu.CompilerParams(vmem_limit_bytes=24 * 2**20),
    )(*args)


def project_kernel(x_ref, down_ref, up_ref, gain_ref, down2_ref, up2_ref, gain2_ref, head_ref, out_ref):
    half, rank = x_ref.shape[0], down_ref.shape[1]
    me = lax.axis_index("section")
    it = 1 - me
    x, up, up2, head = x_ref[...], up_ref[...], up2_ref[...], head_ref[...]
    x32 = x.astype(F32)
    gain, gain2 = gain_ref[...].astype(F32), gain2_ref[...].astype(F32)
    out_ref[rows_of(me * half, half), :] = dot((x32 * gain).astype(BF16), down_ref[...]).astype(BF16)
    out_ref[rows_of(it * half, half), :] = dot((x32 * gain2).astype(BF16), down2_ref[...]).astype(BF16)
    out_ref[rows_of((2 + me) * half, half), :] = dot_nt(x, up).astype(BF16)
    out_ref[rows_of((2 + it) * half, half), :] = dot_nt(x, up2).astype(BF16)
    out_ref[4 * half : 5 * half, :] = dot(x, head).astype(BF16)
    base = 5 * half

    @pl.when(me == 0)
    def _():
        scaled = (up.astype(F32) * gain2).astype(BF16)
        out_ref[base : base + rank, :] = dot(scaled, down2_ref[...]).astype(BF16)

    @pl.when(me != 0)
    def _():
        out_ref[base : base + rank, :] = dot_nt(up, up2).astype(BF16)

    out_ref[base + rank : base + 2 * rank, :] = dot(up, head).astype(BF16)
    out_ref[base + 2 * rank : base + 3 * rank, :] = dot_nt(up, up).astype(BF16)
    squares = jnp.sum(x32 * x32, axis=1, keepdims=True)
    squares = jnp.broadcast_to(squares, (half, rank)).T
    out_ref[base + 3 * rank :, :] = high_low(squares[: PACK // 2])


def prepare_kernel(down_ref, head_ref, down2_ref, up2_ref, gain2_ref, down_t_ref, head_t_ref, mixed_ref):
    down_t_ref[...] = transposed(down_ref[...])
    head_t_ref[...] = transposed(head_ref[...])
    me = lax.axis_index("section")

    @pl.when(me == 0)
    def _():
        mixed_ref[...] = (down2_ref[...].astype(F32).T * gain2_ref[...].astype(F32)).astype(BF16)

    @pl.when(me != 0)
    def _():
        mixed_ref[...] = up2_ref[...]


def chain_kernel(width, count, *refs):
    parts, (gram_ref, gram2_ref, label_ref, valid_ref, mine_ref, theirs_ref) = refs[:count], refs[count:]
    rank = gram_ref.shape[1]
    half = label_ref.shape[1]
    me = lax.axis_index("section")
    first = me == 0

    def total(start, size):
        return sum(r[start : start + size, :].astype(F32) for r in parts)

    def spread(row):
        return jnp.broadcast_to(row, (rank, half)).T

    gram, gram2 = gram_ref[...], gram2_ref[...]
    gram0, gram1 = jnp.where(first, gram, gram2), jnp.where(first, gram2, gram)
    m01, b0h, b0b0 = (gram0[i * rank : (i + 1) * rank] for i in range(3))
    b1b0, b1h, b1b1 = (gram1[i * rank : (i + 1) * rank] for i in range(3))
    tail = total(5 * half + 3 * rank, PACK)
    squares0 = spread(tail[:1] + tail[PACK // 2 : PACK // 2 + 1])
    inv0 = lax.rsqrt(squares0 / width + epsilon)
    proj0 = total(0, half)
    pre0 = inv0 * proj0
    sig0 = jax.nn.sigmoid(pre0)
    hidden0 = (pre0 * sig0).astype(BF16)
    hid0 = hidden0.astype(F32)
    proj1 = total(half, half) + dot(hidden0, m01)
    cross0 = total(2 * half, half)
    one_b0 = cross0 + dot(hidden0, b0b0)
    squares1 = squares0 + jnp.sum(hid0 * (cross0 + one_b0), axis=1, keepdims=True)
    inv1 = lax.rsqrt(squares1 / width + epsilon)
    pre1 = inv1 * proj1
    sig1 = jax.nn.sigmoid(pre1)
    hidden1 = (pre1 * sig1).astype(BF16)
    hid1 = hidden1.astype(F32)
    one_b1 = total(3 * half, half) + dot_nt(hidden0, b1b0)
    two_b0 = one_b0 + dot(hidden1, b1b0)
    two_b1 = one_b1 + dot(hidden1, b1b1)
    squares2 = squares1 + jnp.sum(hid1 * (one_b1 + two_b1), axis=1, keepdims=True)
    inv2 = lax.rsqrt(squares2 / width + epsilon)
    base = total(4 * half, half) + dot(hidden0, b0h) + dot(hidden1, b1h)
    logits = inv2 * base
    expo = jnp.exp(logits - jnp.max(logits, axis=1, keepdims=True))
    prob = expo / jnp.sum(expo, axis=1, keepdims=True)
    labels = spread(label_ref[pl.ds(me, 1), :].astype(F32))
    valid = spread(valid_ref[pl.ds(me, 1), :].astype(F32))
    classes = lax.broadcasted_iota(jnp.int32, logits.shape, 1).astype(F32)
    cot = (prob - (classes == labels).astype(F32)) * valid
    factor2 = inv2 * inv2 * inv2 / width * jnp.sum(cot * base, axis=1, keepdims=True)
    weighted2 = (inv2 * cot).astype(BF16)
    grad1 = dot_nt(weighted2, b1h) - factor2 * two_b1
    act1 = grad1 * sig1 * (1.0 + pre1 * (1.0 - sig1))
    factor1 = inv1 * inv1 * inv1 / width * jnp.sum(act1 * proj1, axis=1, keepdims=True)
    weighted1 = (inv1 * act1).astype(BF16)
    grad0 = dot_nt(weighted2, b0h) - factor2 * two_b0 + dot_nt(weighted1, m01) - factor1 * one_b0
    act0 = grad0 * sig0 * (1.0 + pre0 * (1.0 - sig0))
    weighted0 = (inv0 * act0).astype(BF16)
    scaled0 = ((factor2 + factor1) * hid0).astype(BF16)
    scaled1 = (factor2 * hid1).astype(BF16)
    front = (hidden0, weighted2, scaled0, weighted0, weighted1, scaled1)
    back = (hidden1, weighted2, scaled1, weighted1, hidden0, hidden0)
    for slot, (a, b) in enumerate(zip(front, back)):
        mine_ref[slot * half : (slot + 1) * half, :] = jnp.where(first, a, b)
        theirs_ref[slot * half : (slot + 1) * half, :] = jnp.where(first, b, a)


def mix_kernel(replicas, mine_ref, theirs_ref, *refs):
    out_refs, tall_ref, mix_ref = refs[:replicas], refs[replicas], refs[replicas + 1]
    rank = mine_ref.shape[1]
    half = mine_ref.shape[0] // 6
    slim = rank // replicas
    first = lax.axis_index("section") == 0
    mine, theirs = mine_ref[...], theirs_ref[...]
    front, back = jnp.where(first, mine, theirs), jnp.where(first, theirs, mine)
    hidden, last, scaled, weighted, extra1, extra2 = (
        [v[i * half : (i + 1) * half] for v in (front, back)] for i in range(6)
    )
    hidden_t, scaled_t, weighted_t = ([transposed(v) for v in s] for s in (hidden, scaled, weighted))

    def product(left, right):
        return sum(dot(a, b) for a, b in zip(left, right))

    left_oth = [jnp.where(first, a, b) for a, b in zip(hidden_t, scaled_t)]
    left_mix = [jnp.where(first, a, b) for a, b in zip(hidden_t, weighted_t)]
    mix = product(left_mix, extra1).astype(BF16)
    for slot, value in enumerate(
        (
            product(hidden_t, last).astype(BF16),
            (-product(scaled_t, hidden)).astype(BF16),
            (-product(left_oth, extra2)).astype(BF16),
            mix,
            weighted_t[0],
            weighted_t[1],
            scaled_t[0],
            scaled_t[1],
        )
    ):
        tall_ref[slot * rank : (slot + 1) * rank, :] = value
    mix_ref[:rank, :] = mix
    mix_ref[rank : 2 * rank, :] = weighted_t[0]
    mix_ref[2 * rank :, :] = weighted_t[1]
    me = lax.axis_index("dp")
    for step, out_ref in enumerate(out_refs):
        target = partner(me, step, replicas)
        for slot in range(8):
            out_ref[slot * slim : (slot + 1) * slim, :] = tall_ref[rows_of(slot * rank + target * slim, slim), :]


def gain_kernel(x_ref, mix_ref, part_ref, mixed_ref, down_t_ref, valid_ref, acc_ref, tail_ref):
    features = x_ref.shape[1]
    rank = mix_ref.shape[1]
    half = x_ref.shape[0] // 2
    slim = part_ref.shape[0] // 8
    first = lax.axis_index("section") == 0
    x0, x1 = x_ref[:half, :], x_ref[half:, :]
    mix = jnp.where(first, jnp.zeros((rank, rank), BF16), mix_ref[:rank, :])
    grad = dot(mix_ref[rank : 2 * rank, :], x0) + dot(mix_ref[2 * rank :, :], x1) + dot(mix, mixed_ref[...])
    gain = jnp.sum(grad * down_t_ref[...].astype(F32), axis=0, keepdims=True)
    gain = jnp.concatenate(
        [gain[:, i * rank : (i + 1) * rank] for i in range(features // rank)], axis=0
    )
    count = jnp.sum(valid_ref[...].astype(F32), keepdims=True)
    count = jnp.broadcast_to(count, (PACK // 2, rank))
    tail_ref[...] = jnp.concatenate([high_low(gain), high_low(count)], axis=0)
    accumulate(x0, x1, part_ref, slim, acc_ref)


def accumulate(x0, x1, part_ref, slim, acc_ref, before=None):
    for slot in (0, 1):
        start = (4 + 2 * slot) * slim
        value = dot(part_ref[start : start + slim, :], x0)
        value = value + dot(part_ref[start + slim : start + 2 * slim, :], x1)
        if before is not None:
            value = value + before[slot * slim : (slot + 1) * slim, :]
        acc_ref[slot * slim : (slot + 1) * slim, :] = value


def add_kernel(part_ref, own_ref, far_ref, before_ref, acc_ref):
    first = lax.axis_index("section") == 0
    own, far = own_ref[...], far_ref[...]
    x0, x1 = jnp.where(first, own, far), jnp.where(first, far, own)
    accumulate(x0, x1, part_ref, part_ref.shape[0] // 8, acc_ref, before_ref)


def last_kernel(replicas, *refs):
    parts, refs = refs[:replicas], refs[replicas:]
    tails, refs = refs[:replicas], refs[replicas:]
    acc_ref, head_t_ref, up_ref, up2_ref, mixed_ref, gain_ref, down_out, up_out, gain_out = refs
    slim = parts[0].shape[0] // 8
    rank = parts[0].shape[1]
    first = lax.axis_index("section") == 0
    tail = sum(t[...].astype(F32) for t in tails)
    lines = tail.shape[0] - PACK
    scale = 1.0 / (tail[lines : lines + 1, :1] + tail[lines + PACK // 2 : lines + PACK // 2 + 1, :1])
    gain = (tail[: lines // 2] + tail[lines // 2 : lines]) * scale
    for i in range(lines // 2):
        gain_out[:, i * rank : (i + 1) * rank] = gain[i : i + 1, :]
    head_mix, own_mix, oth_mix, mix = (
        sum(p[slot * slim : (slot + 1) * slim, :].astype(F32) for p in parts).astype(BF16) for slot in range(4)
    )
    mixed = dot(mix, mixed_ref[...])
    none = jnp.zeros_like(mixed)
    down = acc_ref[:slim, :] + jnp.where(first, none, mixed)
    down_out[...] = (down * gain_ref[...].astype(F32) * scale).T
    up = dot(head_mix, head_t_ref[...]) + dot(own_mix, up_ref[...]) + dot(oth_mix, up2_ref[...])
    up_out[...] = (up + jnp.where(first, mixed, none) - acc_ref[slim:, :]) * scale


def local(inputs, adapter_down, adapter_up, gains, head, labels, valid):
    sections, tensors, replicas = (lax.axis_size(a) for a in ("section", "tensor", "dp"))
    me = lax.axis_index("section")
    features = inputs.shape[2]
    width = features * tensors
    rank = adapter_down.shape[2]
    states = inputs.reshape(-1, features)
    half = states.shape[0] // sections
    assert sections == 2 and half == rank and head.shape[1] == rank and features % rank == 0
    slim = rank // replicas
    lines = features // rank
    down, up = adapter_down[0], adapter_up[0]
    labels, valid = labels.reshape(sections, half), valid.reshape(sections, half)
    shape = jax.ShapeDtypeStruct

    down2, up2, gains2 = (from_partner(v, "section", 1) for v in (down, up, gains))
    mine = lax.dynamic_slice_in_dim(states, me * half, half, 0)
    small = 2 * rank * rank * features
    packed = call(
        project_kernel,
        shape((5 * half + 3 * rank + PACK, rank), BF16),
        8 * small,
        mine, down, up, gains, down2, up2, gains2, head,
    )
    wide = [packed] + [from_partner(packed, "tensor", step) for step in range(1, tensors)]
    far = [from_partner(mine, "dp", step) for step in range(1, replicas)]
    down_t, head_t, mixed = call(
        prepare_kernel,
        [shape((rank, features), BF16)] * 3,
        small,
        down, head, down2, up2, gains2,
    )
    gram = sum(w[5 * half : 5 * half + 3 * rank].astype(F32) for w in wide).astype(BF16)
    gram2 = from_partner(gram, "section", 1)
    made, theirs = call(
        functools.partial(chain_kernel, width, tensors),
        [shape((6 * half, rank), BF16)] * 2,
        16 * 2 * half * rank * rank,
        *wide, gram, gram2, labels, valid,
    )
    met = from_partner(theirs, "section", 1)
    *parts, _, mix = call(
        functools.partial(mix_kernel, replicas),
        [shape((8 * slim, rank), BF16)] * replicas
        + [shape((8 * rank, rank), BF16), shape((3 * rank, rank), BF16)],
        16 * 2 * half * rank * rank,
        made, met,
    )
    parts = [parts[0]] + [from_partner(parts[step], "dp", step) for step in range(1, replicas)]
    acc, tail = call(
        gain_kernel,
        [shape((2 * slim, features), F32), shape((2 * lines + PACK, rank), BF16)],
        4 * small,
        states, mix, parts[0], mixed, down_t, valid,
    )
    tails = [tail] + [from_partner(tail, "dp", step) for step in range(1, replicas)]
    crossed = [from_partner(f, "section", 1) for f in far]
    for part, own, other in zip(parts[1:], far, crossed):
        acc = call(add_kernel, shape(acc.shape, F32), small, part, own, other, acc)
    return tuple(
        v[None] if v.shape[0] != 1 else v
        for v in call(
            functools.partial(last_kernel, replicas),
            [shape((features, slim), F32), shape((slim, features), F32), shape((1, features), F32)],
            4 * small,
            *parts, *tails, acc, head_t, up, up2, mixed, gains,
        )
    )


def solution(mesh):
    return jax.shard_map(
        local,
        mesh=mesh,
        in_specs=(
            P(None, "dp", "tensor"),
            P("section", "tensor", None),
            P("section", None, "tensor"),
            P("section", "tensor"),
            P("tensor", None),
            P(None, "dp"),
            P(None, "dp"),
        ),
        out_specs=(
            P("section", "tensor", "dp"),
            P("section", "dp", "tensor"),
            P("section", "tensor"),
        ),
        check_vma=False,
    )
```

time: 69.5 us -> 54 us (0.78)
  starting transfers between devices: 13.1 us -> 27 us
  between operations: 13 us -> 0.8 us
  matrix products: 9.68 us -> 0 us
  Pallas kernels: 0 us -> 5.75 us
  local copies, waits for them, and re-layouts: 7.62 us -> 2.84 us
  waiting for transfers between devices: 21.6 us -> 17.3 us
  other arithmetic: 4.07 us -> 0.06 us
    ppermute x12 -> x20, starting transfers between devices: 13.1 us -> 27 us  [from_partner(): lax.ppermute(value, axis, [(i, partner(i, step, size)) for i in range(siz...]
    dot_general x23 -> x0, matrix products: 9.68 us -> none  [the longest x12 5.97 us: dot(): return jnp.dot(a, b, preferred_element_type=F32)]
    pallas_call x0 -> x9, Pallas kernels: none -> 5.75 us  [call(): pl.pallas_call(kernel, out_shape=out, cost_estimate=pl.CostEstimate(flops...]
    ppermute x12 -> x20, waiting for transfers between devices: 21.6 us -> 17.3 us  [from_partner(): lax.ppermute(value, axis, [(i, partner(i, step, size)) for i in range(siz...]
    reduce_sum x7 -> x0, other arithmetic: 2.3 us -> none  [the longest x1 1.14 us: local(): squares = jnp.sum(mine32 * mine32, axis=1)]
    slice x5 -> x0, local copies, waits for them, and re-layouts: 1.59 us -> none  [the longest x3 1.56 us: local(): count_sum = count_sum + got[2 * slim + 2, 0] + got[2 * slim + 3, 0]]
    unnamed x25 -> x17, local copies, waits for them, and re-layouts: 3.35 us -> 1.81 us
    dynamic_slice x3 -> x1, local copies, waits for them, and re-layouts: 1.76 us -> 1.03 us  [local(): mine = lax.dynamic_slice_in_dim(states, me * half, half, 0)]
  transfers between devices with their start and end apart: 12 -> 20, of which waited for: 5 -> 7; matrix products, arithmetic and copies ran while one was open for 7% -> 2% of each run, Pallas kernels for 0% -> 7%
where the time goes in v2:
time: 54 us; the launch traced here: 53.8 us
  starting transfers between devices  27 us (50%)
  waiting for transfers between devices  17.3 us (32%)
  Pallas kernels  5.75 us (11%)
  local copies, waits for them, and re-layouts  2.84 us (5%)
  between operations  0.8 us (1%)
    ppermute x20, starting transfers between devices, from_partner(): lax.ppermute(value, axis, [(i, partner(i, step, size)) for i in range(siz...  27 us
    ppermute x20, waiting for transfers between devices, from_partner(): lax.ppermute(value, axis, [(i, partner(i, step, size)) for i in range(siz...  17.3 us
    pallas_call x9, Pallas kernels, call(): pl.pallas_call(kernel, out_shape=out, cost_estimate=pl.CostEstimate(flops...  5.75 us
    unnamed x17, local copies, waits for them, and re-layouts  1.81 us
  transfers between devices with their start and end apart: 20, of which 7 were waited for; matrix products, arithmetic and copies ran while one was open for 2% of the time, Pallas kernels for 7%

profile of v2, /device:TPU:0, one launch (start us, length us, event | category | flops | bytes accessed | tf_op | source)
XLA Modules:
  0.0 53.8 jit_solution(18163716891995925299)
XLA Ops:
  1.7 1.0 %constant_dynamic-slice_fusion.x_ref = bf16[128,1024]{1,0:T(8,128)(2,1)S(1)} fusion(bf16[256,1024]{1,0:T(8,128)(2,1)} %bitcast.5, s32[]{:T(128)S(6)} %select_n.3), kind=kLoop, calls=%fused_computation.1 | loop fusion | bytes 524292 | tf_op jit(solution)/shard_map/dynamic_slice | solution.py:289
  3.0 0.9 %copy-done.3 = bf16[1024,128]{1,0:T(8,128)(2,1)S(1)} copy-done((bf16[1024,128]{1,0:T(8,128)(2,1)S(1)}, bf16[1024,128]{1,0:T(8,128)(2,1)}, u32[]{:S(2)}) %copy-start.3) | copy-done | bytes 262168
  3.9 1.0 %shard_map.94.refs_0_ = bf16[1040,128]{1,0:T(8,128)(2,1)S(1)} custom-call(bf16[128,1024]{1,0:T(8,128)(2,1)S(1)} %constant_dynamic-slice_fusion.x_ref, bf16[1024,128]{1,0:T(8,128)(2,1)S(1)} %bitcast.11, bf16[128,1024]{1,0:T(8,128)(2,1)S(1)} %bitcast.8, bf16[1,1024]{1,0:T(2,128)(2,1)S(1)} %copy-done.5, bf16[1024,128]{1,0:T(8,128)(2,1)S(1)} %collective-permute-done.down2_ref, ...), custom_call_target="tpu_custom_call" | custom-call | flops 268435456 | bytes 1576960 | tf_op jit(solution)/shard_map/pallas_call | solution.py:54
  5.0 2.9 %collective-permute-start.3 = (bf16[1040,128]{1,0:T(8,128)(2,1)S(1)}, bf16[1040,128]{1,0:T(8,128)(2,1)S(1)}, u32[]{:S(2)}, u32[]{:S(2)}) collective-permute-start(bf16[1040,128]{1,0:T(8,128)(2,1)S(1)} %shard_map.94.refs_0_), channel_id=1, source_target_pairs={{0,1},{1,0},{2,3},{3,2},{4,5},{5,4},{6,7},{7,6},{8,9},{9,8},{10,11... | collective-permute-start | bytes 798728 | tf_op jit(solution)/shard_map/ppermute | solution.py:44
  7.9 1.5 %collective-permute-start.4 = (bf16[1040,128]{1,0:T(8,128)(2,1)S(1)}, bf16[1040,128]{1,0:T(8,128)(2,1)S(1)}, u32[]{:S(2)}, u32[]{:S(2)}) collective-permute-start(bf16[1040,128]{1,0:T(8,128)(2,1)S(1)} %shard_map.94.refs_0_), channel_id=1, source_target_pairs={{0,2},{1,3},{2,0},{3,1},{4,6},{5,7},{6,4},{7,5},{8,10},{9,11},{10,... | collective-permute-start | bytes 798728 | tf_op jit(solution)/shard_map/ppermute | solution.py:44
  9.4 2.0 %collective-permute-start.18 = (bf16[128,1024]{1,0:T(8,128)(2,1)S(1)}, bf16[128,1024]{1,0:T(8,128)(2,1)S(1)}, u32[]{:S(2)}, u32[]{:S(2)}) collective-permute-start(bf16[128,1024]{1,0:T(8,128)(2,1)S(1)} %constant_dynamic-slice_fusion.x_ref), channel_id=1, source_target_pairs={{0,4},{4,0},{8,12},{12,8},{1,5},{5,1},{9,13},{13,9},{2,6},{6,2},{1... | collective-permute-start | bytes 786440 | tf_op jit(solution)/shard_map/ppermute | solution.py:44
  11.5 2.6 %collective-permute-start.16 = (bf16[128,1024]{1,0:T(8,128)(2,1)S(1)}, bf16[128,1024]{1,0:T(8,128)(2,1)S(1)}, u32[]{:S(2)}, u32[]{:S(2)}) collective-permute-start(bf16[128,1024]{1,0:T(8,128)(2,1)S(1)} %constant_dynamic-slice_fusion.x_ref), channel_id=1, source_target_pairs={{0,8},{4,12},{8,0},{12,4},{1,9},{5,13},{9,1},{13,5},{2,10},{6,14},... | collective-permute-start | bytes 786440 | tf_op jit(solution)/shard_map/ppermute | solution.py:44
  14.1 1.1 %collective-permute-done.3.refs_1_ = bf16[1040,128]{1,0:T(8,128)(2,1)S(1)} collective-permute-done((bf16[1040,128]{1,0:T(8,128)(2,1)S(1)}, bf16[1040,128]{1,0:T(8,128)(2,1)S(1)}, u32[]{:S(2)}, u32[]{:S(2)}) %collective-permute-start.3) | collective-permute-done | bytes 266272 | tf_op jit(solution)/shard_map/ppermute | solution.py:44
  15.1 4.1 %collective-permute-start.14 = (bf16[128,1024]{1,0:T(8,128)(2,1)S(1)}, bf16[128,1024]{1,0:T(8,128)(2,1)S(1)}, u32[]{:S(2)}, u32[]{:S(2)}) collective-permute-start(bf16[128,1024]{1,0:T(8,128)(2,1)S(1)} %constant_dynamic-slice_fusion.x_ref), channel_id=1, source_target_pairs={{0,12},{4,8},{8,4},{12,0},{1,13},{5,9},{9,5},{13,1},{2,14},{6,10},... | collective-permute-start | bytes 786440 | tf_op jit(solution)/shard_map/ppermute | solution.py:44
  19.3 2.5 %collective-permute-done.4.refs_2_ = bf16[1040,128]{1,0:T(8,128)(2,1)S(1)} collective-permute-done((bf16[1040,128]{1,0:T(8,128)(2,1)S(1)}, bf16[1040,128]{1,0:T(8,128)(2,1)S(1)}, u32[]{:S(2)}, u32[]{:S(2)}) %collective-permute-start.4) | collective-permute-done | bytes 266272 | tf_op jit(solution)/shard_map/ppermute | solution.py:44
  22.4 0.8 %collective-permute-done.6.refs_5_ = bf16[384,128]{1,0:T(8,128)(2,1)S(1)} collective-permute-done((bf16[384,128]{1,0:T(8,128)(2,1)S(1)}, bf16[384,128]{1,0:T(8,128)(2,1)S(1)}, u32[]{:S(2)}, u32[]{:S(2)}) %collective-permute-start.6) | collective-permute-done | bytes 98336 | tf_op jit(solution)/shard_map/ppermute | solution.py:44
  23.2 1.1 %shard_map.95 = (bf16[768,128]{1,0:T(8,128)(2,1)S(1)}, bf16[768,128]{1,0:T(8,128)(2,1)S(1)}) custom-call(bf16[1040,128]{1,0:T(8,128)(2,1)S(1)} %shard_map.94.refs_0_, bf16[1040,128]{1,0:T(8,128)(2,1)S(1)} %collective-permute-done.3.refs_1_, bf16[1040,128]{1,0:T(8,128)(2,1)S(1)} %collective-permute-done.4.refs_2_, ...), custom_call_target="tpu_custom_call" | custom-call | flops 67108864 | bytes 1263616 | tf_op jit(solution)/shard_map/pallas_call | solution.py:54
  24.5 8.3 %collective-permute-done.16.own_ref = bf16[128,1024]{1,0:T(8,128)(2,1)S(1)} collective-permute-done((bf16[128,1024]{1,0:T(8,128)(2,1)S(1)}, bf16[128,1024]{1,0:T(8,128)(2,1)S(1)}, u32[]{:S(2)}, u32[]{:S(2)}) %collective-permute-start.16) | collective-permute-done | bytes 262176 | tf_op jit(solution)/shard_map/ppermute | solution.py:44
  33.3 1.0 %shard_map.96 = (bf16[256,128]{1,0:T(8,128)(2,1)S(1)}, bf16[256,128]{1,0:T(8,128)(2,1)S(1)}, bf16[256,128]{1,0:T(8,128)(2,1)S(1)}, bf16[256,128]{1,0:T(8,128)(2,...) custom-call(bf16[768,128]{1,0:T(8,128)(2,1)S(1)} %get-tuple-element.18.mine_ref, ...), custom_call_target="tpu_custom_call" | custom-call | flops 67108864 | bytes 393216 | tf_op jit(solution)/shard_map/pallas_call | solution.py:54
  34.3 3.8 %collective-permute-start.8 = (bf16[256,128]{1,0:T(8,128)(2,1)S(1)}, bf16[256,128]{1,0:T(8,128)(2,1)S(1)}, u32[]{:S(2)}, u32[]{:S(2)}) collective-permute-start(bf16[256,128]{1,0:T(8,128)(2,1)S(1)} %get-tuple-element.21), channel_id=1, source_target_pairs={{0,4},{4,0},{8,12},{12,8},{1,5},{5,1},{9,13},{13,9},{2,6},{6,2},{1... | collective-permute-start | bytes 196616 | tf_op jit(solution)/shard_map/ppermute | solution.py:44
  38.1 1.0 %collective-permute-start.9 = (bf16[256,128]{1,0:T(8,128)(2,1)S(1)}, bf16[256,128]{1,0:T(8,128)(2,1)S(1)}, u32[]{:S(2)}, u32[]{:S(2)}) collective-permute-start(bf16[256,128]{1,0:T(8,128)(2,1)S(1)} %get-tuple-element.22), channel_id=1, source_target_pairs={{0,8},{4,12},{8,0},{12,4},{1,9},{5,13},{9,1},{13,5},{2,10},{6,14},... | collective-permute-start | bytes 196616 | tf_op jit(solution)/shard_map/ppermute | solution.py:44
  39.1 1.5 %collective-permute-start.10 = (bf16[256,128]{1,0:T(8,128)(2,1)S(1)}, bf16[256,128]{1,0:T(8,128)(2,1)S(1)}, u32[]{:S(2)}, u32[]{:S(2)}) collective-permute-start(bf16[256,128]{1,0:T(8,128)(2,1)S(1)} %get-tuple-element.23), channel_id=1, source_target_pairs={{0,12},{4,8},{8,4},{12,0},{1,13},{5,9},{9,5},{13,1},{2,14},{6,10},... | collective-permute-start | bytes 196616 | tf_op jit(solution)/shard_map/ppermute | solution.py:44
  41.5 1.3 %collective-permute-start.11 = (bf16[32,128]{1,0:T(8,128)(2,1)S(1)}, bf16[32,128]{1,0:T(8,128)(2,1)S(1)}, u32[]{:S(2)}, u32[]{:S(2)}) collective-permute-start(bf16[32,128]{1,0:T(8,128)(2,1)S(1)} %get-tuple-element.27.refs_4_), channel_id=1, source_target_pairs={{0,4},{4,0},{8,12},{12,8},{1,5},{5,1},{9,13},{13,9},{2,6},{6,2},{1... | collective-permute-start | bytes 24584 | tf_op jit(solution)/shard_map/ppermute | solution.py:44
  42.7 1.7 %collective-permute-start.12 = (bf16[32,128]{1,0:T(8,128)(2,1)S(1)}, bf16[32,128]{1,0:T(8,128)(2,1)S(1)}, u32[]{:S(2)}, u32[]{:S(2)}) collective-permute-start(bf16[32,128]{1,0:T(8,128)(2,1)S(1)} %get-tuple-element.27.refs_4_), channel_id=1, source_target_pairs={{0,8},{4,12},{8,0},{12,4},{1,9},{5,13},{9,1},{13,5},{2,10},{6,14},... | collective-permute-start | bytes 24584 | tf_op jit(solution)/shard_map/ppermute | solution.py:44
  44.4 2.2 %collective-permute-done.9.part_ref.refs_2_ = bf16[256,128]{1,0:T(8,128)(2,1)S(1)} collective-permute-done((bf16[256,128]{1,0:T(8,128)(2,1)S(1)}, bf16[256,128]{1,0:T(8,128)(2,1)S(1)}, u32[]{:S(2)}, u32[]{:S(2)}) %collective-permute-start.9) | collective-permute-done | bytes 65568 | tf_op jit(solution)/shard_map/ppermute | solution.py:44
  46.6 2.2 %collective-permute-start.13 = (bf16[32,128]{1,0:T(8,128)(2,1)S(1)}, bf16[32,128]{1,0:T(8,128)(2,1)S(1)}, u32[]{:S(2)}, u32[]{:S(2)}) collective-permute-start(bf16[32,128]{1,0:T(8,128)(2,1)S(1)} %get-tuple-element.27.refs_4_), channel_id=1, source_target_pairs={{0,12},{4,8},{8,4},{12,0},{1,13},{5,9},{9,5},{13,1},{2,14},{6,10},... | collective-permute-start | bytes 24584 | tf_op jit(solution)/shard_map/ppermute | solution.py:44
  49.7 2.3 %collective-permute-done.13.refs_7_ = bf16[32,128]{1,0:T(8,128)(2,1)S(1)} collective-permute-done((bf16[32,128]{1,0:T(8,128)(2,1)S(1)}, bf16[32,128]{1,0:T(8,128)(2,1)S(1)}, u32[]{:S(2)}, u32[]{:S(2)}) %collective-permute-start.13) | collective-permute-done | bytes 8224 | tf_op jit(solution)/shard_map/ppermute | solution.py:44
  52.0 0.9 %shard_map.102 = (f32[1024,32]{1,0:T(8,128)S(1)}, f32[32,1024]{1,0:T(8,128)}, f32[1,1024]{1,0:T(1,128)}) custom-call(bf16[256,128]{1,0:T(8,128)(2,1)S(1)} %get-tuple-element.20.part_ref.refs_0_, bf16[256,128]{1,0:T(8,128)(2,1)S(1)} %collective-permute-done.8.part_ref.refs_1_, bf16[256,128]{1,0:T(8,128)(2,1)S(1)} %collective-permute-done.9.part_ref.refs_2_, ...), custom_call_target="tpu_custom_call" | custom-call | flops 134217728 | bytes 1607680 | tf_op jit(solution)/shard_map/pallas_call | solution.py:54
  53.0 0.8 %copy.10 = f32[1,1024,32]{1,2,0:T(8,128)} copy(f32[1,1024,32]{2,1,0:T(8,128)S(1)} %bitcast.13) | data formatting | bytes 262144
  (44 shorter events, 4.4 us)
Async XLA Ops:
  0.6 2.3 %collective-permute-start.1 = (bf16[128,1024]{1,0:T(8,128)(2,1)}, bf16[128,1024]{1,0:T(8,128)(2,1)S(1)}, u32[]{:S(2)}, u32[]{:S(2)}) collective-permute-start(bf16[128,1024]{1,0:T(8,128)(2,1)} %bitcast.7), channel_id=1, source_target_pairs={{0,16},{16,0},{1,17},{17,1},{2,18},{18,2},{3,19},{19,3},{4,20},{20... | collective-permute-start | bytes 786440 | tf_op jit(solution)/shard_map/ppermute | solution.py:44
  1.2 1.8 %collective-permute-start = (bf16[1024,128]{1,0:T(8,128)(2,1)}, bf16[1024,128]{1,0:T(8,128)(2,1)S(1)}, u32[]{:S(2)}, u32[]{:S(2)}) collective-permute-start(bf16[1024,128]{1,0:T(8,128)(2,1)} %bitcast.10), channel_id=1, source_target_pairs={{0,16},{16,0},{1,17},{17,1},{2,18},{18,2},{3,19},{19,3},{4,20},{20... | collective-permute-start | bytes 786440 | tf_op jit(solution)/shard_map/ppermute | solution.py:44
  1.3 1.7 %collective-permute-start.2 = (bf16[1,1024]{1,0:T(2,128)(2,1)}, bf16[1,1024]{1,0:T(2,128)(2,1)S(1)}, u32[]{:S(2)}, u32[]{:S(2)}) collective-permute-start(bf16[1,1024]{1,0:T(2,128)(2,1)} %refs_13_.1), channel_id=1, source_target_pairs={{0,16},{16,0},{1,17},{17,1},{2,18},{18,2},{3,19},{19,3},{4,20},{20... | collective-permute-start | bytes 6152 | tf_op jit(solution)/shard_map/ppermute | solution.py:44
  5.0 18.2 %copy-start.6 = (s32[2,128]{1,0:T(2,128)S(1)}, s32[2,128]{1,0:T(2,128)}, u32[]{:S(2)}) copy-start(s32[2,128]{1,0:T(2,128)} %valid_ref.1) | copy-start | bytes 3076
  5.0 18.2 %copy-start.7 = (s32[2,128]{1,0:T(2,128)S(1)}, s32[2,128]{1,0:T(2,128)}, u32[]{:S(2)}) copy-start(s32[2,128]{1,0:T(2,128)} %refs_6_.1) | copy-start | bytes 3076
  5.0 10.2 %collective-permute-start.3 = (bf16[1040,128]{1,0:T(8,128)(2,1)S(1)}, bf16[1040,128]{1,0:T(8,128)(2,1)S(1)}, u32[]{:S(2)}, u32[]{:S(2)}) collective-permute-start(bf16[1040,128]{1,0:T(8,128)(2,1)S(1)} %shard_map.94.refs_0_), channel_id=1, source_target_pairs={{0,1},{1,0},{2,3},{3,2},{4,5},{5,4},{6,7},{7,6},{8,9},{9,8},{10,11... | collective-permute-start | bytes 798728 | tf_op jit(solution)/shard_map/ppermute | solution.py:44
  7.9 13.9 %collective-permute-start.4 = (bf16[1040,128]{1,0:T(8,128)(2,1)S(1)}, bf16[1040,128]{1,0:T(8,128)(2,1)S(1)}, u32[]{:S(2)}, u32[]{:S(2)}) collective-permute-start(bf16[1040,128]{1,0:T(8,128)(2,1)S(1)} %shard_map.94.refs_0_), channel_id=1, source_target_pairs={{0,2},{1,3},{2,0},{3,1},{4,6},{5,7},{6,4},{7,5},{8,10},{9,11},{10,... | collective-permute-start | bytes 798728 | tf_op jit(solution)/shard_map/ppermute | solution.py:44
  9.4 12.4 %collective-permute-start.5 = (bf16[1040,128]{1,0:T(8,128)(2,1)S(1)}, bf16[1040,128]{1,0:T(8,128)(2,1)S(1)}, u32[]{:S(2)}, u32[]{:S(2)}) collective-permute-start(bf16[1040,128]{1,0:T(8,128)(2,1)S(1)} %shard_map.94.refs_0_), channel_id=1, source_target_pairs={{0,3},{1,2},{2,1},{3,0},{4,7},{5,6},{6,5},{7,4},{8,11},{9,10},{10,... | collective-permute-start | bytes 798728 | tf_op jit(solution)/shard_map/ppermute | solution.py:44
  9.4 12.5 %collective-permute-start.18 = (bf16[128,1024]{1,0:T(8,128)(2,1)S(1)}, bf16[128,1024]{1,0:T(8,128)(2,1)S(1)}, u32[]{:S(2)}, u32[]{:S(2)}) collective-permute-start(bf16[128,1024]{1,0:T(8,128)(2,1)S(1)} %constant_dynamic-slice_fusion.x_ref), channel_id=1, source_target_pairs={{0,4},{4,0},{8,12},{12,8},{1,5},{5,1},{9,13},{13,9},{2,6},{6,2},{1... | collective-permute-start | bytes 786440 | tf_op jit(solution)/shard_map/ppermute | solution.py:44
  11.5 21.3 %collective-permute-start.16 = (bf16[128,1024]{1,0:T(8,128)(2,1)S(1)}, bf16[128,1024]{1,0:T(8,128)(2,1)S(1)}, u32[]{:S(2)}, u32[]{:S(2)}) collective-permute-start(bf16[128,1024]{1,0:T(8,128)(2,1)S(1)} %constant_dynamic-slice_fusion.x_ref), channel_id=1, source_target_pairs={{0,8},{4,12},{8,0},{12,4},{1,9},{5,13},{9,1},{13,5},{2,10},{6,14},... | collective-permute-start | bytes 786440 | tf_op jit(solution)/shard_map/ppermute | solution.py:44
  15.1 17.6 %collective-permute-start.14 = (bf16[128,1024]{1,0:T(8,128)(2,1)S(1)}, bf16[128,1024]{1,0:T(8,128)(2,1)S(1)}, u32[]{:S(2)}, u32[]{:S(2)}) collective-permute-start(bf16[128,1024]{1,0:T(8,128)(2,1)S(1)} %constant_dynamic-slice_fusion.x_ref), channel_id=1, source_target_pairs={{0,12},{4,8},{8,4},{12,0},{1,13},{5,9},{9,5},{13,1},{2,14},{6,10},... | collective-permute-start | bytes 786440 | tf_op jit(solution)/shard_map/ppermute | solution.py:44
  21.8 1.4 %collective-permute-start.6 = (bf16[384,128]{1,0:T(8,128)(2,1)S(1)}, bf16[384,128]{1,0:T(8,128)(2,1)S(1)}, u32[]{:S(2)}, u32[]{:S(2)}) collective-permute-start(bf16[384,128]{1,0:T(8,128)(2,1)S(1)} %add_convert_fusion.refs_4_), channel_id=1, source_target_pairs={{0,16},{16,0},{1,17},{17,1},{2,18},{18,2},{3,19},{19,3},{4,20},{20... | collective-permute-start | bytes 294920 | tf_op jit(solution)/shard_map/ppermute | solution.py:44
  21.9 17.2 %collective-permute-start.19 = (bf16[128,1024]{1,0:T(8,128)(2,1)S(1)}, bf16[128,1024]{1,0:T(8,128)(2,1)S(1)}, u32[]{:S(2)}, u32[]{:S(2)}) collective-permute-start(bf16[128,1024]{1,0:T(8,128)(2,1)S(1)} %collective-permute-done.18.own_ref), channel_id=1, source_target_pairs={{0,16},{16,0},{1,17},{17,1},{2,18},{18,2},{3,19},{19,3},{4,20},{20... | collective-permute-start | bytes 786440 | tf_op jit(solution)/shard_map/ppermute | solution.py:44
  24.3 16.3 %copy-start.4 = (bf16[1024,128]{1,0:T(8,128)(2,1)S(1)}, bf16[1024,128]{1,0:T(8,128)(2,1)}, u32[]{:S(2)}) copy-start(bf16[1024,128]{1,0:T(8,128)(2,1)} %head_ref.3) | copy-start | bytes 786436
  24.3 9.0 %collective-permute-start.7 = (bf16[768,128]{1,0:T(8,128)(2,1)S(1)}, bf16[768,128]{1,0:T(8,128)(2,1)S(1)}, u32[]{:S(2)}, u32[]{:S(2)}) collective-permute-start(bf16[768,128]{1,0:T(8,128)(2,1)S(1)} %get-tuple-element.19), channel_id=1, source_target_pairs={{0,16},{16,0},{1,17},{17,1},{2,18},{18,2},{3,19},{19,3},{4,20},{20... | collective-permute-start | bytes 589832 | tf_op jit(solution)/shard_map/ppermute | solution.py:44
  32.8 8.7 %collective-permute-start.17 = (bf16[128,1024]{1,0:T(8,128)(2,1)S(1)}, bf16[128,1024]{1,0:T(8,128)(2,1)S(1)}, u32[]{:S(2)}, u32[]{:S(2)}) collective-permute-start(bf16[128,1024]{1,0:T(8,128)(2,1)S(1)} %collective-permute-done.16.own_ref), channel_id=1, source_target_pairs={{0,16},{16,0},{1,17},{17,1},{2,18},{18,2},{3,19},{19,3},{4,20},{20... | collective-permute-start | bytes 786440 | tf_op jit(solution)/shard_map/ppermute | solution.py:44
  32.8 16.6 %collective-permute-start.15 = (bf16[128,1024]{1,0:T(8,128)(2,1)S(1)}, bf16[128,1024]{1,0:T(8,128)(2,1)S(1)}, u32[]{:S(2)}, u32[]{:S(2)}) collective-permute-start(bf16[128,1024]{1,0:T(8,128)(2,1)S(1)} %collective-permute-done.14.own_ref), channel_id=1, source_target_pairs={{0,16},{16,0},{1,17},{17,1},{2,18},{18,2},{3,19},{19,3},{4,20},{20... | collective-permute-start | bytes 786440 | tf_op jit(solution)/shard_map/ppermute | solution.py:44
  34.3 8.4 %collective-permute-start.8 = (bf16[256,128]{1,0:T(8,128)(2,1)S(1)}, bf16[256,128]{1,0:T(8,128)(2,1)S(1)}, u32[]{:S(2)}, u32[]{:S(2)}) collective-permute-start(bf16[256,128]{1,0:T(8,128)(2,1)S(1)} %get-tuple-element.21), channel_id=1, source_target_pairs={{0,4},{4,0},{8,12},{12,8},{1,5},{5,1},{9,13},{13,9},{2,6},{6,2},{1... | collective-permute-start | bytes 196616 | tf_op jit(solution)/shard_map/ppermute | solution.py:44
  38.1 8.5 %collective-permute-start.9 = (bf16[256,128]{1,0:T(8,128)(2,1)S(1)}, bf16[256,128]{1,0:T(8,128)(2,1)S(1)}, u32[]{:S(2)}, u32[]{:S(2)}) collective-permute-start(bf16[256,128]{1,0:T(8,128)(2,1)S(1)} %get-tuple-element.22), channel_id=1, source_target_pairs={{0,8},{4,12},{8,0},{12,4},{1,9},{5,13},{9,1},{13,5},{2,10},{6,14},... | collective-permute-start | bytes 196616 | tf_op jit(solution)/shard_map/ppermute | solution.py:44
  39.1 1.9 %copy-start = (bf16[2,128,1024]{2,1,0:T(8,128)(2,1)S(1)}, bf16[2,128,1024]{2,1,0:T(8,128)(2,1)}, u32[]{:S(2)}) copy-start(bf16[2,128,1024]{2,1,0:T(8,128)(2,1)} %param.7) | copy-start | bytes 1572868
  39.1 10.3 %collective-permute-start.10 = (bf16[256,128]{1,0:T(8,128)(2,1)S(1)}, bf16[256,128]{1,0:T(8,128)(2,1)S(1)}, u32[]{:S(2)}, u32[]{:S(2)}) collective-permute-start(bf16[256,128]{1,0:T(8,128)(2,1)S(1)} %get-tuple-element.23), channel_id=1, source_target_pairs={{0,12},{4,8},{8,4},{12,0},{1,13},{5,9},{9,5},{13,1},{2,14},{6,10},... | collective-permute-start | bytes 196616 | tf_op jit(solution)/shard_map/ppermute | solution.py:44
  41.5 8.3 %collective-permute-start.11 = (bf16[32,128]{1,0:T(8,128)(2,1)S(1)}, bf16[32,128]{1,0:T(8,128)(2,1)S(1)}, u32[]{:S(2)}, u32[]{:S(2)}) collective-permute-start(bf16[32,128]{1,0:T(8,128)(2,1)S(1)} %get-tuple-element.27.refs_4_), channel_id=1, source_target_pairs={{0,4},{4,0},{8,12},{12,8},{1,5},{5,1},{9,13},{13,9},{2,6},{6,2},{1... | collective-permute-start | bytes 24584 | tf_op jit(solution)/shard_map/ppermute | solution.py:44
  42.7 7.0 %collective-permute-start.12 = (bf16[32,128]{1,0:T(8,128)(2,1)S(1)}, bf16[32,128]{1,0:T(8,128)(2,1)S(1)}, u32[]{:S(2)}, u32[]{:S(2)}) collective-permute-start(bf16[32,128]{1,0:T(8,128)(2,1)S(1)} %get-tuple-element.27.refs_4_), channel_id=1, source_target_pairs={{0,8},{4,12},{8,0},{12,4},{1,9},{5,13},{9,1},{13,5},{2,10},{6,14},... | collective-permute-start | bytes 24584 | tf_op jit(solution)/shard_map/ppermute | solution.py:44
  46.6 5.4 %collective-permute-start.13 = (bf16[32,128]{1,0:T(8,128)(2,1)S(1)}, bf16[32,128]{1,0:T(8,128)(2,1)S(1)}, u32[]{:S(2)}, u32[]{:S(2)}) collective-permute-start(bf16[32,128]{1,0:T(8,128)(2,1)S(1)} %get-tuple-element.27.refs_4_), channel_id=1, source_target_pairs={{0,12},{4,8},{8,4},{12,0},{1,13},{5,9},{9,5},{13,1},{2,14},{6,10},... | collective-permute-start | bytes 24584 | tf_op jit(solution)/shard_map/ppermute | solution.py:44
  (4 other events, 4.7 us)

commit v3 on v2

--- a/solution.py
+++ b/solution.py
@@ -59,34 +59,50 @@
     )(*args)
 
 
-def project_kernel(x_ref, down_ref, up_ref, gain_ref, down2_ref, up2_ref, gain2_ref, head_ref, out_ref):
-    half, rank = x_ref.shape[0], down_ref.shape[1]
+def gain_kernel(gain_ref, out_ref):
+    out_ref[...] = gain_ref[...].astype(F32)
+
+
+def own_kernel(x_ref, down_ref, up_ref, head_ref, gain_ref, out_ref):
+    rank = down_ref.shape[1]
+    half = x_ref.shape[0] // lax.axis_size("section")
+    x, up, head = x_ref[rows_of(lax.axis_index("section") * half, half), :], up_ref[...], head_ref[...]
+    x32 = x.astype(F32)
+    scaled = (x32 * gain_ref[...]).astype(BF16)
+    out_ref[:half, :] = dot(scaled, down_ref[...]).astype(BF16)
+    out_ref[half : 2 * half, :] = dot_nt(x, up).astype(BF16)
+    out_ref[2 * half : 3 * half, :] = dot(x, head).astype(BF16)
+    out_ref[3 * half : 3 * half + rank, :] = dot(up, head).astype(BF16)
+    out_ref[3 * half + rank : 3 * half + 2 * rank, :] = dot_nt(up, up).astype(BF16)
+    squares = jnp.sum(x32 * x32, axis=1, keepdims=True)
+    squares = jnp.broadcast_to(squares, (half, rank)).T
+    out_ref[3 * half + 2 * rank :, :] = high_low(squares[: PACK // 2])
+
+
+def other_kernel(x_ref, up_ref, own_ref, down2_ref, up2_ref, gain2_ref, out_ref):
+    rank = down2_ref.shape[1]
+    half = x_ref.shape[0] // lax.axis_size("section")
     me = lax.axis_index("section")
     it = 1 - me
-    x, up, up2, head = x_ref[...], up_ref[...], up2_ref[...], head_ref[...]
-    x32 = x.astype(F32)
-    gain, gain2 = gain_ref[...].astype(F32), gain2_ref[...].astype(F32)
-    out_ref[rows_of(me * half, half), :] = dot((x32 * gain).astype(BF16), down_ref[...]).astype(BF16)
-    out_ref[rows_of(it * half, half), :] = dot((x32 * gain2).astype(BF16), down2_ref[...]).astype(BF16)
-    out_ref[rows_of((2 + me) * half, half), :] = dot_nt(x, up).astype(BF16)
-    out_ref[rows_of((2 + it) * half, half), :] = dot_nt(x, up2).astype(BF16)
-    out_ref[4 * half : 5 * half, :] = dot(x, head).astype(BF16)
+    x = x_ref[rows_of(me * half, half), :]
+    gain2 = gain2_ref[...].astype(F32)
     base = 5 * half
+    out_ref[rows_of(me * half, half), :] = own_ref[:half, :]
+    out_ref[rows_of((2 + me) * half, half), :] = own_ref[half : 2 * half, :]
+    out_ref[4 * half : base, :] = own_ref[2 * half : 3 * half, :]
+    out_ref[base + rank :, :] = own_ref[3 * half :, :]
+    scaled = (x.astype(F32) * gain2).astype(BF16)
+    out_ref[rows_of(it * half, half), :] = dot(scaled, down2_ref[...]).astype(BF16)
+    out_ref[rows_of((2 + it) * half, half), :] = dot_nt(x, up2_ref[...]).astype(BF16)
 
     @pl.when(me == 0)
     def _():
-        scaled = (up.astype(F32) * gain2).astype(BF16)
+        scaled = (up_ref[...].astype(F32) * gain2).astype(BF16)
         out_ref[base : base + rank, :] = dot(scaled, down2_ref[...]).astype(BF16)
 
     @pl.when(me != 0)
     def _():
-        out_ref[base : base + rank, :] = dot_nt(up, up2).astype(BF16)
-
-    out_ref[base + rank : base + 2 * rank, :] = dot(up, head).astype(BF16)
-    out_ref[base + 2 * rank : base + 3 * rank, :] = dot_nt(up, up).astype(BF16)
-    squares = jnp.sum(x32 * x32, axis=1, keepdims=True)
-    squares = jnp.broadcast_to(squares, (half, rank)).T
-    out_ref[base + 3 * rank :, :] = high_low(squares[: PACK // 2])
+        out_ref[base : base + rank, :] = dot_nt(up_ref[...], up2_ref[...]).astype(BF16)
 
 
 def prepare_kernel(down_ref, head_ref, down2_ref, up2_ref, gain2_ref, down_t_ref, head_t_ref, mixed_ref):
@@ -168,10 +184,11 @@
         theirs_ref[slot * half : (slot + 1) * half, :] = jnp.where(first, b, a)
 
 
-def mix_kernel(replicas, mine_ref, theirs_ref, *refs):
-    out_refs, tall_ref, mix_ref = refs[:replicas], refs[replicas], refs[replicas + 1]
+def grad_kernel(replicas, mine_ref, theirs_ref, x_ref, down_t_ref, head_t_ref, up_ref, up2_ref, mixed_ref, gain_ref, valid_ref, *refs):
+    out_refs, all_ref = refs[:replicas], refs[replicas]
     rank = mine_ref.shape[1]
     half = mine_ref.shape[0] // 6
+    features = x_ref.shape[1]
     slim = rank // replicas
     first = lax.axis_index("section") == 0
     mine, theirs = mine_ref[...], theirs_ref[...]
@@ -186,88 +203,52 @@
 
     left_oth = [jnp.where(first, a, b) for a, b in zip(hidden_t, scaled_t)]
     left_mix = [jnp.where(first, a, b) for a, b in zip(hidden_t, weighted_t)]
+    head_mix = product(hidden_t, last).astype(BF16)
+    own_mix = product(scaled_t, hidden).astype(BF16)
+    oth_mix = product(left_oth, extra2).astype(BF16)
     mix = product(left_mix, extra1).astype(BF16)
-    for slot, value in enumerate(
-        (
-            product(hidden_t, last).astype(BF16),
-            (-product(scaled_t, hidden)).astype(BF16),
-            (-product(left_oth, extra2)).astype(BF16),
-            mix,
-            weighted_t[0],
-            weighted_t[1],
-            scaled_t[0],
-            scaled_t[1],
-        )
-    ):
-        tall_ref[slot * rank : (slot + 1) * rank, :] = value
-    mix_ref[:rank, :] = mix
-    mix_ref[rank : 2 * rank, :] = weighted_t[0]
-    mix_ref[2 * rank :, :] = weighted_t[1]
+    none = jnp.zeros_like(mix)
+    halves = [x_ref[i * half : (i + 1) * half, :] for i in range(2)]
+    mixed = mixed_ref[...]
+    grad = product(weighted_t, halves) + dot(jnp.where(first, none, mix), mixed)
+    gain = jnp.sum(grad * down_t_ref[...].astype(F32), axis=0, keepdims=True)
+    grad = (grad * gain_ref[...].astype(F32)).astype(BF16)
+    rest = dot(head_mix, head_t_ref[...]) + dot(jnp.where(first, mix, none), mixed)
+    rest = rest - dot(own_mix, up_ref[...]) - dot(oth_mix, up2_ref[...]) - product(scaled_t, halves)
+    rest = rest.astype(BF16)
+    for c in range(replicas):
+        all_ref[2 * c * slim : (2 * c + 1) * slim, :] = grad[c * slim : (c + 1) * slim]
+        all_ref[(2 * c + 1) * slim : (2 * c + 2) * slim, :] = rest[c * slim : (c + 1) * slim]
+    count = jnp.sum(valid_ref[...].astype(F32), keepdims=True)
+    lines = features // rank
+    tail = jnp.concatenate(
+        [gain[:, i * rank : (i + 1) * rank] for i in range(lines)] + [jnp.broadcast_to(count, (PACK - lines, rank))],
+        axis=0,
+    ).astype(BF16)
     me = lax.axis_index("dp")
     for step, out_ref in enumerate(out_refs):
-        target = partner(me, step, replicas)
-        for slot in range(8):
-            out_ref[slot * slim : (slot + 1) * slim, :] = tall_ref[rows_of(slot * rank + target * slim, slim), :]
-
-
-def gain_kernel(x_ref, mix_ref, part_ref, mixed_ref, down_t_ref, valid_ref, acc_ref, tail_ref):
-    features = x_ref.shape[1]
-    rank = mix_ref.shape[1]
-    half = x_ref.shape[0] // 2
-    slim = part_ref.shape[0] // 8
-    first = lax.axis_index("section") == 0
-    x0, x1 = x_ref[:half, :], x_ref[half:, :]
-    mix = jnp.where(first, jnp.zeros((rank, rank), BF16), mix_ref[:rank, :])
-    grad = dot(mix_ref[rank : 2 * rank, :], x0) + dot(mix_ref[2 * rank :, :], x1) + dot(mix, mixed_ref[...])
-    gain = jnp.sum(grad * down_t_ref[...].astype(F32), axis=0, keepdims=True)
-    gain = jnp.concatenate(
-        [gain[:, i * rank : (i + 1) * rank] for i in range(features // rank)], axis=0
-    )
-    count = jnp.sum(valid_ref[...].astype(F32), keepdims=True)
-    count = jnp.broadcast_to(count, (PACK // 2, rank))
-    tail_ref[...] = jnp.concatenate([high_low(gain), high_low(count)], axis=0)
-    accumulate(x0, x1, part_ref, slim, acc_ref)
-
-
-def accumulate(x0, x1, part_ref, slim, acc_ref, before=None):
-    for slot in (0, 1):
-        start = (4 + 2 * slot) * slim
-        value = dot(part_ref[start : start + slim, :], x0)
-        value = value + dot(part_ref[start + slim : start + 2 * slim, :], x1)
-        if before is not None:
-            value = value + before[slot * slim : (slot + 1) * slim, :]
-        acc_ref[slot * slim : (slot + 1) * slim, :] = value
-
-
-def add_kernel(part_ref, own_ref, far_ref, before_ref, acc_ref):
-    first = lax.axis_index("section") == 0
-    own, far = own_ref[...], far_ref[...]
-    x0, x1 = jnp.where(first, own, far), jnp.where(first, far, own)
-    accumulate(x0, x1, part_ref, part_ref.shape[0] // 8, acc_ref, before_ref)
-
-
-def last_kernel(replicas, *refs):
-    parts, refs = refs[:replicas], refs[replicas:]
-    tails, refs = refs[:replicas], refs[replicas:]
-    acc_ref, head_t_ref, up_ref, up2_ref, mixed_ref, gain_ref, down_out, up_out, gain_out = refs
-    slim = parts[0].shape[0] // 8
+        block = all_ref[rows_of(partner(me, step, replicas) * 2 * slim, 2 * slim), :]
+        for i in range(lines):
+            out_ref[i * 2 * slim : (i + 1) * 2 * slim, :] = block[:, i * rank : (i + 1) * rank]
+        out_ref[lines * 2 * slim :, :] = tail
+
+
+def last_kernel(*refs):
+    parts, (down_out, up_out, gain_out) = refs[:-3], refs[-3:]
     rank = parts[0].shape[1]
-    first = lax.axis_index("section") == 0
-    tail = sum(t[...].astype(F32) for t in tails)
-    lines = tail.shape[0] - PACK
-    scale = 1.0 / (tail[lines : lines + 1, :1] + tail[lines + PACK // 2 : lines + PACK // 2 + 1, :1])
-    gain = (tail[: lines // 2] + tail[lines // 2 : lines]) * scale
-    for i in range(lines // 2):
-        gain_out[:, i * rank : (i + 1) * rank] = gain[i : i + 1, :]
-    head_mix, own_mix, oth_mix, mix = (
-        sum(p[slot * slim : (slot + 1) * slim, :].astype(F32) for p in parts).astype(BF16) for slot in range(4)
-    )
-    mixed = dot(mix, mixed_ref[...])
-    none = jnp.zeros_like(mixed)
-    down = acc_ref[:slim, :] + jnp.where(first, none, mixed)
-    down_out[...] = (down * gain_ref[...].astype(F32) * scale).T
-    up = dot(head_mix, head_t_ref[...]) + dot(own_mix, up_ref[...]) + dot(oth_mix, up2_ref[...])
-    up_out[...] = (up + jnp.where(first, mixed, none) - acc_ref[slim:, :]) * scale
+    slim, features = down_out.shape
+    lines = features // rank
+
+    def total(start, size):
+        return sum(p[start : start + size, :].astype(F32) for p in parts)
+
+    tail = total(lines * 2 * slim, PACK)
+    scale = 1.0 / tail[lines : lines + 1, :1]
+    for i in range(lines):
+        lanes = slice(i * rank, (i + 1) * rank)
+        down_out[:, lanes] = total(i * 2 * slim, slim) * scale
+        up_out[:, lanes] = total((2 * i + 1) * slim, slim) * scale
+        gain_out[:, lanes] = tail[i : i + 1, :] * scale
 
 
 def local(inputs, adapter_down, adapter_up, gains, head, labels, valid):
@@ -286,16 +267,20 @@
     shape = jax.ShapeDtypeStruct
 
     down2, up2, gains2 = (from_partner(v, "section", 1) for v in (down, up, gains))
-    mine = lax.dynamic_slice_in_dim(states, me * half, half, 0)
     small = 2 * rank * rank * features
+    own = call(
+        own_kernel,
+        shape((3 * half + 2 * rank + PACK, rank), BF16),
+        5 * small,
+        states, down, up, head, call(gain_kernel, shape(gains.shape, F32), 40 * small, gains),
+    )
     packed = call(
-        project_kernel,
+        other_kernel,
         shape((5 * half + 3 * rank + PACK, rank), BF16),
-        8 * small,
-        mine, down, up, gains, down2, up2, gains2, head,
+        3 * small,
+        states, up, own, down2, up2, gains2,
     )
     wide = [packed] + [from_partner(packed, "tensor", step) for step in range(1, tensors)]
-    far = [from_partner(mine, "dp", step) for step in range(1, replicas)]
     down_t, head_t, mixed = call(
         prepare_kernel,
         [shape((rank, features), BF16)] * 3,
@@ -311,33 +296,20 @@
         *wide, gram, gram2, labels, valid,
     )
     met = from_partner(theirs, "section", 1)
-    *parts, _, mix = call(
-        functools.partial(mix_kernel, replicas),
-        [shape((8 * slim, rank), BF16)] * replicas
-        + [shape((8 * rank, rank), BF16), shape((3 * rank, rank), BF16)],
-        16 * 2 * half * rank * rank,
-        made, met,
+    *parts, _ = call(
+        functools.partial(grad_kernel, replicas),
+        [shape((lines * 2 * slim + PACK, rank), BF16)] * replicas + [shape((2 * rank, features), BF16)],
+        16 * small,
+        made, met, states, down_t, head_t, up, up2, mixed, gains, valid,
     )
     parts = [parts[0]] + [from_partner(parts[step], "dp", step) for step in range(1, replicas)]
-    acc, tail = call(
-        gain_kernel,
-        [shape((2 * slim, features), F32), shape((2 * lines + PACK, rank), BF16)],
-        4 * small,
-        states, mix, parts[0], mixed, down_t, valid,
-    )
-    tails = [tail] + [from_partner(tail, "dp", step) for step in range(1, replicas)]
-    crossed = [from_partner(f, "section", 1) for f in far]
-    for part, own, other in zip(parts[1:], far, crossed):
-        acc = call(add_kernel, shape(acc.shape, F32), small, part, own, other, acc)
-    return tuple(
-        v[None] if v.shape[0] != 1 else v
-        for v in call(
-            functools.partial(last_kernel, replicas),
-            [shape((features, slim), F32), shape((slim, features), F32), shape((1, features), F32)],
-            4 * small,
-            *parts, *tails, acc, head_t, up, up2, mixed, gains,
-        )
-    )
+    down_grad, up_grad, gain_grad = call(
+        last_kernel,
+        [shape((slim, features), F32), shape((slim, features), F32), shape((1, features), F32)],
+        small,
+        *parts,
+    )
+    return down_grad.T[None], up_grad[None], gain_grad
 
 
 def solution(mesh):

time: 54 us -> 41.6 us (0.77)
  starting transfers between devices: 27 us -> 10.2 us
  waiting for transfers between devices: 17.3 us -> 24.7 us
  local copies, waits for them, and re-layouts: 2.84 us -> 0.72 us
  Pallas kernels: 5.75 us -> 4.95 us
    ppermute x20 -> x11, starting transfers between devices: 27 us -> 10.2 us  [from_partner(): lax.ppermute(value, axis, [(i, partner(i, step, size)) for i in range(siz...]
    ppermute x20 -> x11, waiting for transfers between devices: 17.3 us -> 24.7 us  [from_partner(): lax.ppermute(value, axis, [(i, partner(i, step, size)) for i in range(siz...]
    unnamed x17 -> x16, local copies, waits for them, and re-layouts: 1.81 us -> 0.72 us
    dynamic_slice x1 -> x0, local copies, waits for them, and re-layouts: 1.03 us -> none  [local(): mine = lax.dynamic_slice_in_dim(states, me * half, half, 0)]
    pallas_call x9 -> x7, Pallas kernels: 5.75 us -> 4.95 us  [call(): pl.pallas_call(kernel, out_shape=out, cost_estimate=pl.CostEstimate(flops...]
  transfers between devices with their start and end apart: 20 -> 11, of which waited for: 7 -> 7; matrix products, arithmetic and copies ran while one was open for 2% -> 0% of each run, Pallas kernels for 7% -> 2%
where the time goes in v3:
time: 41.6 us; the launch traced here: 41.4 us
  waiting for transfers between devices  24.7 us (59%)
  starting transfers between devices  10.2 us (25%)
  Pallas kernels  4.95 us (12%)
  between operations  0.75 us (2%)
  local copies, waits for them, and re-layouts  0.72 us (2%)
    ppermute x11, waiting for transfers between devices, from_partner(): lax.ppermute(value, axis, [(i, partner(i, step, size)) for i in range(siz...  24.7 us
    ppermute x11, starting transfers between devices, from_partner(): lax.ppermute(value, axis, [(i, partner(i, step, size)) for i in range(siz...  10.2 us
    pallas_call x7, Pallas kernels, call(): pl.pallas_call(kernel, out_shape=out, cost_estimate=pl.CostEstimate(flops...  4.95 us
  transfers between devices with their start and end apart: 11, of which 7 were waited for; matrix products, arithmetic and copies ran while one was open for 0% of the time, Pallas kernels for 2%

profile of v3, /device:TPU:0, one launch (start us, length us, event | category | flops | bytes accessed | tf_op | source)
XLA Modules:
  0.0 41.4 jit_solution(3026346751741901035)
XLA Ops:
  0.6 0.6 %collective-permute-start = (bf16[1024,128]{1,0:T(8,128)(2,1)}, bf16[1024,128]{1,0:T(8,128)(2,1)S(1)}, u32[]{:S(2)}, u32[]{:S(2)}) collective-permute-start(bf16[1024,128]{1,0:T(8,128)(2,1)} %bitcast.14), channel_id=1, source_target_pairs={{0,16},{16,0},{1,17},{17,1},{2,18},{18,2},{3,19},{19,3},{4,20},{20... | collective-permute-start | bytes 786440 | tf_op jit(solution)/shard_map/ppermute | solution.py:44
  1.2 0.1 collective-permute-start.1
  1.3 0.5 %collective-permute-start.2 = (bf16[1,1024]{1,0:T(2,128)(2,1)}, bf16[1,1024]{1,0:T(2,128)(2,1)S(1)}, u32[]{:S(2)}, u32[]{:S(2)}) collective-permute-start(bf16[1,1024]{1,0:T(2,128)(2,1)} %gain_ref.3), channel_id=1, source_target_pairs={{0,16},{16,0},{1,17},{17,1},{2,18},{18,2},{3,19},{19,3},{4,20},{20... | collective-permute-start | bytes 6152 | tf_op jit(solution)/shard_map/ppermute | solution.py:44
  1.8 0.7 %copy-done.4 = bf16[1,1024]{1,0:T(2,128)(2,1)S(1)} copy-done((bf16[1,1024]{1,0:T(2,128)(2,1)S(1)}, bf16[1,1024]{1,0:T(2,128)(2,1)}, u32[]{:S(2)}) %copy-start.4) | copy-done | bytes 2072
  2.5 0.5 %shard_map.95.own_ref = bf16[656,128]{1,0:T(8,128)(2,1)S(1)} custom-call(bf16[256,1024]{1,0:T(8,128)(2,1)S(1)} %bitcast.7, bf16[1024,128]{1,0:T(8,128)(2,1)S(1)} %bitcast.15, bf16[128,1024]{1,0:T(8,128)(2,1)S(1)} %bitcast.11, bf16[1024,128]{1,0:T(8,128)(2,1)S(1)} %copy-done.3, f32[1,1024]{1,0:T(1,128)S(1)} %shard_map.94.gain_ref), custom_call_target="tpu_custom_call" | custom-call | flops 167772160 | bytes 1314816 | tf_op jit(solution)/shard_map/pallas_call | solution.py:54
  3.0 0.5 %shard_map.96.refs_0_ = bf16[1040,128]{1,0:T(8,128)(2,1)S(1)} custom-call(bf16[256,1024]{1,0:T(8,128)(2,1)S(1)} %bitcast.8, bf16[128,1024]{1,0:T(8,128)(2,1)S(1)} %bitcast.12, bf16[656,128]{1,0:T(8,128)(2,1)S(1)} %shard_map.95.own_ref, bf16[1024,128]{1,0:T(8,128)(2,1)S(1)} %collective-permute-done.down2_ref, ...), custom_call_target="tpu_custom_call" | custom-call | flops 100663296 | bytes 1480704 | tf_op jit(solution)/shard_map/pallas_call | solution.py:54
  3.6 3.8 %collective-permute-start.5 = (bf16[1040,128]{1,0:T(8,128)(2,1)S(1)}, bf16[1040,128]{1,0:T(8,128)(2,1)S(1)}, u32[]{:S(2)}, u32[]{:S(2)}) collective-permute-start(bf16[1040,128]{1,0:T(8,128)(2,1)S(1)} %shard_map.96.refs_0_), channel_id=1, source_target_pairs={{0,3},{1,2},{2,1},{3,0},{4,7},{5,6},{6,5},{7,4},{8,11},{9,10},{10,... | collective-permute-start | bytes 798728 | tf_op jit(solution)/shard_map/ppermute | solution.py:44
  7.4 0.5 %collective-permute-start.4 = (bf16[1040,128]{1,0:T(8,128)(2,1)S(1)}, bf16[1040,128]{1,0:T(8,128)(2,1)S(1)}, u32[]{:S(2)}, u32[]{:S(2)}) collective-permute-start(bf16[1040,128]{1,0:T(8,128)(2,1)S(1)} %shard_map.96.refs_0_), channel_id=1, source_target_pairs={{0,2},{1,3},{2,0},{3,1},{4,6},{5,7},{6,4},{7,5},{8,10},{9,11},{10,... | collective-permute-start | bytes 798728 | tf_op jit(solution)/shard_map/ppermute | solution.py:44
  7.9 0.1 collective-permute-start.3
  8.0 6.6 %collective-permute-done.5.refs_3_ = bf16[1040,128]{1,0:T(8,128)(2,1)S(1)} collective-permute-done((bf16[1040,128]{1,0:T(8,128)(2,1)S(1)}, bf16[1040,128]{1,0:T(8,128)(2,1)S(1)}, u32[]{:S(2)}, u32[]{:S(2)}) %collective-permute-start.5) | collective-permute-done | bytes 266272 | tf_op jit(solution)/shard_map/ppermute | solution.py:44
  14.6 5.2 %collective-permute-done.4.refs_2_ = bf16[1040,128]{1,0:T(8,128)(2,1)S(1)} collective-permute-done((bf16[1040,128]{1,0:T(8,128)(2,1)S(1)}, bf16[1040,128]{1,0:T(8,128)(2,1)S(1)}, u32[]{:S(2)}, u32[]{:S(2)}) %collective-permute-start.4) | collective-permute-done | bytes 266272 | tf_op jit(solution)/shard_map/ppermute | solution.py:44
  19.9 0.3 collective-permute-done.3.refs_1_
  20.3 1.3 %collective-permute-done.6.refs_5_ = bf16[384,128]{1,0:T(8,128)(2,1)S(1)} collective-permute-done((bf16[384,128]{1,0:T(8,128)(2,1)S(1)}, bf16[384,128]{1,0:T(8,128)(2,1)S(1)}, u32[]{:S(2)}, u32[]{:S(2)}) %collective-permute-start.6) | collective-permute-done | bytes 98336 | tf_op jit(solution)/shard_map/ppermute | solution.py:44
  21.6 1.1 %shard_map.97 = (bf16[768,128]{1,0:T(8,128)(2,1)S(1)}, bf16[768,128]{1,0:T(8,128)(2,1)S(1)}) custom-call(bf16[1040,128]{1,0:T(8,128)(2,1)S(1)} %shard_map.96.refs_0_, bf16[1040,128]{1,0:T(8,128)(2,1)S(1)} %collective-permute-done.3.refs_1_, bf16[1040,128]{1,0:T(8,128)(2,1)S(1)} %collective-permute-done.4.refs_2_, ...), custom_call_target="tpu_custom_call" | custom-call | flops 67108864 | bytes 1263616 | tf_op jit(solution)/shard_map/pallas_call | solution.py:54
  22.7 0.2 collective-permute-start.7
  22.9 0.3 shard_map.98
  23.2 0.9 %collective-permute-done.7.theirs_ref = bf16[768,128]{1,0:T(8,128)(2,1)S(1)} collective-permute-done((bf16[768,128]{1,0:T(8,128)(2,1)S(1)}, bf16[768,128]{1,0:T(8,128)(2,1)S(1)}, u32[]{:S(2)}, u32[]{:S(2)}) %collective-permute-start.7) | collective-permute-done | bytes 196640 | tf_op jit(solution)/shard_map/ppermute | solution.py:44
  24.2 1.8 %shard_map.99 = (bf16[528,128]{1,0:T(8,128)(2,1)S(1)}, bf16[528,128]{1,0:T(8,128)(2,1)S(1)}, bf16[528,128]{1,0:T(8,128)(2,1)S(1)}, bf16[528,128]{1,0:T(8,128)(2,1)S(1)}, bf16[256,1024]{1,0:T(8,128)(2,1)}) custom-call(bf16[768,128]{1,0:T(8,128)(2,1)S(1)} %get-tuple-element.15.mine_ref, bf16[768,128]{1,0:T(8,128)(2,1)S(1)} %collective-permute-done.7.theirs_ref, ...), custom_call_target="tpu_custom_call" | custom-call | flops 536870912 | bytes 2231296 | tf_op jit(solution)/shard_map/pallas_call | solution.py:54
  26.0 1.6 %collective-permute-start.8 = (bf16[528,128]{1,0:T(8,128)(2,1)S(1)}, bf16[528,128]{1,0:T(8,128)(2,1)S(1)}, u32[]{:S(2)}, u32[]{:S(2)}) collective-permute-start(bf16[528,128]{1,0:T(8,128)(2,1)S(1)} %get-tuple-element.21), channel_id=1, source_target_pairs={{0,4},{4,0},{8,12},{12,8},{1,5},{5,1},{9,13},{13,9},{2,6},{6,2},{1... | collective-permute-start | bytes 405512 | tf_op jit(solution)/shard_map/ppermute | solution.py:44
  27.5 2.6 %collective-permute-start.9 = (bf16[528,128]{1,0:T(8,128)(2,1)S(1)}, bf16[528,128]{1,0:T(8,128)(2,1)S(1)}, u32[]{:S(2)}, u32[]{:S(2)}) collective-permute-start(bf16[528,128]{1,0:T(8,128)(2,1)S(1)} %get-tuple-element.22), channel_id=1, source_target_pairs={{0,8},{4,12},{8,0},{12,4},{1,9},{5,13},{9,1},{13,5},{2,10},{6,14},... | collective-permute-start | bytes 405512 | tf_op jit(solution)/shard_map/ppermute | solution.py:44
  30.1 0.2 collective-permute-start.10
  30.3 3.3 %collective-permute-done.8.refs_1_ = bf16[528,128]{1,0:T(8,128)(2,1)S(1)} collective-permute-done((bf16[528,128]{1,0:T(8,128)(2,1)S(1)}, bf16[528,128]{1,0:T(8,128)(2,1)S(1)}, u32[]{:S(2)}, u32[]{:S(2)}) %collective-permute-start.8) | collective-permute-done | bytes 135200 | tf_op jit(solution)/shard_map/ppermute | solution.py:44
  33.7 7.0 %collective-permute-done.9.refs_2_ = bf16[528,128]{1,0:T(8,128)(2,1)S(1)} collective-permute-done((bf16[528,128]{1,0:T(8,128)(2,1)S(1)}, bf16[528,128]{1,0:T(8,128)(2,1)S(1)}, u32[]{:S(2)}, u32[]{:S(2)}) %collective-permute-start.9) | collective-permute-done | bytes 135200 | tf_op jit(solution)/shard_map/ppermute | solution.py:44
  40.7 0.8 %shard_map.100 = (f32[32,1024]{1,0:T(8,128)}, f32[32,1024]{1,0:T(8,128)}, f32[1,1024]{1,0:T(1,128)}) custom-call(bf16[528,128]{1,0:T(8,128)(2,1)S(1)} %get-tuple-element.20.refs_0_, bf16[528,128]{1,0:T(8,128)(2,1)S(1)} %collective-permute-done.8.refs_1_, bf16[528,128]{1,0:T(8,128)(2,1)S(1)} %collective-permute-done.9.refs_2_, ...), custom_call_target="tpu_custom_call" | custom-call | flops 33554432 | bytes 540672 | tf_op jit(solution)/shard_map/pallas_call | solution.py:54
  (22 shorter events, 0.2 us)
Async XLA Ops:
  0.6 2.4 %collective-permute-start = (bf16[1024,128]{1,0:T(8,128)(2,1)}, bf16[1024,128]{1,0:T(8,128)(2,1)S(1)}, u32[]{:S(2)}, u32[]{:S(2)}) collective-permute-start(bf16[1024,128]{1,0:T(8,128)(2,1)} %bitcast.14), channel_id=1, source_target_pairs={{0,16},{16,0},{1,17},{17,1},{2,18},{18,2},{3,19},{19,3},{4,20},{20... | collective-permute-start | bytes 786440 | tf_op jit(solution)/shard_map/ppermute | solution.py:44
  1.2 1.3 %copy-start = (bf16[2,128,1024]{2,1,0:T(8,128)(2,1)S(1)}, bf16[2,128,1024]{2,1,0:T(8,128)(2,1)}, u32[]{:S(2)}) copy-start(bf16[2,128,1024]{2,1,0:T(8,128)(2,1)} %param.7) | copy-start | bytes 1572868
  1.2 1.3 %copy-start.1 = (bf16[1,128,1024]{2,1,0:T(8,128)(2,1)S(1)}, bf16[1,128,1024]{2,1,0:T(8,128)(2,1)}, u32[]{:S(2)}) copy-start(bf16[1,128,1024]{2,1,0:T(8,128)(2,1)} %param.9) | copy-start | bytes 786436
  1.2 1.3 %copy-start.2 = (bf16[1,1024,128]{2,1,0:T(8,128)(2,1)S(1)}, bf16[1,1024,128]{2,1,0:T(8,128)(2,1)}, u32[]{:S(2)}) copy-start(bf16[1,1024,128]{2,1,0:T(8,128)(2,1)} %param.8) | copy-start | bytes 786436
  1.2 1.3 %copy-start.3 = (bf16[1024,128]{1,0:T(8,128)(2,1)S(1)}, bf16[1024,128]{1,0:T(8,128)(2,1)}, u32[]{:S(2)}) copy-start(bf16[1024,128]{1,0:T(8,128)(2,1)} %head_ref.3) | copy-start | bytes 786436
  1.2 1.8 %collective-permute-start.1 = (bf16[128,1024]{1,0:T(8,128)(2,1)}, bf16[128,1024]{1,0:T(8,128)(2,1)S(1)}, u32[]{:S(2)}, u32[]{:S(2)}) collective-permute-start(bf16[128,1024]{1,0:T(8,128)(2,1)} %bitcast.10), channel_id=1, source_target_pairs={{0,16},{16,0},{1,17},{17,1},{2,18},{18,2},{3,19},{19,3},{4,20},{20... | collective-permute-start | bytes 786440 | tf_op jit(solution)/shard_map/ppermute | solution.py:44
  1.3 1.7 %collective-permute-start.2 = (bf16[1,1024]{1,0:T(2,128)(2,1)}, bf16[1,1024]{1,0:T(2,128)(2,1)S(1)}, u32[]{:S(2)}, u32[]{:S(2)}) collective-permute-start(bf16[1,1024]{1,0:T(2,128)(2,1)} %gain_ref.3), channel_id=1, source_target_pairs={{0,16},{16,0},{1,17},{17,1},{2,18},{18,2},{3,19},{19,3},{4,20},{20... | collective-permute-start | bytes 6152 | tf_op jit(solution)/shard_map/ppermute | solution.py:44
  1.8 0.7 %copy-start.4 = (bf16[1,1024]{1,0:T(2,128)(2,1)S(1)}, bf16[1,1024]{1,0:T(2,128)(2,1)}, u32[]{:S(2)}) copy-start(bf16[1,1024]{1,0:T(2,128)(2,1)} %gain_ref.3) | copy-start | bytes 6148
  3.6 18.0 %copy-start.6 = (s32[2,128]{1,0:T(2,128)S(1)}, s32[2,128]{1,0:T(2,128)}, u32[]{:S(2)}) copy-start(s32[2,128]{1,0:T(2,128)} %valid_ref.1) | copy-start | bytes 3076
  3.6 18.0 %copy-start.7 = (s32[2,128]{1,0:T(2,128)S(1)}, s32[2,128]{1,0:T(2,128)}, u32[]{:S(2)}) copy-start(s32[2,128]{1,0:T(2,128)} %refs_6_.1) | copy-start | bytes 3076
  3.6 11.1 %collective-permute-start.5 = (bf16[1040,128]{1,0:T(8,128)(2,1)S(1)}, bf16[1040,128]{1,0:T(8,128)(2,1)S(1)}, u32[]{:S(2)}, u32[]{:S(2)}) collective-permute-start(bf16[1040,128]{1,0:T(8,128)(2,1)S(1)} %shard_map.96.refs_0_), channel_id=1, source_target_pairs={{0,3},{1,2},{2,1},{3,0},{4,7},{5,6},{6,5},{7,4},{8,11},{9,10},{10,... | collective-permute-start | bytes 798728 | tf_op jit(solution)/shard_map/ppermute | solution.py:44
  7.4 12.5 %collective-permute-start.4 = (bf16[1040,128]{1,0:T(8,128)(2,1)S(1)}, bf16[1040,128]{1,0:T(8,128)(2,1)S(1)}, u32[]{:S(2)}, u32[]{:S(2)}) collective-permute-start(bf16[1040,128]{1,0:T(8,128)(2,1)S(1)} %shard_map.96.refs_0_), channel_id=1, source_target_pairs={{0,2},{1,3},{2,0},{3,1},{4,6},{5,7},{6,4},{7,5},{8,10},{9,11},{10,... | collective-permute-start | bytes 798728 | tf_op jit(solution)/shard_map/ppermute | solution.py:44
  7.9 12.3 %collective-permute-start.3 = (bf16[1040,128]{1,0:T(8,128)(2,1)S(1)}, bf16[1040,128]{1,0:T(8,128)(2,1)S(1)}, u32[]{:S(2)}, u32[]{:S(2)}) collective-permute-start(bf16[1040,128]{1,0:T(8,128)(2,1)S(1)} %shard_map.96.refs_0_), channel_id=1, source_target_pairs={{0,1},{1,0},{2,3},{3,2},{4,5},{5,4},{6,7},{7,6},{8,9},{9,8},{10,11... | collective-permute-start | bytes 798728 | tf_op jit(solution)/shard_map/ppermute | solution.py:44
  20.2 1.4 %collective-permute-start.6 = (bf16[384,128]{1,0:T(8,128)(2,1)S(1)}, bf16[384,128]{1,0:T(8,128)(2,1)S(1)}, u32[]{:S(2)}, u32[]{:S(2)}) collective-permute-start(bf16[384,128]{1,0:T(8,128)(2,1)S(1)} %add_convert_fusion.refs_4_), channel_id=1, source_target_pairs={{0,16},{16,0},{1,17},{17,1},{2,18},{18,2},{3,19},{19,3},{4,20},{20... | collective-permute-start | bytes 294920 | tf_op jit(solution)/shard_map/ppermute | solution.py:44
  22.7 1.5 %collective-permute-start.7 = (bf16[768,128]{1,0:T(8,128)(2,1)S(1)}, bf16[768,128]{1,0:T(8,128)(2,1)S(1)}, u32[]{:S(2)}, u32[]{:S(2)}) collective-permute-start(bf16[768,128]{1,0:T(8,128)(2,1)S(1)} %get-tuple-element.16), channel_id=1, source_target_pairs={{0,16},{16,0},{1,17},{17,1},{2,18},{18,2},{3,19},{19,3},{4,20},{20... | collective-permute-start | bytes 589832 | tf_op jit(solution)/shard_map/ppermute | solution.py:44
  23.2 1.0 %copy-start.5 = (bf16[1,1024]{1,0:T(2,128)(2,1)S(1)}, bf16[1,1024]{1,0:T(2,128)(2,1)}, u32[]{:S(2)}) copy-start(bf16[1,1024]{1,0:T(2,128)(2,1)} %gain_ref.3) | copy-start | bytes 6148
  26.0 7.7 %collective-permute-start.8 = (bf16[528,128]{1,0:T(8,128)(2,1)S(1)}, bf16[528,128]{1,0:T(8,128)(2,1)S(1)}, u32[]{:S(2)}, u32[]{:S(2)}) collective-permute-start(bf16[528,128]{1,0:T(8,128)(2,1)S(1)} %get-tuple-element.21), channel_id=1, source_target_pairs={{0,4},{4,0},{8,12},{12,8},{1,5},{5,1},{9,13},{13,9},{2,6},{6,2},{1... | collective-permute-start | bytes 405512 | tf_op jit(solution)/shard_map/ppermute | solution.py:44
  27.5 13.1 %collective-permute-start.9 = (bf16[528,128]{1,0:T(8,128)(2,1)S(1)}, bf16[528,128]{1,0:T(8,128)(2,1)S(1)}, u32[]{:S(2)}, u32[]{:S(2)}) collective-permute-start(bf16[528,128]{1,0:T(8,128)(2,1)S(1)} %get-tuple-element.22), channel_id=1, source_target_pairs={{0,8},{4,12},{8,0},{12,4},{1,9},{5,13},{9,1},{13,5},{2,10},{6,14},... | collective-permute-start | bytes 405512 | tf_op jit(solution)/shard_map/ppermute | solution.py:44
  30.1 10.6 %collective-permute-start.10 = (bf16[528,128]{1,0:T(8,128)(2,1)S(1)}, bf16[528,128]{1,0:T(8,128)(2,1)S(1)}, u32[]{:S(2)}, u32[]{:S(2)}) collective-permute-start(bf16[528,128]{1,0:T(8,128)(2,1)S(1)} %get-tuple-element.23), channel_id=1, source_target_pairs={{0,12},{4,8},{8,4},{12,0},{1,13},{5,9},{9,5},{13,1},{2,14},{6,10},... | collective-permute-start | bytes 405512 | tf_op jit(solution)/shard_map/ppermute | solution.py:44

commit v4 on v3

--- a/solution.py
+++ b/solution.py
@@ -7,6 +7,7 @@
 from jax.experimental.pallas import tpu as pltpu
 from jax.sharding import PartitionSpec as P
 
+
 epsilon = 1e-05
 F32 = jnp.float32
 BF16 = jnp.bfloat16
@@ -19,10 +20,6 @@
 
 def dot_nt(a, b):
     return lax.dot_general(a, b, (((1,), (1,)), ((), ())), preferred_element_type=F32)
-
-
-def dot_tn(a, b):
-    return lax.dot_general(a, b, (((0,), (0,)), ((), ())), preferred_element_type=F32)
 
 
 def rows_of(start, count):
@@ -79,18 +76,18 @@
     out_ref[3 * half + 2 * rank :, :] = high_low(squares[: PACK // 2])
 
 
-def other_kernel(x_ref, up_ref, own_ref, down2_ref, up2_ref, gain2_ref, out_ref):
+def other_kernel(x_ref, up_ref, own_ref, down2_ref, up2_ref, gain2_ref, out_ref, gram_ref):
     rank = down2_ref.shape[1]
     half = x_ref.shape[0] // lax.axis_size("section")
     me = lax.axis_index("section")
     it = 1 - me
     x = x_ref[rows_of(me * half, half), :]
     gain2 = gain2_ref[...].astype(F32)
-    base = 5 * half
     out_ref[rows_of(me * half, half), :] = own_ref[:half, :]
     out_ref[rows_of((2 + me) * half, half), :] = own_ref[half : 2 * half, :]
-    out_ref[4 * half : base, :] = own_ref[2 * half : 3 * half, :]
-    out_ref[base + rank :, :] = own_ref[3 * half :, :]
+    out_ref[4 * half : 5 * half, :] = own_ref[2 * half : 3 * half, :]
+    out_ref[5 * half :, :] = own_ref[3 * half + 2 * rank :, :]
+    gram_ref[rank:, :] = own_ref[3 * half : 3 * half + 2 * rank, :]
     scaled = (x.astype(F32) * gain2).astype(BF16)
     out_ref[rows_of(it * half, half), :] = dot(scaled, down2_ref[...]).astype(BF16)
     out_ref[rows_of((2 + it) * half, half), :] = dot_nt(x, up2_ref[...]).astype(BF16)
@@ -98,11 +95,15 @@
     @pl.when(me == 0)
     def _():
         scaled = (up_ref[...].astype(F32) * gain2).astype(BF16)
-        out_ref[base : base + rank, :] = dot(scaled, down2_ref[...]).astype(BF16)
+        gram_ref[:rank, :] = dot(scaled, down2_ref[...]).astype(BF16)
 
     @pl.when(me != 0)
     def _():
-        out_ref[base : base + rank, :] = dot_nt(up_ref[...], up2_ref[...]).astype(BF16)
+        gram_ref[:rank, :] = dot_nt(up_ref[...], up2_ref[...]).astype(BF16)
+
+
+def add_kernel(*refs):
+    refs[-1][...] = sum(r[...].astype(F32) for r in refs[:-1]).astype(BF16)
 
 
 def prepare_kernel(down_ref, head_ref, down2_ref, up2_ref, gain2_ref, down_t_ref, head_t_ref, mixed_ref):
@@ -136,7 +137,7 @@
     gram0, gram1 = jnp.where(first, gram, gram2), jnp.where(first, gram2, gram)
     m01, b0h, b0b0 = (gram0[i * rank : (i + 1) * rank] for i in range(3))
     b1b0, b1h, b1b1 = (gram1[i * rank : (i + 1) * rank] for i in range(3))
-    tail = total(5 * half + 3 * rank, PACK)
+    tail = total(5 * half, PACK)
     squares0 = spread(tail[:1] + tail[PACK // 2 : PACK // 2 + 1])
     inv0 = lax.rsqrt(squares0 / width + epsilon)
     proj0 = total(0, half)
@@ -184,37 +185,54 @@
         theirs_ref[slot * half : (slot + 1) * half, :] = jnp.where(first, b, a)
 
 
-def grad_kernel(replicas, mine_ref, theirs_ref, x_ref, down_t_ref, head_t_ref, up_ref, up2_ref, mixed_ref, gain_ref, valid_ref, *refs):
+def products(made, x):
+    half = x.shape[0]
+    first = lax.axis_index("section") == 0
+    hidden, last, scaled, weighted, extra1, extra2 = (made[i * half : (i + 1) * half] for i in range(6))
+    hidden_t, scaled_t, weighted_t = (transposed(v) for v in (hidden, scaled, weighted))
+    mixes = (
+        dot(hidden_t, last),
+        dot(scaled_t, hidden),
+        dot(jnp.where(first, hidden_t, scaled_t), extra2),
+        dot(jnp.where(first, hidden_t, weighted_t), extra1),
+    )
+    return mixes, dot(weighted_t, x), dot(scaled_t, x)
+
+
+def mine_kernel(made_ref, x_ref, mix_ref, acc_ref):
+    rank = made_ref.shape[1]
+    half = made_ref.shape[0] // 6
+    x = x_ref[rows_of(lax.axis_index("section") * half, half), :]
+    mixes, grad, rest = products(made_ref[...], x)
+    for i, mix in enumerate(mixes):
+        mix_ref[i * rank : (i + 1) * rank, :] = mix
+    acc_ref[:rank, :] = grad
+    acc_ref[rank:, :] = rest
+
+
+def grad_kernel(
+    replicas, made_ref, mix_ref, acc_ref, x_ref, down_t_ref, head_t_ref, up_ref, up2_ref, mixed_ref, gain_ref,
+    valid_ref, *refs
+):
     out_refs, all_ref = refs[:replicas], refs[replicas]
-    rank = mine_ref.shape[1]
-    half = mine_ref.shape[0] // 6
+    rank = made_ref.shape[1]
+    half = made_ref.shape[0] // 6
     features = x_ref.shape[1]
     slim = rank // replicas
-    first = lax.axis_index("section") == 0
-    mine, theirs = mine_ref[...], theirs_ref[...]
-    front, back = jnp.where(first, mine, theirs), jnp.where(first, theirs, mine)
-    hidden, last, scaled, weighted, extra1, extra2 = (
-        [v[i * half : (i + 1) * half] for v in (front, back)] for i in range(6)
-    )
-    hidden_t, scaled_t, weighted_t = ([transposed(v) for v in s] for s in (hidden, scaled, weighted))
-
-    def product(left, right):
-        return sum(dot(a, b) for a, b in zip(left, right))
-
-    left_oth = [jnp.where(first, a, b) for a, b in zip(hidden_t, scaled_t)]
-    left_mix = [jnp.where(first, a, b) for a, b in zip(hidden_t, weighted_t)]
-    head_mix = product(hidden_t, last).astype(BF16)
-    own_mix = product(scaled_t, hidden).astype(BF16)
-    oth_mix = product(left_oth, extra2).astype(BF16)
-    mix = product(left_mix, extra1).astype(BF16)
+    me = lax.axis_index("section")
+    first = me == 0
+    x = x_ref[rows_of((1 - me) * half, half), :]
+    mixes, grad, rest = products(made_ref[...], x)
+    head_mix, own_mix, oth_mix, mix = (
+        (m + mix_ref[i * rank : (i + 1) * rank, :]).astype(BF16) for i, m in enumerate(mixes)
+    )
     none = jnp.zeros_like(mix)
-    halves = [x_ref[i * half : (i + 1) * half, :] for i in range(2)]
     mixed = mixed_ref[...]
-    grad = product(weighted_t, halves) + dot(jnp.where(first, none, mix), mixed)
+    grad = grad + acc_ref[:rank, :] + dot(jnp.where(first, none, mix), mixed)
     gain = jnp.sum(grad * down_t_ref[...].astype(F32), axis=0, keepdims=True)
-    grad = (grad * gain_ref[...].astype(F32)).astype(BF16)
-    rest = dot(head_mix, head_t_ref[...]) + dot(jnp.where(first, mix, none), mixed)
-    rest = rest - dot(own_mix, up_ref[...]) - dot(oth_mix, up2_ref[...]) - product(scaled_t, halves)
+    grad = (grad * gain_ref[...]).astype(BF16)
+    rest = dot(head_mix, head_t_ref[...]) + dot(jnp.where(first, mix, none), mixed) - rest - acc_ref[rank:, :]
+    rest = rest - dot(own_mix, up_ref[...]) - dot(oth_mix, up2_ref[...])
     rest = rest.astype(BF16)
     for c in range(replicas):
         all_ref[2 * c * slim : (2 * c + 1) * slim, :] = grad[c * slim : (c + 1) * slim]
@@ -225,9 +243,9 @@
         [gain[:, i * rank : (i + 1) * rank] for i in range(lines)] + [jnp.broadcast_to(count, (PACK - lines, rank))],
         axis=0,
     ).astype(BF16)
-    me = lax.axis_index("dp")
+    place = lax.axis_index("dp")
     for step, out_ref in enumerate(out_refs):
-        block = all_ref[rows_of(partner(me, step, replicas) * 2 * slim, 2 * slim), :]
+        block = all_ref[rows_of(partner(place, step, replicas) * 2 * slim, 2 * slim), :]
         for i in range(lines):
             out_ref[i * 2 * slim : (i + 1) * 2 * slim, :] = block[:, i * rank : (i + 1) * rank]
         out_ref[lines * 2 * slim :, :] = tail
@@ -253,7 +271,6 @@
 
 def local(inputs, adapter_down, adapter_up, gains, head, labels, valid):
     sections, tensors, replicas = (lax.axis_size(a) for a in ("section", "tensor", "dp"))
-    me = lax.axis_index("section")
     features = inputs.shape[2]
     width = features * tensors
     rank = adapter_down.shape[2]
@@ -268,26 +285,41 @@
 
     down2, up2, gains2 = (from_partner(v, "section", 1) for v in (down, up, gains))
     small = 2 * rank * rank * features
+    wide_gain = call(gain_kernel, shape(gains.shape, F32), 40 * small, gains)
     own = call(
         own_kernel,
         shape((3 * half + 2 * rank + PACK, rank), BF16),
         5 * small,
-        states, down, up, head, call(gain_kernel, shape(gains.shape, F32), 40 * small, gains),
-    )
-    packed = call(
+        states, down, up, head, wide_gain,
+    )
+    packed, gram = call(
         other_kernel,
-        shape((5 * half + 3 * rank + PACK, rank), BF16),
+        [shape((5 * half + PACK, rank), BF16), shape((3 * rank, rank), BF16)],
         3 * small,
         states, up, own, down2, up2, gains2,
     )
-    wide = [packed] + [from_partner(packed, "tensor", step) for step in range(1, tensors)]
+    wide = [packed]
+    for step in range(1, tensors):
+        wide.append(from_partner(packed, "tensor", step))
     down_t, head_t, mixed = call(
         prepare_kernel,
         [shape((rank, features), BF16)] * 3,
         small,
         down, head, down2, up2, gains2,
     )
-    gram = sum(w[5 * half : 5 * half + 3 * rank].astype(F32) for w in wide).astype(BF16)
+    if tensors & (tensors - 1) == 0:
+        step = 1
+        while step < tensors:
+            gram = call(add_kernel, shape(gram.shape, BF16), small // 8, gram, from_partner(gram, "tensor", step))
+            step *= 2
+    else:
+        gram = call(
+            add_kernel,
+            shape(gram.shape, BF16),
+            small // 8,
+            gram,
+            *(from_partner(gram, "tensor", step) for step in range(1, tensors)),
+        )
     gram2 = from_partner(gram, "section", 1)
     made, theirs = call(
         functools.partial(chain_kernel, width, tensors),
@@ -296,13 +328,20 @@
         *wide, gram, gram2, labels, valid,
     )
     met = from_partner(theirs, "section", 1)
+    mixes, acc = call(
+        mine_kernel,
+        [shape((4 * rank, rank), F32), shape((2 * rank, features), F32)],
+        4 * small,
+        made, states,
+    )
     *parts, _ = call(
         functools.partial(grad_kernel, replicas),
         [shape((lines * 2 * slim + PACK, rank), BF16)] * replicas + [shape((2 * rank, features), BF16)],
         16 * small,
-        made, met, states, down_t, head_t, up, up2, mixed, gains, valid,
-    )
-    parts = [parts[0]] + [from_partner(parts[step], "dp", step) for step in range(1, replicas)]
+        met, mixes, acc, states, down_t, head_t, up, up2, mixed, wide_gain, valid,
+    )
+    for step in range(1, replicas):
+        parts[step] = from_partner(parts[step], "dp", step)
     down_grad, up_grad, gain_grad = call(
         last_kernel,
         [shape((slim, features), F32), shape((slim, features), F32), shape((1, features), F32)],

time: 41.6 us -> 41.7 us (level)
  waiting for transfers between devices: 24.7 us -> 20.9 us
  starting transfers between devices: 10.2 us -> 13.8 us
    ppermute x11 -> x13, waiting for transfers between devices: 24.7 us -> 20.9 us  [from_partner(): lax.ppermute(value, axis, [(i, partner(i, step, size)) for i in range(siz...]
    ppermute x11 -> x13, starting transfers between devices: 10.2 us -> 13.8 us  [from_partner(): lax.ppermute(value, axis, [(i, partner(i, step, size)) for i in range(siz...]
    pallas_call x7 -> x10, Pallas kernels: 4.95 us -> 5.3 us  [call(): pl.pallas_call(kernel, out_shape=out, cost_estimate=pl.CostEstimate(flops...]
  transfers between devices with their start and end apart: 11 -> 13, of which waited for: 7 -> 7; matrix products, arithmetic and copies ran while one was open for 0% -> 0% of each run, Pallas kernels for 2% -> 3%
where the time goes in v4:
time: 41.7 us; the launch traced here: 41.5 us
  waiting for transfers between devices  20.9 us (50%)
  starting transfers between devices  13.8 us (33%)
  Pallas kernels  5.3 us (13%)
  between operations  0.76 us (2%)
  local copies, waits for them, and re-layouts  0.71 us (2%)
    ppermute x13, waiting for transfers between devices, from_partner(): lax.ppermute(value, axis, [(i, partner(i, step, size)) for i in range(siz...  20.9 us
    ppermute x13, starting transfers between devices, from_partner(): lax.ppermute(value, axis, [(i, partner(i, step, size)) for i in range(siz...  13.8 us
    pallas_call x10, Pallas kernels, call(): pl.pallas_call(kernel, out_shape=out, cost_estimate=pl.CostEstimate(flops...  5.3 us
  transfers between devices with their start and end apart: 13, of which 7 were waited for; matrix products, arithmetic and copies ran while one was open for 0% of the time, Pallas kernels for 3%

profile of v4, /device:TPU:0, one launch (start us, length us, event | category | flops | bytes accessed | tf_op | source)
XLA Modules:
  0.0 41.5 jit_solution(1211103600548349388)
XLA Ops:
  0.6 0.6 %collective-permute-start = (bf16[1024,128]{1,0:T(8,128)(2,1)}, bf16[1024,128]{1,0:T(8,128)(2,1)S(1)}, u32[]{:S(2)}, u32[]{:S(2)}) collective-permute-start(bf16[1024,128]{1,0:T(8,128)(2,1)} %bitcast.15), channel_id=1, source_target_pairs={{0,16},{16,0},{1,17},{17,1},{2,18},{18,2},{3,19},{19,3},{4,20},{20... | collective-permute-start | bytes 786440 | tf_op jit(solution)/shard_map/ppermute | solution.py:41
  1.3 0.5 %collective-permute-start.2 = (bf16[1,1024]{1,0:T(2,128)(2,1)}, bf16[1,1024]{1,0:T(2,128)(2,1)S(1)}, u32[]{:S(2)}, u32[]{:S(2)}) collective-permute-start(bf16[1,1024]{1,0:T(2,128)(2,1)} %gain_ref.1), channel_id=1, source_target_pairs={{0,16},{16,0},{1,17},{17,1},{2,18},{18,2},{3,19},{19,3},{4,20},{20... | collective-permute-start | bytes 6152 | tf_op jit(solution)/shard_map/ppermute | solution.py:41
  1.8 0.7 %copy-done.6 = bf16[1,1024]{1,0:T(2,128)(2,1)S(1)} copy-done((bf16[1,1024]{1,0:T(2,128)(2,1)S(1)}, bf16[1,1024]{1,0:T(2,128)(2,1)}, u32[]{:S(2)}) %copy-start.6) | copy-done | bytes 2072
  2.5 0.5 %shard_map.95.own_ref = bf16[656,128]{1,0:T(8,128)(2,1)S(1)} custom-call(bf16[256,1024]{1,0:T(8,128)(2,1)S(1)} %bitcast.7, bf16[1024,128]{1,0:T(8,128)(2,1)S(1)} %bitcast.16, bf16[128,1024]{1,0:T(8,128)(2,1)S(1)} %bitcast.12, bf16[1024,128]{1,0:T(8,128)(2,1)S(1)} %copy-done.3, f32[1,1024]{1,0:T(1,128)S(1)} %shard_map.94.gain_ref), custom_call_target="tpu_custom_call" | custom-call | flops 167772160 | bytes 1314816 | tf_op jit(solution)/shard_map/pallas_call | solution.py:51
  3.0 0.5 %shard_map.96 = (bf16[656,128]{1,0:T(8,128)(2,1)S(1)}, bf16[384,128]{1,0:T(8,128)(2,1)S(1)}) custom-call(bf16[256,1024]{1,0:T(8,128)(2,1)S(1)} %bitcast.8, bf16[128,1024]{1,0:T(8,128)(2,1)S(1)} %bitcast.13, bf16[656,128]{1,0:T(8,128)(2,1)S(1)} %shard_map.95.own_ref, bf16[1024,128]{1,0:T(8,128)(2,1)S(1)} %collective-permute-done.down2_ref, ...), custom_call_target="tpu_custom_call" | custom-call | flops 100663296 | bytes 1480704 | tf_op jit(solution)/shard_map/pallas_call | solution.py:51
  3.6 2.8 %collective-permute-start.6 = (bf16[384,128]{1,0:T(8,128)(2,1)S(1)}, bf16[384,128]{1,0:T(8,128)(2,1)S(1)}, u32[]{:S(2)}, u32[]{:S(2)}) collective-permute-start(bf16[384,128]{1,0:T(8,128)(2,1)S(1)} %get-tuple-element.20.refs_0_), channel_id=1, source_target_pairs={{0,1},{1,0},{2,3},{3,2},{4,5},{5,4},{6,7},{7,6},{8,9},{9,8},{10,11... | collective-permute-start | bytes 294920 | tf_op jit(solution)/shard_map/ppermute | solution.py:41
  6.4 3.2 %collective-permute-done.6.refs_1_ = bf16[384,128]{1,0:T(8,128)(2,1)S(1)} collective-permute-done((bf16[384,128]{1,0:T(8,128)(2,1)S(1)}, bf16[384,128]{1,0:T(8,128)(2,1)S(1)}, u32[]{:S(2)}, u32[]{:S(2)}) %collective-permute-start.6) | collective-permute-done | bytes 98336 | tf_op jit(solution)/shard_map/ppermute | solution.py:41
  9.6 1.8 %collective-permute-start.7 = (bf16[384,128]{1,0:T(8,128)(2,1)S(1)}, bf16[384,128]{1,0:T(8,128)(2,1)S(1)}, u32[]{:S(2)}, u32[]{:S(2)}) collective-permute-start(bf16[384,128]{1,0:T(8,128)(2,1)S(1)} %shard_map.97.refs_0_), channel_id=1, source_target_pairs={{0,2},{1,3},{2,0},{3,1},{4,6},{5,7},{6,4},{7,5},{8,10},{9,11},{10,... | collective-permute-start | bytes 294920 | tf_op jit(solution)/shard_map/ppermute | solution.py:41
  11.5 1.4 %collective-permute-start.5 = (bf16[656,128]{1,0:T(8,128)(2,1)S(1)}, bf16[656,128]{1,0:T(8,128)(2,1)S(1)}, u32[]{:S(2)}, u32[]{:S(2)}) collective-permute-start(bf16[656,128]{1,0:T(8,128)(2,1)S(1)} %get-tuple-element.19.refs_0_), channel_id=1, source_target_pairs={{0,3},{1,2},{2,1},{3,0},{4,7},{5,6},{6,5},{7,4},{8,11},{9,10},{10,... | collective-permute-start | bytes 503816 | tf_op jit(solution)/shard_map/ppermute | solution.py:41
  12.9 1.5 %collective-permute-start.4 = (bf16[656,128]{1,0:T(8,128)(2,1)S(1)}, bf16[656,128]{1,0:T(8,128)(2,1)S(1)}, u32[]{:S(2)}, u32[]{:S(2)}) collective-permute-start(bf16[656,128]{1,0:T(8,128)(2,1)S(1)} %get-tuple-element.19.refs_0_), channel_id=1, source_target_pairs={{0,2},{1,3},{2,0},{3,1},{4,6},{5,7},{6,4},{7,5},{8,10},{9,11},{10,... | collective-permute-start | bytes 503816 | tf_op jit(solution)/shard_map/ppermute | solution.py:41
  14.4 0.5 %collective-permute-start.3 = (bf16[656,128]{1,0:T(8,128)(2,1)S(1)}, bf16[656,128]{1,0:T(8,128)(2,1)S(1)}, u32[]{:S(2)}, u32[]{:S(2)}) collective-permute-start(bf16[656,128]{1,0:T(8,128)(2,1)S(1)} %get-tuple-element.19.refs_0_), channel_id=1, source_target_pairs={{0,1},{1,0},{2,3},{3,2},{4,5},{5,4},{6,7},{7,6},{8,9},{9,8},{10,11... | collective-permute-start | bytes 503816 | tf_op jit(solution)/shard_map/ppermute | solution.py:41
  14.9 2.7 %collective-permute-done.7.refs_1_ = bf16[384,128]{1,0:T(8,128)(2,1)S(1)} collective-permute-done((bf16[384,128]{1,0:T(8,128)(2,1)S(1)}, bf16[384,128]{1,0:T(8,128)(2,1)S(1)}, u32[]{:S(2)}, u32[]{:S(2)}) %collective-permute-start.7) | collective-permute-done | bytes 98336 | tf_op jit(solution)/shard_map/ppermute | solution.py:41
  17.7 1.8 %collective-permute-done.5.refs_3_ = bf16[656,128]{1,0:T(8,128)(2,1)S(1)} collective-permute-done((bf16[656,128]{1,0:T(8,128)(2,1)S(1)}, bf16[656,128]{1,0:T(8,128)(2,1)S(1)}, u32[]{:S(2)}, u32[]{:S(2)}) %collective-permute-start.5) | collective-permute-done | bytes 167968 | tf_op jit(solution)/shard_map/ppermute | solution.py:41
  19.5 2.0 %collective-permute-done.4.refs_2_ = bf16[656,128]{1,0:T(8,128)(2,1)S(1)} collective-permute-done((bf16[656,128]{1,0:T(8,128)(2,1)S(1)}, bf16[656,128]{1,0:T(8,128)(2,1)S(1)}, u32[]{:S(2)}, u32[]{:S(2)}) %collective-permute-start.4) | collective-permute-done | bytes 167968 | tf_op jit(solution)/shard_map/ppermute | solution.py:41
  21.5 1.1 %shard_map.99 = (bf16[768,128]{1,0:T(8,128)(2,1)S(1)}, bf16[768,128]{1,0:T(8,128)(2,1)S(1)}) custom-call(bf16[656,128]{1,0:T(8,128)(2,1)S(1)} %get-tuple-element.19.refs_0_, bf16[656,128]{1,0:T(8,128)(2,1)S(1)} %collective-permute-done.3.refs_1_, bf16[656,128]{1,0:T(8,128)(2,1)S(1)} %collective-permute-done.4.refs_2_, ...), custom_call_target="tpu_custom_call" | custom-call | flops 67108864 | bytes 870400 | tf_op jit(solution)/shard_map/pallas_call | solution.py:51
  22.7 0.3 shard_map.101
  23.0 0.4 shard_map.100
  23.4 0.7 %collective-permute-done.9.made_ref = bf16[768,128]{1,0:T(8,128)(2,1)S(1)} collective-permute-done((bf16[768,128]{1,0:T(8,128)(2,1)S(1)}, bf16[768,128]{1,0:T(8,128)(2,1)S(1)}, u32[]{:S(2)}, u32[]{:S(2)}) %collective-permute-start.9) | collective-permute-done | bytes 196640 | tf_op jit(solution)/shard_map/ppermute | solution.py:41
  24.1 1.7 %shard_map.102 = (bf16[528,128]{1,0:T(8,128)(2,1)S(1)}, bf16[528,128]{1,0:T(8,128)(2,1)S(1)}, bf16[528,128]{1,0:T(8,128)(2,1)S(1)}, bf16[528,128]{1,0:T(8,128)(2,1)S(1)}, bf16[256,1024]{1,0:T(8,128)(2,1)}) custom-call(bf16[768,128]{1,0:T(8,128)(2,1)S(1)} %collective-permute-done.9.made_ref, f32[512,128]{1,0:T(8,128)S(1)} %get-tuple-element.23.mix_ref, ...), custom_call_target="tpu_custom_call" | custom-call | flops 536870912 | bytes 3347456 | tf_op jit(solution)/shard_map/pallas_call | solution.py:51
  25.8 1.8 %collective-permute-start.10 = (bf16[528,128]{1,0:T(8,128)(2,1)S(1)}, bf16[528,128]{1,0:T(8,128)(2,1)S(1)}, u32[]{:S(2)}, u32[]{:S(2)}) collective-permute-start(bf16[528,128]{1,0:T(8,128)(2,1)S(1)} %get-tuple-element.29), channel_id=1, source_target_pairs={{0,4},{4,0},{8,12},{12,8},{1,5},{5,1},{9,13},{13,9},{2,6},{6,2},{1... | collective-permute-start | bytes 405512 | tf_op jit(solution)/shard_map/ppermute | solution.py:41
  27.6 2.6 %collective-permute-start.11 = (bf16[528,128]{1,0:T(8,128)(2,1)S(1)}, bf16[528,128]{1,0:T(8,128)(2,1)S(1)}, u32[]{:S(2)}, u32[]{:S(2)}) collective-permute-start(bf16[528,128]{1,0:T(8,128)(2,1)S(1)} %get-tuple-element.30), channel_id=1, source_target_pairs={{0,8},{4,12},{8,0},{12,4},{1,9},{5,13},{9,1},{13,5},{2,10},{6,14},... | collective-permute-start | bytes 405512 | tf_op jit(solution)/shard_map/ppermute | solution.py:41
  30.2 3.3 %collective-permute-done.10.refs_1_ = bf16[528,128]{1,0:T(8,128)(2,1)S(1)} collective-permute-done((bf16[528,128]{1,0:T(8,128)(2,1)S(1)}, bf16[528,128]{1,0:T(8,128)(2,1)S(1)}, u32[]{:S(2)}, u32[]{:S(2)}) %collective-permute-start.10) | collective-permute-done | bytes 135200 | tf_op jit(solution)/shard_map/ppermute | solution.py:41
  33.5 7.3 %collective-permute-done.11.refs_2_ = bf16[528,128]{1,0:T(8,128)(2,1)S(1)} collective-permute-done((bf16[528,128]{1,0:T(8,128)(2,1)S(1)}, bf16[528,128]{1,0:T(8,128)(2,1)S(1)}, u32[]{:S(2)}, u32[]{:S(2)}) %collective-permute-start.11) | collective-permute-done | bytes 135200 | tf_op jit(solution)/shard_map/ppermute | solution.py:41
  40.8 0.8 %shard_map.103 = (f32[32,1024]{1,0:T(8,128)}, f32[32,1024]{1,0:T(8,128)}, f32[1,1024]{1,0:T(1,128)}) custom-call(bf16[528,128]{1,0:T(8,128)(2,1)S(1)} %get-tuple-element.28.refs_0_, bf16[528,128]{1,0:T(8,128)(2,1)S(1)} %collective-permute-done.10.refs_1_, bf16[528,128]{1,0:T(8,128)(2,1)S(1)} %collective-permute-done.11.refs_2_, ...), custom_call_target="tpu_custom_call" | custom-call | flops 33554432 | bytes 540672 | tf_op jit(solution)/shard_map/pallas_call | solution.py:51
  (26 shorter events, 0.4 us)
Async XLA Ops:
  0.6 2.4 %collective-permute-start = (bf16[1024,128]{1,0:T(8,128)(2,1)}, bf16[1024,128]{1,0:T(8,128)(2,1)S(1)}, u32[]{:S(2)}, u32[]{:S(2)}) collective-permute-start(bf16[1024,128]{1,0:T(8,128)(2,1)} %bitcast.15), channel_id=1, source_target_pairs={{0,16},{16,0},{1,17},{17,1},{2,18},{18,2},{3,19},{19,3},{4,20},{20... | collective-permute-start | bytes 786440 | tf_op jit(solution)/shard_map/ppermute | solution.py:41
  1.2 1.3 %copy-start = (bf16[2,128,1024]{2,1,0:T(8,128)(2,1)S(1)}, bf16[2,128,1024]{2,1,0:T(8,128)(2,1)}, u32[]{:S(2)}) copy-start(bf16[2,128,1024]{2,1,0:T(8,128)(2,1)} %param.7) | copy-start | bytes 1572868
  1.2 1.3 %copy-start.1 = (bf16[1,128,1024]{2,1,0:T(8,128)(2,1)S(1)}, bf16[1,128,1024]{2,1,0:T(8,128)(2,1)}, u32[]{:S(2)}) copy-start(bf16[1,128,1024]{2,1,0:T(8,128)(2,1)} %param.9) | copy-start | bytes 786436
  1.2 1.3 %copy-start.2 = (bf16[1,1024,128]{2,1,0:T(8,128)(2,1)S(1)}, bf16[1,1024,128]{2,1,0:T(8,128)(2,1)}, u32[]{:S(2)}) copy-start(bf16[1,1024,128]{2,1,0:T(8,128)(2,1)} %param.8) | copy-start | bytes 786436
  1.2 1.3 %copy-start.3 = (bf16[1024,128]{1,0:T(8,128)(2,1)S(1)}, bf16[1024,128]{1,0:T(8,128)(2,1)}, u32[]{:S(2)}) copy-start(bf16[1024,128]{1,0:T(8,128)(2,1)} %head_ref.3) | copy-start | bytes 786436
  1.2 1.8 %collective-permute-start.1 = (bf16[128,1024]{1,0:T(8,128)(2,1)}, bf16[128,1024]{1,0:T(8,128)(2,1)S(1)}, u32[]{:S(2)}, u32[]{:S(2)}) collective-permute-start(bf16[128,1024]{1,0:T(8,128)(2,1)} %bitcast.11), channel_id=1, source_target_pairs={{0,16},{16,0},{1,17},{17,1},{2,18},{18,2},{3,19},{19,3},{4,20},{20... | collective-permute-start | bytes 786440 | tf_op jit(solution)/shard_map/ppermute | solution.py:41
  1.3 1.7 %collective-permute-start.2 = (bf16[1,1024]{1,0:T(2,128)(2,1)}, bf16[1,1024]{1,0:T(2,128)(2,1)S(1)}, u32[]{:S(2)}, u32[]{:S(2)}) collective-permute-start(bf16[1,1024]{1,0:T(2,128)(2,1)} %gain_ref.1), channel_id=1, source_target_pairs={{0,16},{16,0},{1,17},{17,1},{2,18},{18,2},{3,19},{19,3},{4,20},{20... | collective-permute-start | bytes 6152 | tf_op jit(solution)/shard_map/ppermute | solution.py:41
  1.8 0.7 %copy-start.6 = (bf16[1,1024]{1,0:T(2,128)(2,1)S(1)}, bf16[1,1024]{1,0:T(2,128)(2,1)}, u32[]{:S(2)}) copy-start(bf16[1,1024]{1,0:T(2,128)(2,1)} %gain_ref.1) | copy-start | bytes 6148
  3.6 6.0 %collective-permute-start.6 = (bf16[384,128]{1,0:T(8,128)(2,1)S(1)}, bf16[384,128]{1,0:T(8,128)(2,1)S(1)}, u32[]{:S(2)}, u32[]{:S(2)}) collective-permute-start(bf16[384,128]{1,0:T(8,128)(2,1)S(1)} %get-tuple-element.20.refs_0_), channel_id=1, source_target_pairs={{0,1},{1,0},{2,3},{3,2},{4,5},{5,4},{6,7},{7,6},{8,9},{9,8},{10,11... | collective-permute-start | bytes 294920 | tf_op jit(solution)/shard_map/ppermute | solution.py:41
  9.6 8.0 %collective-permute-start.7 = (bf16[384,128]{1,0:T(8,128)(2,1)S(1)}, bf16[384,128]{1,0:T(8,128)(2,1)S(1)}, u32[]{:S(2)}, u32[]{:S(2)}) collective-permute-start(bf16[384,128]{1,0:T(8,128)(2,1)S(1)} %shard_map.97.refs_0_), channel_id=1, source_target_pairs={{0,2},{1,3},{2,0},{3,1},{4,6},{5,7},{6,4},{7,5},{8,10},{9,11},{10,... | collective-permute-start | bytes 294920 | tf_op jit(solution)/shard_map/ppermute | solution.py:41
  11.5 10.1 %copy-start.4 = (s32[2,128]{1,0:T(2,128)S(1)}, s32[2,128]{1,0:T(2,128)}, u32[]{:S(2)}) copy-start(s32[2,128]{1,0:T(2,128)} %valid_ref.1) | copy-start | bytes 3076
  11.5 10.1 %copy-start.5 = (s32[2,128]{1,0:T(2,128)S(1)}, s32[2,128]{1,0:T(2,128)}, u32[]{:S(2)}) copy-start(s32[2,128]{1,0:T(2,128)} %refs_6_.1) | copy-start | bytes 3076
  11.5 8.1 %collective-permute-start.5 = (bf16[656,128]{1,0:T(8,128)(2,1)S(1)}, bf16[656,128]{1,0:T(8,128)(2,1)S(1)}, u32[]{:S(2)}, u32[]{:S(2)}) collective-permute-start(bf16[656,128]{1,0:T(8,128)(2,1)S(1)} %get-tuple-element.19.refs_0_), channel_id=1, source_target_pairs={{0,3},{1,2},{2,1},{3,0},{4,7},{5,6},{6,5},{7,4},{8,11},{9,10},{10,... | collective-permute-start | bytes 503816 | tf_op jit(solution)/shard_map/ppermute | solution.py:41
  12.9 8.6 %collective-permute-start.4 = (bf16[656,128]{1,0:T(8,128)(2,1)S(1)}, bf16[656,128]{1,0:T(8,128)(2,1)S(1)}, u32[]{:S(2)}, u32[]{:S(2)}) collective-permute-start(bf16[656,128]{1,0:T(8,128)(2,1)S(1)} %get-tuple-element.19.refs_0_), channel_id=1, source_target_pairs={{0,2},{1,3},{2,0},{3,1},{4,6},{5,7},{6,4},{7,5},{8,10},{9,11},{10,... | collective-permute-start | bytes 503816 | tf_op jit(solution)/shard_map/ppermute | solution.py:41
  14.4 7.1 %collective-permute-start.3 = (bf16[656,128]{1,0:T(8,128)(2,1)S(1)}, bf16[656,128]{1,0:T(8,128)(2,1)S(1)}, u32[]{:S(2)}, u32[]{:S(2)}) collective-permute-start(bf16[656,128]{1,0:T(8,128)(2,1)S(1)} %get-tuple-element.19.refs_0_), channel_id=1, source_target_pairs={{0,1},{1,0},{2,3},{3,2},{4,5},{5,4},{6,7},{7,6},{8,9},{9,8},{10,11... | collective-permute-start | bytes 503816 | tf_op jit(solution)/shard_map/ppermute | solution.py:41
  17.6 3.9 %collective-permute-start.8 = (bf16[384,128]{1,0:T(8,128)(2,1)S(1)}, bf16[384,128]{1,0:T(8,128)(2,1)S(1)}, u32[]{:S(2)}, u32[]{:S(2)}) collective-permute-start(bf16[384,128]{1,0:T(8,128)(2,1)S(1)} %shard_map.98.refs_4_), channel_id=1, source_target_pairs={{0,16},{16,0},{1,17},{17,1},{2,18},{18,2},{3,19},{19,3},{4,20},{20... | collective-permute-start | bytes 294920 | tf_op jit(solution)/shard_map/ppermute | solution.py:41
  22.6 1.5 %collective-permute-start.9 = (bf16[768,128]{1,0:T(8,128)(2,1)S(1)}, bf16[768,128]{1,0:T(8,128)(2,1)S(1)}, u32[]{:S(2)}, u32[]{:S(2)}) collective-permute-start(bf16[768,128]{1,0:T(8,128)(2,1)S(1)} %get-tuple-element.21), channel_id=1, source_target_pairs={{0,16},{16,0},{1,17},{17,1},{2,18},{18,2},{3,19},{19,3},{4,20},{20... | collective-permute-start | bytes 589832 | tf_op jit(solution)/shard_map/ppermute | solution.py:41
  25.8 7.7 %collective-permute-start.10 = (bf16[528,128]{1,0:T(8,128)(2,1)S(1)}, bf16[528,128]{1,0:T(8,128)(2,1)S(1)}, u32[]{:S(2)}, u32[]{:S(2)}) collective-permute-start(bf16[528,128]{1,0:T(8,128)(2,1)S(1)} %get-tuple-element.29), channel_id=1, source_target_pairs={{0,4},{4,0},{8,12},{12,8},{1,5},{5,1},{9,13},{13,9},{2,6},{6,2},{1... | collective-permute-start | bytes 405512 | tf_op jit(solution)/shard_map/ppermute | solution.py:41
  27.6 13.2 %collective-permute-start.11 = (bf16[528,128]{1,0:T(8,128)(2,1)S(1)}, bf16[528,128]{1,0:T(8,128)(2,1)S(1)}, u32[]{:S(2)}, u32[]{:S(2)}) collective-permute-start(bf16[528,128]{1,0:T(8,128)(2,1)S(1)} %get-tuple-element.30), channel_id=1, source_target_pairs={{0,8},{4,12},{8,0},{12,4},{1,9},{5,13},{9,1},{13,5},{2,10},{6,14},... | collective-permute-start | bytes 405512 | tf_op jit(solution)/shard_map/ppermute | solution.py:41
  30.2 10.6 %collective-permute-start.12 = (bf16[528,128]{1,0:T(8,128)(2,1)S(1)}, bf16[528,128]{1,0:T(8,128)(2,1)S(1)}, u32[]{:S(2)}, u32[]{:S(2)}) collective-permute-start(bf16[528,128]{1,0:T(8,128)(2,1)S(1)} %get-tuple-element.31), channel_id=1, source_target_pairs={{0,12},{4,8},{8,4},{12,0},{1,13},{5,9},{9,5},{13,1},{2,14},{6,10},... | collective-permute-start | bytes 405512 | tf_op jit(solution)/shard_map/ppermute | solution.py:41

commit v5 on v4

--- a/solution.py
+++ b/solution.py
@@ -106,18 +106,24 @@
     refs[-1][...] = sum(r[...].astype(F32) for r in refs[:-1]).astype(BF16)
 
 
-def prepare_kernel(down_ref, head_ref, down2_ref, up2_ref, gain2_ref, down_t_ref, head_t_ref, mixed_ref):
+def prepare_kernel(down_ref, head_ref, up_ref, down2_ref, up2_ref, gain2_ref, x_ref, down_t_ref, stack_ref):
+    rank = up_ref.shape[0]
+    half = x_ref.shape[0] // lax.axis_size("section")
     down_t_ref[...] = transposed(down_ref[...])
-    head_t_ref[...] = transposed(head_ref[...])
+    stack_ref[:rank, :] = transposed(head_ref[...])
+    stack_ref[rank : 2 * rank, :] = up_ref[...]
+    stack_ref[2 * rank : 3 * rank, :] = up2_ref[...]
     me = lax.axis_index("section")
 
     @pl.when(me == 0)
     def _():
-        mixed_ref[...] = (down2_ref[...].astype(F32).T * gain2_ref[...].astype(F32)).astype(BF16)
+        stack_ref[3 * rank : 4 * rank, :] = (down2_ref[...].astype(F32).T * gain2_ref[...].astype(F32)).astype(BF16)
 
     @pl.when(me != 0)
     def _():
-        mixed_ref[...] = up2_ref[...]
+        stack_ref[3 * rank : 4 * rank, :] = up2_ref[...]
+
+    stack_ref[4 * rank :, :] = x_ref[rows_of((1 - me) * half, half), :]
 
 
 def chain_kernel(width, count, *refs):
@@ -185,55 +191,47 @@
         theirs_ref[slot * half : (slot + 1) * half, :] = jnp.where(first, b, a)
 
 
-def products(made, x):
-    half = x.shape[0]
+def products(made):
+    half = made.shape[0] // 6
     first = lax.axis_index("section") == 0
     hidden, last, scaled, weighted, extra1, extra2 = (made[i * half : (i + 1) * half] for i in range(6))
-    hidden_t, scaled_t, weighted_t = (transposed(v) for v in (hidden, scaled, weighted))
+    hidden_t, scaled_t, weighted_t = (transposed(v) for v in (hidden, -scaled, weighted))
     mixes = (
         dot(hidden_t, last),
         dot(scaled_t, hidden),
-        dot(jnp.where(first, hidden_t, scaled_t), extra2),
+        dot(jnp.where(first, -hidden_t, scaled_t), extra2),
         dot(jnp.where(first, hidden_t, weighted_t), extra1),
     )
-    return mixes, dot(weighted_t, x), dot(scaled_t, x)
+    return mixes, weighted_t, scaled_t
 
 
 def mine_kernel(made_ref, x_ref, mix_ref, acc_ref):
     rank = made_ref.shape[1]
     half = made_ref.shape[0] // 6
     x = x_ref[rows_of(lax.axis_index("section") * half, half), :]
-    mixes, grad, rest = products(made_ref[...], x)
+    mixes, weighted_t, scaled_t = products(made_ref[...])
     for i, mix in enumerate(mixes):
         mix_ref[i * rank : (i + 1) * rank, :] = mix
-    acc_ref[:rank, :] = grad
-    acc_ref[rank:, :] = rest
-
-
-def grad_kernel(
-    replicas, made_ref, mix_ref, acc_ref, x_ref, down_t_ref, head_t_ref, up_ref, up2_ref, mixed_ref, gain_ref,
-    valid_ref, *refs
-):
+    acc_ref[:rank, :] = dot(weighted_t, x)
+    acc_ref[rank:, :] = dot(scaled_t, x)
+
+
+def grad_kernel(replicas, made_ref, mix_ref, acc_ref, stack_ref, down_t_ref, gain_ref, valid_ref, *refs):
     out_refs, all_ref = refs[:replicas], refs[replicas]
-    rank = made_ref.shape[1]
-    half = made_ref.shape[0] // 6
-    features = x_ref.shape[1]
+    rank, features = down_t_ref.shape
     slim = rank // replicas
-    me = lax.axis_index("section")
-    first = me == 0
-    x = x_ref[rows_of((1 - me) * half, half), :]
-    mixes, grad, rest = products(made_ref[...], x)
+    first = lax.axis_index("section") == 0
+    mixes, weighted_t, scaled_t = products(made_ref[...])
     head_mix, own_mix, oth_mix, mix = (
         (m + mix_ref[i * rank : (i + 1) * rank, :]).astype(BF16) for i, m in enumerate(mixes)
     )
     none = jnp.zeros_like(mix)
-    mixed = mixed_ref[...]
-    grad = grad + acc_ref[:rank, :] + dot(jnp.where(first, none, mix), mixed)
+    left = jnp.concatenate([jnp.where(first, none, mix), weighted_t], axis=1)
+    grad = acc_ref[:rank, :] + dot(left, stack_ref[3 * rank :, :])
     gain = jnp.sum(grad * down_t_ref[...].astype(F32), axis=0, keepdims=True)
     grad = (grad * gain_ref[...]).astype(BF16)
-    rest = dot(head_mix, head_t_ref[...]) + dot(jnp.where(first, mix, none), mixed) - rest - acc_ref[rank:, :]
-    rest = rest - dot(own_mix, up_ref[...]) - dot(oth_mix, up2_ref[...])
-    rest = rest.astype(BF16)
+    left = jnp.concatenate([head_mix, own_mix, oth_mix, jnp.where(first, mix, none), scaled_t], axis=1)
+    rest = (acc_ref[rank:, :] + dot(left, stack_ref[...])).astype(BF16)
     for c in range(replicas):
         all_ref[2 * c * slim : (2 * c + 1) * slim, :] = grad[c * slim : (c + 1) * slim]
         all_ref[(2 * c + 1) * slim : (2 * c + 2) * slim, :] = rest[c * slim : (c + 1) * slim]
@@ -301,11 +299,11 @@
     wide = [packed]
     for step in range(1, tensors):
         wide.append(from_partner(packed, "tensor", step))
-    down_t, head_t, mixed = call(
+    down_t, stack = call(
         prepare_kernel,
-        [shape((rank, features), BF16)] * 3,
+        [shape((rank, features), BF16), shape((4 * rank + half, features), BF16)],
         small,
-        down, head, down2, up2, gains2,
+        down, head, up, down2, up2, gains2, states,
     )
     if tensors & (tensors - 1) == 0:
         step = 1
@@ -338,7 +336,7 @@
         functools.partial(grad_kernel, replicas),
         [shape((lines * 2 * slim + PACK, rank), BF16)] * replicas + [shape((2 * rank, features), BF16)],
         16 * small,
-        met, mixes, acc, states, down_t, head_t, up, up2, mixed, wide_gain, valid,
+        met, mixes, acc, stack, down_t, wide_gain, valid,
     )
     for step in range(1, replicas):
         parts[step] = from_partner(parts[step], "dp", step)

time: 41.7 us -> 41.6 us (level)
  no operation moved by 1% of the time
where the time goes in v5:
time: 41.6 us; the launch traced here: 41.4 us
  waiting for transfers between devices  20.9 us (50%)
  starting transfers between devices  13.8 us (33%)
  Pallas kernels  5.2 us (12%)
  between operations  0.77 us (2%)
  local copies, waits for them, and re-layouts  0.71 us (2%)
    ppermute x13, waiting for transfers between devices, from_partner(): lax.ppermute(value, axis, [(i, partner(i, step, size)) for i in range(siz...  20.9 us
    ppermute x13, starting transfers between devices, from_partner(): lax.ppermute(value, axis, [(i, partner(i, step, size)) for i in range(siz...  13.8 us
    pallas_call x10, Pallas kernels, call(): pl.pallas_call(kernel, out_shape=out, cost_estimate=pl.CostEstimate(flops...  5.2 us
  transfers between devices with their start and end apart: 13, of which 7 were waited for; matrix products, arithmetic and copies ran while one was open for 0% of the time, Pallas kernels for 3%

profile of v5, /device:TPU:0, one launch (start us, length us, event | category | flops | bytes accessed | tf_op | source)
XLA Modules:
  0.0 41.4 jit_solution(1303384828615602229)
XLA Ops:
  0.6 0.6 %collective-permute-start = (bf16[1024,128]{1,0:T(8,128)(2,1)}, bf16[1024,128]{1,0:T(8,128)(2,1)S(1)}, u32[]{:S(2)}, u32[]{:S(2)}) collective-permute-start(bf16[1024,128]{1,0:T(8,128)(2,1)} %bitcast.15), channel_id=1, source_target_pairs={{0,16},{16,0},{1,17},{17,1},{2,18},{18,2},{3,19},{19,3},{4,20},{20... | collective-permute-start | bytes 786440 | tf_op jit(solution)/shard_map/ppermute | solution.py:41
  1.3 0.5 %collective-permute-start.2 = (bf16[1,1024]{1,0:T(2,128)(2,1)}, bf16[1,1024]{1,0:T(2,128)(2,1)S(1)}, u32[]{:S(2)}, u32[]{:S(2)}) collective-permute-start(bf16[1,1024]{1,0:T(2,128)(2,1)} %gain_ref.1), channel_id=1, source_target_pairs={{0,16},{16,0},{1,17},{17,1},{2,18},{18,2},{3,19},{19,3},{4,20},{20... | collective-permute-start | bytes 6152 | tf_op jit(solution)/shard_map/ppermute | solution.py:41
  1.8 0.7 %copy-done.6 = bf16[1,1024]{1,0:T(2,128)(2,1)S(1)} copy-done((bf16[1,1024]{1,0:T(2,128)(2,1)S(1)}, bf16[1,1024]{1,0:T(2,128)(2,1)}, u32[]{:S(2)}) %copy-start.6) | copy-done | bytes 2072
  2.5 0.5 %shard_map.95.own_ref = bf16[656,128]{1,0:T(8,128)(2,1)S(1)} custom-call(bf16[256,1024]{1,0:T(8,128)(2,1)S(1)} %bitcast.7, bf16[1024,128]{1,0:T(8,128)(2,1)S(1)} %bitcast.16, bf16[128,1024]{1,0:T(8,128)(2,1)S(1)} %bitcast.12, bf16[1024,128]{1,0:T(8,128)(2,1)S(1)} %copy-done.3, f32[1,1024]{1,0:T(1,128)S(1)} %shard_map.94.gain_ref), custom_call_target="tpu_custom_call" | custom-call | flops 167772160 | bytes 1314816 | tf_op jit(solution)/shard_map/pallas_call | solution.py:51
  3.1 0.5 %shard_map.96 = (bf16[656,128]{1,0:T(8,128)(2,1)S(1)}, bf16[384,128]{1,0:T(8,128)(2,1)S(1)}) custom-call(bf16[256,1024]{1,0:T(8,128)(2,1)S(1)} %bitcast.8, bf16[128,1024]{1,0:T(8,128)(2,1)S(1)} %bitcast.13, bf16[656,128]{1,0:T(8,128)(2,1)S(1)} %shard_map.95.own_ref, bf16[1024,128]{1,0:T(8,128)(2,1)S(1)} %collective-permute-done.down2_ref, ...), custom_call_target="tpu_custom_call" | custom-call | flops 100663296 | bytes 1480704 | tf_op jit(solution)/shard_map/pallas_call | solution.py:51
  3.6 2.8 %collective-permute-start.6 = (bf16[384,128]{1,0:T(8,128)(2,1)S(1)}, bf16[384,128]{1,0:T(8,128)(2,1)S(1)}, u32[]{:S(2)}, u32[]{:S(2)}) collective-permute-start(bf16[384,128]{1,0:T(8,128)(2,1)S(1)} %get-tuple-element.19.refs_0_), channel_id=1, source_target_pairs={{0,1},{1,0},{2,3},{3,2},{4,5},{5,4},{6,7},{7,6},{8,9},{9,8},{10,11... | collective-permute-start | bytes 294920 | tf_op jit(solution)/shard_map/ppermute | solution.py:41
  6.4 3.2 %collective-permute-done.6.refs_1_ = bf16[384,128]{1,0:T(8,128)(2,1)S(1)} collective-permute-done((bf16[384,128]{1,0:T(8,128)(2,1)S(1)}, bf16[384,128]{1,0:T(8,128)(2,1)S(1)}, u32[]{:S(2)}, u32[]{:S(2)}) %collective-permute-start.6) | collective-permute-done | bytes 98336 | tf_op jit(solution)/shard_map/ppermute | solution.py:41
  9.6 1.8 %collective-permute-start.7 = (bf16[384,128]{1,0:T(8,128)(2,1)S(1)}, bf16[384,128]{1,0:T(8,128)(2,1)S(1)}, u32[]{:S(2)}, u32[]{:S(2)}) collective-permute-start(bf16[384,128]{1,0:T(8,128)(2,1)S(1)} %shard_map.97.refs_0_), channel_id=1, source_target_pairs={{0,2},{1,3},{2,0},{3,1},{4,6},{5,7},{6,4},{7,5},{8,10},{9,11},{10,... | collective-permute-start | bytes 294920 | tf_op jit(solution)/shard_map/ppermute | solution.py:41
  11.5 1.4 %collective-permute-start.5 = (bf16[656,128]{1,0:T(8,128)(2,1)S(1)}, bf16[656,128]{1,0:T(8,128)(2,1)S(1)}, u32[]{:S(2)}, u32[]{:S(2)}) collective-permute-start(bf16[656,128]{1,0:T(8,128)(2,1)S(1)} %get-tuple-element.18.refs_0_), channel_id=1, source_target_pairs={{0,3},{1,2},{2,1},{3,0},{4,7},{5,6},{6,5},{7,4},{8,11},{9,10},{10,... | collective-permute-start | bytes 503816 | tf_op jit(solution)/shard_map/ppermute | solution.py:41
  12.9 1.5 %collective-permute-start.4 = (bf16[656,128]{1,0:T(8,128)(2,1)S(1)}, bf16[656,128]{1,0:T(8,128)(2,1)S(1)}, u32[]{:S(2)}, u32[]{:S(2)}) collective-permute-start(bf16[656,128]{1,0:T(8,128)(2,1)S(1)} %get-tuple-element.18.refs_0_), channel_id=1, source_target_pairs={{0,2},{1,3},{2,0},{3,1},{4,6},{5,7},{6,4},{7,5},{8,10},{9,11},{10,... | collective-permute-start | bytes 503816 | tf_op jit(solution)/shard_map/ppermute | solution.py:41
  14.4 0.5 %collective-permute-start.3 = (bf16[656,128]{1,0:T(8,128)(2,1)S(1)}, bf16[656,128]{1,0:T(8,128)(2,1)S(1)}, u32[]{:S(2)}, u32[]{:S(2)}) collective-permute-start(bf16[656,128]{1,0:T(8,128)(2,1)S(1)} %get-tuple-element.18.refs_0_), channel_id=1, source_target_pairs={{0,1},{1,0},{2,3},{3,2},{4,5},{5,4},{6,7},{7,6},{8,9},{9,8},{10,11... | collective-permute-start | bytes 503816 | tf_op jit(solution)/shard_map/ppermute | solution.py:41
  15.0 2.7 %collective-permute-done.7.refs_1_ = bf16[384,128]{1,0:T(8,128)(2,1)S(1)} collective-permute-done((bf16[384,128]{1,0:T(8,128)(2,1)S(1)}, bf16[384,128]{1,0:T(8,128)(2,1)S(1)}, u32[]{:S(2)}, u32[]{:S(2)}) %collective-permute-start.7) | collective-permute-done | bytes 98336 | tf_op jit(solution)/shard_map/ppermute | solution.py:41
  17.7 1.8 %collective-permute-done.5.refs_3_ = bf16[656,128]{1,0:T(8,128)(2,1)S(1)} collective-permute-done((bf16[656,128]{1,0:T(8,128)(2,1)S(1)}, bf16[656,128]{1,0:T(8,128)(2,1)S(1)}, u32[]{:S(2)}, u32[]{:S(2)}) %collective-permute-start.5) | collective-permute-done | bytes 167968 | tf_op jit(solution)/shard_map/ppermute | solution.py:41
  19.5 2.0 %collective-permute-done.4.refs_2_ = bf16[656,128]{1,0:T(8,128)(2,1)S(1)} collective-permute-done((bf16[656,128]{1,0:T(8,128)(2,1)S(1)}, bf16[656,128]{1,0:T(8,128)(2,1)S(1)}, u32[]{:S(2)}, u32[]{:S(2)}) %collective-permute-start.4) | collective-permute-done | bytes 167968 | tf_op jit(solution)/shard_map/ppermute | solution.py:41
  21.5 1.1 %shard_map.99 = (bf16[768,128]{1,0:T(8,128)(2,1)S(1)}, bf16[768,128]{1,0:T(8,128)(2,1)S(1)}) custom-call(bf16[656,128]{1,0:T(8,128)(2,1)S(1)} %get-tuple-element.18.refs_0_, bf16[656,128]{1,0:T(8,128)(2,1)S(1)} %collective-permute-done.3.refs_1_, bf16[656,128]{1,0:T(8,128)(2,1)S(1)} %collective-permute-done.4.refs_2_, ...), custom_call_target="tpu_custom_call" | custom-call | flops 67108864 | bytes 870400 | tf_op jit(solution)/shard_map/pallas_call | solution.py:51
  22.7 0.4 shard_map.101
  23.0 0.4 shard_map.100
  23.4 0.7 %collective-permute-done.9.made_ref = bf16[768,128]{1,0:T(8,128)(2,1)S(1)} collective-permute-done((bf16[768,128]{1,0:T(8,128)(2,1)S(1)}, bf16[768,128]{1,0:T(8,128)(2,1)S(1)}, u32[]{:S(2)}, u32[]{:S(2)}) %collective-permute-start.9) | collective-permute-done | bytes 196640 | tf_op jit(solution)/shard_map/ppermute | solution.py:41
  24.1 1.6 %shard_map.102 = (bf16[528,128]{1,0:T(8,128)(2,1)S(1)}, bf16[528,128]{1,0:T(8,128)(2,1)S(1)}, bf16[528,128]{1,0:T(8,128)(2,1)S(1)}, bf16[528,128]{1,0:T(8,128)(2,1)S(1)}, bf16[256,1024]{1,0:T(8,128)(2,1)}) custom-call(bf16[768,128]{1,0:T(8,128)(2,1)S(1)} %collective-permute-done.9.made_ref, f32[512,128]{1,0:T(8,128)S(1)} %get-tuple-element.22.mix_ref, ...), custom_call_target="tpu_custom_call" | custom-call | flops 536870912 | bytes 3085312 | tf_op jit(solution)/shard_map/pallas_call | solution.py:51
  25.7 1.8 %collective-permute-start.10 = (bf16[528,128]{1,0:T(8,128)(2,1)S(1)}, bf16[528,128]{1,0:T(8,128)(2,1)S(1)}, u32[]{:S(2)}, u32[]{:S(2)}) collective-permute-start(bf16[528,128]{1,0:T(8,128)(2,1)S(1)} %get-tuple-element.27), channel_id=1, source_target_pairs={{0,4},{4,0},{8,12},{12,8},{1,5},{5,1},{9,13},{13,9},{2,6},{6,2},{1... | collective-permute-start | bytes 405512 | tf_op jit(solution)/shard_map/ppermute | solution.py:41
  27.5 2.6 %collective-permute-start.11 = (bf16[528,128]{1,0:T(8,128)(2,1)S(1)}, bf16[528,128]{1,0:T(8,128)(2,1)S(1)}, u32[]{:S(2)}, u32[]{:S(2)}) collective-permute-start(bf16[528,128]{1,0:T(8,128)(2,1)S(1)} %get-tuple-element.28), channel_id=1, source_target_pairs={{0,8},{4,12},{8,0},{12,4},{1,9},{5,13},{9,1},{13,5},{2,10},{6,14},... | collective-permute-start | bytes 405512 | tf_op jit(solution)/shard_map/ppermute | solution.py:41
  30.1 3.3 %collective-permute-done.10.refs_1_ = bf16[528,128]{1,0:T(8,128)(2,1)S(1)} collective-permute-done((bf16[528,128]{1,0:T(8,128)(2,1)S(1)}, bf16[528,128]{1,0:T(8,128)(2,1)S(1)}, u32[]{:S(2)}, u32[]{:S(2)}) %collective-permute-start.10) | collective-permute-done | bytes 135200 | tf_op jit(solution)/shard_map/ppermute | solution.py:41
  33.4 7.2 %collective-permute-done.11.refs_2_ = bf16[528,128]{1,0:T(8,128)(2,1)S(1)} collective-permute-done((bf16[528,128]{1,0:T(8,128)(2,1)S(1)}, bf16[528,128]{1,0:T(8,128)(2,1)S(1)}, u32[]{:S(2)}, u32[]{:S(2)}) %collective-permute-start.11) | collective-permute-done | bytes 135200 | tf_op jit(solution)/shard_map/ppermute | solution.py:41
  40.6 0.8 %shard_map.103 = (f32[32,1024]{1,0:T(8,128)}, f32[32,1024]{1,0:T(8,128)}, f32[1,1024]{1,0:T(1,128)}) custom-call(bf16[528,128]{1,0:T(8,128)(2,1)S(1)} %get-tuple-element.26.refs_0_, bf16[528,128]{1,0:T(8,128)(2,1)S(1)} %collective-permute-done.10.refs_1_, bf16[528,128]{1,0:T(8,128)(2,1)S(1)} %collective-permute-done.11.refs_2_, ...), custom_call_target="tpu_custom_call" | custom-call | flops 33554432 | bytes 540672 | tf_op jit(solution)/shard_map/pallas_call | solution.py:51
  (26 shorter events, 0.4 us)
Async XLA Ops:
  0.6 2.4 %collective-permute-start = (bf16[1024,128]{1,0:T(8,128)(2,1)}, bf16[1024,128]{1,0:T(8,128)(2,1)S(1)}, u32[]{:S(2)}, u32[]{:S(2)}) collective-permute-start(bf16[1024,128]{1,0:T(8,128)(2,1)} %bitcast.15), channel_id=1, source_target_pairs={{0,16},{16,0},{1,17},{17,1},{2,18},{18,2},{3,19},{19,3},{4,20},{20... | collective-permute-start | bytes 786440 | tf_op jit(solution)/shard_map/ppermute | solution.py:41
  1.2 1.3 %copy-start = (bf16[2,128,1024]{2,1,0:T(8,128)(2,1)S(1)}, bf16[2,128,1024]{2,1,0:T(8,128)(2,1)}, u32[]{:S(2)}) copy-start(bf16[2,128,1024]{2,1,0:T(8,128)(2,1)} %param.7) | copy-start | bytes 1572868
  1.2 1.3 %copy-start.1 = (bf16[1,128,1024]{2,1,0:T(8,128)(2,1)S(1)}, bf16[1,128,1024]{2,1,0:T(8,128)(2,1)}, u32[]{:S(2)}) copy-start(bf16[1,128,1024]{2,1,0:T(8,128)(2,1)} %param.9) | copy-start | bytes 786436
  1.2 1.3 %copy-start.2 = (bf16[1,1024,128]{2,1,0:T(8,128)(2,1)S(1)}, bf16[1,1024,128]{2,1,0:T(8,128)(2,1)}, u32[]{:S(2)}) copy-start(bf16[1,1024,128]{2,1,0:T(8,128)(2,1)} %param.8) | copy-start | bytes 786436
  1.2 1.3 %copy-start.3 = (bf16[1024,128]{1,0:T(8,128)(2,1)S(1)}, bf16[1024,128]{1,0:T(8,128)(2,1)}, u32[]{:S(2)}) copy-start(bf16[1024,128]{1,0:T(8,128)(2,1)} %head_ref.3) | copy-start | bytes 786436
  1.2 1.9 %collective-permute-start.1 = (bf16[128,1024]{1,0:T(8,128)(2,1)}, bf16[128,1024]{1,0:T(8,128)(2,1)S(1)}, u32[]{:S(2)}, u32[]{:S(2)}) collective-permute-start(bf16[128,1024]{1,0:T(8,128)(2,1)} %bitcast.11), channel_id=1, source_target_pairs={{0,16},{16,0},{1,17},{17,1},{2,18},{18,2},{3,19},{19,3},{4,20},{20... | collective-permute-start | bytes 786440 | tf_op jit(solution)/shard_map/ppermute | solution.py:41
  1.3 1.7 %collective-permute-start.2 = (bf16[1,1024]{1,0:T(2,128)(2,1)}, bf16[1,1024]{1,0:T(2,128)(2,1)S(1)}, u32[]{:S(2)}, u32[]{:S(2)}) collective-permute-start(bf16[1,1024]{1,0:T(2,128)(2,1)} %gain_ref.1), channel_id=1, source_target_pairs={{0,16},{16,0},{1,17},{17,1},{2,18},{18,2},{3,19},{19,3},{4,20},{20... | collective-permute-start | bytes 6152 | tf_op jit(solution)/shard_map/ppermute | solution.py:41
  1.8 0.7 %copy-start.6 = (bf16[1,1024]{1,0:T(2,128)(2,1)S(1)}, bf16[1,1024]{1,0:T(2,128)(2,1)}, u32[]{:S(2)}) copy-start(bf16[1,1024]{1,0:T(2,128)(2,1)} %gain_ref.1) | copy-start | bytes 6148
  3.0 18.5 %copy-start.4 = (s32[2,128]{1,0:T(2,128)S(1)}, s32[2,128]{1,0:T(2,128)}, u32[]{:S(2)}) copy-start(s32[2,128]{1,0:T(2,128)} %valid_ref.1) | copy-start | bytes 3076
  3.0 18.5 %copy-start.5 = (s32[2,128]{1,0:T(2,128)S(1)}, s32[2,128]{1,0:T(2,128)}, u32[]{:S(2)}) copy-start(s32[2,128]{1,0:T(2,128)} %refs_6_.1) | copy-start | bytes 3076
  3.6 6.0 %collective-permute-start.6 = (bf16[384,128]{1,0:T(8,128)(2,1)S(1)}, bf16[384,128]{1,0:T(8,128)(2,1)S(1)}, u32[]{:S(2)}, u32[]{:S(2)}) collective-permute-start(bf16[384,128]{1,0:T(8,128)(2,1)S(1)} %get-tuple-element.19.refs_0_), channel_id=1, source_target_pairs={{0,1},{1,0},{2,3},{3,2},{4,5},{5,4},{6,7},{7,6},{8,9},{9,8},{10,11... | collective-permute-start | bytes 294920 | tf_op jit(solution)/shard_map/ppermute | solution.py:41
  9.6 8.0 %collective-permute-start.7 = (bf16[384,128]{1,0:T(8,128)(2,1)S(1)}, bf16[384,128]{1,0:T(8,128)(2,1)S(1)}, u32[]{:S(2)}, u32[]{:S(2)}) collective-permute-start(bf16[384,128]{1,0:T(8,128)(2,1)S(1)} %shard_map.97.refs_0_), channel_id=1, source_target_pairs={{0,2},{1,3},{2,0},{3,1},{4,6},{5,7},{6,4},{7,5},{8,10},{9,11},{10,... | collective-permute-start | bytes 294920 | tf_op jit(solution)/shard_map/ppermute | solution.py:41
  11.5 8.1 %collective-permute-start.5 = (bf16[656,128]{1,0:T(8,128)(2,1)S(1)}, bf16[656,128]{1,0:T(8,128)(2,1)S(1)}, u32[]{:S(2)}, u32[]{:S(2)}) collective-permute-start(bf16[656,128]{1,0:T(8,128)(2,1)S(1)} %get-tuple-element.18.refs_0_), channel_id=1, source_target_pairs={{0,3},{1,2},{2,1},{3,0},{4,7},{5,6},{6,5},{7,4},{8,11},{9,10},{10,... | collective-permute-start | bytes 503816 | tf_op jit(solution)/shard_map/ppermute | solution.py:41
  12.9 8.6 %collective-permute-start.4 = (bf16[656,128]{1,0:T(8,128)(2,1)S(1)}, bf16[656,128]{1,0:T(8,128)(2,1)S(1)}, u32[]{:S(2)}, u32[]{:S(2)}) collective-permute-start(bf16[656,128]{1,0:T(8,128)(2,1)S(1)} %get-tuple-element.18.refs_0_), channel_id=1, source_target_pairs={{0,2},{1,3},{2,0},{3,1},{4,6},{5,7},{6,4},{7,5},{8,10},{9,11},{10,... | collective-permute-start | bytes 503816 | tf_op jit(solution)/shard_map/ppermute | solution.py:41
  14.4 7.1 %collective-permute-start.3 = (bf16[656,128]{1,0:T(8,128)(2,1)S(1)}, bf16[656,128]{1,0:T(8,128)(2,1)S(1)}, u32[]{:S(2)}, u32[]{:S(2)}) collective-permute-start(bf16[656,128]{1,0:T(8,128)(2,1)S(1)} %get-tuple-element.18.refs_0_), channel_id=1, source_target_pairs={{0,1},{1,0},{2,3},{3,2},{4,5},{5,4},{6,7},{7,6},{8,9},{9,8},{10,11... | collective-permute-start | bytes 503816 | tf_op jit(solution)/shard_map/ppermute | solution.py:41
  17.7 3.9 %collective-permute-start.8 = (bf16[384,128]{1,0:T(8,128)(2,1)S(1)}, bf16[384,128]{1,0:T(8,128)(2,1)S(1)}, u32[]{:S(2)}, u32[]{:S(2)}) collective-permute-start(bf16[384,128]{1,0:T(8,128)(2,1)S(1)} %shard_map.98.refs_4_), channel_id=1, source_target_pairs={{0,16},{16,0},{1,17},{17,1},{2,18},{18,2},{3,19},{19,3},{4,20},{20... | collective-permute-start | bytes 294920 | tf_op jit(solution)/shard_map/ppermute | solution.py:41
  22.6 1.5 %collective-permute-start.9 = (bf16[768,128]{1,0:T(8,128)(2,1)S(1)}, bf16[768,128]{1,0:T(8,128)(2,1)S(1)}, u32[]{:S(2)}, u32[]{:S(2)}) collective-permute-start(bf16[768,128]{1,0:T(8,128)(2,1)S(1)} %get-tuple-element.20), channel_id=1, source_target_pairs={{0,16},{16,0},{1,17},{17,1},{2,18},{18,2},{3,19},{19,3},{4,20},{20... | collective-permute-start | bytes 589832 | tf_op jit(solution)/shard_map/ppermute | solution.py:41
  25.7 7.7 %collective-permute-start.10 = (bf16[528,128]{1,0:T(8,128)(2,1)S(1)}, bf16[528,128]{1,0:T(8,128)(2,1)S(1)}, u32[]{:S(2)}, u32[]{:S(2)}) collective-permute-start(bf16[528,128]{1,0:T(8,128)(2,1)S(1)} %get-tuple-element.27), channel_id=1, source_target_pairs={{0,4},{4,0},{8,12},{12,8},{1,5},{5,1},{9,13},{13,9},{2,6},{6,2},{1... | collective-permute-start | bytes 405512 | tf_op jit(solution)/shard_map/ppermute | solution.py:41
  27.5 13.1 %collective-permute-start.11 = (bf16[528,128]{1,0:T(8,128)(2,1)S(1)}, bf16[528,128]{1,0:T(8,128)(2,1)S(1)}, u32[]{:S(2)}, u32[]{:S(2)}) collective-permute-start(bf16[528,128]{1,0:T(8,128)(2,1)S(1)} %get-tuple-element.28), channel_id=1, source_target_pairs={{0,8},{4,12},{8,0},{12,4},{1,9},{5,13},{9,1},{13,5},{2,10},{6,14},... | collective-permute-start | bytes 405512 | tf_op jit(solution)/shard_map/ppermute | solution.py:41
  30.1 10.6 %collective-permute-start.12 = (bf16[528,128]{1,0:T(8,128)(2,1)S(1)}, bf16[528,128]{1,0:T(8,128)(2,1)S(1)}, u32[]{:S(2)}, u32[]{:S(2)}) collective-permute-start(bf16[528,128]{1,0:T(8,128)(2,1)S(1)} %get-tuple-element.29), channel_id=1, source_target_pairs={{0,12},{4,8},{8,4},{12,0},{1,13},{5,9},{9,5},{13,1},{2,14},{6,10},... | collective-permute-start | bytes 405512 | tf_op jit(solution)/shard_map/ppermute | solution.py:41

commit v6 on v5

--- a/solution.py
+++ b/solution.py
@@ -205,26 +205,36 @@
     return mixes, weighted_t, scaled_t
 
 
-def mine_kernel(made_ref, x_ref, mix_ref, acc_ref):
+def mine_kernel(made_ref, x_ref, mix_ref, acc_ref, left_ref):
     rank = made_ref.shape[1]
     half = made_ref.shape[0] // 6
     x = x_ref[rows_of(lax.axis_index("section") * half, half), :]
     mixes, weighted_t, scaled_t = products(made_ref[...])
     for i, mix in enumerate(mixes):
         mix_ref[i * rank : (i + 1) * rank, :] = mix
+    left_ref[:rank, :] = weighted_t
+    left_ref[rank:, :] = scaled_t
     acc_ref[:rank, :] = dot(weighted_t, x)
     acc_ref[rank:, :] = dot(scaled_t, x)
 
 
-def grad_kernel(replicas, made_ref, mix_ref, acc_ref, stack_ref, down_t_ref, gain_ref, valid_ref, *refs):
-    out_refs, all_ref = refs[:replicas], refs[replicas]
+def grad_kernel(
+    replicas, sections, made_ref, mix_ref, acc_ref, left_ref, stack_ref, down_t_ref, gain_ref, valid_ref, *refs
+):
+    out_refs, (all_ref, tall_ref) = refs[:replicas], refs[replicas:]
     rank, features = down_t_ref.shape
     slim = rank // replicas
-    first = lax.axis_index("section") == 0
+    section = lax.axis_index("section")
+    first = section == 0
     mixes, weighted_t, scaled_t = products(made_ref[...])
-    head_mix, own_mix, oth_mix, mix = (
-        (m + mix_ref[i * rank : (i + 1) * rank, :]).astype(BF16) for i, m in enumerate(mixes)
-    )
+    mixes = [(m + mix_ref[i * rank : (i + 1) * rank, :]).astype(BF16) for i, m in enumerate(mixes)]
+    for i, mix in enumerate(mixes):
+        tall_ref[i * rank : (i + 1) * rank, :] = mix
+    tall_ref[rows_of((4 + section) * rank, rank), :] = left_ref[:rank, :]
+    tall_ref[rows_of((5 - section) * rank, rank), :] = weighted_t
+    tall_ref[rows_of((6 + section) * rank, rank), :] = left_ref[rank:, :]
+    tall_ref[rows_of((7 - section) * rank, rank), :] = scaled_t
+    head_mix, own_mix, oth_mix, mix = mixes
     none = jnp.zeros_like(mix)
     left = jnp.concatenate([jnp.where(first, none, mix), weighted_t], axis=1)
     grad = acc_ref[:rank, :] + dot(left, stack_ref[3 * rank :, :])
@@ -243,27 +253,50 @@
     ).astype(BF16)
     place = lax.axis_index("dp")
     for step, out_ref in enumerate(out_refs):
-        block = all_ref[rows_of(partner(place, step, replicas) * 2 * slim, 2 * slim), :]
-        for i in range(lines):
-            out_ref[i * 2 * slim : (i + 1) * 2 * slim, :] = block[:, i * rank : (i + 1) * rank]
-        out_ref[lines * 2 * slim :, :] = tail
-
-
-def last_kernel(*refs):
-    parts, (down_out, up_out, gain_out) = refs[:-3], refs[-3:]
-    rank = parts[0].shape[1]
+        target = partner(place, step, replicas)
+        if step < replicas - sections:
+            block = all_ref[rows_of(target * 2 * slim, 2 * slim), :]
+            for i in range(lines):
+                out_ref[i * 2 * slim : (i + 1) * 2 * slim, :] = block[:, i * rank : (i + 1) * rank]
+        else:
+            for i in range(8):
+                out_ref[i * slim : (i + 1) * slim, :] = tall_ref[rows_of(i * rank + target * slim, slim), :]
+        out_ref[-PACK:, :] = tail
+
+
+def last_kernel(whole, *refs):
+    parts, (far_ref, cross_ref, stack_ref, gain_ref, down_out, up_out, gain_out) = refs[:-7], refs[-7:]
+    near, (a_ref, b_ref) = parts[:whole], parts[whole:]
+    rank = a_ref.shape[1]
     slim, features = down_out.shape
     lines = features // rank
+    first = lax.axis_index("section") == 0
 
     def total(start, size):
-        return sum(p[start : start + size, :].astype(F32) for p in parts)
-
-    tail = total(lines * 2 * slim, PACK)
+        return sum(p[start : start + size, :].astype(F32) for p in near)
+
+    def left(ref):
+        rows = [ref[i * slim : (i + 1) * slim, :] for i in range(4, 8)]
+        return jnp.concatenate([jnp.concatenate(rows[:2], axis=1), jnp.concatenate(rows[2:], axis=1)], axis=0)
+
+    tail = sum(p[-PACK:, :].astype(F32) for p in parts)
     scale = 1.0 / tail[lines : lines + 1, :1]
+    left_a, left_b = left(a_ref), left(b_ref)
+    moved = dot(jnp.where(first, left_a, left_b), far_ref[...])
+    moved = moved + dot(jnp.where(first, left_b, left_a), cross_ref[...])
+    mixes = [
+        (a_ref[i * slim : (i + 1) * slim, :].astype(F32) + b_ref[i * slim : (i + 1) * slim, :].astype(F32)).astype(BF16)
+        for i in range(4)
+    ]
+    none = jnp.zeros_like(mixes[3])
+    down = moved[:slim] + dot(jnp.where(first, none, mixes[3]), stack_ref[3 * rank : 4 * rank, :])
+    down = down * gain_ref[...]
+    mixes = jnp.concatenate(mixes[:3] + [jnp.where(first, mixes[3], none)], axis=1)
+    up = moved[slim:] + dot(mixes, stack_ref[: 4 * rank, :])
     for i in range(lines):
         lanes = slice(i * rank, (i + 1) * rank)
-        down_out[:, lanes] = total(i * 2 * slim, slim) * scale
-        up_out[:, lanes] = total((2 * i + 1) * slim, slim) * scale
+        down_out[:, lanes] = (total(i * 2 * slim, slim) + down[:, lanes]) * scale
+        up_out[:, lanes] = (total((2 * i + 1) * slim, slim) + up[:, lanes]) * scale
         gain_out[:, lanes] = tail[i : i + 1, :] * scale
 
 
@@ -281,7 +314,17 @@
     labels, valid = labels.reshape(sections, half), valid.reshape(sections, half)
     shape = jax.ShapeDtypeStruct
 
-    down2, up2, gains2 = (from_partner(v, "section", 1) for v in (down, up, gains))
+    others = []
+    for value in (down, up, gains):
+        others.append(from_partner(value, "section", 1))
+    down2, up2, gains2 = others
+    whole = replicas - sections
+    assert whole > 0
+    far = lax.ppermute(
+        states,
+        ("section", "dp"),
+        [(s * replicas + i, s * replicas + partner(i, whole + s, replicas)) for s in range(sections) for i in range(replicas)],
+    )
     small = 2 * rank * rank * features
     wide_gain = call(gain_kernel, shape(gains.shape, F32), 40 * small, gains)
     own = call(
@@ -326,25 +369,28 @@
         *wide, gram, gram2, labels, valid,
     )
     met = from_partner(theirs, "section", 1)
-    mixes, acc = call(
+    mixes, acc, left = call(
         mine_kernel,
-        [shape((4 * rank, rank), F32), shape((2 * rank, features), F32)],
+        [shape((4 * rank, rank), F32), shape((2 * rank, features), F32), shape((2 * rank, half), BF16)],
         4 * small,
         made, states,
     )
-    *parts, _ = call(
-        functools.partial(grad_kernel, replicas),
-        [shape((lines * 2 * slim + PACK, rank), BF16)] * replicas + [shape((2 * rank, features), BF16)],
+    *parts, _, _ = call(
+        functools.partial(grad_kernel, replicas, sections),
+        [shape((lines * 2 * slim + PACK, rank), BF16)] * whole
+        + [shape((8 * slim + PACK, rank), BF16)] * sections
+        + [shape((2 * rank, features), BF16), shape((8 * rank, rank), BF16)],
         16 * small,
-        met, mixes, acc, stack, down_t, wide_gain, valid,
+        met, mixes, acc, left, stack, down_t, wide_gain, valid,
     )
     for step in range(1, replicas):
         parts[step] = from_partner(parts[step], "dp", step)
+    cross = from_partner(far, "section", 1)
     down_grad, up_grad, gain_grad = call(
-        last_kernel,
+        functools.partial(last_kernel, whole),
         [shape((slim, features), F32), shape((slim, features), F32), shape((1, features), F32)],
-        small,
-        *parts,
+        2 * small,
+        *parts, far, cross, stack, wide_gain,
     )
     return down_grad.T[None], up_grad[None], gain_grad
 

time: 41.6 us -> 45.3 us (1.089)
  starting transfers between devices: 13.8 us -> 17.1 us
    ppermute x0 -> x1, waiting for transfers between devices: none -> 10.4 us  [local(): lax.ppermute(states, ('section', 'dp'), [(s * replicas + i, s * replicas...]
    ppermute x13 -> x14, waiting for transfers between devices: 20.9 us -> 10.5 us  [from_partner(): lax.ppermute(value, axis, [(i, partner(i, step, size)) for i in range(siz...]
    ppermute x0 -> x1, starting transfers between devices: none -> 4.13 us  [local(): lax.ppermute(states, ('section', 'dp'), [(s * replicas + i, s * replicas...]
    ppermute x13 -> x14, starting transfers between devices: 13.8 us -> 12.9 us  [from_partner(): lax.ppermute(value, axis, [(i, partner(i, step, size)) for i in range(siz...]
  transfers between devices with their start and end apart: 13 -> 15, of which waited for: 7 -> 6; matrix products, arithmetic and copies ran while one was open for 0% -> 0% of each run, Pallas kernels for 3% -> 10%
where the time goes in v6:
time: 45.3 us; the launch traced here: 45.1 us
  waiting for transfers between devices  21 us (46%)
  starting transfers between devices  17.1 us (38%)
  Pallas kernels  5.63 us (12%)
  between operations  0.76 us (2%)
  local copies, waits for them, and re-layouts  0.71 us (2%)
    ppermute x14, starting transfers between devices, from_partner(): lax.ppermute(value, axis, [(i, partner(i, step, size)) for i in range(siz...  12.9 us
    ppermute x14, waiting for transfers between devices, from_partner(): lax.ppermute(value, axis, [(i, partner(i, step, size)) for i in range(siz...  10.5 us
    ppermute x1, waiting for transfers between devices, local(): lax.ppermute(states, ('section', 'dp'), [(s * replicas + i, s * replicas...  10.4 us
    pallas_call x10, Pallas kernels, call(): pl.pallas_call(kernel, out_shape=out, cost_estimate=pl.CostEstimate(flops...  5.63 us
    ppermute x1, starting transfers between devices, local(): lax.ppermute(states, ('section', 'dp'), [(s * replicas + i, s * replicas...  4.13 us
  transfers between devices with their start and end apart: 15, of which 6 were waited for; matrix products, arithmetic and copies ran while one was open for 0% of the time, Pallas kernels for 10%

profile of v6, /device:TPU:0, one launch (start us, length us, event | category | flops | bytes accessed | tf_op | source)
XLA Modules:
  0.0 45.1 jit_solution(15819892208220920187)
XLA Ops:
  0.6 4.1 %collective-permute-start.13 = (bf16[256,1024]{1,0:T(8,128)(2,1)}, bf16[256,1024]{1,0:T(8,128)(2,1)S(1)}, u32[]{:S(2)}, u32[]{:S(2)}) collective-permute-start(bf16[256,1024]{1,0:T(8,128)(2,1)} %bitcast.7), channel_id=1, source_target_pairs={{0,8},{4,12},{8,0},{12,4},{16,28},{20,24},{24,20},{28,16},{1,9},{5... | collective-permute-start | bytes 1572872 | tf_op jit(solution)/shard_map/ppermute | solution.py:323
  4.8 0.6 %collective-permute-start.1 = (bf16[128,1024]{1,0:T(8,128)(2,1)}, bf16[128,1024]{1,0:T(8,128)(2,1)S(1)}, u32[]{:S(2)}, u32[]{:S(2)}) collective-permute-start(bf16[128,1024]{1,0:T(8,128)(2,1)} %bitcast.12), channel_id=1, source_target_pairs={{0,16},{16,0},{1,17},{17,1},{2,18},{18,2},{3,19},{19,3},{4,20},{20... | collective-permute-start | bytes 786440 | tf_op jit(solution)/shard_map/ppermute | solution.py:41
  5.4 0.5 %collective-permute-start.2 = (bf16[1,1024]{1,0:T(2,128)(2,1)}, bf16[1,1024]{1,0:T(2,128)(2,1)S(1)}, u32[]{:S(2)}, u32[]{:S(2)}) collective-permute-start(bf16[1,1024]{1,0:T(2,128)(2,1)} %gain_ref.1), channel_id=1, source_target_pairs={{0,16},{16,0},{1,17},{17,1},{2,18},{18,2},{3,19},{19,3},{4,20},{20... | collective-permute-start | bytes 6152 | tf_op jit(solution)/shard_map/ppermute | solution.py:41
  5.9 0.7 %copy-done.6 = bf16[1,1024]{1,0:T(2,128)(2,1)S(1)} copy-done((bf16[1,1024]{1,0:T(2,128)(2,1)S(1)}, bf16[1,1024]{1,0:T(2,128)(2,1)}, u32[]{:S(2)}) %copy-start.6) | copy-done | bytes 2072
  6.6 0.5 %shard_map.95.own_ref = bf16[656,128]{1,0:T(8,128)(2,1)S(1)} custom-call(bf16[256,1024]{1,0:T(8,128)(2,1)S(1)} %bitcast.8, bf16[1024,128]{1,0:T(8,128)(2,1)S(1)} %bitcast.17, bf16[128,1024]{1,0:T(8,128)(2,1)S(1)} %bitcast.13, bf16[1024,128]{1,0:T(8,128)(2,1)S(1)} %copy-done.3, f32[1,1024]{1,0:T(1,128)S(1)} %shard_map.94.gain_ref.refs_7_), custom_call_target="tpu_custom_call" | custom-call | flops 167772160 | bytes 1314816 | tf_op jit(solution)/shard_map/pallas_call | solution.py:51
  7.2 0.5 %shard_map.96 = (bf16[656,128]{1,0:T(8,128)(2,1)S(1)}, bf16[384,128]{1,0:T(8,128)(2,1)S(1)}) custom-call(bf16[256,1024]{1,0:T(8,128)(2,1)S(1)} %bitcast.9, bf16[128,1024]{1,0:T(8,128)(2,1)S(1)} %bitcast.14, bf16[656,128]{1,0:T(8,128)(2,1)S(1)} %shard_map.95.own_ref, bf16[1024,128]{1,0:T(8,128)(2,1)S(1)} %collective-permute-done.down2_ref, ...), custom_call_target="tpu_custom_call" | custom-call | flops 100663296 | bytes 1480704 | tf_op jit(solution)/shard_map/pallas_call | solution.py:51
  7.7 1.6 %collective-permute-start.6 = (bf16[384,128]{1,0:T(8,128)(2,1)S(1)}, bf16[384,128]{1,0:T(8,128)(2,1)S(1)}, u32[]{:S(2)}, u32[]{:S(2)}) collective-permute-start(bf16[384,128]{1,0:T(8,128)(2,1)S(1)} %get-tuple-element.20.refs_0_), channel_id=1, source_target_pairs={{0,1},{1,0},{2,3},{3,2},{4,5},{5,4},{6,7},{7,6},{8,9},{9,8},{10,11... | collective-permute-start | bytes 294920 | tf_op jit(solution)/shard_map/ppermute | solution.py:41
  9.3 3.5 %collective-permute-done.6.refs_1_ = bf16[384,128]{1,0:T(8,128)(2,1)S(1)} collective-permute-done((bf16[384,128]{1,0:T(8,128)(2,1)S(1)}, bf16[384,128]{1,0:T(8,128)(2,1)S(1)}, u32[]{:S(2)}, u32[]{:S(2)}) %collective-permute-start.6) | collective-permute-done | bytes 98336 | tf_op jit(solution)/shard_map/ppermute | solution.py:41
  12.8 1.6 %collective-permute-start.7 = (bf16[384,128]{1,0:T(8,128)(2,1)S(1)}, bf16[384,128]{1,0:T(8,128)(2,1)S(1)}, u32[]{:S(2)}, u32[]{:S(2)}) collective-permute-start(bf16[384,128]{1,0:T(8,128)(2,1)S(1)} %shard_map.97.refs_0_), channel_id=1, source_target_pairs={{0,2},{1,3},{2,0},{3,1},{4,6},{5,7},{6,4},{7,5},{8,10},{9,11},{10,... | collective-permute-start | bytes 294920 | tf_op jit(solution)/shard_map/ppermute | solution.py:41
  14.4 1.5 %collective-permute-start.3 = (bf16[656,128]{1,0:T(8,128)(2,1)S(1)}, bf16[656,128]{1,0:T(8,128)(2,1)S(1)}, u32[]{:S(2)}, u32[]{:S(2)}) collective-permute-start(bf16[656,128]{1,0:T(8,128)(2,1)S(1)} %get-tuple-element.19.refs_0_), channel_id=1, source_target_pairs={{0,1},{1,0},{2,3},{3,2},{4,5},{5,4},{6,7},{7,6},{8,9},{9,8},{10,11... | collective-permute-start | bytes 503816 | tf_op jit(solution)/shard_map/ppermute | solution.py:41
  15.9 0.5 %collective-permute-start.4 = (bf16[656,128]{1,0:T(8,128)(2,1)S(1)}, bf16[656,128]{1,0:T(8,128)(2,1)S(1)}, u32[]{:S(2)}, u32[]{:S(2)}) collective-permute-start(bf16[656,128]{1,0:T(8,128)(2,1)S(1)} %get-tuple-element.19.refs_0_), channel_id=1, source_target_pairs={{0,2},{1,3},{2,0},{3,1},{4,6},{5,7},{6,4},{7,5},{8,10},{9,11},{10,... | collective-permute-start | bytes 503816 | tf_op jit(solution)/shard_map/ppermute | solution.py:41
  16.4 1.5 %collective-permute-start.5 = (bf16[656,128]{1,0:T(8,128)(2,1)S(1)}, bf16[656,128]{1,0:T(8,128)(2,1)S(1)}, u32[]{:S(2)}, u32[]{:S(2)}) collective-permute-start(bf16[656,128]{1,0:T(8,128)(2,1)S(1)} %get-tuple-element.19.refs_0_), channel_id=1, source_target_pairs={{0,3},{1,2},{2,1},{3,0},{4,7},{5,6},{6,5},{7,4},{8,11},{9,10},{10,... | collective-permute-start | bytes 503816 | tf_op jit(solution)/shard_map/ppermute | solution.py:41
  17.9 10.4 %collective-permute-done.13.refs_4_ = bf16[256,1024]{1,0:T(8,128)(2,1)S(1)} collective-permute-done((bf16[256,1024]{1,0:T(8,128)(2,1)}, bf16[256,1024]{1,0:T(8,128)(2,1)S(1)}, u32[]{:S(2)}, u32[]{:S(2)}) %collective-permute-start.13) | collective-permute-done | bytes 524320 | tf_op jit(solution)/shard_map/ppermute | solution.py:323
  28.3 0.6 %collective-permute-start.8 = (bf16[384,128]{1,0:T(8,128)(2,1)S(1)}, bf16[384,128]{1,0:T(8,128)(2,1)S(1)}, u32[]{:S(2)}, u32[]{:S(2)}) collective-permute-start(bf16[384,128]{1,0:T(8,128)(2,1)S(1)} %shard_map.98.refs_4_), channel_id=1, source_target_pairs={{0,16},{16,0},{1,17},{17,1},{2,18},{18,2},{3,19},{19,3},{4,20},{20... | collective-permute-start | bytes 294920 | tf_op jit(solution)/shard_map/ppermute | solution.py:41
  28.9 1.4 %collective-permute-done.8.refs_5_ = bf16[384,128]{1,0:T(8,128)(2,1)S(1)} collective-permute-done((bf16[384,128]{1,0:T(8,128)(2,1)S(1)}, bf16[384,128]{1,0:T(8,128)(2,1)S(1)}, u32[]{:S(2)}, u32[]{:S(2)}) %collective-permute-start.8) | collective-permute-done | bytes 98336 | tf_op jit(solution)/shard_map/ppermute | solution.py:41
  30.4 1.1 %shard_map.99 = (bf16[768,128]{1,0:T(8,128)(2,1)S(1)}, bf16[768,128]{1,0:T(8,128)(2,1)S(1)}) custom-call(bf16[656,128]{1,0:T(8,128)(2,1)S(1)} %get-tuple-element.19.refs_0_, bf16[656,128]{1,0:T(8,128)(2,1)S(1)} %collective-permute-done.3.refs_1_, bf16[656,128]{1,0:T(8,128)(2,1)S(1)} %collective-permute-done.4.refs_2_, ...), custom_call_target="tpu_custom_call" | custom-call | flops 67108864 | bytes 870400 | tf_op jit(solution)/shard_map/pallas_call | solution.py:51
  32.0 0.4 shard_map.100
  32.4 0.5 %collective-permute-done.9.made_ref = bf16[768,128]{1,0:T(8,128)(2,1)S(1)} collective-permute-done((bf16[768,128]{1,0:T(8,128)(2,1)S(1)}, bf16[768,128]{1,0:T(8,128)(2,1)S(1)}, u32[]{:S(2)}, u32[]{:S(2)}) %collective-permute-start.9) | collective-permute-done | bytes 196640 | tf_op jit(solution)/shard_map/ppermute | solution.py:41
  32.9 1.6 %shard_map.102 = (bf16[528,128]{1,0:T(8,128)(2,1)S(1)}, bf16[528,128]{1,0:T(8,128)(2,1)S(1)}, bf16[272,128]{1,0:T(8,128)(2,1)S(1)}, bf16[272,128]{1,0:T(8,128)(2...) custom-call(bf16[768,128]{1,0:T(8,128)(2,1)S(1)} %collective-permute-done.9.made_ref, ...), custom_call_target="tpu_custom_call" | custom-call | flops 536870912 | bytes 3150848 | tf_op jit(solution)/shard_map/pallas_call | solution.py:51
  34.5 3.0 %collective-permute-start.11 = (bf16[272,128]{1,0:T(8,128)(2,1)S(1)}, bf16[272,128]{1,0:T(8,128)(2,1)S(1)}, u32[]{:S(2)}, u32[]{:S(2)}) collective-permute-start(bf16[272,128]{1,0:T(8,128)(2,1)S(1)} %get-tuple-element.30), channel_id=1, source_target_pairs={{0,8},{4,12},{8,0},{12,4},{1,9},{5,13},{9,1},{13,5},{2,10},{6,14},... | collective-permute-start | bytes 208904 | tf_op jit(solution)/shard_map/ppermute | solution.py:41
  37.5 1.3 %collective-permute-start.12 = (bf16[272,128]{1,0:T(8,128)(2,1)S(1)}, bf16[272,128]{1,0:T(8,128)(2,1)S(1)}, u32[]{:S(2)}, u32[]{:S(2)}) collective-permute-start(bf16[272,128]{1,0:T(8,128)(2,1)S(1)} %get-tuple-element.31), channel_id=1, source_target_pairs={{0,12},{4,8},{8,4},{12,0},{1,13},{5,9},{9,5},{13,1},{2,14},{6,10},... | collective-permute-start | bytes 208904 | tf_op jit(solution)/shard_map/ppermute | solution.py:41
  38.9 1.3 %collective-permute-done.11.refs_2_ = bf16[272,128]{1,0:T(8,128)(2,1)S(1)} collective-permute-done((bf16[272,128]{1,0:T(8,128)(2,1)S(1)}, bf16[272,128]{1,0:T(8,128)(2,1)S(1)}, u32[]{:S(2)}, u32[]{:S(2)}) %collective-permute-start.11) | collective-permute-done | bytes 69664 | tf_op jit(solution)/shard_map/ppermute | solution.py:41
  40.2 3.7 %collective-permute-done.12.refs_3_ = bf16[272,128]{1,0:T(8,128)(2,1)S(1)} collective-permute-done((bf16[272,128]{1,0:T(8,128)(2,1)S(1)}, bf16[272,128]{1,0:T(8,128)(2,1)S(1)}, u32[]{:S(2)}, u32[]{:S(2)}) %collective-permute-start.12) | collective-permute-done | bytes 69664 | tf_op jit(solution)/shard_map/ppermute | solution.py:41
  44.0 1.2 %shard_map.103 = (f32[32,1024]{1,0:T(8,128)}, f32[32,1024]{1,0:T(8,128)}, f32[1,1024]{1,0:T(1,128)}) custom-call(bf16[528,128]{1,0:T(8,128)(2,1)S(1)} %get-tuple-element.28.refs_0_, bf16[528,128]{1,0:T(8,128)(2,1)S(1)} %collective-permute-done.10.refs_1_, bf16[272,128]{1,0:T(8,128)(2,1)S(1)} %collective-permute-done.11.refs_2_, ...), custom_call_target="tpu_custom_call" | custom-call | flops 67108864 | bytes 2772992 | tf_op jit(solution)/shard_map/pallas_call | solution.py:51
  (30 shorter events, 0.7 us)
Async XLA Ops:
  0.6 27.7 %collective-permute-start.13 = (bf16[256,1024]{1,0:T(8,128)(2,1)}, bf16[256,1024]{1,0:T(8,128)(2,1)S(1)}, u32[]{:S(2)}, u32[]{:S(2)}) collective-permute-start(bf16[256,1024]{1,0:T(8,128)(2,1)} %bitcast.7), channel_id=1, source_target_pairs={{0,8},{4,12},{8,0},{12,4},{16,28},{20,24},{24,20},{28,16},{1,9},{5... | collective-permute-start | bytes 1572872 | tf_op jit(solution)/shard_map/ppermute | solution.py:323
  4.8 2.4 %collective-permute-start.1 = (bf16[128,1024]{1,0:T(8,128)(2,1)}, bf16[128,1024]{1,0:T(8,128)(2,1)S(1)}, u32[]{:S(2)}, u32[]{:S(2)}) collective-permute-start(bf16[128,1024]{1,0:T(8,128)(2,1)} %bitcast.12), channel_id=1, source_target_pairs={{0,16},{16,0},{1,17},{17,1},{2,18},{18,2},{3,19},{19,3},{4,20},{20... | collective-permute-start | bytes 786440 | tf_op jit(solution)/shard_map/ppermute | solution.py:41
  5.3 1.3 %copy-start = (bf16[2,128,1024]{2,1,0:T(8,128)(2,1)S(1)}, bf16[2,128,1024]{2,1,0:T(8,128)(2,1)}, u32[]{:S(2)}) copy-start(bf16[2,128,1024]{2,1,0:T(8,128)(2,1)} %param.7) | copy-start | bytes 1572868
  5.3 1.3 %copy-start.1 = (bf16[1,128,1024]{2,1,0:T(8,128)(2,1)S(1)}, bf16[1,128,1024]{2,1,0:T(8,128)(2,1)}, u32[]{:S(2)}) copy-start(bf16[1,128,1024]{2,1,0:T(8,128)(2,1)} %param.9) | copy-start | bytes 786436
  5.3 1.3 %copy-start.2 = (bf16[1,1024,128]{2,1,0:T(8,128)(2,1)S(1)}, bf16[1,1024,128]{2,1,0:T(8,128)(2,1)}, u32[]{:S(2)}) copy-start(bf16[1,1024,128]{2,1,0:T(8,128)(2,1)} %param.8) | copy-start | bytes 786436
  5.3 1.3 %copy-start.3 = (bf16[1024,128]{1,0:T(8,128)(2,1)S(1)}, bf16[1024,128]{1,0:T(8,128)(2,1)}, u32[]{:S(2)}) copy-start(bf16[1024,128]{1,0:T(8,128)(2,1)} %head_ref.3) | copy-start | bytes 786436
  5.3 1.9 %collective-permute-start = (bf16[1024,128]{1,0:T(8,128)(2,1)}, bf16[1024,128]{1,0:T(8,128)(2,1)S(1)}, u32[]{:S(2)}, u32[]{:S(2)}) collective-permute-start(bf16[1024,128]{1,0:T(8,128)(2,1)} %bitcast.16), channel_id=1, source_target_pairs={{0,16},{16,0},{1,17},{17,1},{2,18},{18,2},{3,19},{19,3},{4,20},{20... | collective-permute-start | bytes 786440 | tf_op jit(solution)/shard_map/ppermute | solution.py:41
  5.4 1.8 %collective-permute-start.2 = (bf16[1,1024]{1,0:T(2,128)(2,1)}, bf16[1,1024]{1,0:T(2,128)(2,1)S(1)}, u32[]{:S(2)}, u32[]{:S(2)}) collective-permute-start(bf16[1,1024]{1,0:T(2,128)(2,1)} %gain_ref.1), channel_id=1, source_target_pairs={{0,16},{16,0},{1,17},{17,1},{2,18},{18,2},{3,19},{19,3},{4,20},{20... | collective-permute-start | bytes 6152 | tf_op jit(solution)/shard_map/ppermute | solution.py:41
  5.9 0.7 %copy-start.6 = (bf16[1,1024]{1,0:T(2,128)(2,1)S(1)}, bf16[1,1024]{1,0:T(2,128)(2,1)}, u32[]{:S(2)}) copy-start(bf16[1,1024]{1,0:T(2,128)(2,1)} %gain_ref.1) | copy-start | bytes 6148
  7.2 23.2 %copy-start.4 = (s32[2,128]{1,0:T(2,128)S(1)}, s32[2,128]{1,0:T(2,128)}, u32[]{:S(2)}) copy-start(s32[2,128]{1,0:T(2,128)} %valid_ref.1) | copy-start | bytes 3076
  7.2 23.2 %copy-start.5 = (s32[2,128]{1,0:T(2,128)S(1)}, s32[2,128]{1,0:T(2,128)}, u32[]{:S(2)}) copy-start(s32[2,128]{1,0:T(2,128)} %refs_6_.1) | copy-start | bytes 3076
  7.7 5.0 %collective-permute-start.6 = (bf16[384,128]{1,0:T(8,128)(2,1)S(1)}, bf16[384,128]{1,0:T(8,128)(2,1)S(1)}, u32[]{:S(2)}, u32[]{:S(2)}) collective-permute-start(bf16[384,128]{1,0:T(8,128)(2,1)S(1)} %get-tuple-element.20.refs_0_), channel_id=1, source_target_pairs={{0,1},{1,0},{2,3},{3,2},{4,5},{5,4},{6,7},{7,6},{8,9},{9,8},{10,11... | collective-permute-start | bytes 294920 | tf_op jit(solution)/shard_map/ppermute | solution.py:41
  12.8 15.5 %collective-permute-start.7 = (bf16[384,128]{1,0:T(8,128)(2,1)S(1)}, bf16[384,128]{1,0:T(8,128)(2,1)S(1)}, u32[]{:S(2)}, u32[]{:S(2)}) collective-permute-start(bf16[384,128]{1,0:T(8,128)(2,1)S(1)} %shard_map.97.refs_0_), channel_id=1, source_target_pairs={{0,2},{1,3},{2,0},{3,1},{4,6},{5,7},{6,4},{7,5},{8,10},{9,11},{10,... | collective-permute-start | bytes 294920 | tf_op jit(solution)/shard_map/ppermute | solution.py:41
  14.4 14.5 %collective-permute-start.3 = (bf16[656,128]{1,0:T(8,128)(2,1)S(1)}, bf16[656,128]{1,0:T(8,128)(2,1)S(1)}, u32[]{:S(2)}, u32[]{:S(2)}) collective-permute-start(bf16[656,128]{1,0:T(8,128)(2,1)S(1)} %get-tuple-element.19.refs_0_), channel_id=1, source_target_pairs={{0,1},{1,0},{2,3},{3,2},{4,5},{5,4},{6,7},{7,6},{8,9},{9,8},{10,11... | collective-permute-start | bytes 503816 | tf_op jit(solution)/shard_map/ppermute | solution.py:41
  15.9 13.0 %collective-permute-start.4 = (bf16[656,128]{1,0:T(8,128)(2,1)S(1)}, bf16[656,128]{1,0:T(8,128)(2,1)S(1)}, u32[]{:S(2)}, u32[]{:S(2)}) collective-permute-start(bf16[656,128]{1,0:T(8,128)(2,1)S(1)} %get-tuple-element.19.refs_0_), channel_id=1, source_target_pairs={{0,2},{1,3},{2,0},{3,1},{4,6},{5,7},{6,4},{7,5},{8,10},{9,11},{10,... | collective-permute-start | bytes 503816 | tf_op jit(solution)/shard_map/ppermute | solution.py:41
  16.4 12.5 %collective-permute-start.5 = (bf16[656,128]{1,0:T(8,128)(2,1)S(1)}, bf16[656,128]{1,0:T(8,128)(2,1)S(1)}, u32[]{:S(2)}, u32[]{:S(2)}) collective-permute-start(bf16[656,128]{1,0:T(8,128)(2,1)S(1)} %get-tuple-element.19.refs_0_), channel_id=1, source_target_pairs={{0,3},{1,2},{2,1},{3,0},{4,7},{5,6},{6,5},{7,4},{8,11},{9,10},{10,... | collective-permute-start | bytes 503816 | tf_op jit(solution)/shard_map/ppermute | solution.py:41
  28.3 15.7 %collective-permute-start.14 = (bf16[256,1024]{1,0:T(8,128)(2,1)S(1)}, bf16[256,1024]{1,0:T(8,128)(2,1)S(1)}, u32[]{:S(2)}, u32[]{:S(2)}) collective-permute-start(bf16[256,1024]{1,0:T(8,128)(2,1)S(1)} %collective-permute-done.13.refs_4_), channel_id=1, source_target_pairs={{0,16},{16,0},{1,17},{17,1},{2,18},{18,2},{3,19},{19,3},{4,20},{20... | collective-permute-start | bytes 1572872 | tf_op jit(solution)/shard_map/ppermute | solution.py:41
  28.3 2.0 %collective-permute-start.8 = (bf16[384,128]{1,0:T(8,128)(2,1)S(1)}, bf16[384,128]{1,0:T(8,128)(2,1)S(1)}, u32[]{:S(2)}, u32[]{:S(2)}) collective-permute-start(bf16[384,128]{1,0:T(8,128)(2,1)S(1)} %shard_map.98.refs_4_), channel_id=1, source_target_pairs={{0,16},{16,0},{1,17},{17,1},{2,18},{18,2},{3,19},{19,3},{4,20},{20... | collective-permute-start | bytes 294920 | tf_op jit(solution)/shard_map/ppermute | solution.py:41
  31.4 1.5 %collective-permute-start.9 = (bf16[768,128]{1,0:T(8,128)(2,1)S(1)}, bf16[768,128]{1,0:T(8,128)(2,1)S(1)}, u32[]{:S(2)}, u32[]{:S(2)}) collective-permute-start(bf16[768,128]{1,0:T(8,128)(2,1)S(1)} %get-tuple-element.21), channel_id=1, source_target_pairs={{0,16},{16,0},{1,17},{17,1},{2,18},{18,2},{3,19},{19,3},{4,20},{20... | collective-permute-start | bytes 589832 | tf_op jit(solution)/shard_map/ppermute | solution.py:41
  34.5 9.5 %collective-permute-start.10 = (bf16[528,128]{1,0:T(8,128)(2,1)S(1)}, bf16[528,128]{1,0:T(8,128)(2,1)S(1)}, u32[]{:S(2)}, u32[]{:S(2)}) collective-permute-start(bf16[528,128]{1,0:T(8,128)(2,1)S(1)} %get-tuple-element.29), channel_id=1, source_target_pairs={{0,4},{4,0},{8,12},{12,8},{1,5},{5,1},{9,13},{13,9},{2,6},{6,2},{1... | collective-permute-start | bytes 405512 | tf_op jit(solution)/shard_map/ppermute | solution.py:41
  34.5 5.7 %collective-permute-start.11 = (bf16[272,128]{1,0:T(8,128)(2,1)S(1)}, bf16[272,128]{1,0:T(8,128)(2,1)S(1)}, u32[]{:S(2)}, u32[]{:S(2)}) collective-permute-start(bf16[272,128]{1,0:T(8,128)(2,1)S(1)} %get-tuple-element.30), channel_id=1, source_target_pairs={{0,8},{4,12},{8,0},{12,4},{1,9},{5,13},{9,1},{13,5},{2,10},{6,14},... | collective-permute-start | bytes 208904 | tf_op jit(solution)/shard_map/ppermute | solution.py:41
  37.5 6.4 %collective-permute-start.12 = (bf16[272,128]{1,0:T(8,128)(2,1)S(1)}, bf16[272,128]{1,0:T(8,128)(2,1)S(1)}, u32[]{:S(2)}, u32[]{:S(2)}) collective-permute-start(bf16[272,128]{1,0:T(8,128)(2,1)S(1)} %get-tuple-element.31), channel_id=1, source_target_pairs={{0,12},{4,8},{8,4},{12,0},{1,13},{5,9},{9,5},{13,1},{2,14},{6,10},... | collective-permute-start | bytes 208904 | tf_op jit(solution)/shard_map/ppermute | solution.py:41

commit v7 on v6

--- a/solution.py
+++ b/solution.py
@@ -76,21 +76,23 @@
     out_ref[3 * half + 2 * rank :, :] = high_low(squares[: PACK // 2])
 
 
-def other_kernel(x_ref, up_ref, own_ref, down2_ref, up2_ref, gain2_ref, out_ref, gram_ref):
+def other_kernel(x_ref, up_ref, own_ref, down2_ref, up2_ref, gain2_ref, a_ref, b_ref, gram_ref):
     rank = down2_ref.shape[1]
     half = x_ref.shape[0] // lax.axis_size("section")
     me = lax.axis_index("section")
     it = 1 - me
     x = x_ref[rows_of(me * half, half), :]
     gain2 = gain2_ref[...].astype(F32)
-    out_ref[rows_of(me * half, half), :] = own_ref[:half, :]
-    out_ref[rows_of((2 + me) * half, half), :] = own_ref[half : 2 * half, :]
-    out_ref[4 * half : 5 * half, :] = own_ref[2 * half : 3 * half, :]
-    out_ref[5 * half :, :] = own_ref[3 * half + 2 * rank :, :]
+    middle = 5 * half // 2
+    a_ref[rows_of(me * half, half), :] = own_ref[:half, :]
+    b_ref[rows_of(me * half, half), :] = own_ref[half : 2 * half, :]
+    a_ref[2 * half : middle, :] = own_ref[2 * half : middle, :]
+    b_ref[2 * half : middle, :] = own_ref[middle : 3 * half, :]
+    a_ref[middle:, :] = own_ref[3 * half + 2 * rank :, :]
     gram_ref[rank:, :] = own_ref[3 * half : 3 * half + 2 * rank, :]
     scaled = (x.astype(F32) * gain2).astype(BF16)
-    out_ref[rows_of(it * half, half), :] = dot(scaled, down2_ref[...]).astype(BF16)
-    out_ref[rows_of((2 + it) * half, half), :] = dot_nt(x, up2_ref[...]).astype(BF16)
+    a_ref[rows_of(it * half, half), :] = dot(scaled, down2_ref[...]).astype(BF16)
+    b_ref[rows_of(it * half, half), :] = dot_nt(x, up2_ref[...]).astype(BF16)
 
     @pl.when(me == 0)
     def _():
@@ -127,13 +129,14 @@
 
 
 def chain_kernel(width, count, *refs):
-    parts, (gram_ref, gram2_ref, label_ref, valid_ref, mine_ref, theirs_ref) = refs[:count], refs[count:]
+    a_refs, b_refs = refs[:count], refs[count : 2 * count]
+    gram_ref, gram2_ref, label_ref, valid_ref, mine_ref, theirs_ref = refs[2 * count :]
     rank = gram_ref.shape[1]
     half = label_ref.shape[1]
     me = lax.axis_index("section")
     first = me == 0
 
-    def total(start, size):
+    def total(parts, start, size):
         return sum(r[start : start + size, :].astype(F32) for r in parts)
 
     def spread(row):
@@ -143,16 +146,17 @@
     gram0, gram1 = jnp.where(first, gram, gram2), jnp.where(first, gram2, gram)
     m01, b0h, b0b0 = (gram0[i * rank : (i + 1) * rank] for i in range(3))
     b1b0, b1h, b1b1 = (gram1[i * rank : (i + 1) * rank] for i in range(3))
-    tail = total(5 * half, PACK)
+    middle = 5 * half // 2
+    tail = total(a_refs, middle, PACK)
     squares0 = spread(tail[:1] + tail[PACK // 2 : PACK // 2 + 1])
     inv0 = lax.rsqrt(squares0 / width + epsilon)
-    proj0 = total(0, half)
+    proj0 = total(a_refs, 0, half)
     pre0 = inv0 * proj0
     sig0 = jax.nn.sigmoid(pre0)
     hidden0 = (pre0 * sig0).astype(BF16)
     hid0 = hidden0.astype(F32)
-    proj1 = total(half, half) + dot(hidden0, m01)
-    cross0 = total(2 * half, half)
+    proj1 = total(a_refs, half, half) + dot(hidden0, m01)
+    cross0 = total(b_refs, 0, half)
     one_b0 = cross0 + dot(hidden0, b0b0)
     squares1 = squares0 + jnp.sum(hid0 * (cross0 + one_b0), axis=1, keepdims=True)
     inv1 = lax.rsqrt(squares1 / width + epsilon)
@@ -160,12 +164,13 @@
     sig1 = jax.nn.sigmoid(pre1)
     hidden1 = (pre1 * sig1).astype(BF16)
     hid1 = hidden1.astype(F32)
-    one_b1 = total(3 * half, half) + dot_nt(hidden0, b1b0)
+    one_b1 = total(b_refs, half, half) + dot_nt(hidden0, b1b0)
     two_b0 = one_b0 + dot(hidden1, b1b0)
     two_b1 = one_b1 + dot(hidden1, b1b1)
     squares2 = squares1 + jnp.sum(hid1 * (one_b1 + two_b1), axis=1, keepdims=True)
     inv2 = lax.rsqrt(squares2 / width + epsilon)
-    base = total(4 * half, half) + dot(hidden0, b0h) + dot(hidden1, b1h)
+    base = jnp.concatenate([total(r, 2 * half, half // 2) for r in (a_refs, b_refs)], axis=0)
+    base = base + dot(hidden0, b0h) + dot(hidden1, b1h)
     logits = inv2 * base
     expo = jnp.exp(logits - jnp.max(logits, axis=1, keepdims=True))
     prob = expo / jnp.sum(expo, axis=1, keepdims=True)
@@ -333,40 +338,40 @@
         5 * small,
         states, down, up, head, wide_gain,
     )
-    packed, gram = call(
+    lower = 5 * half // 2
+    first_part, second_part, gram = call(
         other_kernel,
-        [shape((5 * half + PACK, rank), BF16), shape((3 * rank, rank), BF16)],
+        [shape((lower + PACK, rank), BF16), shape((lower, rank), BF16), shape((3 * rank, rank), BF16)],
         3 * small,
         states, up, own, down2, up2, gains2,
     )
-    wide = [packed]
-    for step in range(1, tensors):
-        wide.append(from_partner(packed, "tensor", step))
+    doubling = [1 << i for i in range(tensors.bit_length() - 1)]
+
+    def terms(value, steps):
+        if tensors & (tensors - 1):
+            return [value] + [from_partner(value, "tensor", step) for step in range(1, tensors)]
+        for hop, step in enumerate(steps):
+            got = from_partner(value, "tensor", step)
+            if hop + 1 == len(steps):
+                return [value, got]
+            value = call(add_kernel, shape(value.shape, BF16), small // 8, value, got)
+
+    gram = terms(gram, doubling)
+    second_part = terms(second_part, doubling[::-1])
+    first_part = terms(first_part, doubling)
+    gram = call(add_kernel, shape(gram[0].shape, BF16), small // 8, *gram)
     down_t, stack = call(
         prepare_kernel,
         [shape((rank, features), BF16), shape((4 * rank + half, features), BF16)],
         small,
         down, head, up, down2, up2, gains2, states,
     )
-    if tensors & (tensors - 1) == 0:
-        step = 1
-        while step < tensors:
-            gram = call(add_kernel, shape(gram.shape, BF16), small // 8, gram, from_partner(gram, "tensor", step))
-            step *= 2
-    else:
-        gram = call(
-            add_kernel,
-            shape(gram.shape, BF16),
-            small // 8,
-            gram,
-            *(from_partner(gram, "tensor", step) for step in range(1, tensors)),
-        )
     gram2 = from_partner(gram, "section", 1)
     made, theirs = call(
-        functools.partial(chain_kernel, width, tensors),
+        functools.partial(chain_kernel, width, len(first_part)),
         [shape((6 * half, rank), BF16)] * 2,
         16 * 2 * half * rank * rank,
-        *wide, gram, gram2, labels, valid,
+        *first_part, *second_part, gram, gram2, labels, valid,
     )
     met = from_partner(theirs, "section", 1)
     mixes, acc, left = call(

time: 45.3 us -> 50.1 us (1.11)
  waiting for transfers between devices: 21 us -> 24.1 us
  starting transfers between devices: 17.1 us -> 18.6 us
    ppermute x14 -> x15, waiting for transfers between devices: 10.5 us -> 12.2 us  [from_partner(): lax.ppermute(value, axis, [(i, partner(i, step, size)) for i in range(siz...]
    ppermute x14 -> x15, starting transfers between devices: 12.9 us -> 14.5 us  [from_partner(): lax.ppermute(value, axis, [(i, partner(i, step, size)) for i in range(siz...]
    ppermute x1, waiting for transfers between devices: 10.4 us -> 11.9 us  [local(): lax.ppermute(states, ('section', 'dp'), [(s * replicas + i, s * replicas...]
    pallas_call x10 -> x12, Pallas kernels: 5.63 us -> 5.7 us  [call(): pl.pallas_call(kernel, out_shape=out, cost_estimate=pl.CostEstimate(flops...]
  transfers between devices with their start and end apart: 15 -> 16, of which waited for: 6 -> 6; matrix products, arithmetic and copies ran while one was open for 0% -> 0% of each run, Pallas kernels for 10% -> 9%
where the time goes in v7:
time: 50.1 us; the launch traced here: 49.9 us
  waiting for transfers between devices  24.1 us (48%)
  starting transfers between devices  18.6 us (37%)
  Pallas kernels  5.7 us (11%)
  between operations  0.78 us (2%)
  local copies, waits for them, and re-layouts  0.71 us (1%)
    ppermute x15, starting transfers between devices, from_partner(): lax.ppermute(value, axis, [(i, partner(i, step, size)) for i in range(siz...  14.5 us
    ppermute x15, waiting for transfers between devices, from_partner(): lax.ppermute(value, axis, [(i, partner(i, step, size)) for i in range(siz...  12.2 us
    ppermute x1, waiting for transfers between devices, local(): lax.ppermute(states, ('section', 'dp'), [(s * replicas + i, s * replicas...  11.9 us
    pallas_call x12, Pallas kernels, call(): pl.pallas_call(kernel, out_shape=out, cost_estimate=pl.CostEstimate(flops...  5.7 us
    ppermute x1, starting transfers between devices, local(): lax.ppermute(states, ('section', 'dp'), [(s * replicas + i, s * replicas...  4.13 us
  transfers between devices with their start and end apart: 16, of which 6 were waited for; matrix products, arithmetic and copies ran while one was open for 0% of the time, Pallas kernels for 9%

profile of v7, /device:TPU:0, one launch (start us, length us, event | category | flops | bytes accessed | tf_op | source)
XLA Modules:
  0.0 49.9 jit_solution(15895618938921789508)
XLA Ops:
  0.6 4.1 %collective-permute-start.14 = (bf16[256,1024]{1,0:T(8,128)(2,1)}, bf16[256,1024]{1,0:T(8,128)(2,1)S(1)}, u32[]{:S(2)}, u32[]{:S(2)}) collective-permute-start(bf16[256,1024]{1,0:T(8,128)(2,1)} %bitcast.7), channel_id=1, source_target_pairs={{0,8},{4,12},{8,0},{12,4},{16,28},{20,24},{24,20},{28,16},{1,9},{5... | collective-permute-start | bytes 1572872 | tf_op jit(solution)/shard_map/ppermute | solution.py:328
  4.8 0.6 %collective-permute-start.1 = (bf16[128,1024]{1,0:T(8,128)(2,1)}, bf16[128,1024]{1,0:T(8,128)(2,1)S(1)}, u32[]{:S(2)}, u32[]{:S(2)}) collective-permute-start(bf16[128,1024]{1,0:T(8,128)(2,1)} %bitcast.12), channel_id=1, source_target_pairs={{0,16},{16,0},{1,17},{17,1},{2,18},{18,2},{3,19},{19,3},{4,20},{20... | collective-permute-start | bytes 786440 | tf_op jit(solution)/shard_map/ppermute | solution.py:41
  5.4 0.5 collective-permute-start.2
  5.9 0.7 %copy-done.6 = bf16[1,1024]{1,0:T(2,128)(2,1)S(1)} copy-done((bf16[1,1024]{1,0:T(2,128)(2,1)S(1)}, bf16[1,1024]{1,0:T(2,128)(2,1)}, u32[]{:S(2)}) %copy-start.6) | copy-done | bytes 2072
  6.6 0.5 %shard_map.95.own_ref = bf16[656,128]{1,0:T(8,128)(2,1)S(1)} custom-call(bf16[256,1024]{1,0:T(8,128)(2,1)S(1)} %bitcast.8, bf16[1024,128]{1,0:T(8,128)(2,1)S(1)} %bitcast.17, bf16[128,1024]{1,0:T(8,128)(2,1)S(1)} %bitcast.13, bf16[1024,128]{1,0:T(8,128)(2,1)S(1)} %copy-done.3, f32[1,1024]{1,0:T(1,128)S(1)} %shard_map.94.gain_ref.refs_7_), custom_call_target="tpu_custom_call" | custom-call | flops 167772160 | bytes 1314816 | tf_op jit(solution)/shard_map/pallas_call | solution.py:51
  7.2 0.5 %shard_map.96 = (bf16[336,128]{1,0:T(8,128)(2,1)S(1)}, bf16[320,128]{1,0:T(8,128)(2,1)S(1)}, bf16[384,128]{1,0:T(8,128)(2,1)S(1)}) custom-call(bf16[256,1024]{1,0:T(8,128)(2,1)S(1)} %bitcast.9, bf16[128,1024]{1,0:T(8,128)(2,1)S(1)} %bitcast.14, bf16[656,128]{1,0:T(8,128)(2,1)S(1)} %shard_map.95.own_ref, ...), custom_call_target="tpu_custom_call" | custom-call | flops 100663296 | bytes 1480704 | tf_op jit(solution)/shard_map/pallas_call | solution.py:51
  7.7 1.6 %collective-permute-start.7 = (bf16[384,128]{1,0:T(8,128)(2,1)S(1)}, bf16[384,128]{1,0:T(8,128)(2,1)S(1)}, u32[]{:S(2)}, u32[]{:S(2)}) collective-permute-start(bf16[384,128]{1,0:T(8,128)(2,1)S(1)} %get-tuple-element.22.refs_0_), channel_id=1, source_target_pairs={{0,1},{1,0},{2,3},{3,2},{4,5},{5,4},{6,7},{7,6},{8,9},{9,8},{10,11... | collective-permute-start | bytes 294920 | tf_op jit(solution)/shard_map/ppermute | solution.py:41
  9.3 3.5 %collective-permute-done.7.refs_1_ = bf16[384,128]{1,0:T(8,128)(2,1)S(1)} collective-permute-done((bf16[384,128]{1,0:T(8,128)(2,1)S(1)}, bf16[384,128]{1,0:T(8,128)(2,1)S(1)}, u32[]{:S(2)}, u32[]{:S(2)}) %collective-permute-start.7) | collective-permute-done | bytes 98336 | tf_op jit(solution)/shard_map/ppermute | solution.py:41
  12.8 1.6 %collective-permute-start.8 = (bf16[384,128]{1,0:T(8,128)(2,1)S(1)}, bf16[384,128]{1,0:T(8,128)(2,1)S(1)}, u32[]{:S(2)}, u32[]{:S(2)}) collective-permute-start(bf16[384,128]{1,0:T(8,128)(2,1)S(1)} %shard_map.99.refs_0_), channel_id=1, source_target_pairs={{0,2},{1,3},{2,0},{3,1},{4,6},{5,7},{6,4},{7,5},{8,10},{9,11},{10,... | collective-permute-start | bytes 294920 | tf_op jit(solution)/shard_map/ppermute | solution.py:41
  14.4 1.5 %collective-permute-start.3 = (bf16[336,128]{1,0:T(8,128)(2,1)S(1)}, bf16[336,128]{1,0:T(8,128)(2,1)S(1)}, u32[]{:S(2)}, u32[]{:S(2)}) collective-permute-start(bf16[336,128]{1,0:T(8,128)(2,1)S(1)} %get-tuple-element.20.refs_0_), channel_id=1, source_target_pairs={{0,1},{1,0},{2,3},{3,2},{4,5},{5,4},{6,7},{7,6},{8,9},{9,8},{10,11... | collective-permute-start | bytes 258056 | tf_op jit(solution)/shard_map/ppermute | solution.py:41
  15.9 0.5 %collective-permute-start.5 = (bf16[320,128]{1,0:T(8,128)(2,1)S(1)}, bf16[320,128]{1,0:T(8,128)(2,1)S(1)}, u32[]{:S(2)}, u32[]{:S(2)}) collective-permute-start(bf16[320,128]{1,0:T(8,128)(2,1)S(1)} %get-tuple-element.21.refs_0_), channel_id=1, source_target_pairs={{0,2},{1,3},{2,0},{3,1},{4,6},{5,7},{6,4},{7,5},{8,10},{9,11},{10,... | collective-permute-start | bytes 245768 | tf_op jit(solution)/shard_map/ppermute | solution.py:41
  16.4 11.9 %collective-permute-done.14.refs_4_ = bf16[256,1024]{1,0:T(8,128)(2,1)S(1)} collective-permute-done((bf16[256,1024]{1,0:T(8,128)(2,1)}, bf16[256,1024]{1,0:T(8,128)(2,1)S(1)}, u32[]{:S(2)}, u32[]{:S(2)}) %collective-permute-start.14) | collective-permute-done | bytes 524320 | tf_op jit(solution)/shard_map/ppermute | solution.py:328
  28.3 0.6 %collective-permute-start.9 = (bf16[384,128]{1,0:T(8,128)(2,1)S(1)}, bf16[384,128]{1,0:T(8,128)(2,1)S(1)}, u32[]{:S(2)}, u32[]{:S(2)}) collective-permute-start(bf16[384,128]{1,0:T(8,128)(2,1)S(1)} %shard_map.100.refs_4_), channel_id=1, source_target_pairs={{0,16},{16,0},{1,17},{17,1},{2,18},{18,2},{3,19},{19,3},{4,20},{20... | collective-permute-start | bytes 294920 | tf_op jit(solution)/shard_map/ppermute | solution.py:41
  28.9 1.6 %collective-permute-start.4 = (bf16[336,128]{1,0:T(8,128)(2,1)S(1)}, bf16[336,128]{1,0:T(8,128)(2,1)S(1)}, u32[]{:S(2)}, u32[]{:S(2)}) collective-permute-start(bf16[336,128]{1,0:T(8,128)(2,1)S(1)} %shard_map.97.refs_0_), channel_id=1, source_target_pairs={{0,2},{1,3},{2,0},{3,1},{4,6},{5,7},{6,4},{7,5},{8,10},{9,11},{10,... | collective-permute-start | bytes 258056 | tf_op jit(solution)/shard_map/ppermute | solution.py:41
  30.5 1.6 %collective-permute-start.6 = (bf16[320,128]{1,0:T(8,128)(2,1)S(1)}, bf16[320,128]{1,0:T(8,128)(2,1)S(1)}, u32[]{:S(2)}, u32[]{:S(2)}) collective-permute-start(bf16[320,128]{1,0:T(8,128)(2,1)S(1)} %shard_map.98.refs_2_), channel_id=1, source_target_pairs={{0,1},{1,0},{2,3},{3,2},{4,5},{5,4},{6,7},{7,6},{8,9},{9,8},{10,11... | collective-permute-start | bytes 245768 | tf_op jit(solution)/shard_map/ppermute | solution.py:41
  32.1 2.9 %collective-permute-done.6.refs_3_ = bf16[320,128]{1,0:T(8,128)(2,1)S(1)} collective-permute-done((bf16[320,128]{1,0:T(8,128)(2,1)S(1)}, bf16[320,128]{1,0:T(8,128)(2,1)S(1)}, u32[]{:S(2)}, u32[]{:S(2)}) %collective-permute-start.6) | collective-permute-done | bytes 81952 | tf_op jit(solution)/shard_map/ppermute | solution.py:41
  35.1 1.1 %shard_map.101 = (bf16[768,128]{1,0:T(8,128)(2,1)S(1)}, bf16[768,128]{1,0:T(8,128)(2,1)S(1)}) custom-call(bf16[336,128]{1,0:T(8,128)(2,1)S(1)} %shard_map.97.refs_0_, bf16[336,128]{1,0:T(8,128)(2,1)S(1)} %collective-permute-done.4.refs_1_, bf16[320,128]{1,0:T(8,128)(2,1)S(1)} %shard_map.98.refs_2_, bf16[320,128]{1,0:T(8,128)(2,1)S(1)} %collective-permute-done.6.refs_3_, ...), custom_call_target="tpu_custom_call" | custom-call | flops 67108864 | bytes 534528 | tf_op jit(solution)/shard_map/pallas_call | solution.py:51
  37.0 0.7 %collective-permute-done.10.made_ref = bf16[768,128]{1,0:T(8,128)(2,1)S(1)} collective-permute-done((bf16[768,128]{1,0:T(8,128)(2,1)S(1)}, bf16[768,128]{1,0:T(8,128)(2,1)S(1)}, u32[]{:S(2)}, u32[]{:S(2)}) %collective-permute-start.10) | collective-permute-done | bytes 196640 | tf_op jit(solution)/shard_map/ppermute | solution.py:41
  37.6 1.6 %shard_map.104 = (bf16[528,128]{1,0:T(8,128)(2,1)S(1)}, bf16[528,128]{1,0:T(8,128)(2,1)S(1)}, bf16[272,128]{1,0:T(8,128)(2,1)S(1)}, bf16[272,128]{1,0:T(8,128)(2...) custom-call(bf16[768,128]{1,0:T(8,128)(2,1)S(1)} %collective-permute-done.10.made_ref, ...), custom_call_target="tpu_custom_call" | custom-call | flops 536870912 | bytes 3150848 | tf_op jit(solution)/shard_map/pallas_call | solution.py:51
  39.2 3.0 %collective-permute-start.12 = (bf16[272,128]{1,0:T(8,128)(2,1)S(1)}, bf16[272,128]{1,0:T(8,128)(2,1)S(1)}, u32[]{:S(2)}, u32[]{:S(2)}) collective-permute-start(bf16[272,128]{1,0:T(8,128)(2,1)S(1)} %get-tuple-element.32), channel_id=1, source_target_pairs={{0,8},{4,12},{8,0},{12,4},{1,9},{5,13},{9,1},{13,5},{2,10},{6,14},... | collective-permute-start | bytes 208904 | tf_op jit(solution)/shard_map/ppermute | solution.py:41
  42.3 1.4 %collective-permute-start.13 = (bf16[272,128]{1,0:T(8,128)(2,1)S(1)}, bf16[272,128]{1,0:T(8,128)(2,1)S(1)}, u32[]{:S(2)}, u32[]{:S(2)}) collective-permute-start(bf16[272,128]{1,0:T(8,128)(2,1)S(1)} %get-tuple-element.33), channel_id=1, source_target_pairs={{0,12},{4,8},{8,4},{12,0},{1,13},{5,9},{9,5},{13,1},{2,14},{6,10},... | collective-permute-start | bytes 208904 | tf_op jit(solution)/shard_map/ppermute | solution.py:41
  43.6 1.3 %collective-permute-done.12.refs_2_ = bf16[272,128]{1,0:T(8,128)(2,1)S(1)} collective-permute-done((bf16[272,128]{1,0:T(8,128)(2,1)S(1)}, bf16[272,128]{1,0:T(8,128)(2,1)S(1)}, u32[]{:S(2)}, u32[]{:S(2)}) %collective-permute-start.12) | collective-permute-done | bytes 69664 | tf_op jit(solution)/shard_map/ppermute | solution.py:41
  44.9 3.7 %collective-permute-done.13.refs_3_ = bf16[272,128]{1,0:T(8,128)(2,1)S(1)} collective-permute-done((bf16[272,128]{1,0:T(8,128)(2,1)S(1)}, bf16[272,128]{1,0:T(8,128)(2,1)S(1)}, u32[]{:S(2)}, u32[]{:S(2)}) %collective-permute-start.13) | collective-permute-done | bytes 69664 | tf_op jit(solution)/shard_map/ppermute | solution.py:41
  48.7 1.2 %shard_map.105 = (f32[32,1024]{1,0:T(8,128)}, f32[32,1024]{1,0:T(8,128)}, f32[1,1024]{1,0:T(1,128)}) custom-call(bf16[528,128]{1,0:T(8,128)(2,1)S(1)} %get-tuple-element.30.refs_0_, bf16[528,128]{1,0:T(8,128)(2,1)S(1)} %collective-permute-done.11.refs_1_, bf16[272,128]{1,0:T(8,128)(2,1)S(1)} %collective-permute-done.12.refs_2_, ...), custom_call_target="tpu_custom_call" | custom-call | flops 67108864 | bytes 2772992 | tf_op jit(solution)/shard_map/pallas_call | solution.py:51
  (34 shorter events, 1.1 us)
Async XLA Ops:
  0.6 27.7 %collective-permute-start.14 = (bf16[256,1024]{1,0:T(8,128)(2,1)}, bf16[256,1024]{1,0:T(8,128)(2,1)S(1)}, u32[]{:S(2)}, u32[]{:S(2)}) collective-permute-start(bf16[256,1024]{1,0:T(8,128)(2,1)} %bitcast.7), channel_id=1, source_target_pairs={{0,8},{4,12},{8,0},{12,4},{16,28},{20,24},{24,20},{28,16},{1,9},{5... | collective-permute-start | bytes 1572872 | tf_op jit(solution)/shard_map/ppermute | solution.py:328
  4.8 2.4 %collective-permute-start.1 = (bf16[128,1024]{1,0:T(8,128)(2,1)}, bf16[128,1024]{1,0:T(8,128)(2,1)S(1)}, u32[]{:S(2)}, u32[]{:S(2)}) collective-permute-start(bf16[128,1024]{1,0:T(8,128)(2,1)} %bitcast.12), channel_id=1, source_target_pairs={{0,16},{16,0},{1,17},{17,1},{2,18},{18,2},{3,19},{19,3},{4,20},{20... | collective-permute-start | bytes 786440 | tf_op jit(solution)/shard_map/ppermute | solution.py:41
  5.3 1.3 %copy-start = (bf16[2,128,1024]{2,1,0:T(8,128)(2,1)S(1)}, bf16[2,128,1024]{2,1,0:T(8,128)(2,1)}, u32[]{:S(2)}) copy-start(bf16[2,128,1024]{2,1,0:T(8,128)(2,1)} %param.7) | copy-start | bytes 1572868
  5.3 1.3 %copy-start.1 = (bf16[1,128,1024]{2,1,0:T(8,128)(2,1)S(1)}, bf16[1,128,1024]{2,1,0:T(8,128)(2,1)}, u32[]{:S(2)}) copy-start(bf16[1,128,1024]{2,1,0:T(8,128)(2,1)} %param.9) | copy-start | bytes 786436
  5.3 1.3 %copy-start.2 = (bf16[1,1024,128]{2,1,0:T(8,128)(2,1)S(1)}, bf16[1,1024,128]{2,1,0:T(8,128)(2,1)}, u32[]{:S(2)}) copy-start(bf16[1,1024,128]{2,1,0:T(8,128)(2,1)} %param.8) | copy-start | bytes 786436
  5.3 1.3 %copy-start.3 = (bf16[1024,128]{1,0:T(8,128)(2,1)S(1)}, bf16[1024,128]{1,0:T(8,128)(2,1)}, u32[]{:S(2)}) copy-start(bf16[1024,128]{1,0:T(8,128)(2,1)} %head_ref.3) | copy-start | bytes 786436
  5.3 1.9 %collective-permute-start = (bf16[1024,128]{1,0:T(8,128)(2,1)}, bf16[1024,128]{1,0:T(8,128)(2,1)S(1)}, u32[]{:S(2)}, u32[]{:S(2)}) collective-permute-start(bf16[1024,128]{1,0:T(8,128)(2,1)} %bitcast.16), channel_id=1, source_target_pairs={{0,16},{16,0},{1,17},{17,1},{2,18},{18,2},{3,19},{19,3},{4,20},{20... | collective-permute-start | bytes 786440 | tf_op jit(solution)/shard_map/ppermute | solution.py:41
  5.4 1.8 %collective-permute-start.2 = (bf16[1,1024]{1,0:T(2,128)(2,1)}, bf16[1,1024]{1,0:T(2,128)(2,1)S(1)}, u32[]{:S(2)}, u32[]{:S(2)}) collective-permute-start(bf16[1,1024]{1,0:T(2,128)(2,1)} %gain_ref.1), channel_id=1, source_target_pairs={{0,16},{16,0},{1,17},{17,1},{2,18},{18,2},{3,19},{19,3},{4,20},{20... | collective-permute-start | bytes 6152 | tf_op jit(solution)/shard_map/ppermute | solution.py:41
  5.9 0.7 %copy-start.6 = (bf16[1,1024]{1,0:T(2,128)(2,1)S(1)}, bf16[1,1024]{1,0:T(2,128)(2,1)}, u32[]{:S(2)}) copy-start(bf16[1,1024]{1,0:T(2,128)(2,1)} %gain_ref.1) | copy-start | bytes 6148
  7.2 27.9 %copy-start.4 = (s32[2,128]{1,0:T(2,128)S(1)}, s32[2,128]{1,0:T(2,128)}, u32[]{:S(2)}) copy-start(s32[2,128]{1,0:T(2,128)} %valid_ref.1) | copy-start | bytes 3076
  7.2 27.9 %copy-start.5 = (s32[2,128]{1,0:T(2,128)S(1)}, s32[2,128]{1,0:T(2,128)}, u32[]{:S(2)}) copy-start(s32[2,128]{1,0:T(2,128)} %refs_6_.1) | copy-start | bytes 3076
  7.7 5.0 %collective-permute-start.7 = (bf16[384,128]{1,0:T(8,128)(2,1)S(1)}, bf16[384,128]{1,0:T(8,128)(2,1)S(1)}, u32[]{:S(2)}, u32[]{:S(2)}) collective-permute-start(bf16[384,128]{1,0:T(8,128)(2,1)S(1)} %get-tuple-element.22.refs_0_), channel_id=1, source_target_pairs={{0,1},{1,0},{2,3},{3,2},{4,5},{5,4},{6,7},{7,6},{8,9},{9,8},{10,11... | collective-permute-start | bytes 294920 | tf_op jit(solution)/shard_map/ppermute | solution.py:41
  12.8 15.5 %collective-permute-start.8 = (bf16[384,128]{1,0:T(8,128)(2,1)S(1)}, bf16[384,128]{1,0:T(8,128)(2,1)S(1)}, u32[]{:S(2)}, u32[]{:S(2)}) collective-permute-start(bf16[384,128]{1,0:T(8,128)(2,1)S(1)} %shard_map.99.refs_0_), channel_id=1, source_target_pairs={{0,2},{1,3},{2,0},{3,1},{4,6},{5,7},{6,4},{7,5},{8,10},{9,11},{10,... | collective-permute-start | bytes 294920 | tf_op jit(solution)/shard_map/ppermute | solution.py:41
  14.4 14.5 %collective-permute-start.3 = (bf16[336,128]{1,0:T(8,128)(2,1)S(1)}, bf16[336,128]{1,0:T(8,128)(2,1)S(1)}, u32[]{:S(2)}, u32[]{:S(2)}) collective-permute-start(bf16[336,128]{1,0:T(8,128)(2,1)S(1)} %get-tuple-element.20.refs_0_), channel_id=1, source_target_pairs={{0,1},{1,0},{2,3},{3,2},{4,5},{5,4},{6,7},{7,6},{8,9},{9,8},{10,11... | collective-permute-start | bytes 258056 | tf_op jit(solution)/shard_map/ppermute | solution.py:41
  15.9 14.7 %collective-permute-start.5 = (bf16[320,128]{1,0:T(8,128)(2,1)S(1)}, bf16[320,128]{1,0:T(8,128)(2,1)S(1)}, u32[]{:S(2)}, u32[]{:S(2)}) collective-permute-start(bf16[320,128]{1,0:T(8,128)(2,1)S(1)} %get-tuple-element.21.refs_0_), channel_id=1, source_target_pairs={{0,2},{1,3},{2,0},{3,1},{4,6},{5,7},{6,4},{7,5},{8,10},{9,11},{10,... | collective-permute-start | bytes 245768 | tf_op jit(solution)/shard_map/ppermute | solution.py:41
  28.3 20.4 %collective-permute-start.15 = (bf16[256,1024]{1,0:T(8,128)(2,1)S(1)}, bf16[256,1024]{1,0:T(8,128)(2,1)S(1)}, u32[]{:S(2)}, u32[]{:S(2)}) collective-permute-start(bf16[256,1024]{1,0:T(8,128)(2,1)S(1)} %collective-permute-done.14.refs_4_), channel_id=1, source_target_pairs={{0,16},{16,0},{1,17},{17,1},{2,18},{18,2},{3,19},{19,3},{4,20},{20... | collective-permute-start | bytes 1572872 | tf_op jit(solution)/shard_map/ppermute | solution.py:41
  28.3 6.7 %collective-permute-start.9 = (bf16[384,128]{1,0:T(8,128)(2,1)S(1)}, bf16[384,128]{1,0:T(8,128)(2,1)S(1)}, u32[]{:S(2)}, u32[]{:S(2)}) collective-permute-start(bf16[384,128]{1,0:T(8,128)(2,1)S(1)} %shard_map.100.refs_4_), channel_id=1, source_target_pairs={{0,16},{16,0},{1,17},{17,1},{2,18},{18,2},{3,19},{19,3},{4,20},{20... | collective-permute-start | bytes 294920 | tf_op jit(solution)/shard_map/ppermute | solution.py:41
  28.9 6.1 %collective-permute-start.4 = (bf16[336,128]{1,0:T(8,128)(2,1)S(1)}, bf16[336,128]{1,0:T(8,128)(2,1)S(1)}, u32[]{:S(2)}, u32[]{:S(2)}) collective-permute-start(bf16[336,128]{1,0:T(8,128)(2,1)S(1)} %shard_map.97.refs_0_), channel_id=1, source_target_pairs={{0,2},{1,3},{2,0},{3,1},{4,6},{5,7},{6,4},{7,5},{8,10},{9,11},{10,... | collective-permute-start | bytes 258056 | tf_op jit(solution)/shard_map/ppermute | solution.py:41
  30.5 4.5 %collective-permute-start.6 = (bf16[320,128]{1,0:T(8,128)(2,1)S(1)}, bf16[320,128]{1,0:T(8,128)(2,1)S(1)}, u32[]{:S(2)}, u32[]{:S(2)}) collective-permute-start(bf16[320,128]{1,0:T(8,128)(2,1)S(1)} %shard_map.98.refs_2_), channel_id=1, source_target_pairs={{0,1},{1,0},{2,3},{3,2},{4,5},{5,4},{6,7},{7,6},{8,9},{9,8},{10,11... | collective-permute-start | bytes 245768 | tf_op jit(solution)/shard_map/ppermute | solution.py:41
  36.1 1.5 %collective-permute-start.10 = (bf16[768,128]{1,0:T(8,128)(2,1)S(1)}, bf16[768,128]{1,0:T(8,128)(2,1)S(1)}, u32[]{:S(2)}, u32[]{:S(2)}) collective-permute-start(bf16[768,128]{1,0:T(8,128)(2,1)S(1)} %get-tuple-element.23), channel_id=1, source_target_pairs={{0,16},{16,0},{1,17},{17,1},{2,18},{18,2},{3,19},{19,3},{4,20},{20... | collective-permute-start | bytes 589832 | tf_op jit(solution)/shard_map/ppermute | solution.py:41
  39.2 9.4 %collective-permute-start.11 = (bf16[528,128]{1,0:T(8,128)(2,1)S(1)}, bf16[528,128]{1,0:T(8,128)(2,1)S(1)}, u32[]{:S(2)}, u32[]{:S(2)}) collective-permute-start(bf16[528,128]{1,0:T(8,128)(2,1)S(1)} %get-tuple-element.31), channel_id=1, source_target_pairs={{0,4},{4,0},{8,12},{12,8},{1,5},{5,1},{9,13},{13,9},{2,6},{6,2},{1... | collective-permute-start | bytes 405512 | tf_op jit(solution)/shard_map/ppermute | solution.py:41
  39.2 5.7 %collective-permute-start.12 = (bf16[272,128]{1,0:T(8,128)(2,1)S(1)}, bf16[272,128]{1,0:T(8,128)(2,1)S(1)}, u32[]{:S(2)}, u32[]{:S(2)}) collective-permute-start(bf16[272,128]{1,0:T(8,128)(2,1)S(1)} %get-tuple-element.32), channel_id=1, source_target_pairs={{0,8},{4,12},{8,0},{12,4},{1,9},{5,13},{9,1},{13,5},{2,10},{6,14},... | collective-permute-start | bytes 208904 | tf_op jit(solution)/shard_map/ppermute | solution.py:41
  42.3 6.4 %collective-permute-start.13 = (bf16[272,128]{1,0:T(8,128)(2,1)S(1)}, bf16[272,128]{1,0:T(8,128)(2,1)S(1)}, u32[]{:S(2)}, u32[]{:S(2)}) collective-permute-start(bf16[272,128]{1,0:T(8,128)(2,1)S(1)} %get-tuple-element.33), channel_id=1, source_target_pairs={{0,12},{4,8},{8,4},{12,0},{1,13},{5,9},{9,5},{13,1},{2,14},{6,10},... | collective-permute-start | bytes 208904 | tf_op jit(solution)/shard_map/ppermute | solution.py:41

commit v8 on v7

--- a/solution.py
+++ b/solution.py
@@ -60,10 +60,11 @@
     out_ref[...] = gain_ref[...].astype(F32)
 
 
-def own_kernel(x_ref, down_ref, up_ref, head_ref, gain_ref, out_ref):
+def own_kernel(x_ref, down_ref, up_ref, head_ref, gain_ref, out_ref, half_ref):
     rank = down_ref.shape[1]
     half = x_ref.shape[0] // lax.axis_size("section")
     x, up, head = x_ref[rows_of(lax.axis_index("section") * half, half), :], up_ref[...], head_ref[...]
+    half_ref[...] = x
     x32 = x.astype(F32)
     scaled = (x32 * gain_ref[...]).astype(BF16)
     out_ref[:half, :] = dot(scaled, down_ref[...]).astype(BF16)
@@ -270,7 +271,7 @@
 
 
 def last_kernel(whole, *refs):
-    parts, (far_ref, cross_ref, stack_ref, gain_ref, down_out, up_out, gain_out) = refs[:-7], refs[-7:]
+    parts, (far_refs, stack_ref, gain_ref, down_out, up_out, gain_out) = refs[:-9], (refs[-9:-5], *refs[-5:])
     near, (a_ref, b_ref) = parts[:whole], parts[whole:]
     rank = a_ref.shape[1]
     slim, features = down_out.shape
@@ -280,15 +281,17 @@
     def total(start, size):
         return sum(p[start : start + size, :].astype(F32) for p in near)
 
-    def left(ref):
-        rows = [ref[i * slim : (i + 1) * slim, :] for i in range(4, 8)]
-        return jnp.concatenate([jnp.concatenate(rows[:2], axis=1), jnp.concatenate(rows[2:], axis=1)], axis=0)
+    def left(ref, i):
+        rows = [ref[j * slim : (j + 1) * slim, :] for j in (4 + i, 6 + i)]
+        return jnp.concatenate(rows, axis=0)
 
     tail = sum(p[-PACK:, :].astype(F32) for p in parts)
     scale = 1.0 / tail[lines : lines + 1, :1]
-    left_a, left_b = left(a_ref), left(b_ref)
-    moved = dot(jnp.where(first, left_a, left_b), far_ref[...])
-    moved = moved + dot(jnp.where(first, left_b, left_a), cross_ref[...])
+    moved = 0.0
+    for i, ref in enumerate((a_ref, b_ref)):
+        one, two = left(ref, 0), left(ref, 1)
+        moved = moved + dot(jnp.where(first, one, two), far_refs[i][...])
+        moved = moved + dot(jnp.where(first, two, one), far_refs[2 + i][...])
     mixes = [
         (a_ref[i * slim : (i + 1) * slim, :].astype(F32) + b_ref[i * slim : (i + 1) * slim, :].astype(F32)).astype(BF16)
         for i in range(4)
@@ -325,19 +328,15 @@
     down2, up2, gains2 = others
     whole = replicas - sections
     assert whole > 0
-    far = lax.ppermute(
-        states,
-        ("section", "dp"),
-        [(s * replicas + i, s * replicas + partner(i, whole + s, replicas)) for s in range(sections) for i in range(replicas)],
-    )
     small = 2 * rank * rank * features
     wide_gain = call(gain_kernel, shape(gains.shape, F32), 40 * small, gains)
-    own = call(
+    own, mine = call(
         own_kernel,
-        shape((3 * half + 2 * rank + PACK, rank), BF16),
+        [shape((3 * half + 2 * rank + PACK, rank), BF16), shape((half, features), BF16)],
         5 * small,
         states, down, up, head, wide_gain,
     )
+    far = from_partner(mine, "dp", whole)
     lower = 5 * half // 2
     first_part, second_part, gram = call(
         other_kernel,
@@ -374,6 +373,7 @@
         *first_part, *second_part, gram, gram2, labels, valid,
     )
     met = from_partner(theirs, "section", 1)
+    fars = [far, from_partner(far, "dp", 1)]
     mixes, acc, left = call(
         mine_kernel,
         [shape((4 * rank, rank), F32), shape((2 * rank, features), F32), shape((2 * rank, half), BF16)],
@@ -390,12 +390,13 @@
     )
     for step in range(1, replicas):
         parts[step] = from_partner(parts[step], "dp", step)
-    cross = from_partner(far, "section", 1)
+    for i in range(2):
+        fars.append(from_partner(fars[i], "section", 1))
     down_grad, up_grad, gain_grad = call(
         functools.partial(last_kernel, whole),
         [shape((slim, features), F32), shape((slim, features), F32), shape((1, features), F32)],
         2 * small,
-        *parts, far, cross, stack, wide_gain,
+        *parts, *fars, stack, wide_gain,
     )
     return down_grad.T[None], up_grad[None], gain_grad
 

time: 50.1 us -> 43.5 us (0.87)
  waiting for transfers between devices: 24.1 us -> 16.7 us
    ppermute x1 -> x0, waiting for transfers between devices: 11.9 us -> none  [local(): lax.ppermute(states, ('section', 'dp'), [(s * replicas + i, s * replicas...]
    ppermute x15 -> x18, starting transfers between devices: 14.5 us -> 19.1 us  [from_partner(): lax.ppermute(value, axis, [(i, partner(i, step, size)) for i in range(siz...]
    ppermute x15 -> x18, waiting for transfers between devices: 12.2 us -> 16.7 us  [from_partner(): lax.ppermute(value, axis, [(i, partner(i, step, size)) for i in range(siz...]
    ppermute x1 -> x0, starting transfers between devices: 4.13 us -> none  [local(): lax.ppermute(states, ('section', 'dp'), [(s * replicas + i, s * replicas...]
    unnamed x14 -> x16, local copies, waits for them, and re-layouts: 0.71 us -> 1.17 us
  transfers between devices with their start and end apart: 16 -> 18, of which waited for: 6 -> 7; matrix products, arithmetic and copies ran while one was open for 0% -> 0% of each run, Pallas kernels for 9% -> 10%
where the time goes in v8:
time: 43.5 us; the launch traced here: 43.3 us
  starting transfers between devices  19.1 us (44%)
  waiting for transfers between devices  16.7 us (38%)
  Pallas kernels  5.66 us (13%)
  local copies, waits for them, and re-layouts  1.17 us (3%)
  between operations  0.76 us (2%)
    ppermute x18, starting transfers between devices, from_partner(): lax.ppermute(value, axis, [(i, partner(i, step, size)) for i in range(siz...  19.1 us
    ppermute x18, waiting for transfers between devices, from_partner(): lax.ppermute(value, axis, [(i, partner(i, step, size)) for i in range(siz...  16.7 us
    pallas_call x12, Pallas kernels, call(): pl.pallas_call(kernel, out_shape=out, cost_estimate=pl.CostEstimate(flops...  5.66 us
    unnamed x16, local copies, waits for them, and re-layouts  1.17 us
  transfers between devices with their start and end apart: 18, of which 7 were waited for; matrix products, arithmetic and copies ran while one was open for 0% of the time, Pallas kernels for 10%

profile of v8, /device:TPU:0, one launch (start us, length us, event | category | flops | bytes accessed | tf_op | source)
XLA Modules:
  0.0 43.3 jit_solution(17408033008501175345)
XLA Ops:
  0.6 0.6 %collective-permute-start.1 = (bf16[128,1024]{1,0:T(8,128)(2,1)}, bf16[128,1024]{1,0:T(8,128)(2,1)S(1)}, u32[]{:S(2)}, u32[]{:S(2)}) collective-permute-start(bf16[128,1024]{1,0:T(8,128)(2,1)} %bitcast.11), channel_id=1, source_target_pairs={{0,16},{16,0},{1,17},{17,1},{2,18},{18,2},{3,19},{19,3},{4,20},{20... | collective-permute-start | bytes 786440 | tf_op jit(solution)/shard_map/ppermute | solution.py:41
  1.3 0.8 %copy-done.6 = bf16[1,1024]{1,0:T(2,128)(2,1)S(1)} copy-done((bf16[1,1024]{1,0:T(2,128)(2,1)S(1)}, bf16[1,1024]{1,0:T(2,128)(2,1)}, u32[]{:S(2)}) %copy-start.6) | copy-done | bytes 2072
  2.5 0.5 %shard_map.95 = (bf16[656,128]{1,0:T(8,128)(2,1)S(1)}, bf16[128,1024]{1,0:T(8,128)(2,1)S(1)}) custom-call(bf16[256,1024]{1,0:T(8,128)(2,1)S(1)} %bitcast.7, bf16[1024,128]{1,0:T(8,128)(2,1)S(1)} %bitcast.16, bf16[128,1024]{1,0:T(8,128)(2,1)S(1)} %bitcast.12, bf16[1024,128]{1,0:T(8,128)(2,1)S(1)} %copy-done.3, f32[1,1024]{1,0:T(1,128)S(1)} %shard_map.94.gain_ref.refs_9_), custom_call_target="tpu_custom_call" | custom-call | flops 167772160 | bytes 1314816 | tf_op jit(solution)/shard_map/pallas_call | solution.py:51
  3.0 3.7 %collective-permute-start.14 = (bf16[128,1024]{1,0:T(8,128)(2,1)S(1)}, bf16[128,1024]{1,0:T(8,128)(2,1)S(1)}, u32[]{:S(2)}, u32[]{:S(2)}) collective-permute-start(bf16[128,1024]{1,0:T(8,128)(2,1)S(1)} %get-tuple-element.37), channel_id=1, source_target_pairs={{0,8},{4,12},{8,0},{12,4},{1,9},{5,13},{9,1},{13,5},{2,10},{6,14},... | collective-permute-start | bytes 786440 | tf_op jit(solution)/shard_map/ppermute | solution.py:41
  6.9 1.0 %collective-permute-done.2.gain2_ref = bf16[1,1024]{1,0:T(2,128)(2,1)S(1)} collective-permute-done((bf16[1,1024]{1,0:T(2,128)(2,1)S(1)}, bf16[1,1024]{1,0:T(2,128)(2,1)S(1)}, u32[]{:S(2)}, u32[]{:S(2)}) %collective-permute-start.2) | collective-permute-done | bytes 2080 | tf_op jit(solution)/shard_map/ppermute | solution.py:41
  7.9 0.5 %shard_map.96 = (bf16[336,128]{1,0:T(8,128)(2,1)S(1)}, bf16[320,128]{1,0:T(8,128)(2,1)S(1)}, bf16[384,128]{1,0:T(8,128)(2,1)S(1)}) custom-call(bf16[256,1024]{1,0:T(8,128)(2,1)S(1)} %bitcast.8, bf16[128,1024]{1,0:T(8,128)(2,1)S(1)} %bitcast.13, bf16[656,128]{1,0:T(8,128)(2,1)S(1)} %get-tuple-element.22.own_ref, ...), custom_call_target="tpu_custom_call" | custom-call | flops 100663296 | bytes 1480704 | tf_op jit(solution)/shard_map/pallas_call | solution.py:51
  8.4 1.6 %collective-permute-start.7 = (bf16[384,128]{1,0:T(8,128)(2,1)S(1)}, bf16[384,128]{1,0:T(8,128)(2,1)S(1)}, u32[]{:S(2)}, u32[]{:S(2)}) collective-permute-start(bf16[384,128]{1,0:T(8,128)(2,1)S(1)} %get-tuple-element.25.refs_0_), channel_id=1, source_target_pairs={{0,1},{1,0},{2,3},{3,2},{4,5},{5,4},{6,7},{7,6},{8,9},{9,8},{10,11... | collective-permute-start | bytes 294920 | tf_op jit(solution)/shard_map/ppermute | solution.py:41
  9.9 3.4 %collective-permute-done.7.refs_1_ = bf16[384,128]{1,0:T(8,128)(2,1)S(1)} collective-permute-done((bf16[384,128]{1,0:T(8,128)(2,1)S(1)}, bf16[384,128]{1,0:T(8,128)(2,1)S(1)}, u32[]{:S(2)}, u32[]{:S(2)}) %collective-permute-start.7) | collective-permute-done | bytes 98336 | tf_op jit(solution)/shard_map/ppermute | solution.py:41
  13.4 1.6 %collective-permute-start.8 = (bf16[384,128]{1,0:T(8,128)(2,1)S(1)}, bf16[384,128]{1,0:T(8,128)(2,1)S(1)}, u32[]{:S(2)}, u32[]{:S(2)}) collective-permute-start(bf16[384,128]{1,0:T(8,128)(2,1)S(1)} %shard_map.99.refs_0_), channel_id=1, source_target_pairs={{0,2},{1,3},{2,0},{3,1},{4,6},{5,7},{6,4},{7,5},{8,10},{9,11},{10,... | collective-permute-start | bytes 294920 | tf_op jit(solution)/shard_map/ppermute | solution.py:41
  15.0 1.5 %collective-permute-start.3 = (bf16[336,128]{1,0:T(8,128)(2,1)S(1)}, bf16[336,128]{1,0:T(8,128)(2,1)S(1)}, u32[]{:S(2)}, u32[]{:S(2)}) collective-permute-start(bf16[336,128]{1,0:T(8,128)(2,1)S(1)} %get-tuple-element.23.refs_0_), channel_id=1, source_target_pairs={{0,1},{1,0},{2,3},{3,2},{4,5},{5,4},{6,7},{7,6},{8,9},{9,8},{10,11... | collective-permute-start | bytes 258056 | tf_op jit(solution)/shard_map/ppermute | solution.py:41
  16.5 0.5 %collective-permute-start.5 = (bf16[320,128]{1,0:T(8,128)(2,1)S(1)}, bf16[320,128]{1,0:T(8,128)(2,1)S(1)}, u32[]{:S(2)}, u32[]{:S(2)}) collective-permute-start(bf16[320,128]{1,0:T(8,128)(2,1)S(1)} %get-tuple-element.24.refs_0_), channel_id=1, source_target_pairs={{0,2},{1,3},{2,0},{3,1},{4,6},{5,7},{6,4},{7,5},{8,10},{9,11},{10,... | collective-permute-start | bytes 245768 | tf_op jit(solution)/shard_map/ppermute | solution.py:41
  17.0 2.3 %collective-permute-done.14.refs_4_ = bf16[128,1024]{1,0:T(8,128)(2,1)S(1)} collective-permute-done((bf16[128,1024]{1,0:T(8,128)(2,1)S(1)}, bf16[128,1024]{1,0:T(8,128)(2,1)S(1)}, u32[]{:S(2)}, u32[]{:S(2)}) %collective-permute-start.14) | collective-permute-done | bytes 262176 | tf_op jit(solution)/shard_map/ppermute | solution.py:41
  19.2 0.7 %collective-permute-start.15 = (bf16[128,1024]{1,0:T(8,128)(2,1)S(1)}, bf16[128,1024]{1,0:T(8,128)(2,1)S(1)}, u32[]{:S(2)}, u32[]{:S(2)}) collective-permute-start(bf16[128,1024]{1,0:T(8,128)(2,1)S(1)} %collective-permute-done.14.refs_4_), channel_id=1, source_target_pairs={{0,4},{4,0},{8,12},{12,8},{1,5},{5,1},{9,13},{13,9},{2,6},{6,2},{1... | collective-permute-start | bytes 786440 | tf_op jit(solution)/shard_map/ppermute | solution.py:41
  20.1 1.6 %collective-permute-start.4 = (bf16[336,128]{1,0:T(8,128)(2,1)S(1)}, bf16[336,128]{1,0:T(8,128)(2,1)S(1)}, u32[]{:S(2)}, u32[]{:S(2)}) collective-permute-start(bf16[336,128]{1,0:T(8,128)(2,1)S(1)} %shard_map.97.refs_0_), channel_id=1, source_target_pairs={{0,2},{1,3},{2,0},{3,1},{4,6},{5,7},{6,4},{7,5},{8,10},{9,11},{10,... | collective-permute-start | bytes 258056 | tf_op jit(solution)/shard_map/ppermute | solution.py:41
  21.8 1.5 %collective-permute-start.6 = (bf16[320,128]{1,0:T(8,128)(2,1)S(1)}, bf16[320,128]{1,0:T(8,128)(2,1)S(1)}, u32[]{:S(2)}, u32[]{:S(2)}) collective-permute-start(bf16[320,128]{1,0:T(8,128)(2,1)S(1)} %shard_map.98.refs_2_), channel_id=1, source_target_pairs={{0,1},{1,0},{2,3},{3,2},{4,5},{5,4},{6,7},{7,6},{8,9},{9,8},{10,11... | collective-permute-start | bytes 245768 | tf_op jit(solution)/shard_map/ppermute | solution.py:41
  23.3 3.1 %collective-permute-done.6.refs_3_ = bf16[320,128]{1,0:T(8,128)(2,1)S(1)} collective-permute-done((bf16[320,128]{1,0:T(8,128)(2,1)S(1)}, bf16[320,128]{1,0:T(8,128)(2,1)S(1)}, u32[]{:S(2)}, u32[]{:S(2)}) %collective-permute-start.6) | collective-permute-done | bytes 81952 | tf_op jit(solution)/shard_map/ppermute | solution.py:41
  26.4 1.1 %shard_map.101 = (bf16[768,128]{1,0:T(8,128)(2,1)S(1)}, bf16[768,128]{1,0:T(8,128)(2,1)S(1)}) custom-call(bf16[336,128]{1,0:T(8,128)(2,1)S(1)} %shard_map.97.refs_0_, bf16[336,128]{1,0:T(8,128)(2,1)S(1)} %collective-permute-done.4.refs_1_, bf16[320,128]{1,0:T(8,128)(2,1)S(1)} %shard_map.98.refs_2_, bf16[320,128]{1,0:T(8,128)(2,1)S(1)} %collective-permute-done.6.refs_3_, ...), custom_call_target="tpu_custom_call" | custom-call | flops 67108864 | bytes 534528 | tf_op jit(solution)/shard_map/pallas_call | solution.py:51
  29.0 1.6 %shard_map.104 = (bf16[528,128]{1,0:T(8,128)(2,1)S(1)}, bf16[528,128]{1,0:T(8,128)(2,1)S(1)}, bf16[272,128]{1,0:T(8,128)(2,1)S(1)}, bf16[272,128]{1,0:T(8,128)(2...) custom-call(bf16[768,128]{1,0:T(8,128)(2,1)S(1)} %collective-permute-done.10.made_ref, ...), custom_call_target="tpu_custom_call" | custom-call | flops 536870912 | bytes 3150848 | tf_op jit(solution)/shard_map/pallas_call | solution.py:51
  30.5 1.3 %collective-permute-start.11 = (bf16[528,128]{1,0:T(8,128)(2,1)S(1)}, bf16[528,128]{1,0:T(8,128)(2,1)S(1)}, u32[]{:S(2)}, u32[]{:S(2)}) collective-permute-start(bf16[528,128]{1,0:T(8,128)(2,1)S(1)} %get-tuple-element.34), channel_id=1, source_target_pairs={{0,4},{4,0},{8,12},{12,8},{1,5},{5,1},{9,13},{13,9},{2,6},{6,2},{1... | collective-permute-start | bytes 405512 | tf_op jit(solution)/shard_map/ppermute | solution.py:41
  31.9 2.1 %collective-permute-start.12 = (bf16[272,128]{1,0:T(8,128)(2,1)S(1)}, bf16[272,128]{1,0:T(8,128)(2,1)S(1)}, u32[]{:S(2)}, u32[]{:S(2)}) collective-permute-start(bf16[272,128]{1,0:T(8,128)(2,1)S(1)} %get-tuple-element.35), channel_id=1, source_target_pairs={{0,8},{4,12},{8,0},{12,4},{1,9},{5,13},{9,1},{13,5},{2,10},{6,14},... | collective-permute-start | bytes 208904 | tf_op jit(solution)/shard_map/ppermute | solution.py:41
  34.0 1.4 %collective-permute-start.13 = (bf16[272,128]{1,0:T(8,128)(2,1)S(1)}, bf16[272,128]{1,0:T(8,128)(2,1)S(1)}, u32[]{:S(2)}, u32[]{:S(2)}) collective-permute-start(bf16[272,128]{1,0:T(8,128)(2,1)S(1)} %get-tuple-element.36), channel_id=1, source_target_pairs={{0,12},{4,8},{8,4},{12,0},{1,13},{5,9},{9,5},{13,1},{2,14},{6,10},... | collective-permute-start | bytes 208904 | tf_op jit(solution)/shard_map/ppermute | solution.py:41
  35.4 2.0 %collective-permute-done.12.refs_2_ = bf16[272,128]{1,0:T(8,128)(2,1)S(1)} collective-permute-done((bf16[272,128]{1,0:T(8,128)(2,1)S(1)}, bf16[272,128]{1,0:T(8,128)(2,1)S(1)}, u32[]{:S(2)}, u32[]{:S(2)}) %collective-permute-start.12) | collective-permute-done | bytes 69664 | tf_op jit(solution)/shard_map/ppermute | solution.py:41
  37.4 4.8 %collective-permute-done.13.refs_3_ = bf16[272,128]{1,0:T(8,128)(2,1)S(1)} collective-permute-done((bf16[272,128]{1,0:T(8,128)(2,1)S(1)}, bf16[272,128]{1,0:T(8,128)(2,1)S(1)}, u32[]{:S(2)}, u32[]{:S(2)}) %collective-permute-start.13) | collective-permute-done | bytes 69664 | tf_op jit(solution)/shard_map/ppermute | solution.py:41
  42.2 1.2 %shard_map.105 = (f32[32,1024]{1,0:T(8,128)}, f32[32,1024]{1,0:T(8,128)}, f32[1,1024]{1,0:T(1,128)}) custom-call(bf16[528,128]{1,0:T(8,128)(2,1)S(1)} %get-tuple-element.33.refs_0_, bf16[528,128]{1,0:T(8,128)(2,1)S(1)} %collective-permute-done.11.refs_1_, bf16[272,128]{1,0:T(8,128)(2,1)S(1)} %collective-permute-done.12.refs_2_, ...), custom_call_target="tpu_custom_call" | custom-call | flops 67108864 | bytes 2772992 | tf_op jit(solution)/shard_map/pallas_call | solution.py:51
  (40 shorter events, 2.4 us)
Async XLA Ops:
  0.6 7.2 %collective-permute-start.1 = (bf16[128,1024]{1,0:T(8,128)(2,1)}, bf16[128,1024]{1,0:T(8,128)(2,1)S(1)}, u32[]{:S(2)}, u32[]{:S(2)}) collective-permute-start(bf16[128,1024]{1,0:T(8,128)(2,1)} %bitcast.11), channel_id=1, source_target_pairs={{0,16},{16,0},{1,17},{17,1},{2,18},{18,2},{3,19},{19,3},{4,20},{20... | collective-permute-start | bytes 786440 | tf_op jit(solution)/shard_map/ppermute | solution.py:41
  1.2 1.1 %copy-start.1 = (bf16[1,128,1024]{2,1,0:T(8,128)(2,1)S(1)}, bf16[1,128,1024]{2,1,0:T(8,128)(2,1)}, u32[]{:S(2)}) copy-start(bf16[1,128,1024]{2,1,0:T(8,128)(2,1)} %param.9) | copy-start | bytes 786436
  1.2 1.2 %copy-start.2 = (bf16[1,1024,128]{2,1,0:T(8,128)(2,1)S(1)}, bf16[1,1024,128]{2,1,0:T(8,128)(2,1)}, u32[]{:S(2)}) copy-start(bf16[1,1024,128]{2,1,0:T(8,128)(2,1)} %param.8) | copy-start | bytes 786436
  1.2 1.3 %copy-start.3 = (bf16[1024,128]{1,0:T(8,128)(2,1)S(1)}, bf16[1024,128]{1,0:T(8,128)(2,1)}, u32[]{:S(2)}) copy-start(bf16[1024,128]{1,0:T(8,128)(2,1)} %head_ref.3) | copy-start | bytes 786436
  1.2 6.7 %collective-permute-start = (bf16[1024,128]{1,0:T(8,128)(2,1)}, bf16[1024,128]{1,0:T(8,128)(2,1)S(1)}, u32[]{:S(2)}, u32[]{:S(2)}) collective-permute-start(bf16[1024,128]{1,0:T(8,128)(2,1)} %bitcast.15), channel_id=1, source_target_pairs={{0,16},{16,0},{1,17},{17,1},{2,18},{18,2},{3,19},{19,3},{4,20},{20... | collective-permute-start | bytes 786440 | tf_op jit(solution)/shard_map/ppermute | solution.py:41
  2.1 4.6 %copy-start.7 = (bf16[1,1024]{1,0:T(2,128)(2,1)S(1)}, bf16[1,1024]{1,0:T(2,128)(2,1)}, u32[]{:S(2)}) copy-start(bf16[1,1024]{1,0:T(2,128)(2,1)} %gain_ref.1) | copy-start | bytes 6148
  3.0 23.4 %copy-start.4 = (s32[2,128]{1,0:T(2,128)S(1)}, s32[2,128]{1,0:T(2,128)}, u32[]{:S(2)}) copy-start(s32[2,128]{1,0:T(2,128)} %valid_ref.1) | copy-start | bytes 3076
  3.0 23.4 %copy-start.5 = (s32[2,128]{1,0:T(2,128)S(1)}, s32[2,128]{1,0:T(2,128)}, u32[]{:S(2)}) copy-start(s32[2,128]{1,0:T(2,128)} %refs_6_.1) | copy-start | bytes 3076
  3.0 16.2 %collective-permute-start.14 = (bf16[128,1024]{1,0:T(8,128)(2,1)S(1)}, bf16[128,1024]{1,0:T(8,128)(2,1)S(1)}, u32[]{:S(2)}, u32[]{:S(2)}) collective-permute-start(bf16[128,1024]{1,0:T(8,128)(2,1)S(1)} %get-tuple-element.37), channel_id=1, source_target_pairs={{0,8},{4,12},{8,0},{12,4},{1,9},{5,13},{9,1},{13,5},{2,10},{6,14},... | collective-permute-start | bytes 786440 | tf_op jit(solution)/shard_map/ppermute | solution.py:41
  6.7 1.2 %collective-permute-start.2 = (bf16[1,1024]{1,0:T(2,128)(2,1)S(1)}, bf16[1,1024]{1,0:T(2,128)(2,1)S(1)}, u32[]{:S(2)}, u32[]{:S(2)}) collective-permute-start(bf16[1,1024]{1,0:T(2,128)(2,1)S(1)} %copy-done.7), channel_id=1, source_target_pairs={{0,16},{16,0},{1,17},{17,1},{2,18},{18,2},{3,19},{19,3},{4,20},{20... | collective-permute-start | bytes 6152 | tf_op jit(solution)/shard_map/ppermute | solution.py:41
  8.4 5.0 %collective-permute-start.7 = (bf16[384,128]{1,0:T(8,128)(2,1)S(1)}, bf16[384,128]{1,0:T(8,128)(2,1)S(1)}, u32[]{:S(2)}, u32[]{:S(2)}) collective-permute-start(bf16[384,128]{1,0:T(8,128)(2,1)S(1)} %get-tuple-element.25.refs_0_), channel_id=1, source_target_pairs={{0,1},{1,0},{2,3},{3,2},{4,5},{5,4},{6,7},{7,6},{8,9},{9,8},{10,11... | collective-permute-start | bytes 294920 | tf_op jit(solution)/shard_map/ppermute | solution.py:41
  13.4 6.6 %collective-permute-start.8 = (bf16[384,128]{1,0:T(8,128)(2,1)S(1)}, bf16[384,128]{1,0:T(8,128)(2,1)S(1)}, u32[]{:S(2)}, u32[]{:S(2)}) collective-permute-start(bf16[384,128]{1,0:T(8,128)(2,1)S(1)} %shard_map.99.refs_0_), channel_id=1, source_target_pairs={{0,2},{1,3},{2,0},{3,1},{4,6},{5,7},{6,4},{7,5},{8,10},{9,11},{10,... | collective-permute-start | bytes 294920 | tf_op jit(solution)/shard_map/ppermute | solution.py:41
  15.0 5.1 %collective-permute-start.3 = (bf16[336,128]{1,0:T(8,128)(2,1)S(1)}, bf16[336,128]{1,0:T(8,128)(2,1)S(1)}, u32[]{:S(2)}, u32[]{:S(2)}) collective-permute-start(bf16[336,128]{1,0:T(8,128)(2,1)S(1)} %get-tuple-element.23.refs_0_), channel_id=1, source_target_pairs={{0,1},{1,0},{2,3},{3,2},{4,5},{5,4},{6,7},{7,6},{8,9},{9,8},{10,11... | collective-permute-start | bytes 258056 | tf_op jit(solution)/shard_map/ppermute | solution.py:41
  16.5 5.3 %collective-permute-start.5 = (bf16[320,128]{1,0:T(8,128)(2,1)S(1)}, bf16[320,128]{1,0:T(8,128)(2,1)S(1)}, u32[]{:S(2)}, u32[]{:S(2)}) collective-permute-start(bf16[320,128]{1,0:T(8,128)(2,1)S(1)} %get-tuple-element.24.refs_0_), channel_id=1, source_target_pairs={{0,2},{1,3},{2,0},{3,1},{4,6},{5,7},{6,4},{7,5},{8,10},{9,11},{10,... | collective-permute-start | bytes 245768 | tf_op jit(solution)/shard_map/ppermute | solution.py:41
  19.2 8.8 %collective-permute-start.15 = (bf16[128,1024]{1,0:T(8,128)(2,1)S(1)}, bf16[128,1024]{1,0:T(8,128)(2,1)S(1)}, u32[]{:S(2)}, u32[]{:S(2)}) collective-permute-start(bf16[128,1024]{1,0:T(8,128)(2,1)S(1)} %collective-permute-done.14.refs_4_), channel_id=1, source_target_pairs={{0,4},{4,0},{8,12},{12,8},{1,5},{5,1},{9,13},{13,9},{2,6},{6,2},{1... | collective-permute-start | bytes 786440 | tf_op jit(solution)/shard_map/ppermute | solution.py:41
  20.0 6.4 %collective-permute-start.9 = (bf16[384,128]{1,0:T(8,128)(2,1)S(1)}, bf16[384,128]{1,0:T(8,128)(2,1)S(1)}, u32[]{:S(2)}, u32[]{:S(2)}) collective-permute-start(bf16[384,128]{1,0:T(8,128)(2,1)S(1)} %shard_map.100.refs_4_), channel_id=1, source_target_pairs={{0,16},{16,0},{1,17},{17,1},{2,18},{18,2},{3,19},{19,3},{4,20},{20... | collective-permute-start | bytes 294920 | tf_op jit(solution)/shard_map/ppermute | solution.py:41
  20.1 6.2 %collective-permute-start.4 = (bf16[336,128]{1,0:T(8,128)(2,1)S(1)}, bf16[336,128]{1,0:T(8,128)(2,1)S(1)}, u32[]{:S(2)}, u32[]{:S(2)}) collective-permute-start(bf16[336,128]{1,0:T(8,128)(2,1)S(1)} %shard_map.97.refs_0_), channel_id=1, source_target_pairs={{0,2},{1,3},{2,0},{3,1},{4,6},{5,7},{6,4},{7,5},{8,10},{9,11},{10,... | collective-permute-start | bytes 258056 | tf_op jit(solution)/shard_map/ppermute | solution.py:41
  21.8 4.6 %collective-permute-start.6 = (bf16[320,128]{1,0:T(8,128)(2,1)S(1)}, bf16[320,128]{1,0:T(8,128)(2,1)S(1)}, u32[]{:S(2)}, u32[]{:S(2)}) collective-permute-start(bf16[320,128]{1,0:T(8,128)(2,1)S(1)} %shard_map.98.refs_2_), channel_id=1, source_target_pairs={{0,1},{1,0},{2,3},{3,2},{4,5},{5,4},{6,7},{7,6},{8,9},{9,8},{10,11... | collective-permute-start | bytes 245768 | tf_op jit(solution)/shard_map/ppermute | solution.py:41
  27.5 1.5 %collective-permute-start.10 = (bf16[768,128]{1,0:T(8,128)(2,1)S(1)}, bf16[768,128]{1,0:T(8,128)(2,1)S(1)}, u32[]{:S(2)}, u32[]{:S(2)}) collective-permute-start(bf16[768,128]{1,0:T(8,128)(2,1)S(1)} %get-tuple-element.26), channel_id=1, source_target_pairs={{0,16},{16,0},{1,17},{17,1},{2,18},{18,2},{3,19},{19,3},{4,20},{20... | collective-permute-start | bytes 589832 | tf_op jit(solution)/shard_map/ppermute | solution.py:41
  27.5 7.8 %collective-permute-start.16 = (bf16[128,1024]{1,0:T(8,128)(2,1)S(1)}, bf16[128,1024]{1,0:T(8,128)(2,1)S(1)}, u32[]{:S(2)}, u32[]{:S(2)}) collective-permute-start(bf16[128,1024]{1,0:T(8,128)(2,1)S(1)} %collective-permute-done.14.refs_4_), channel_id=1, source_target_pairs={{0,16},{16,0},{1,17},{17,1},{2,18},{18,2},{3,19},{19,3},{4,20},{20... | collective-permute-start | bytes 786440 | tf_op jit(solution)/shard_map/ppermute | solution.py:41
  28.0 7.3 %collective-permute-start.17 = (bf16[128,1024]{1,0:T(8,128)(2,1)S(1)}, bf16[128,1024]{1,0:T(8,128)(2,1)S(1)}, u32[]{:S(2)}, u32[]{:S(2)}) collective-permute-start(bf16[128,1024]{1,0:T(8,128)(2,1)S(1)} %collective-permute-done.15.refs_5_), channel_id=1, source_target_pairs={{0,16},{16,0},{1,17},{17,1},{2,18},{18,2},{3,19},{19,3},{4,20},{20... | collective-permute-start | bytes 786440 | tf_op jit(solution)/shard_map/ppermute | solution.py:41
  30.5 11.6 %collective-permute-start.11 = (bf16[528,128]{1,0:T(8,128)(2,1)S(1)}, bf16[528,128]{1,0:T(8,128)(2,1)S(1)}, u32[]{:S(2)}, u32[]{:S(2)}) collective-permute-start(bf16[528,128]{1,0:T(8,128)(2,1)S(1)} %get-tuple-element.34), channel_id=1, source_target_pairs={{0,4},{4,0},{8,12},{12,8},{1,5},{5,1},{9,13},{13,9},{2,6},{6,2},{1... | collective-permute-start | bytes 405512 | tf_op jit(solution)/shard_map/ppermute | solution.py:41
  31.9 5.5 %collective-permute-start.12 = (bf16[272,128]{1,0:T(8,128)(2,1)S(1)}, bf16[272,128]{1,0:T(8,128)(2,1)S(1)}, u32[]{:S(2)}, u32[]{:S(2)}) collective-permute-start(bf16[272,128]{1,0:T(8,128)(2,1)S(1)} %get-tuple-element.35), channel_id=1, source_target_pairs={{0,8},{4,12},{8,0},{12,4},{1,9},{5,13},{9,1},{13,5},{2,10},{6,14},... | collective-permute-start | bytes 208904 | tf_op jit(solution)/shard_map/ppermute | solution.py:41
  34.0 8.2 %collective-permute-start.13 = (bf16[272,128]{1,0:T(8,128)(2,1)S(1)}, bf16[272,128]{1,0:T(8,128)(2,1)S(1)}, u32[]{:S(2)}, u32[]{:S(2)}) collective-permute-start(bf16[272,128]{1,0:T(8,128)(2,1)S(1)} %get-tuple-element.36), channel_id=1, source_target_pairs={{0,12},{4,8},{8,4},{12,0},{1,13},{5,9},{9,5},{13,1},{2,14},{6,10},... | collective-permute-start | bytes 208904 | tf_op jit(solution)/shard_map/ppermute | solution.py:41
  (2 other events, 1.8 us)

commit v9 on v7

--- a/solution.py
+++ b/solution.py
@@ -39,6 +39,12 @@
 def from_partner(value, axis, step):
     size = lax.axis_size(axis)
     return lax.ppermute(value, axis, [(i, partner(i, step, size)) for i in range(size)])
+
+
+def from_section(value, steps):
+    size = lax.axis_size("dp")
+    pairs = [(s * size + i, s * size + partner(i, step, size)) for s, step in enumerate(steps) for i in range(size)]
+    return lax.ppermute(value, ("section", "dp"), pairs)
 
 
 def high_low(value):
@@ -56,16 +62,16 @@
     )(*args)
 
 
-def gain_kernel(gain_ref, out_ref):
-    out_ref[...] = gain_ref[...].astype(F32)
-
-
-def own_kernel(x_ref, down_ref, up_ref, head_ref, gain_ref, out_ref):
+def open_kernel(out_ref):
+    out_ref[...] = jnp.zeros_like(out_ref)
+
+
+def own_kernel(x_ref, down_ref, up_ref, head_ref, gain_ref, _, out_ref):
     rank = down_ref.shape[1]
     half = x_ref.shape[0] // lax.axis_size("section")
     x, up, head = x_ref[rows_of(lax.axis_index("section") * half, half), :], up_ref[...], head_ref[...]
     x32 = x.astype(F32)
-    scaled = (x32 * gain_ref[...]).astype(BF16)
+    scaled = (x32 * gain_ref[...].astype(F32)).astype(BF16)
     out_ref[:half, :] = dot(scaled, down_ref[...]).astype(BF16)
     out_ref[half : 2 * half, :] = dot_nt(x, up).astype(BF16)
     out_ref[2 * half : 3 * half, :] = dot(x, head).astype(BF16)
@@ -76,36 +82,35 @@
     out_ref[3 * half + 2 * rank :, :] = high_low(squares[: PACK // 2])
 
 
-def other_kernel(x_ref, up_ref, own_ref, down2_ref, up2_ref, gain2_ref, a_ref, b_ref, gram_ref):
+def other_kernel(x_ref, up_ref, own_ref, down2_ref, up2_ref, gain2_ref, a_ref, b_ref):
     rank = down2_ref.shape[1]
     half = x_ref.shape[0] // lax.axis_size("section")
     me = lax.axis_index("section")
     it = 1 - me
     x = x_ref[rows_of(me * half, half), :]
     gain2 = gain2_ref[...].astype(F32)
-    middle = 5 * half // 2
-    a_ref[rows_of(me * half, half), :] = own_ref[:half, :]
-    b_ref[rows_of(me * half, half), :] = own_ref[half : 2 * half, :]
-    a_ref[2 * half : middle, :] = own_ref[2 * half : middle, :]
-    b_ref[2 * half : middle, :] = own_ref[middle : 3 * half, :]
-    a_ref[middle:, :] = own_ref[3 * half + 2 * rank :, :]
-    gram_ref[rank:, :] = own_ref[3 * half : 3 * half + 2 * rank, :]
+    b_ref[rows_of(me * half, half), :] = own_ref[:half, :]
+    b_ref[rows_of((2 + me) * half, half), :] = own_ref[half : 2 * half, :]
+    a_ref[rank : 3 * rank, :] = own_ref[3 * half : 3 * half + 2 * rank, :]
+    a_ref[3 * rank : 3 * rank + half, :] = own_ref[2 * half : 3 * half, :]
+    a_ref[3 * rank + half :, :] = own_ref[3 * half + 2 * rank :, :]
     scaled = (x.astype(F32) * gain2).astype(BF16)
-    a_ref[rows_of(it * half, half), :] = dot(scaled, down2_ref[...]).astype(BF16)
-    b_ref[rows_of(it * half, half), :] = dot_nt(x, up2_ref[...]).astype(BF16)
+    b_ref[rows_of(it * half, half), :] = dot(scaled, down2_ref[...]).astype(BF16)
+    b_ref[rows_of((2 + it) * half, half), :] = dot_nt(x, up2_ref[...]).astype(BF16)
 
     @pl.when(me == 0)
     def _():
         scaled = (up_ref[...].astype(F32) * gain2).astype(BF16)
-        gram_ref[:rank, :] = dot(scaled, down2_ref[...]).astype(BF16)
+        a_ref[:rank, :] = dot(scaled, down2_ref[...]).astype(BF16)
 
     @pl.when(me != 0)
     def _():
-        gram_ref[:rank, :] = dot_nt(up_ref[...], up2_ref[...]).astype(BF16)
+        a_ref[:rank, :] = dot_nt(up_ref[...], up2_ref[...]).astype(BF16)
 
 
 def add_kernel(*refs):
-    refs[-1][...] = sum(r[...].astype(F32) for r in refs[:-1]).astype(BF16)
+    rows = refs[-1].shape[0]
+    refs[-1][...] = sum(r[:rows, :].astype(F32) for r in refs[:-1]).astype(BF16)
 
 
 def prepare_kernel(down_ref, head_ref, up_ref, down2_ref, up2_ref, gain2_ref, x_ref, down_t_ref, stack_ref):
@@ -146,17 +151,16 @@
     gram0, gram1 = jnp.where(first, gram, gram2), jnp.where(first, gram2, gram)
     m01, b0h, b0b0 = (gram0[i * rank : (i + 1) * rank] for i in range(3))
     b1b0, b1h, b1b1 = (gram1[i * rank : (i + 1) * rank] for i in range(3))
-    middle = 5 * half // 2
-    tail = total(a_refs, middle, PACK)
+    tail = total(a_refs, 3 * rank + half, PACK)
     squares0 = spread(tail[:1] + tail[PACK // 2 : PACK // 2 + 1])
     inv0 = lax.rsqrt(squares0 / width + epsilon)
-    proj0 = total(a_refs, 0, half)
+    proj0 = total(b_refs, 0, half)
     pre0 = inv0 * proj0
     sig0 = jax.nn.sigmoid(pre0)
     hidden0 = (pre0 * sig0).astype(BF16)
     hid0 = hidden0.astype(F32)
-    proj1 = total(a_refs, half, half) + dot(hidden0, m01)
-    cross0 = total(b_refs, 0, half)
+    proj1 = total(b_refs, half, half) + dot(hidden0, m01)
+    cross0 = total(b_refs, 2 * half, half)
     one_b0 = cross0 + dot(hidden0, b0b0)
     squares1 = squares0 + jnp.sum(hid0 * (cross0 + one_b0), axis=1, keepdims=True)
     inv1 = lax.rsqrt(squares1 / width + epsilon)
@@ -164,13 +168,12 @@
     sig1 = jax.nn.sigmoid(pre1)
     hidden1 = (pre1 * sig1).astype(BF16)
     hid1 = hidden1.astype(F32)
-    one_b1 = total(b_refs, half, half) + dot_nt(hidden0, b1b0)
+    one_b1 = total(b_refs, 3 * half, half) + dot_nt(hidden0, b1b0)
     two_b0 = one_b0 + dot(hidden1, b1b0)
     two_b1 = one_b1 + dot(hidden1, b1b1)
     squares2 = squares1 + jnp.sum(hid1 * (one_b1 + two_b1), axis=1, keepdims=True)
     inv2 = lax.rsqrt(squares2 / width + epsilon)
-    base = jnp.concatenate([total(r, 2 * half, half // 2) for r in (a_refs, b_refs)], axis=0)
-    base = base + dot(hidden0, b0h) + dot(hidden1, b1h)
+    base = total(a_refs, 3 * rank, half) + dot(hidden0, b0h) + dot(hidden1, b1h)
     logits = inv2 * base
     expo = jnp.exp(logits - jnp.max(logits, axis=1, keepdims=True))
     prob = expo / jnp.sum(expo, axis=1, keepdims=True)
@@ -210,7 +213,7 @@
     return mixes, weighted_t, scaled_t
 
 
-def mine_kernel(made_ref, x_ref, mix_ref, acc_ref, left_ref):
+def mine_kernel(near, made_ref, x_ref, mix_ref, acc_ref, left_ref):
     rank = made_ref.shape[1]
     half = made_ref.shape[0] // 6
     x = x_ref[rows_of(lax.axis_index("section") * half, half), :]
@@ -220,13 +223,17 @@
     left_ref[:rank, :] = weighted_t
     left_ref[rank:, :] = scaled_t
     acc_ref[:rank, :] = dot(weighted_t, x)
-    acc_ref[rank:, :] = dot(scaled_t, x)
+    slim = (acc_ref.shape[0] - rank) // len(near)
+    place = lax.axis_index("dp")
+    for i, step in enumerate(near):
+        rows = left_ref[rows_of(rank + partner(place, step, rank // slim) * slim, slim), :]
+        acc_ref[rank + i * slim : rank + (i + 1) * slim, :] = dot(rows, x)
 
 
 def grad_kernel(
-    replicas, sections, made_ref, mix_ref, acc_ref, left_ref, stack_ref, down_t_ref, gain_ref, valid_ref, *refs
+    replicas, near, made_ref, mix_ref, acc_ref, left_ref, stack_ref, down_t_ref, gain_ref, valid_ref, *refs
 ):
-    out_refs, (all_ref, tall_ref) = refs[:replicas], refs[replicas:]
+    out_refs, (all_ref, tall_ref, wide_ref) = refs[:replicas], refs[replicas:]
     rank, features = down_t_ref.shape
     slim = rank // replicas
     section = lax.axis_index("section")
@@ -244,35 +251,38 @@
     left = jnp.concatenate([jnp.where(first, none, mix), weighted_t], axis=1)
     grad = acc_ref[:rank, :] + dot(left, stack_ref[3 * rank :, :])
     gain = jnp.sum(grad * down_t_ref[...].astype(F32), axis=0, keepdims=True)
-    grad = (grad * gain_ref[...]).astype(BF16)
-    left = jnp.concatenate([head_mix, own_mix, oth_mix, jnp.where(first, mix, none), scaled_t], axis=1)
+    grad = (grad * gain_ref[...].astype(F32)).astype(BF16)
+    all_ref[...] = grad
+    for i, value in enumerate((head_mix, own_mix, oth_mix, jnp.where(first, mix, none), scaled_t)):
+        wide_ref[:, i * rank : (i + 1) * rank] = value
+    place = lax.axis_index("dp")
+    targets = [partner(place, step, replicas) for step in range(replicas)]
+    left = jnp.concatenate([wide_ref[rows_of(t * slim, slim), :] for t in (targets[i] for i in near)], axis=0)
     rest = (acc_ref[rank:, :] + dot(left, stack_ref[...])).astype(BF16)
-    for c in range(replicas):
-        all_ref[2 * c * slim : (2 * c + 1) * slim, :] = grad[c * slim : (c + 1) * slim]
-        all_ref[(2 * c + 1) * slim : (2 * c + 2) * slim, :] = rest[c * slim : (c + 1) * slim]
     count = jnp.sum(valid_ref[...].astype(F32), keepdims=True)
     lines = features // rank
     tail = jnp.concatenate(
         [gain[:, i * rank : (i + 1) * rank] for i in range(lines)] + [jnp.broadcast_to(count, (PACK - lines, rank))],
         axis=0,
     ).astype(BF16)
-    place = lax.axis_index("dp")
     for step, out_ref in enumerate(out_refs):
-        target = partner(place, step, replicas)
-        if step < replicas - sections:
-            block = all_ref[rows_of(target * 2 * slim, 2 * slim), :]
+        if step in near:
+            at = near.index(step) * slim
+            block = all_ref[rows_of(targets[step] * slim, slim), :]
             for i in range(lines):
-                out_ref[i * 2 * slim : (i + 1) * 2 * slim, :] = block[:, i * rank : (i + 1) * rank]
+                lanes = slice(i * rank, (i + 1) * rank)
+                out_ref[i * 2 * slim : (2 * i + 1) * slim, :] = block[:, lanes]
+                out_ref[(2 * i + 1) * slim : (i + 1) * 2 * slim, :] = rest[at : at + slim, lanes]
         else:
             for i in range(8):
-                out_ref[i * slim : (i + 1) * slim, :] = tall_ref[rows_of(i * rank + target * slim, slim), :]
+                out_ref[i * slim : (i + 1) * slim, :] = tall_ref[rows_of(i * rank + targets[step] * slim, slim), :]
         out_ref[-PACK:, :] = tail
 
 
-def last_kernel(whole, *refs):
-    parts, (far_ref, cross_ref, stack_ref, gain_ref, down_out, up_out, gain_out) = refs[:-7], refs[-7:]
-    near, (a_ref, b_ref) = parts[:whole], parts[whole:]
-    rank = a_ref.shape[1]
+def last_kernel(count, *refs):
+    near, fars, refs = refs[:count], refs[count : count + 3], refs[count + 3 :]
+    sent_ref, relay_ref, cross_ref, cross2_ref, stack_ref, gain_ref, down_out, up_out, gain_out = refs
+    rank = fars[0].shape[1]
     slim, features = down_out.shape
     lines = features // rank
     first = lax.axis_index("section") == 0
@@ -284,18 +294,15 @@
         rows = [ref[i * slim : (i + 1) * slim, :] for i in range(4, 8)]
         return jnp.concatenate([jnp.concatenate(rows[:2], axis=1), jnp.concatenate(rows[2:], axis=1)], axis=0)
 
-    tail = sum(p[-PACK:, :].astype(F32) for p in parts)
+    tail = sum(p[-PACK:, :].astype(F32) for p in near + fars)
     scale = 1.0 / tail[lines : lines + 1, :1]
-    left_a, left_b = left(a_ref), left(b_ref)
-    moved = dot(jnp.where(first, left_a, left_b), far_ref[...])
-    moved = moved + dot(jnp.where(first, left_b, left_a), cross_ref[...])
-    mixes = [
-        (a_ref[i * slim : (i + 1) * slim, :].astype(F32) + b_ref[i * slim : (i + 1) * slim, :].astype(F32)).astype(BF16)
-        for i in range(4)
-    ]
+    left_a, left_b, left_c = (left(r) for r in fars)
+    moved = dot(jnp.where(first, left_a, left_c), sent_ref[...]) + dot(jnp.where(first, left_c, left_a), cross_ref[...])
+    moved = moved + dot(left_b, jnp.where(first, relay_ref[...], cross2_ref[...]))
+    mixes = [sum(r[i * slim : (i + 1) * slim, :].astype(F32) for r in fars).astype(BF16) for i in range(4)]
     none = jnp.zeros_like(mixes[3])
     down = moved[:slim] + dot(jnp.where(first, none, mixes[3]), stack_ref[3 * rank : 4 * rank, :])
-    down = down * gain_ref[...]
+    down = down * gain_ref[...].astype(F32)
     mixes = jnp.concatenate(mixes[:3] + [jnp.where(first, mixes[3], none)], axis=1)
     up = moved[slim:] + dot(mixes, stack_ref[: 4 * rank, :])
     for i in range(lines):
@@ -323,25 +330,21 @@
     for value in (down, up, gains):
         others.append(from_partner(value, "section", 1))
     down2, up2, gains2 = others
-    whole = replicas - sections
-    assert whole > 0
-    far = lax.ppermute(
-        states,
-        ("section", "dp"),
-        [(s * replicas + i, s * replicas + partner(i, whole + s, replicas)) for s in range(sections) for i in range(replicas)],
-    )
+    assert replicas > 3
+    far = [replicas - 2, replicas - 1, 1]
+    near = [step for step in range(replicas) if step not in far]
+    gathered = [from_section(states, [replicas - 2, 1])]
     small = 2 * rank * rank * features
-    wide_gain = call(gain_kernel, shape(gains.shape, F32), 40 * small, gains)
+    opened = call(open_kernel, shape((8, rank), F32), 40 * small)
     own = call(
         own_kernel,
         shape((3 * half + 2 * rank + PACK, rank), BF16),
         5 * small,
-        states, down, up, head, wide_gain,
-    )
-    lower = 5 * half // 2
-    first_part, second_part, gram = call(
+        states, down, up, head, gains, opened,
+    )
+    first_part, second_part = call(
         other_kernel,
-        [shape((lower + PACK, rank), BF16), shape((lower, rank), BF16), shape((3 * rank, rank), BF16)],
+        [shape((3 * rank + half + PACK, rank), BF16), shape((4 * half, rank), BF16)],
         3 * small,
         states, up, own, down2, up2, gains2,
     )
@@ -356,10 +359,9 @@
                 return [value, got]
             value = call(add_kernel, shape(value.shape, BF16), small // 8, value, got)
 
-    gram = terms(gram, doubling)
+    first_part = terms(first_part, doubling)
     second_part = terms(second_part, doubling[::-1])
-    first_part = terms(first_part, doubling)
-    gram = call(add_kernel, shape(gram[0].shape, BF16), small // 8, *gram)
+    gram = call(add_kernel, shape((3 * rank, rank), BF16), small // 8, *first_part)
     down_t, stack = call(
         prepare_kernel,
         [shape((rank, features), BF16), shape((4 * rank + half, features), BF16)],
@@ -374,28 +376,29 @@
         *first_part, *second_part, gram, gram2, labels, valid,
     )
     met = from_partner(theirs, "section", 1)
+    gathered.append(from_section(gathered[0], [1]))
     mixes, acc, left = call(
-        mine_kernel,
-        [shape((4 * rank, rank), F32), shape((2 * rank, features), F32), shape((2 * rank, half), BF16)],
+        functools.partial(mine_kernel, near),
+        [shape((4 * rank, rank), F32), shape((rank + len(near) * slim, features), F32), shape((2 * rank, half), BF16)],
         4 * small,
         made, states,
     )
-    *parts, _, _ = call(
-        functools.partial(grad_kernel, replicas, sections),
-        [shape((lines * 2 * slim + PACK, rank), BF16)] * whole
-        + [shape((8 * slim + PACK, rank), BF16)] * sections
-        + [shape((2 * rank, features), BF16), shape((8 * rank, rank), BF16)],
+    *parts, _, _, _ = call(
+        functools.partial(grad_kernel, replicas, near),
+        [shape(((lines * 2 if i in near else 8) * slim + PACK, rank), BF16) for i in range(replicas)]
+        + [shape((rank, features), BF16), shape((8 * rank, rank), BF16), shape((rank, 5 * rank), BF16)],
         16 * small,
-        met, mixes, acc, left, stack, down_t, wide_gain, valid,
+        met, mixes, acc, left, stack, down_t, gains, valid,
     )
     for step in range(1, replicas):
         parts[step] = from_partner(parts[step], "dp", step)
-    cross = from_partner(far, "section", 1)
+    for i in range(2):
+        gathered.append(from_partner(gathered[i], "section", 1))
     down_grad, up_grad, gain_grad = call(
-        functools.partial(last_kernel, whole),
+        functools.partial(last_kernel, len(near)),
         [shape((slim, features), F32), shape((slim, features), F32), shape((1, features), F32)],
         2 * small,
-        *parts, far, cross, stack, wide_gain,
+        *(parts[i] for i in near + far), *gathered, stack, gains,
     )
     return down_grad.T[None], up_grad[None], gain_grad
 

time: 50.1 us -> 52.7 us (1.052)
  starting transfers between devices: 18.6 us -> 20.4 us
  waiting for transfers between devices: 24.1 us -> 25.1 us
    ppermute x1 -> x2, starting transfers between devices: 4.13 us -> 8.45 us  [from_section(): return lax.ppermute(value, ('section', 'dp'), pairs)]
    ppermute x15 -> x14, starting transfers between devices: 14.5 us -> 11.9 us  [from_partner(): lax.ppermute(value, axis, [(i, partner(i, step, size)) for i in range(siz...]
    ppermute x15 -> x14, waiting for transfers between devices: 12.2 us -> 13.4 us  [from_partner(): lax.ppermute(value, axis, [(i, partner(i, step, size)) for i in range(siz...]
    ppermute x1 -> x2, waiting for transfers between devices: 11.9 us -> 11.7 us  [from_section(): return lax.ppermute(value, ('section', 'dp'), pairs)]
    pallas_call x12 -> x11, Pallas kernels: 5.7 us -> 5.6 us  [call(): pl.pallas_call(kernel, out_shape=out, cost_estimate=pl.CostEstimate(flops...]
  transfers between devices with their start and end apart: 16 -> 16, of which waited for: 6 -> 9; matrix products, arithmetic and copies ran while one was open for 0% -> 0% of each run, Pallas kernels for 9% -> 8%
where the time goes in v9:
time: 52.7 us; the launch traced here: 52.5 us
  waiting for transfers between devices  25.1 us (48%)
  starting transfers between devices  20.4 us (39%)
  Pallas kernels  5.6 us (11%)
  between operations  0.78 us (1%)
  local copies, waits for them, and re-layouts  0.63 us (1%)
    ppermute x14, waiting for transfers between devices, from_partner(): lax.ppermute(value, axis, [(i, partner(i, step, size)) for i in range(siz...  13.4 us
    ppermute x14, starting transfers between devices, from_partner(): lax.ppermute(value, axis, [(i, partner(i, step, size)) for i in range(siz...  11.9 us
    ppermute x2, waiting for transfers between devices, from_section(): return lax.ppermute(value, ('section', 'dp'), pairs)  11.7 us
    ppermute x2, starting transfers between devices, from_section(): return lax.ppermute(value, ('section', 'dp'), pairs)  8.45 us
    pallas_call x11, Pallas kernels, call(): pl.pallas_call(kernel, out_shape=out, cost_estimate=pl.CostEstimate(flops...  5.6 us
  transfers between devices with their start and end apart: 16, of which 9 were waited for; matrix products, arithmetic and copies ran while one was open for 0% of the time, Pallas kernels for 8%

profile of v9, /device:TPU:0, one launch (start us, length us, event | category | flops | bytes accessed | tf_op | source)
XLA Modules:
  0.0 52.5 jit_solution(9622109365294906637)
XLA Ops:
  0.6 4.1 %collective-permute-start.12 = (bf16[256,1024]{1,0:T(8,128)(2,1)}, bf16[256,1024]{1,0:T(8,128)(2,1)S(1)}, u32[]{:S(2)}, u32[]{:S(2)}) collective-permute-start(bf16[256,1024]{1,0:T(8,128)(2,1)} %bitcast.7), channel_id=1, source_target_pairs={{0,8},{4,12},{8,0},{12,4},{16,20},{20,16},{24,28},{28,24},{1,9},{5... | collective-permute-start | bytes 1572872 | tf_op jit(solution)/shard_map/ppermute | solution.py:47
  4.8 11.7 %collective-permute-done.12.refs_4_ = bf16[256,1024]{1,0:T(8,128)(2,1)S(1)} collective-permute-done((bf16[256,1024]{1,0:T(8,128)(2,1)}, bf16[256,1024]{1,0:T(8,128)(2,1)S(1)}, u32[]{:S(2)}, u32[]{:S(2)}) %collective-permute-start.12) | collective-permute-done | bytes 524320 | tf_op jit(solution)/shard_map/ppermute | solution.py:47
  16.5 4.3 %collective-permute-start.13 = (bf16[256,1024]{1,0:T(8,128)(2,1)S(1)}, bf16[256,1024]{1,0:T(8,128)(2,1)S(1)}, u32[]{:S(2)}, u32[]{:S(2)}) collective-permute-start(bf16[256,1024]{1,0:T(8,128)(2,1)S(1)} %collective-permute-done.12.refs_4_), channel_id=1, source_target_pairs={{0,4},{4,0},{8,12},{12,8},{1,5},{5,1},{9,13},{13,9},{2,6},{6,2},{1... | collective-permute-start | bytes 1572872 | tf_op jit(solution)/shard_map/ppermute | solution.py:47
  20.9 0.5 %collective-permute-start = (bf16[1024,128]{1,0:T(8,128)(2,1)}, bf16[1024,128]{1,0:T(8,128)(2,1)S(1)}, u32[]{:S(2)}, u32[]{:S(2)}) collective-permute-start(bf16[1024,128]{1,0:T(8,128)(2,1)} %bitcast.16), channel_id=1, source_target_pairs={{0,16},{16,0},{1,17},{17,1},{2,18},{18,2},{3,19},{19,3},{4,20},{20... | collective-permute-start | bytes 786440 | tf_op jit(solution)/shard_map/ppermute | solution.py:41
  22.2 0.5 shard_map.95.own_ref
  23.0 0.5 shard_map.96
  23.5 1.6 %collective-permute-start.3 = (bf16[528,128]{1,0:T(8,128)(2,1)S(1)}, bf16[528,128]{1,0:T(8,128)(2,1)S(1)}, u32[]{:S(2)}, u32[]{:S(2)}) collective-permute-start(bf16[528,128]{1,0:T(8,128)(2,1)S(1)} %get-tuple-element.19.refs_0_), channel_id=1, source_target_pairs={{0,1},{1,0},{2,3},{3,2},{4,5},{5,4},{6,7},{7,6},{8,9},{9,8},{10,11... | collective-permute-start | bytes 405512 | tf_op jit(solution)/shard_map/ppermute | solution.py:41
  25.1 1.5 %collective-permute-start.5 = (bf16[512,128]{1,0:T(8,128)(2,1)S(1)}, bf16[512,128]{1,0:T(8,128)(2,1)S(1)}, u32[]{:S(2)}, u32[]{:S(2)}) collective-permute-start(bf16[512,128]{1,0:T(8,128)(2,1)S(1)} %get-tuple-element.20.refs_0_), channel_id=1, source_target_pairs={{0,2},{1,3},{2,0},{3,1},{4,6},{5,7},{6,4},{7,5},{8,10},{9,11},{10,... | collective-permute-start | bytes 393224 | tf_op jit(solution)/shard_map/ppermute | solution.py:41
  26.6 2.7 %collective-permute-done.3.refs_1_ = bf16[528,128]{1,0:T(8,128)(2,1)S(1)} collective-permute-done((bf16[528,128]{1,0:T(8,128)(2,1)S(1)}, bf16[528,128]{1,0:T(8,128)(2,1)S(1)}, u32[]{:S(2)}, u32[]{:S(2)}) %collective-permute-start.3) | collective-permute-done | bytes 135200 | tf_op jit(solution)/shard_map/ppermute | solution.py:41
  29.4 1.6 %collective-permute-start.4 = (bf16[528,128]{1,0:T(8,128)(2,1)S(1)}, bf16[528,128]{1,0:T(8,128)(2,1)S(1)}, u32[]{:S(2)}, u32[]{:S(2)}) collective-permute-start(bf16[528,128]{1,0:T(8,128)(2,1)S(1)} %shard_map.97.refs_0_), channel_id=1, source_target_pairs={{0,2},{1,3},{2,0},{3,1},{4,6},{5,7},{6,4},{7,5},{8,10},{9,11},{10,... | collective-permute-start | bytes 405512 | tf_op jit(solution)/shard_map/ppermute | solution.py:41
  31.0 0.5 collective-permute-start.15
  31.5 1.6 %collective-permute-start.6 = (bf16[512,128]{1,0:T(8,128)(2,1)S(1)}, bf16[512,128]{1,0:T(8,128)(2,1)S(1)}, u32[]{:S(2)}, u32[]{:S(2)}) collective-permute-start(bf16[512,128]{1,0:T(8,128)(2,1)S(1)} %shard_map.98.refs_2_), channel_id=1, source_target_pairs={{0,1},{1,0},{2,3},{3,2},{4,5},{5,4},{6,7},{7,6},{8,9},{9,8},{10,11... | collective-permute-start | bytes 393224 | tf_op jit(solution)/shard_map/ppermute | solution.py:41
  33.1 1.4 %collective-permute-done.4.refs_1_ = bf16[528,128]{1,0:T(8,128)(2,1)S(1)} collective-permute-done((bf16[528,128]{1,0:T(8,128)(2,1)S(1)}, bf16[528,128]{1,0:T(8,128)(2,1)S(1)}, u32[]{:S(2)}, u32[]{:S(2)}) %collective-permute-start.4) | collective-permute-done | bytes 135200 | tf_op jit(solution)/shard_map/ppermute | solution.py:41
  34.5 2.4 %collective-permute-done.6.refs_3_ = bf16[512,128]{1,0:T(8,128)(2,1)S(1)} collective-permute-done((bf16[512,128]{1,0:T(8,128)(2,1)S(1)}, bf16[512,128]{1,0:T(8,128)(2,1)S(1)}, u32[]{:S(2)}, u32[]{:S(2)}) %collective-permute-start.6) | collective-permute-done | bytes 131104 | tf_op jit(solution)/shard_map/ppermute | solution.py:41
  37.0 1.1 %shard_map.100 = (bf16[768,128]{1,0:T(8,128)(2,1)S(1)}, bf16[768,128]{1,0:T(8,128)(2,1)S(1)}) custom-call(bf16[528,128]{1,0:T(8,128)(2,1)S(1)} %shard_map.97.refs_0_, bf16[528,128]{1,0:T(8,128)(2,1)S(1)} %collective-permute-done.4.refs_1_, bf16[512,128]{1,0:T(8,128)(2,1)S(1)} %shard_map.98.refs_2_, bf16[512,128]{1,0:T(8,128)(2,1)S(1)} %collective-permute-done.6.refs_3_, ...), custom_call_target="tpu_custom_call" | custom-call | flops 67108864 | bytes 731136 | tf_op jit(solution)/shard_map/pallas_call | solution.py:57
  38.9 0.7 %collective-permute-done.8.made_ref = bf16[768,128]{1,0:T(8,128)(2,1)S(1)} collective-permute-done((bf16[768,128]{1,0:T(8,128)(2,1)S(1)}, bf16[768,128]{1,0:T(8,128)(2,1)S(1)}, u32[]{:S(2)}, u32[]{:S(2)}) %collective-permute-start.8) | collective-permute-done | bytes 196640 | tf_op jit(solution)/shard_map/ppermute | solution.py:41
  39.6 1.5 %shard_map.103 = (bf16[528,128]{1,0:T(8,128)(2,1)S(1)}, bf16[272,128]{1,0:T(8,128)(2,1)S(1)}, bf16[272,128]{1,0:T(8,128)(2,1)S(1)}, bf16[272,128]{1,0:T(8,128)(2...) custom-call(bf16[768,128]{1,0:T(8,128)(2,1)S(1)} %collective-permute-done.8.made_ref, ...), custom_call_target="tpu_custom_call" | custom-call | flops 536870912 | bytes 2755584 | tf_op jit(solution)/shard_map/pallas_call | solution.py:57
  41.0 2.7 %collective-permute-start.10 = (bf16[272,128]{1,0:T(8,128)(2,1)S(1)}, bf16[272,128]{1,0:T(8,128)(2,1)S(1)}, u32[]{:S(2)}, u32[]{:S(2)}) collective-permute-start(bf16[272,128]{1,0:T(8,128)(2,1)S(1)} %get-tuple-element.30), channel_id=1, source_target_pairs={{0,12},{4,8},{8,4},{12,0},{1,13},{5,9},{9,5},{13,1},{2,14},{6,10},... | collective-permute-start | bytes 208904 | tf_op jit(solution)/shard_map/ppermute | solution.py:41
  43.7 1.1 %collective-permute-start.11 = (bf16[272,128]{1,0:T(8,128)(2,1)S(1)}, bf16[272,128]{1,0:T(8,128)(2,1)S(1)}, u32[]{:S(2)}, u32[]{:S(2)}) collective-permute-start(bf16[272,128]{1,0:T(8,128)(2,1)S(1)} %get-tuple-element.31), channel_id=1, source_target_pairs={{0,4},{4,0},{8,12},{12,8},{1,5},{5,1},{9,13},{13,9},{2,6},{6,2},{1... | collective-permute-start | bytes 208904 | tf_op jit(solution)/shard_map/ppermute | solution.py:41
  44.9 0.5 %collective-permute-start.9 = (bf16[272,128]{1,0:T(8,128)(2,1)S(1)}, bf16[272,128]{1,0:T(8,128)(2,1)S(1)}, u32[]{:S(2)}, u32[]{:S(2)}) collective-permute-start(bf16[272,128]{1,0:T(8,128)(2,1)S(1)} %get-tuple-element.29), channel_id=1, source_target_pairs={{0,8},{4,12},{8,0},{12,4},{1,9},{5,13},{9,1},{13,5},{2,10},{6,14},... | collective-permute-start | bytes 208904 | tf_op jit(solution)/shard_map/ppermute | solution.py:41
  45.4 2.4 %collective-permute-done.10.refs_2_ = bf16[272,128]{1,0:T(8,128)(2,1)S(1)} collective-permute-done((bf16[272,128]{1,0:T(8,128)(2,1)S(1)}, bf16[272,128]{1,0:T(8,128)(2,1)S(1)}, u32[]{:S(2)}, u32[]{:S(2)}) %collective-permute-start.10) | collective-permute-done | bytes 69664 | tf_op jit(solution)/shard_map/ppermute | solution.py:41
  47.8 1.3 %collective-permute-done.11.refs_3_ = bf16[272,128]{1,0:T(8,128)(2,1)S(1)} collective-permute-done((bf16[272,128]{1,0:T(8,128)(2,1)S(1)}, bf16[272,128]{1,0:T(8,128)(2,1)S(1)}, u32[]{:S(2)}, u32[]{:S(2)}) %collective-permute-start.11) | collective-permute-done | bytes 69664 | tf_op jit(solution)/shard_map/ppermute | solution.py:41
  49.1 2.1 %collective-permute-done.9.refs_1_ = bf16[272,128]{1,0:T(8,128)(2,1)S(1)} collective-permute-done((bf16[272,128]{1,0:T(8,128)(2,1)S(1)}, bf16[272,128]{1,0:T(8,128)(2,1)S(1)}, u32[]{:S(2)}, u32[]{:S(2)}) %collective-permute-start.9) | collective-permute-done | bytes 69664 | tf_op jit(solution)/shard_map/ppermute | solution.py:41
  51.2 1.3 %shard_map.104 = (f32[32,1024]{1,0:T(8,128)}, f32[32,1024]{1,0:T(8,128)}, f32[1,1024]{1,0:T(1,128)}) custom-call(bf16[528,128]{1,0:T(8,128)(2,1)S(1)} %get-tuple-element.28.refs_0_, bf16[272,128]{1,0:T(8,128)(2,1)S(1)} %collective-permute-done.9.refs_1_, bf16[272,128]{1,0:T(8,128)(2,1)S(1)} %collective-permute-done.10.refs_2_, ...), custom_call_target="tpu_custom_call" | custom-call | flops 67108864 | bytes 3753984 | tf_op jit(solution)/shard_map/pallas_call | solution.py:57
  (33 shorter events, 2.1 us)
Async XLA Ops:
  0.6 15.9 %collective-permute-start.12 = (bf16[256,1024]{1,0:T(8,128)(2,1)}, bf16[256,1024]{1,0:T(8,128)(2,1)S(1)}, u32[]{:S(2)}, u32[]{:S(2)}) collective-permute-start(bf16[256,1024]{1,0:T(8,128)(2,1)} %bitcast.7), channel_id=1, source_target_pairs={{0,8},{4,12},{8,0},{12,4},{16,20},{20,16},{24,28},{28,24},{1,9},{5... | collective-permute-start | bytes 1572872 | tf_op jit(solution)/shard_map/ppermute | solution.py:47
  16.5 14.5 %collective-permute-start.13 = (bf16[256,1024]{1,0:T(8,128)(2,1)S(1)}, bf16[256,1024]{1,0:T(8,128)(2,1)S(1)}, u32[]{:S(2)}, u32[]{:S(2)}) collective-permute-start(bf16[256,1024]{1,0:T(8,128)(2,1)S(1)} %collective-permute-done.12.refs_4_), channel_id=1, source_target_pairs={{0,4},{4,0},{8,12},{12,8},{1,5},{5,1},{9,13},{13,9},{2,6},{6,2},{1... | collective-permute-start | bytes 1572872 | tf_op jit(solution)/shard_map/ppermute | solution.py:47
  20.8 2.2 %collective-permute-start.1 = (bf16[128,1024]{1,0:T(8,128)(2,1)}, bf16[128,1024]{1,0:T(8,128)(2,1)S(1)}, u32[]{:S(2)}, u32[]{:S(2)}) collective-permute-start(bf16[128,1024]{1,0:T(8,128)(2,1)} %bitcast.12), channel_id=1, source_target_pairs={{0,16},{16,0},{1,17},{17,1},{2,18},{18,2},{3,19},{19,3},{4,20},{20... | collective-permute-start | bytes 786440 | tf_op jit(solution)/shard_map/ppermute | solution.py:41
  20.9 1.0 %copy-start = (bf16[2,128,1024]{2,1,0:T(8,128)(2,1)S(1)}, bf16[2,128,1024]{2,1,0:T(8,128)(2,1)}, u32[]{:S(2)}) copy-start(bf16[2,128,1024]{2,1,0:T(8,128)(2,1)} %param.7) | copy-start | bytes 1572868
  20.9 1.1 %copy-start.1 = (bf16[1,128,1024]{2,1,0:T(8,128)(2,1)S(1)}, bf16[1,128,1024]{2,1,0:T(8,128)(2,1)}, u32[]{:S(2)}) copy-start(bf16[1,128,1024]{2,1,0:T(8,128)(2,1)} %param.9) | copy-start | bytes 786436
  20.9 1.2 %copy-start.2 = (bf16[1,1024,128]{2,1,0:T(8,128)(2,1)S(1)}, bf16[1,1024,128]{2,1,0:T(8,128)(2,1)}, u32[]{:S(2)}) copy-start(bf16[1,1024,128]{2,1,0:T(8,128)(2,1)} %param.8) | copy-start | bytes 786436
  20.9 1.2 %copy-start.3 = (bf16[1024,128]{1,0:T(8,128)(2,1)S(1)}, bf16[1024,128]{1,0:T(8,128)(2,1)}, u32[]{:S(2)}) copy-start(bf16[1024,128]{1,0:T(8,128)(2,1)} %head_ref.3) | copy-start | bytes 786436
  20.9 1.2 %copy-start.4 = (bf16[1,1024]{1,0:T(2,128)(2,1)S(1)}, bf16[1,1024]{1,0:T(2,128)(2,1)}, u32[]{:S(2)}) copy-start(bf16[1,1024]{1,0:T(2,128)(2,1)} %refs_9_.1) | copy-start | bytes 6148
  20.9 2.1 %collective-permute-start = (bf16[1024,128]{1,0:T(8,128)(2,1)}, bf16[1024,128]{1,0:T(8,128)(2,1)S(1)}, u32[]{:S(2)}, u32[]{:S(2)}) collective-permute-start(bf16[1024,128]{1,0:T(8,128)(2,1)} %bitcast.16), channel_id=1, source_target_pairs={{0,16},{16,0},{1,17},{17,1},{2,18},{18,2},{3,19},{19,3},{4,20},{20... | collective-permute-start | bytes 786440 | tf_op jit(solution)/shard_map/ppermute | solution.py:41
  21.5 1.5 %collective-permute-start.2 = (bf16[1,1024]{1,0:T(2,128)(2,1)}, bf16[1,1024]{1,0:T(2,128)(2,1)S(1)}, u32[]{:S(2)}, u32[]{:S(2)}) collective-permute-start(bf16[1,1024]{1,0:T(2,128)(2,1)} %refs_9_.1), channel_id=1, source_target_pairs={{0,16},{16,0},{1,17},{17,1},{2,18},{18,2},{3,19},{19,3},{4,20},{20... | collective-permute-start | bytes 6152 | tf_op jit(solution)/shard_map/ppermute | solution.py:41
  22.7 14.3 %copy-start.5 = (s32[2,128]{1,0:T(2,128)S(1)}, s32[2,128]{1,0:T(2,128)}, u32[]{:S(2)}) copy-start(s32[2,128]{1,0:T(2,128)} %valid_ref.1) | copy-start | bytes 3076
  22.7 14.3 %copy-start.6 = (s32[2,128]{1,0:T(2,128)S(1)}, s32[2,128]{1,0:T(2,128)}, u32[]{:S(2)}) copy-start(s32[2,128]{1,0:T(2,128)} %refs_6_.1) | copy-start | bytes 3076
  23.5 5.8 %collective-permute-start.3 = (bf16[528,128]{1,0:T(8,128)(2,1)S(1)}, bf16[528,128]{1,0:T(8,128)(2,1)S(1)}, u32[]{:S(2)}, u32[]{:S(2)}) collective-permute-start(bf16[528,128]{1,0:T(8,128)(2,1)S(1)} %get-tuple-element.19.refs_0_), channel_id=1, source_target_pairs={{0,1},{1,0},{2,3},{3,2},{4,5},{5,4},{6,7},{7,6},{8,9},{9,8},{10,11... | collective-permute-start | bytes 405512 | tf_op jit(solution)/shard_map/ppermute | solution.py:41
  25.1 6.4 %collective-permute-start.5 = (bf16[512,128]{1,0:T(8,128)(2,1)S(1)}, bf16[512,128]{1,0:T(8,128)(2,1)S(1)}, u32[]{:S(2)}, u32[]{:S(2)}) collective-permute-start(bf16[512,128]{1,0:T(8,128)(2,1)S(1)} %get-tuple-element.20.refs_0_), channel_id=1, source_target_pairs={{0,2},{1,3},{2,0},{3,1},{4,6},{5,7},{6,4},{7,5},{8,10},{9,11},{10,... | collective-permute-start | bytes 393224 | tf_op jit(solution)/shard_map/ppermute | solution.py:41
  29.4 5.1 %collective-permute-start.4 = (bf16[528,128]{1,0:T(8,128)(2,1)S(1)}, bf16[528,128]{1,0:T(8,128)(2,1)S(1)}, u32[]{:S(2)}, u32[]{:S(2)}) collective-permute-start(bf16[528,128]{1,0:T(8,128)(2,1)S(1)} %shard_map.97.refs_0_), channel_id=1, source_target_pairs={{0,2},{1,3},{2,0},{3,1},{4,6},{5,7},{6,4},{7,5},{8,10},{9,11},{10,... | collective-permute-start | bytes 405512 | tf_op jit(solution)/shard_map/ppermute | solution.py:41
  30.9 20.3 %collective-permute-start.14 = (bf16[256,1024]{1,0:T(8,128)(2,1)S(1)}, bf16[256,1024]{1,0:T(8,128)(2,1)S(1)}, u32[]{:S(2)}, u32[]{:S(2)}) collective-permute-start(bf16[256,1024]{1,0:T(8,128)(2,1)S(1)} %collective-permute-done.12.refs_4_), channel_id=1, source_target_pairs={{0,16},{16,0},{1,17},{17,1},{2,18},{18,2},{3,19},{19,3},{4,20},{20... | collective-permute-start | bytes 1572872 | tf_op jit(solution)/shard_map/ppermute | solution.py:41
  31.0 20.3 %collective-permute-start.15 = (bf16[256,1024]{1,0:T(8,128)(2,1)S(1)}, bf16[256,1024]{1,0:T(8,128)(2,1)S(1)}, u32[]{:S(2)}, u32[]{:S(2)}) collective-permute-start(bf16[256,1024]{1,0:T(8,128)(2,1)S(1)} %collective-permute-done.13.refs_5_), channel_id=1, source_target_pairs={{0,16},{16,0},{1,17},{17,1},{2,18},{18,2},{3,19},{19,3},{4,20},{20... | collective-permute-start | bytes 1572872 | tf_op jit(solution)/shard_map/ppermute | solution.py:41
  31.5 5.5 %collective-permute-start.6 = (bf16[512,128]{1,0:T(8,128)(2,1)S(1)}, bf16[512,128]{1,0:T(8,128)(2,1)S(1)}, u32[]{:S(2)}, u32[]{:S(2)}) collective-permute-start(bf16[512,128]{1,0:T(8,128)(2,1)S(1)} %shard_map.98.refs_2_), channel_id=1, source_target_pairs={{0,1},{1,0},{2,3},{3,2},{4,5},{5,4},{6,7},{7,6},{8,9},{9,8},{10,11... | collective-permute-start | bytes 393224 | tf_op jit(solution)/shard_map/ppermute | solution.py:41
  34.5 2.5 %collective-permute-start.7 = (bf16[384,128]{1,0:T(8,128)(2,1)S(1)}, bf16[384,128]{1,0:T(8,128)(2,1)S(1)}, u32[]{:S(2)}, u32[]{:S(2)}) collective-permute-start(bf16[384,128]{1,0:T(8,128)(2,1)S(1)} %shard_map.99.refs_4_), channel_id=1, source_target_pairs={{0,16},{16,0},{1,17},{17,1},{2,18},{18,2},{3,19},{19,3},{4,20},{20... | collective-permute-start | bytes 294920 | tf_op jit(solution)/shard_map/ppermute | solution.py:41
  38.1 1.5 %collective-permute-start.8 = (bf16[768,128]{1,0:T(8,128)(2,1)S(1)}, bf16[768,128]{1,0:T(8,128)(2,1)S(1)}, u32[]{:S(2)}, u32[]{:S(2)}) collective-permute-start(bf16[768,128]{1,0:T(8,128)(2,1)S(1)} %get-tuple-element.21), channel_id=1, source_target_pairs={{0,16},{16,0},{1,17},{17,1},{2,18},{18,2},{3,19},{19,3},{4,20},{20... | collective-permute-start | bytes 589832 | tf_op jit(solution)/shard_map/ppermute | solution.py:41
  41.0 6.8 %collective-permute-start.10 = (bf16[272,128]{1,0:T(8,128)(2,1)S(1)}, bf16[272,128]{1,0:T(8,128)(2,1)S(1)}, u32[]{:S(2)}, u32[]{:S(2)}) collective-permute-start(bf16[272,128]{1,0:T(8,128)(2,1)S(1)} %get-tuple-element.30), channel_id=1, source_target_pairs={{0,12},{4,8},{8,4},{12,0},{1,13},{5,9},{9,5},{13,1},{2,14},{6,10},... | collective-permute-start | bytes 208904 | tf_op jit(solution)/shard_map/ppermute | solution.py:41
  43.7 5.3 %collective-permute-start.11 = (bf16[272,128]{1,0:T(8,128)(2,1)S(1)}, bf16[272,128]{1,0:T(8,128)(2,1)S(1)}, u32[]{:S(2)}, u32[]{:S(2)}) collective-permute-start(bf16[272,128]{1,0:T(8,128)(2,1)S(1)} %get-tuple-element.31), channel_id=1, source_target_pairs={{0,4},{4,0},{8,12},{12,8},{1,5},{5,1},{9,13},{13,9},{2,6},{6,2},{1... | collective-permute-start | bytes 208904 | tf_op jit(solution)/shard_map/ppermute | solution.py:41
  44.9 6.4 %collective-permute-start.9 = (bf16[272,128]{1,0:T(8,128)(2,1)S(1)}, bf16[272,128]{1,0:T(8,128)(2,1)S(1)}, u32[]{:S(2)}, u32[]{:S(2)}) collective-permute-start(bf16[272,128]{1,0:T(8,128)(2,1)S(1)} %get-tuple-element.29), channel_id=1, source_target_pairs={{0,8},{4,12},{8,0},{12,4},{1,9},{5,13},{9,1},{13,5},{2,10},{6,14},... | collective-permute-start | bytes 208904 | tf_op jit(solution)/shard_map/ppermute | solution.py:41

commit v10 on v9

--- a/solution.py
+++ b/solution.py
@@ -39,12 +39,6 @@
 def from_partner(value, axis, step):
     size = lax.axis_size(axis)
     return lax.ppermute(value, axis, [(i, partner(i, step, size)) for i in range(size)])
-
-
-def from_section(value, steps):
-    size = lax.axis_size("dp")
-    pairs = [(s * size + i, s * size + partner(i, step, size)) for s, step in enumerate(steps) for i in range(size)]
-    return lax.ppermute(value, ("section", "dp"), pairs)
 
 
 def high_low(value):
@@ -66,10 +60,11 @@
     out_ref[...] = jnp.zeros_like(out_ref)
 
 
-def own_kernel(x_ref, down_ref, up_ref, head_ref, gain_ref, _, out_ref):
+def own_kernel(x_ref, down_ref, up_ref, head_ref, gain_ref, _, out_ref, half_ref):
     rank = down_ref.shape[1]
     half = x_ref.shape[0] // lax.axis_size("section")
     x, up, head = x_ref[rows_of(lax.axis_index("section") * half, half), :], up_ref[...], head_ref[...]
+    half_ref[...] = x
     x32 = x.astype(F32)
     scaled = (x32 * gain_ref[...].astype(F32)).astype(BF16)
     out_ref[:half, :] = dot(scaled, down_ref[...]).astype(BF16)
@@ -213,7 +208,7 @@
     return mixes, weighted_t, scaled_t
 
 
-def mine_kernel(near, made_ref, x_ref, mix_ref, acc_ref, left_ref):
+def mine_kernel(whole, made_ref, x_ref, mix_ref, acc_ref, left_ref):
     rank = made_ref.shape[1]
     half = made_ref.shape[0] // 6
     x = x_ref[rows_of(lax.axis_index("section") * half, half), :]
@@ -223,17 +218,18 @@
     left_ref[:rank, :] = weighted_t
     left_ref[rank:, :] = scaled_t
     acc_ref[:rank, :] = dot(weighted_t, x)
-    slim = (acc_ref.shape[0] - rank) // len(near)
+    slim = (acc_ref.shape[0] - rank) // whole
     place = lax.axis_index("dp")
-    for i, step in enumerate(near):
+    for step in range(whole):
         rows = left_ref[rows_of(rank + partner(place, step, rank // slim) * slim, slim), :]
-        acc_ref[rank + i * slim : rank + (i + 1) * slim, :] = dot(rows, x)
+        acc_ref[rank + step * slim : rank + (step + 1) * slim, :] = dot(rows, x)
 
 
 def grad_kernel(
-    replicas, near, made_ref, mix_ref, acc_ref, left_ref, stack_ref, down_t_ref, gain_ref, valid_ref, *refs
+    replicas, sections, made_ref, mix_ref, acc_ref, left_ref, stack_ref, down_t_ref, gain_ref, valid_ref, *refs
 ):
     out_refs, (all_ref, tall_ref, wide_ref) = refs[:replicas], refs[replicas:]
+    whole = replicas - sections
     rank, features = down_t_ref.shape
     slim = rank // replicas
     section = lax.axis_index("section")
@@ -257,7 +253,7 @@
         wide_ref[:, i * rank : (i + 1) * rank] = value
     place = lax.axis_index("dp")
     targets = [partner(place, step, replicas) for step in range(replicas)]
-    left = jnp.concatenate([wide_ref[rows_of(t * slim, slim), :] for t in (targets[i] for i in near)], axis=0)
+    left = jnp.concatenate([wide_ref[rows_of(t * slim, slim), :] for t in targets[:whole]], axis=0)
     rest = (acc_ref[rank:, :] + dot(left, stack_ref[...])).astype(BF16)
     count = jnp.sum(valid_ref[...].astype(F32), keepdims=True)
     lines = features // rank
@@ -266,23 +262,22 @@
         axis=0,
     ).astype(BF16)
     for step, out_ref in enumerate(out_refs):
-        if step in near:
-            at = near.index(step) * slim
+        if step < whole:
             block = all_ref[rows_of(targets[step] * slim, slim), :]
             for i in range(lines):
                 lanes = slice(i * rank, (i + 1) * rank)
                 out_ref[i * 2 * slim : (2 * i + 1) * slim, :] = block[:, lanes]
-                out_ref[(2 * i + 1) * slim : (i + 1) * 2 * slim, :] = rest[at : at + slim, lanes]
+                out_ref[(2 * i + 1) * slim : (i + 1) * 2 * slim, :] = rest[step * slim : (step + 1) * slim, lanes]
         else:
             for i in range(8):
                 out_ref[i * slim : (i + 1) * slim, :] = tall_ref[rows_of(i * rank + targets[step] * slim, slim), :]
         out_ref[-PACK:, :] = tail
 
 
-def last_kernel(count, *refs):
-    near, fars, refs = refs[:count], refs[count : count + 3], refs[count + 3 :]
-    sent_ref, relay_ref, cross_ref, cross2_ref, stack_ref, gain_ref, down_out, up_out, gain_out = refs
-    rank = fars[0].shape[1]
+def last_kernel(whole, *refs):
+    parts, (far_refs, stack_ref, gain_ref, down_out, up_out, gain_out) = refs[:-9], (refs[-9:-5], *refs[-5:])
+    near, (a_ref, b_ref) = parts[:whole], parts[whole:]
+    rank = a_ref.shape[1]
     slim, features = down_out.shape
     lines = features // rank
     first = lax.axis_index("section") == 0
@@ -290,16 +285,21 @@
     def total(start, size):
         return sum(p[start : start + size, :].astype(F32) for p in near)
 
-    def left(ref):
-        rows = [ref[i * slim : (i + 1) * slim, :] for i in range(4, 8)]
-        return jnp.concatenate([jnp.concatenate(rows[:2], axis=1), jnp.concatenate(rows[2:], axis=1)], axis=0)
-
-    tail = sum(p[-PACK:, :].astype(F32) for p in near + fars)
+    def left(ref, i):
+        rows = [ref[j * slim : (j + 1) * slim, :] for j in (4 + i, 6 + i)]
+        return jnp.concatenate(rows, axis=0)
+
+    tail = sum(p[-PACK:, :].astype(F32) for p in parts)
     scale = 1.0 / tail[lines : lines + 1, :1]
-    left_a, left_b, left_c = (left(r) for r in fars)
-    moved = dot(jnp.where(first, left_a, left_c), sent_ref[...]) + dot(jnp.where(first, left_c, left_a), cross_ref[...])
-    moved = moved + dot(left_b, jnp.where(first, relay_ref[...], cross2_ref[...]))
-    mixes = [sum(r[i * slim : (i + 1) * slim, :].astype(F32) for r in fars).astype(BF16) for i in range(4)]
+    moved = 0.0
+    for i, ref in enumerate((a_ref, b_ref)):
+        one, two = left(ref, 0), left(ref, 1)
+        moved = moved + dot(jnp.where(first, one, two), far_refs[i][...])
+        moved = moved + dot(jnp.where(first, two, one), far_refs[2 + i][...])
+    mixes = [
+        (a_ref[i * slim : (i + 1) * slim, :].astype(F32) + b_ref[i * slim : (i + 1) * slim, :].astype(F32)).astype(BF16)
+        for i in range(4)
+    ]
     none = jnp.zeros_like(mixes[3])
     down = moved[:slim] + dot(jnp.where(first, none, mixes[3]), stack_ref[3 * rank : 4 * rank, :])
     down = down * gain_ref[...].astype(F32)
@@ -330,18 +330,17 @@
     for value in (down, up, gains):
         others.append(from_partner(value, "section", 1))
     down2, up2, gains2 = others
-    assert replicas > 3
-    far = [replicas - 2, replicas - 1, 1]
-    near = [step for step in range(replicas) if step not in far]
-    gathered = [from_section(states, [replicas - 2, 1])]
+    whole = replicas - sections
+    assert whole > 0
     small = 2 * rank * rank * features
     opened = call(open_kernel, shape((8, rank), F32), 40 * small)
-    own = call(
+    own, mine = call(
         own_kernel,
-        shape((3 * half + 2 * rank + PACK, rank), BF16),
+        [shape((3 * half + 2 * rank + PACK, rank), BF16), shape((half, features), BF16)],
         5 * small,
         states, down, up, head, gains, opened,
     )
+    far = from_partner(mine, "dp", whole)
     first_part, second_part = call(
         other_kernel,
         [shape((3 * rank + half + PACK, rank), BF16), shape((4 * half, rank), BF16)],
@@ -376,16 +375,17 @@
         *first_part, *second_part, gram, gram2, labels, valid,
     )
     met = from_partner(theirs, "section", 1)
-    gathered.append(from_section(gathered[0], [1]))
+    fars = [far, from_partner(far, "dp", 1)]
     mixes, acc, left = call(
-        functools.partial(mine_kernel, near),
-        [shape((4 * rank, rank), F32), shape((rank + len(near) * slim, features), F32), shape((2 * rank, half), BF16)],
+        functools.partial(mine_kernel, whole),
+        [shape((4 * rank, rank), F32), shape((rank + whole * slim, features), F32), shape((2 * rank, half), BF16)],
         4 * small,
         made, states,
     )
     *parts, _, _, _ = call(
-        functools.partial(grad_kernel, replicas, near),
-        [shape(((lines * 2 if i in near else 8) * slim + PACK, rank), BF16) for i in range(replicas)]
+        functools.partial(grad_kernel, replicas, sections),
+        [shape((lines * 2 * slim + PACK, rank), BF16)] * whole
+        + [shape((8 * slim + PACK, rank), BF16)] * sections
         + [shape((rank, features), BF16), shape((8 * rank, rank), BF16), shape((rank, 5 * rank), BF16)],
         16 * small,
         met, mixes, acc, left, stack, down_t, gains, valid,
@@ -393,12 +393,12 @@
     for step in range(1, replicas):
         parts[step] = from_partner(parts[step], "dp", step)
     for i in range(2):
-        gathered.append(from_partner(gathered[i], "section", 1))
+        fars.append(from_partner(fars[i], "section", 1))
     down_grad, up_grad, gain_grad = call(
-        functools.partial(last_kernel, len(near)),
+        functools.partial(last_kernel, whole),
         [shape((slim, features), F32), shape((slim, features), F32), shape((1, features), F32)],
         2 * small,
-        *(parts[i] for i in near + far), *gathered, stack, gains,
+        *parts, *fars, stack, gains,
     )
     return down_grad.T[None], up_grad[None], gain_grad
 

time: 52.7 us -> 42.2 us (0.80)
  waiting for transfers between devices: 25.1 us -> 18 us
  starting transfers between devices: 20.4 us -> 16.7 us
    ppermute x2 -> x0, waiting for transfers between devices: 11.7 us -> none  [from_section(): return lax.ppermute(value, ('section', 'dp'), pairs)]
    ppermute x2 -> x0, starting transfers between devices: 8.45 us -> none  [from_section(): return lax.ppermute(value, ('section', 'dp'), pairs)]
    ppermute x14 -> x16, starting transfers between devices: 11.9 us -> 16.7 us  [from_partner(): lax.ppermute(value, axis, [(i, partner(i, step, size)) for i in range(siz...]
    ppermute x14 -> x16, waiting for transfers between devices: 13.4 us -> 18 us  [from_partner(): lax.ppermute(value, axis, [(i, partner(i, step, size)) for i in range(siz...]
  transfers between devices with their start and end apart: 16 -> 16, of which waited for: 9 -> 7; matrix products, arithmetic and copies ran while one was open for 0% -> 0% of each run, Pallas kernels for 8% -> 10%
where the time goes in v10:
time: 42.2 us; the launch traced here: 42 us
  waiting for transfers between devices  18 us (43%)
  starting transfers between devices  16.7 us (40%)
  Pallas kernels  5.47 us (13%)
  local copies, waits for them, and re-layouts  1.15 us (3%)
  between operations  0.73 us (2%)
    ppermute x16, waiting for transfers between devices, from_partner(): lax.ppermute(value, axis, [(i, partner(i, step, size)) for i in range(siz...  18 us
    ppermute x16, starting transfers between devices, from_partner(): lax.ppermute(value, axis, [(i, partner(i, step, size)) for i in range(siz...  16.7 us
    pallas_call x11, Pallas kernels, call(): pl.pallas_call(kernel, out_shape=out, cost_estimate=pl.CostEstimate(flops...  5.47 us
    unnamed x14, local copies, waits for them, and re-layouts  1.15 us
  transfers between devices with their start and end apart: 16, of which 7 were waited for; matrix products, arithmetic and copies ran while one was open for 0% of the time, Pallas kernels for 10%

profile of v10, /device:TPU:0, one launch (start us, length us, event | category | flops | bytes accessed | tf_op | source)
XLA Modules:
  0.0 42.0 jit_solution(12875770773568333089)
XLA Ops:
  0.6 0.6 %collective-permute-start.1 = (bf16[128,1024]{1,0:T(8,128)(2,1)}, bf16[128,1024]{1,0:T(8,128)(2,1)S(1)}, u32[]{:S(2)}, u32[]{:S(2)}) collective-permute-start(bf16[128,1024]{1,0:T(8,128)(2,1)} %bitcast.11), channel_id=1, source_target_pairs={{0,16},{16,0},{1,17},{17,1},{2,18},{18,2},{3,19},{19,3},{4,20},{20... | collective-permute-start | bytes 786440 | tf_op jit(solution)/shard_map/ppermute | solution.py:41
  1.3 0.9 %copy-done = bf16[2,128,1024]{2,1,0:T(8,128)(2,1)S(1)} copy-done((bf16[2,128,1024]{2,1,0:T(8,128)(2,1)S(1)}, bf16[2,128,1024]{2,1,0:T(8,128)(2,1)}, u32[]{:S(2)}) %copy-start) | copy-done | bytes 524312
  2.5 0.5 %shard_map.95 = (bf16[656,128]{1,0:T(8,128)(2,1)S(1)}, bf16[128,1024]{1,0:T(8,128)(2,1)S(1)}) custom-call(bf16[256,1024]{1,0:T(8,128)(2,1)S(1)} %bitcast.7, bf16[1024,128]{1,0:T(8,128)(2,1)S(1)} %bitcast.16, bf16[128,1024]{1,0:T(8,128)(2,1)S(1)} %bitcast.12, bf16[1024,128]{1,0:T(8,128)(2,1)S(1)} %copy-done.3, bf16[1,1024]{1,0:T(2,128)(2,1)S(1)} %copy-done.4, ...), custom_call_target="tpu_custom_call" | custom-call | flops 167772160 | bytes 1316864 | tf_op jit(solution)/shard_map/pallas_call | solution.py:51
  3.0 3.6 %collective-permute-start.12 = (bf16[128,1024]{1,0:T(8,128)(2,1)S(1)}, bf16[128,1024]{1,0:T(8,128)(2,1)S(1)}, u32[]{:S(2)}, u32[]{:S(2)}) collective-permute-start(bf16[128,1024]{1,0:T(8,128)(2,1)S(1)} %get-tuple-element.35), channel_id=1, source_target_pairs={{0,8},{4,12},{8,0},{12,4},{1,9},{5,13},{9,1},{13,5},{2,10},{6,14},... | collective-permute-start | bytes 786440 | tf_op jit(solution)/shard_map/ppermute | solution.py:41
  6.8 0.9 %collective-permute-done.2.gain2_ref = bf16[1,1024]{1,0:T(2,128)(2,1)S(1)} collective-permute-done((bf16[1,1024]{1,0:T(2,128)(2,1)S(1)}, bf16[1,1024]{1,0:T(2,128)(2,1)S(1)}, u32[]{:S(2)}, u32[]{:S(2)}) %collective-permute-start.2) | collective-permute-done | bytes 2080 | tf_op jit(solution)/shard_map/ppermute | solution.py:41
  7.8 0.5 %shard_map.96 = (bf16[528,128]{1,0:T(8,128)(2,1)S(1)}, bf16[512,128]{1,0:T(8,128)(2,1)S(1)}) custom-call(bf16[256,1024]{1,0:T(8,128)(2,1)S(1)} %bitcast.8, bf16[128,1024]{1,0:T(8,128)(2,1)S(1)} %bitcast.13, bf16[656,128]{1,0:T(8,128)(2,1)S(1)} %get-tuple-element.21.own_ref, bf16[1024,128]{1,0:T(8,128)(2,1)S(1)} %collective-permute-done.down2_ref, ...), custom_call_target="tpu_custom_call" | custom-call | flops 100663296 | bytes 1480704 | tf_op jit(solution)/shard_map/pallas_call | solution.py:51
  8.3 1.6 %collective-permute-start.3 = (bf16[528,128]{1,0:T(8,128)(2,1)S(1)}, bf16[528,128]{1,0:T(8,128)(2,1)S(1)}, u32[]{:S(2)}, u32[]{:S(2)}) collective-permute-start(bf16[528,128]{1,0:T(8,128)(2,1)S(1)} %get-tuple-element.22.refs_0_), channel_id=1, source_target_pairs={{0,1},{1,0},{2,3},{3,2},{4,5},{5,4},{6,7},{7,6},{8,9},{9,8},{10,11... | collective-permute-start | bytes 405512 | tf_op jit(solution)/shard_map/ppermute | solution.py:41
  9.9 1.5 %collective-permute-start.5 = (bf16[512,128]{1,0:T(8,128)(2,1)S(1)}, bf16[512,128]{1,0:T(8,128)(2,1)S(1)}, u32[]{:S(2)}, u32[]{:S(2)}) collective-permute-start(bf16[512,128]{1,0:T(8,128)(2,1)S(1)} %get-tuple-element.23.refs_0_), channel_id=1, source_target_pairs={{0,2},{1,3},{2,0},{3,1},{4,6},{5,7},{6,4},{7,5},{8,10},{9,11},{10,... | collective-permute-start | bytes 393224 | tf_op jit(solution)/shard_map/ppermute | solution.py:41
  11.4 2.7 %collective-permute-done.3.refs_1_ = bf16[528,128]{1,0:T(8,128)(2,1)S(1)} collective-permute-done((bf16[528,128]{1,0:T(8,128)(2,1)S(1)}, bf16[528,128]{1,0:T(8,128)(2,1)S(1)}, u32[]{:S(2)}, u32[]{:S(2)}) %collective-permute-start.3) | collective-permute-done | bytes 135200 | tf_op jit(solution)/shard_map/ppermute | solution.py:41
  14.2 1.6 %collective-permute-start.4 = (bf16[528,128]{1,0:T(8,128)(2,1)S(1)}, bf16[528,128]{1,0:T(8,128)(2,1)S(1)}, u32[]{:S(2)}, u32[]{:S(2)}) collective-permute-start(bf16[528,128]{1,0:T(8,128)(2,1)S(1)} %shard_map.97.refs_0_), channel_id=1, source_target_pairs={{0,2},{1,3},{2,0},{3,1},{4,6},{5,7},{6,4},{7,5},{8,10},{9,11},{10,... | collective-permute-start | bytes 405512 | tf_op jit(solution)/shard_map/ppermute | solution.py:41
  15.7 3.5 %collective-permute-done.12.refs_4_ = bf16[128,1024]{1,0:T(8,128)(2,1)S(1)} collective-permute-done((bf16[128,1024]{1,0:T(8,128)(2,1)S(1)}, bf16[128,1024]{1,0:T(8,128)(2,1)S(1)}, u32[]{:S(2)}, u32[]{:S(2)}) %collective-permute-start.12) | collective-permute-done | bytes 262176 | tf_op jit(solution)/shard_map/ppermute | solution.py:41
  19.2 0.7 %collective-permute-start.13 = (bf16[128,1024]{1,0:T(8,128)(2,1)S(1)}, bf16[128,1024]{1,0:T(8,128)(2,1)S(1)}, u32[]{:S(2)}, u32[]{:S(2)}) collective-permute-start(bf16[128,1024]{1,0:T(8,128)(2,1)S(1)} %collective-permute-done.12.refs_4_), channel_id=1, source_target_pairs={{0,4},{4,0},{8,12},{12,8},{1,5},{5,1},{9,13},{13,9},{2,6},{6,2},{1... | collective-permute-start | bytes 786440 | tf_op jit(solution)/shard_map/ppermute | solution.py:41
  20.0 1.6 %collective-permute-start.6 = (bf16[512,128]{1,0:T(8,128)(2,1)S(1)}, bf16[512,128]{1,0:T(8,128)(2,1)S(1)}, u32[]{:S(2)}, u32[]{:S(2)}) collective-permute-start(bf16[512,128]{1,0:T(8,128)(2,1)S(1)} %shard_map.98.refs_2_), channel_id=1, source_target_pairs={{0,1},{1,0},{2,3},{3,2},{4,5},{5,4},{6,7},{7,6},{8,9},{9,8},{10,11... | collective-permute-start | bytes 393224 | tf_op jit(solution)/shard_map/ppermute | solution.py:41
  21.7 3.6 %collective-permute-done.6.refs_3_ = bf16[512,128]{1,0:T(8,128)(2,1)S(1)} collective-permute-done((bf16[512,128]{1,0:T(8,128)(2,1)S(1)}, bf16[512,128]{1,0:T(8,128)(2,1)S(1)}, u32[]{:S(2)}, u32[]{:S(2)}) %collective-permute-start.6) | collective-permute-done | bytes 131104 | tf_op jit(solution)/shard_map/ppermute | solution.py:41
  25.2 1.1 %shard_map.100 = (bf16[768,128]{1,0:T(8,128)(2,1)S(1)}, bf16[768,128]{1,0:T(8,128)(2,1)S(1)}) custom-call(bf16[528,128]{1,0:T(8,128)(2,1)S(1)} %shard_map.97.refs_0_, bf16[528,128]{1,0:T(8,128)(2,1)S(1)} %collective-permute-done.4.refs_1_, bf16[512,128]{1,0:T(8,128)(2,1)S(1)} %shard_map.98.refs_2_, bf16[512,128]{1,0:T(8,128)(2,1)S(1)} %collective-permute-done.6.refs_3_, ...), custom_call_target="tpu_custom_call" | custom-call | flops 67108864 | bytes 731136 | tf_op jit(solution)/shard_map/pallas_call | solution.py:51
  26.4 0.5 %collective-permute-start.14 = (bf16[128,1024]{1,0:T(8,128)(2,1)S(1)}, bf16[128,1024]{1,0:T(8,128)(2,1)S(1)}, u32[]{:S(2)}, u32[]{:S(2)}) collective-permute-start(bf16[128,1024]{1,0:T(8,128)(2,1)S(1)} %collective-permute-done.12.refs_4_), channel_id=1, source_target_pairs={{0,16},{16,0},{1,17},{17,1},{2,18},{18,2},{3,19},{19,3},{4,20},{20... | collective-permute-start | bytes 786440 | tf_op jit(solution)/shard_map/ppermute | solution.py:41
  26.9 0.5 %collective-permute-done.13.refs_5_ = bf16[128,1024]{1,0:T(8,128)(2,1)S(1)} collective-permute-done((bf16[128,1024]{1,0:T(8,128)(2,1)S(1)}, bf16[128,1024]{1,0:T(8,128)(2,1)S(1)}, u32[]{:S(2)}, u32[]{:S(2)}) %collective-permute-start.13) | collective-permute-done | bytes 262176 | tf_op jit(solution)/shard_map/ppermute | solution.py:41
  27.7 0.4 shard_map.101
  28.1 1.4 %shard_map.103 = (bf16[528,128]{1,0:T(8,128)(2,1)S(1)}, bf16[528,128]{1,0:T(8,128)(2,1)S(1)}, bf16[272,128]{1,0:T(8,128)(2,1)S(1)}, bf16[272,128]{1,0:T(8,128)(2...) custom-call(bf16[768,128]{1,0:T(8,128)(2,1)S(1)} %collective-permute-done.8.made_ref, ...), custom_call_target="tpu_custom_call" | custom-call | flops 536870912 | bytes 2886656 | tf_op jit(solution)/shard_map/pallas_call | solution.py:51
  29.5 0.9 %collective-permute-start.9 = (bf16[528,128]{1,0:T(8,128)(2,1)S(1)}, bf16[528,128]{1,0:T(8,128)(2,1)S(1)}, u32[]{:S(2)}, u32[]{:S(2)}) collective-permute-start(bf16[528,128]{1,0:T(8,128)(2,1)S(1)} %get-tuple-element.32), channel_id=1, source_target_pairs={{0,4},{4,0},{8,12},{12,8},{1,5},{5,1},{9,13},{13,9},{2,6},{6,2},{1... | collective-permute-start | bytes 405512 | tf_op jit(solution)/shard_map/ppermute | solution.py:41
  30.4 3.4 %collective-permute-start.10 = (bf16[272,128]{1,0:T(8,128)(2,1)S(1)}, bf16[272,128]{1,0:T(8,128)(2,1)S(1)}, u32[]{:S(2)}, u32[]{:S(2)}) collective-permute-start(bf16[272,128]{1,0:T(8,128)(2,1)S(1)} %get-tuple-element.33), channel_id=1, source_target_pairs={{0,8},{4,12},{8,0},{12,4},{1,9},{5,13},{9,1},{13,5},{2,10},{6,14},... | collective-permute-start | bytes 208904 | tf_op jit(solution)/shard_map/ppermute | solution.py:41
  34.0 2.3 %collective-permute-done.10.refs_2_ = bf16[272,128]{1,0:T(8,128)(2,1)S(1)} collective-permute-done((bf16[272,128]{1,0:T(8,128)(2,1)S(1)}, bf16[272,128]{1,0:T(8,128)(2,1)S(1)}, u32[]{:S(2)}, u32[]{:S(2)}) %collective-permute-start.10) | collective-permute-done | bytes 69664 | tf_op jit(solution)/shard_map/ppermute | solution.py:41
  36.3 4.5 %collective-permute-done.11.refs_3_ = bf16[272,128]{1,0:T(8,128)(2,1)S(1)} collective-permute-done((bf16[272,128]{1,0:T(8,128)(2,1)S(1)}, bf16[272,128]{1,0:T(8,128)(2,1)S(1)}, u32[]{:S(2)}, u32[]{:S(2)}) %collective-permute-start.11) | collective-permute-done | bytes 69664 | tf_op jit(solution)/shard_map/ppermute | solution.py:41
  40.8 1.2 %shard_map.104 = (f32[32,1024]{1,0:T(8,128)}, f32[32,1024]{1,0:T(8,128)}, f32[1,1024]{1,0:T(1,128)}) custom-call(bf16[528,128]{1,0:T(8,128)(2,1)S(1)} %get-tuple-element.31.refs_0_, bf16[528,128]{1,0:T(8,128)(2,1)S(1)} %collective-permute-done.9.refs_1_, bf16[272,128]{1,0:T(8,128)(2,1)S(1)} %collective-permute-done.10.refs_2_, ...), custom_call_target="tpu_custom_call" | custom-call | flops 67108864 | bytes 2770944 | tf_op jit(solution)/shard_map/pallas_call | solution.py:51
  (33 shorter events, 1.5 us)
Async XLA Ops:
  0.6 7.2 %collective-permute-start.1 = (bf16[128,1024]{1,0:T(8,128)(2,1)}, bf16[128,1024]{1,0:T(8,128)(2,1)S(1)}, u32[]{:S(2)}, u32[]{:S(2)}) collective-permute-start(bf16[128,1024]{1,0:T(8,128)(2,1)} %bitcast.11), channel_id=1, source_target_pairs={{0,16},{16,0},{1,17},{17,1},{2,18},{18,2},{3,19},{19,3},{4,20},{20... | collective-permute-start | bytes 786440 | tf_op jit(solution)/shard_map/ppermute | solution.py:41
  1.2 1.0 %copy-start = (bf16[2,128,1024]{2,1,0:T(8,128)(2,1)S(1)}, bf16[2,128,1024]{2,1,0:T(8,128)(2,1)}, u32[]{:S(2)}) copy-start(bf16[2,128,1024]{2,1,0:T(8,128)(2,1)} %param.7) | copy-start | bytes 1572868
  1.2 1.1 %copy-start.1 = (bf16[1,128,1024]{2,1,0:T(8,128)(2,1)S(1)}, bf16[1,128,1024]{2,1,0:T(8,128)(2,1)}, u32[]{:S(2)}) copy-start(bf16[1,128,1024]{2,1,0:T(8,128)(2,1)} %param.9) | copy-start | bytes 786436
  1.2 1.2 %copy-start.2 = (bf16[1,1024,128]{2,1,0:T(8,128)(2,1)S(1)}, bf16[1,1024,128]{2,1,0:T(8,128)(2,1)}, u32[]{:S(2)}) copy-start(bf16[1,1024,128]{2,1,0:T(8,128)(2,1)} %param.8) | copy-start | bytes 786436
  1.2 1.3 %copy-start.3 = (bf16[1024,128]{1,0:T(8,128)(2,1)S(1)}, bf16[1024,128]{1,0:T(8,128)(2,1)}, u32[]{:S(2)}) copy-start(bf16[1024,128]{1,0:T(8,128)(2,1)} %head_ref.3) | copy-start | bytes 786436
  1.2 1.3 %copy-start.4 = (bf16[1,1024]{1,0:T(2,128)(2,1)S(1)}, bf16[1,1024]{1,0:T(2,128)(2,1)}, u32[]{:S(2)}) copy-start(bf16[1,1024]{1,0:T(2,128)(2,1)} %refs_9_.1) | copy-start | bytes 6148
  1.2 6.6 %collective-permute-start = (bf16[1024,128]{1,0:T(8,128)(2,1)}, bf16[1024,128]{1,0:T(8,128)(2,1)S(1)}, u32[]{:S(2)}, u32[]{:S(2)}) collective-permute-start(bf16[1024,128]{1,0:T(8,128)(2,1)} %bitcast.15), channel_id=1, source_target_pairs={{0,16},{16,0},{1,17},{17,1},{2,18},{18,2},{3,19},{19,3},{4,20},{20... | collective-permute-start | bytes 786440 | tf_op jit(solution)/shard_map/ppermute | solution.py:41
  3.0 16.2 %collective-permute-start.12 = (bf16[128,1024]{1,0:T(8,128)(2,1)S(1)}, bf16[128,1024]{1,0:T(8,128)(2,1)S(1)}, u32[]{:S(2)}, u32[]{:S(2)}) collective-permute-start(bf16[128,1024]{1,0:T(8,128)(2,1)S(1)} %get-tuple-element.35), channel_id=1, source_target_pairs={{0,8},{4,12},{8,0},{12,4},{1,9},{5,13},{9,1},{13,5},{2,10},{6,14},... | collective-permute-start | bytes 786440 | tf_op jit(solution)/shard_map/ppermute | solution.py:41
  6.6 1.2 %collective-permute-start.2 = (bf16[1,1024]{1,0:T(2,128)(2,1)S(1)}, bf16[1,1024]{1,0:T(2,128)(2,1)S(1)}, u32[]{:S(2)}, u32[]{:S(2)}) collective-permute-start(bf16[1,1024]{1,0:T(2,128)(2,1)S(1)} %copy-done.4), channel_id=1, source_target_pairs={{0,16},{16,0},{1,17},{17,1},{2,18},{18,2},{3,19},{19,3},{4,20},{20... | collective-permute-start | bytes 6152 | tf_op jit(solution)/shard_map/ppermute | solution.py:41
  7.8 17.4 %copy-start.5 = (s32[2,128]{1,0:T(2,128)S(1)}, s32[2,128]{1,0:T(2,128)}, u32[]{:S(2)}) copy-start(s32[2,128]{1,0:T(2,128)} %valid_ref.1) | copy-start | bytes 3076
  7.8 17.4 %copy-start.6 = (s32[2,128]{1,0:T(2,128)S(1)}, s32[2,128]{1,0:T(2,128)}, u32[]{:S(2)}) copy-start(s32[2,128]{1,0:T(2,128)} %refs_6_.1) | copy-start | bytes 3076
  8.3 5.8 %collective-permute-start.3 = (bf16[528,128]{1,0:T(8,128)(2,1)S(1)}, bf16[528,128]{1,0:T(8,128)(2,1)S(1)}, u32[]{:S(2)}, u32[]{:S(2)}) collective-permute-start(bf16[528,128]{1,0:T(8,128)(2,1)S(1)} %get-tuple-element.22.refs_0_), channel_id=1, source_target_pairs={{0,1},{1,0},{2,3},{3,2},{4,5},{5,4},{6,7},{7,6},{8,9},{9,8},{10,11... | collective-permute-start | bytes 405512 | tf_op jit(solution)/shard_map/ppermute | solution.py:41
  9.9 10.1 %collective-permute-start.5 = (bf16[512,128]{1,0:T(8,128)(2,1)S(1)}, bf16[512,128]{1,0:T(8,128)(2,1)S(1)}, u32[]{:S(2)}, u32[]{:S(2)}) collective-permute-start(bf16[512,128]{1,0:T(8,128)(2,1)S(1)} %get-tuple-element.23.refs_0_), channel_id=1, source_target_pairs={{0,2},{1,3},{2,0},{3,1},{4,6},{5,7},{6,4},{7,5},{8,10},{9,11},{10,... | collective-permute-start | bytes 393224 | tf_op jit(solution)/shard_map/ppermute | solution.py:41
  14.2 7.4 %collective-permute-start.4 = (bf16[528,128]{1,0:T(8,128)(2,1)S(1)}, bf16[528,128]{1,0:T(8,128)(2,1)S(1)}, u32[]{:S(2)}, u32[]{:S(2)}) collective-permute-start(bf16[528,128]{1,0:T(8,128)(2,1)S(1)} %shard_map.97.refs_0_), channel_id=1, source_target_pairs={{0,2},{1,3},{2,0},{3,1},{4,6},{5,7},{6,4},{7,5},{8,10},{9,11},{10,... | collective-permute-start | bytes 405512 | tf_op jit(solution)/shard_map/ppermute | solution.py:41
  19.2 8.1 %collective-permute-start.13 = (bf16[128,1024]{1,0:T(8,128)(2,1)S(1)}, bf16[128,1024]{1,0:T(8,128)(2,1)S(1)}, u32[]{:S(2)}, u32[]{:S(2)}) collective-permute-start(bf16[128,1024]{1,0:T(8,128)(2,1)S(1)} %collective-permute-done.12.refs_4_), channel_id=1, source_target_pairs={{0,4},{4,0},{8,12},{12,8},{1,5},{5,1},{9,13},{13,9},{2,6},{6,2},{1... | collective-permute-start | bytes 786440 | tf_op jit(solution)/shard_map/ppermute | solution.py:41
  20.0 5.2 %collective-permute-start.6 = (bf16[512,128]{1,0:T(8,128)(2,1)S(1)}, bf16[512,128]{1,0:T(8,128)(2,1)S(1)}, u32[]{:S(2)}, u32[]{:S(2)}) collective-permute-start(bf16[512,128]{1,0:T(8,128)(2,1)S(1)} %shard_map.98.refs_2_), channel_id=1, source_target_pairs={{0,1},{1,0},{2,3},{3,2},{4,5},{5,4},{6,7},{7,6},{8,9},{9,8},{10,11... | collective-permute-start | bytes 393224 | tf_op jit(solution)/shard_map/ppermute | solution.py:41
  21.6 3.6 %collective-permute-start.7 = (bf16[384,128]{1,0:T(8,128)(2,1)S(1)}, bf16[384,128]{1,0:T(8,128)(2,1)S(1)}, u32[]{:S(2)}, u32[]{:S(2)}) collective-permute-start(bf16[384,128]{1,0:T(8,128)(2,1)S(1)} %shard_map.99.refs_4_), channel_id=1, source_target_pairs={{0,16},{16,0},{1,17},{17,1},{2,18},{18,2},{3,19},{19,3},{4,20},{20... | collective-permute-start | bytes 294920 | tf_op jit(solution)/shard_map/ppermute | solution.py:41
  26.3 1.8 %collective-permute-start.8 = (bf16[768,128]{1,0:T(8,128)(2,1)S(1)}, bf16[768,128]{1,0:T(8,128)(2,1)S(1)}, u32[]{:S(2)}, u32[]{:S(2)}) collective-permute-start(bf16[768,128]{1,0:T(8,128)(2,1)S(1)} %get-tuple-element.24), channel_id=1, source_target_pairs={{0,16},{16,0},{1,17},{17,1},{2,18},{18,2},{3,19},{19,3},{4,20},{20... | collective-permute-start | bytes 589832 | tf_op jit(solution)/shard_map/ppermute | solution.py:41
  26.4 7.7 %collective-permute-start.14 = (bf16[128,1024]{1,0:T(8,128)(2,1)S(1)}, bf16[128,1024]{1,0:T(8,128)(2,1)S(1)}, u32[]{:S(2)}, u32[]{:S(2)}) collective-permute-start(bf16[128,1024]{1,0:T(8,128)(2,1)S(1)} %collective-permute-done.12.refs_4_), channel_id=1, source_target_pairs={{0,16},{16,0},{1,17},{17,1},{2,18},{18,2},{3,19},{19,3},{4,20},{20... | collective-permute-start | bytes 786440 | tf_op jit(solution)/shard_map/ppermute | solution.py:41
  27.3 6.7 %collective-permute-start.15 = (bf16[128,1024]{1,0:T(8,128)(2,1)S(1)}, bf16[128,1024]{1,0:T(8,128)(2,1)S(1)}, u32[]{:S(2)}, u32[]{:S(2)}) collective-permute-start(bf16[128,1024]{1,0:T(8,128)(2,1)S(1)} %collective-permute-done.13.refs_5_), channel_id=1, source_target_pairs={{0,16},{16,0},{1,17},{17,1},{2,18},{18,2},{3,19},{19,3},{4,20},{20... | collective-permute-start | bytes 786440 | tf_op jit(solution)/shard_map/ppermute | solution.py:41
  29.5 11.3 %collective-permute-start.9 = (bf16[528,128]{1,0:T(8,128)(2,1)S(1)}, bf16[528,128]{1,0:T(8,128)(2,1)S(1)}, u32[]{:S(2)}, u32[]{:S(2)}) collective-permute-start(bf16[528,128]{1,0:T(8,128)(2,1)S(1)} %get-tuple-element.32), channel_id=1, source_target_pairs={{0,4},{4,0},{8,12},{12,8},{1,5},{5,1},{9,13},{13,9},{2,6},{6,2},{1... | collective-permute-start | bytes 405512 | tf_op jit(solution)/shard_map/ppermute | solution.py:41
  30.4 5.9 %collective-permute-start.10 = (bf16[272,128]{1,0:T(8,128)(2,1)S(1)}, bf16[272,128]{1,0:T(8,128)(2,1)S(1)}, u32[]{:S(2)}, u32[]{:S(2)}) collective-permute-start(bf16[272,128]{1,0:T(8,128)(2,1)S(1)} %get-tuple-element.33), channel_id=1, source_target_pairs={{0,8},{4,12},{8,0},{12,4},{1,9},{5,13},{9,1},{13,5},{2,10},{6,14},... | collective-permute-start | bytes 208904 | tf_op jit(solution)/shard_map/ppermute | solution.py:41
  33.7 7.1 %collective-permute-start.11 = (bf16[272,128]{1,0:T(8,128)(2,1)S(1)}, bf16[272,128]{1,0:T(8,128)(2,1)S(1)}, u32[]{:S(2)}, u32[]{:S(2)}) collective-permute-start(bf16[272,128]{1,0:T(8,128)(2,1)S(1)} %get-tuple-element.34), channel_id=1, source_target_pairs={{0,12},{4,8},{8,4},{12,0},{1,13},{5,9},{9,5},{13,1},{2,14},{6,10},... | collective-permute-start | bytes 208904 | tf_op jit(solution)/shard_map/ppermute | solution.py:41

commit v11 on v9

--- a/solution.py
+++ b/solution.py
@@ -39,12 +39,6 @@
 def from_partner(value, axis, step):
     size = lax.axis_size(axis)
     return lax.ppermute(value, axis, [(i, partner(i, step, size)) for i in range(size)])
-
-
-def from_section(value, steps):
-    size = lax.axis_size("dp")
-    pairs = [(s * size + i, s * size + partner(i, step, size)) for s, step in enumerate(steps) for i in range(size)]
-    return lax.ppermute(value, ("section", "dp"), pairs)
 
 
 def high_low(value):
@@ -66,10 +60,11 @@
     out_ref[...] = jnp.zeros_like(out_ref)
 
 
-def own_kernel(x_ref, down_ref, up_ref, head_ref, gain_ref, _, out_ref):
+def own_kernel(x_ref, down_ref, up_ref, head_ref, gain_ref, _, out_ref, half_ref):
     rank = down_ref.shape[1]
     half = x_ref.shape[0] // lax.axis_size("section")
     x, up, head = x_ref[rows_of(lax.axis_index("section") * half, half), :], up_ref[...], head_ref[...]
+    half_ref[...] = x
     x32 = x.astype(F32)
     scaled = (x32 * gain_ref[...].astype(F32)).astype(BF16)
     out_ref[:half, :] = dot(scaled, down_ref[...]).astype(BF16)
@@ -280,9 +275,9 @@
 
 
 def last_kernel(count, *refs):
-    near, fars, refs = refs[:count], refs[count : count + 3], refs[count + 3 :]
-    sent_ref, relay_ref, cross_ref, cross2_ref, stack_ref, gain_ref, down_out, up_out, gain_out = refs
-    rank = fars[0].shape[1]
+    near, refs = refs[:count], refs[count:]
+    far_ref, sent_ref, cross_ref, stack_ref, gain_ref, down_out, up_out, gain_out = refs
+    rank = far_ref.shape[1]
     slim, features = down_out.shape
     lines = features // rank
     first = lax.axis_index("section") == 0
@@ -290,16 +285,14 @@
     def total(start, size):
         return sum(p[start : start + size, :].astype(F32) for p in near)
 
-    def left(ref):
-        rows = [ref[i * slim : (i + 1) * slim, :] for i in range(4, 8)]
-        return jnp.concatenate([jnp.concatenate(rows[:2], axis=1), jnp.concatenate(rows[2:], axis=1)], axis=0)
-
-    tail = sum(p[-PACK:, :].astype(F32) for p in near + fars)
+    def left(i):
+        return jnp.concatenate([far_ref[j * slim : (j + 1) * slim, :] for j in (4 + i, 6 + i)], axis=0)
+
+    tail = sum(p[-PACK:, :].astype(F32) for p in (*near, far_ref))
     scale = 1.0 / tail[lines : lines + 1, :1]
-    left_a, left_b, left_c = (left(r) for r in fars)
-    moved = dot(jnp.where(first, left_a, left_c), sent_ref[...]) + dot(jnp.where(first, left_c, left_a), cross_ref[...])
-    moved = moved + dot(left_b, jnp.where(first, relay_ref[...], cross2_ref[...]))
-    mixes = [sum(r[i * slim : (i + 1) * slim, :].astype(F32) for r in fars).astype(BF16) for i in range(4)]
+    one, two = left(0), left(1)
+    moved = dot(jnp.where(first, one, two), sent_ref[...]) + dot(jnp.where(first, two, one), cross_ref[...])
+    mixes = [far_ref[i * slim : (i + 1) * slim, :] for i in range(4)]
     none = jnp.zeros_like(mixes[3])
     down = moved[:slim] + dot(jnp.where(first, none, mixes[3]), stack_ref[3 * rank : 4 * rank, :])
     down = down * gain_ref[...].astype(F32)
@@ -330,18 +323,18 @@
     for value in (down, up, gains):
         others.append(from_partner(value, "section", 1))
     down2, up2, gains2 = others
-    assert replicas > 3
-    far = [replicas - 2, replicas - 1, 1]
-    near = [step for step in range(replicas) if step not in far]
-    gathered = [from_section(states, [replicas - 2, 1])]
+    assert replicas > 1
+    far = replicas // 2
+    near = [step for step in range(replicas) if step != far]
     small = 2 * rank * rank * features
     opened = call(open_kernel, shape((8, rank), F32), 40 * small)
-    own = call(
+    own, mine = call(
         own_kernel,
-        shape((3 * half + 2 * rank + PACK, rank), BF16),
+        [shape((3 * half + 2 * rank + PACK, rank), BF16), shape((half, features), BF16)],
         5 * small,
         states, down, up, head, gains, opened,
     )
+    sent = from_partner(mine, "dp", far)
     first_part, second_part = call(
         other_kernel,
         [shape((3 * rank + half + PACK, rank), BF16), shape((4 * half, rank), BF16)],
@@ -376,7 +369,6 @@
         *first_part, *second_part, gram, gram2, labels, valid,
     )
     met = from_partner(theirs, "section", 1)
-    gathered.append(from_section(gathered[0], [1]))
     mixes, acc, left = call(
         functools.partial(mine_kernel, near),
         [shape((4 * rank, rank), F32), shape((rank + len(near) * slim, features), F32), shape((2 * rank, half), BF16)],
@@ -392,13 +384,12 @@
     )
     for step in range(1, replicas):
         parts[step] = from_partner(parts[step], "dp", step)
-    for i in range(2):
-        gathered.append(from_partner(gathered[i], "section", 1))
+    cross = from_partner(sent, "section", 1)
     down_grad, up_grad, gain_grad = call(
         functools.partial(last_kernel, len(near)),
         [shape((slim, features), F32), shape((slim, features), F32), shape((1, features), F32)],
         2 * small,
-        *(parts[i] for i in near + far), *gathered, stack, gains,
+        *(parts[i] for i in near), parts[far], sent, cross, stack, gains,
     )
     return down_grad.T[None], up_grad[None], gain_grad
 

time: 52.7 us -> 41.7 us (0.79)
  waiting for transfers between devices: 25.1 us -> 18.7 us
  starting transfers between devices: 20.4 us -> 16 us
    ppermute x2 -> x0, waiting for transfers between devices: 11.7 us -> none  [from_section(): return lax.ppermute(value, ('section', 'dp'), pairs)]
    ppermute x2 -> x0, starting transfers between devices: 8.45 us -> none  [from_section(): return lax.ppermute(value, ('section', 'dp'), pairs)]
    ppermute x14, waiting for transfers between devices: 13.4 us -> 18.7 us  [from_partner(): lax.ppermute(value, axis, [(i, partner(i, step, size)) for i in range(siz...]
    ppermute x14, starting transfers between devices: 11.9 us -> 16 us  [from_partner(): lax.ppermute(value, axis, [(i, partner(i, step, size)) for i in range(siz...]
  transfers between devices with their start and end apart: 16 -> 14, of which waited for: 9 -> 6; matrix products, arithmetic and copies ran while one was open for 0% -> 0% of each run, Pallas kernels for 8% -> 9%
where the time goes in v11:
time: 41.7 us; the launch traced here: 41.6 us
  waiting for transfers between devices  18.7 us (45%)
  starting transfers between devices  16 us (38%)
  Pallas kernels  5.47 us (13%)
  between operations  0.73 us (2%)
  local copies, waits for them, and re-layouts  0.68 us (2%)
    ppermute x14, waiting for transfers between devices, from_partner(): lax.ppermute(value, axis, [(i, partner(i, step, size)) for i in range(siz...  18.7 us
    ppermute x14, starting transfers between devices, from_partner(): lax.ppermute(value, axis, [(i, partner(i, step, size)) for i in range(siz...  16 us
    pallas_call x11, Pallas kernels, call(): pl.pallas_call(kernel, out_shape=out, cost_estimate=pl.CostEstimate(flops...  5.47 us
  transfers between devices with their start and end apart: 14, of which 6 were waited for; matrix products, arithmetic and copies ran while one was open for 0% of the time, Pallas kernels for 9%

profile of v11, /device:TPU:0, one launch (start us, length us, event | category | flops | bytes accessed | tf_op | source)
XLA Modules:
  0.0 41.6 jit_solution(620555355990012589)
XLA Ops:
  0.6 0.6 %collective-permute-start.1 = (bf16[128,1024]{1,0:T(8,128)(2,1)}, bf16[128,1024]{1,0:T(8,128)(2,1)S(1)}, u32[]{:S(2)}, u32[]{:S(2)}) collective-permute-start(bf16[128,1024]{1,0:T(8,128)(2,1)} %bitcast.11), channel_id=1, source_target_pairs={{0,16},{16,0},{1,17},{17,1},{2,18},{18,2},{3,19},{19,3},{4,20},{20... | collective-permute-start | bytes 786440 | tf_op jit(solution)/shard_map/ppermute | solution.py:41
  1.2 0.1 collective-permute-start
  1.3 0.5 %collective-permute-start.2 = (bf16[1,1024]{1,0:T(2,128)(2,1)}, bf16[1,1024]{1,0:T(2,128)(2,1)S(1)}, u32[]{:S(2)}, u32[]{:S(2)}) collective-permute-start(bf16[1,1024]{1,0:T(2,128)(2,1)} %refs_7_.3), channel_id=1, source_target_pairs={{0,16},{16,0},{1,17},{17,1},{2,18},{18,2},{3,19},{19,3},{4,20},{20... | collective-permute-start | bytes 6152 | tf_op jit(solution)/shard_map/ppermute | solution.py:41
  1.8 0.4 %copy-done = bf16[2,128,1024]{2,1,0:T(8,128)(2,1)S(1)} copy-done((bf16[2,128,1024]{2,1,0:T(8,128)(2,1)S(1)}, bf16[2,128,1024]{2,1,0:T(8,128)(2,1)}, u32[]{:S(2)}) %copy-start) | copy-done | bytes 524312
  2.3 0.1 copy-done.2
  2.5 0.5 %shard_map.95 = (bf16[656,128]{1,0:T(8,128)(2,1)S(1)}, bf16[128,1024]{1,0:T(8,128)(2,1)S(1)}) custom-call(bf16[256,1024]{1,0:T(8,128)(2,1)S(1)} %bitcast.7, bf16[1024,128]{1,0:T(8,128)(2,1)S(1)} %bitcast.16, bf16[128,1024]{1,0:T(8,128)(2,1)S(1)} %bitcast.12, bf16[1024,128]{1,0:T(8,128)(2,1)S(1)} %copy-done.3, bf16[1,1024]{1,0:T(2,128)(2,1)S(1)} %copy-done.4, ...), custom_call_target="tpu_custom_call" | custom-call | flops 167772160 | bytes 1316864 | tf_op jit(solution)/shard_map/pallas_call | solution.py:51
  3.1 0.5 %shard_map.96 = (bf16[528,128]{1,0:T(8,128)(2,1)S(1)}, bf16[512,128]{1,0:T(8,128)(2,1)S(1)}) custom-call(bf16[256,1024]{1,0:T(8,128)(2,1)S(1)} %bitcast.8, bf16[128,1024]{1,0:T(8,128)(2,1)S(1)} %bitcast.13, bf16[656,128]{1,0:T(8,128)(2,1)S(1)} %get-tuple-element.21.own_ref, bf16[1024,128]{1,0:T(8,128)(2,1)S(1)} %collective-permute-done.down2_ref, ...), custom_call_target="tpu_custom_call" | custom-call | flops 100663296 | bytes 1480704 | tf_op jit(solution)/shard_map/pallas_call | solution.py:51
  3.6 2.8 %collective-permute-start.3 = (bf16[528,128]{1,0:T(8,128)(2,1)S(1)}, bf16[528,128]{1,0:T(8,128)(2,1)S(1)}, u32[]{:S(2)}, u32[]{:S(2)}) collective-permute-start(bf16[528,128]{1,0:T(8,128)(2,1)S(1)} %get-tuple-element.22.refs_0_), channel_id=1, source_target_pairs={{0,1},{1,0},{2,3},{3,2},{4,5},{5,4},{6,7},{7,6},{8,9},{9,8},{10,11... | collective-permute-start | bytes 405512 | tf_op jit(solution)/shard_map/ppermute | solution.py:41
  6.4 1.5 %collective-permute-start.5 = (bf16[512,128]{1,0:T(8,128)(2,1)S(1)}, bf16[512,128]{1,0:T(8,128)(2,1)S(1)}, u32[]{:S(2)}, u32[]{:S(2)}) collective-permute-start(bf16[512,128]{1,0:T(8,128)(2,1)S(1)} %get-tuple-element.23.refs_0_), channel_id=1, source_target_pairs={{0,2},{1,3},{2,0},{3,1},{4,6},{5,7},{6,4},{7,5},{8,10},{9,11},{10,... | collective-permute-start | bytes 393224 | tf_op jit(solution)/shard_map/ppermute | solution.py:41
  7.9 2.5 %collective-permute-done.3.refs_1_ = bf16[528,128]{1,0:T(8,128)(2,1)S(1)} collective-permute-done((bf16[528,128]{1,0:T(8,128)(2,1)S(1)}, bf16[528,128]{1,0:T(8,128)(2,1)S(1)}, u32[]{:S(2)}, u32[]{:S(2)}) %collective-permute-start.3) | collective-permute-done | bytes 135200 | tf_op jit(solution)/shard_map/ppermute | solution.py:41
  10.4 1.8 %collective-permute-start.4 = (bf16[528,128]{1,0:T(8,128)(2,1)S(1)}, bf16[528,128]{1,0:T(8,128)(2,1)S(1)}, u32[]{:S(2)}, u32[]{:S(2)}) collective-permute-start(bf16[528,128]{1,0:T(8,128)(2,1)S(1)} %shard_map.97.refs_0_), channel_id=1, source_target_pairs={{0,2},{1,3},{2,0},{3,1},{4,6},{5,7},{6,4},{7,5},{8,10},{9,11},{10,... | collective-permute-start | bytes 405512 | tf_op jit(solution)/shard_map/ppermute | solution.py:41
  12.2 2.6 %collective-permute-start.12 = (bf16[128,1024]{1,0:T(8,128)(2,1)S(1)}, bf16[128,1024]{1,0:T(8,128)(2,1)S(1)}, u32[]{:S(2)}, u32[]{:S(2)}) collective-permute-start(bf16[128,1024]{1,0:T(8,128)(2,1)S(1)} %get-tuple-element.35), channel_id=1, source_target_pairs={{0,8},{4,12},{8,0},{12,4},{1,9},{5,13},{9,1},{13,5},{2,10},{6,14},... | collective-permute-start | bytes 786440 | tf_op jit(solution)/shard_map/ppermute | solution.py:41
  14.9 1.6 %collective-permute-start.6 = (bf16[512,128]{1,0:T(8,128)(2,1)S(1)}, bf16[512,128]{1,0:T(8,128)(2,1)S(1)}, u32[]{:S(2)}, u32[]{:S(2)}) collective-permute-start(bf16[512,128]{1,0:T(8,128)(2,1)S(1)} %shard_map.98.refs_2_), channel_id=1, source_target_pairs={{0,1},{1,0},{2,3},{3,2},{4,5},{5,4},{6,7},{7,6},{8,9},{9,8},{10,11... | collective-permute-start | bytes 393224 | tf_op jit(solution)/shard_map/ppermute | solution.py:41
  16.5 3.4 %collective-permute-done.6.refs_3_ = bf16[512,128]{1,0:T(8,128)(2,1)S(1)} collective-permute-done((bf16[512,128]{1,0:T(8,128)(2,1)S(1)}, bf16[512,128]{1,0:T(8,128)(2,1)S(1)}, u32[]{:S(2)}, u32[]{:S(2)}) %collective-permute-start.6) | collective-permute-done | bytes 131104 | tf_op jit(solution)/shard_map/ppermute | solution.py:41
  19.9 1.1 %shard_map.100 = (bf16[768,128]{1,0:T(8,128)(2,1)S(1)}, bf16[768,128]{1,0:T(8,128)(2,1)S(1)}) custom-call(bf16[528,128]{1,0:T(8,128)(2,1)S(1)} %shard_map.97.refs_0_, bf16[528,128]{1,0:T(8,128)(2,1)S(1)} %collective-permute-done.4.refs_1_, bf16[512,128]{1,0:T(8,128)(2,1)S(1)} %shard_map.98.refs_2_, bf16[512,128]{1,0:T(8,128)(2,1)S(1)} %collective-permute-done.6.refs_3_, ...), custom_call_target="tpu_custom_call" | custom-call | flops 67108864 | bytes 731136 | tf_op jit(solution)/shard_map/pallas_call | solution.py:51
  21.1 5.0 %collective-permute-done.12.refs_4_ = bf16[128,1024]{1,0:T(8,128)(2,1)S(1)} collective-permute-done((bf16[128,1024]{1,0:T(8,128)(2,1)S(1)}, bf16[128,1024]{1,0:T(8,128)(2,1)S(1)}, u32[]{:S(2)}, u32[]{:S(2)}) %collective-permute-start.12) | collective-permute-done | bytes 262176 | tf_op jit(solution)/shard_map/ppermute | solution.py:41
  26.1 0.4 shard_map.102
  26.4 0.4 %shard_map.101 = (f32[512,128]{1,0:T(8,128)S(1)}, f32[224,1024]{1,0:T(8,128)S(1)}, bf16[256,128]{1,0:T(8,128)(2,1)S(1)}) custom-call(bf16[768,128]{1,0:T(8,128)(2,1)S(1)} %get-tuple-element.25.made_ref, bf16[256,1024]{1,0:T(8,128)(2,1)S(1)} %bitcast.10), custom_call_target="tpu_custom_call" | custom-call | flops 134217728 | bytes 720896 | tf_op jit(solution)/shard_map/pallas_call | solution.py:51
  26.9 1.4 %shard_map.103 = (bf16[528,128]{1,0:T(8,128)(2,1)S(1)}, bf16[528,128]{1,0:T(8,128)(2,1)S(1)}, bf16[272,128]{1,0:T(8,128)(2,1)S(1)}, bf16[528,128]{1,0:T(8,128)(2...) custom-call(bf16[768,128]{1,0:T(8,128)(2,1)S(1)} %collective-permute-done.8.made_ref, ...), custom_call_target="tpu_custom_call" | custom-call | flops 536870912 | bytes 3017728 | tf_op jit(solution)/shard_map/pallas_call | solution.py:51
  28.3 3.5 %collective-permute-start.10 = (bf16[528,128]{1,0:T(8,128)(2,1)S(1)}, bf16[528,128]{1,0:T(8,128)(2,1)S(1)}, u32[]{:S(2)}, u32[]{:S(2)}) collective-permute-start(bf16[528,128]{1,0:T(8,128)(2,1)S(1)} %get-tuple-element.33), channel_id=1, source_target_pairs={{0,12},{4,8},{8,4},{12,0},{1,13},{5,9},{9,5},{13,1},{2,14},{6,10},... | collective-permute-start | bytes 405512 | tf_op jit(solution)/shard_map/ppermute | solution.py:41
  31.8 0.9 %collective-permute-start.11 = (bf16[272,128]{1,0:T(8,128)(2,1)S(1)}, bf16[272,128]{1,0:T(8,128)(2,1)S(1)}, u32[]{:S(2)}, u32[]{:S(2)}) collective-permute-start(bf16[272,128]{1,0:T(8,128)(2,1)S(1)} %get-tuple-element.34), channel_id=1, source_target_pairs={{0,8},{4,12},{8,0},{12,4},{1,9},{5,13},{9,1},{13,5},{2,10},{6,14},... | collective-permute-start | bytes 208904 | tf_op jit(solution)/shard_map/ppermute | solution.py:41
  32.7 7.0 %collective-permute-done.11.refs_3_ = bf16[272,128]{1,0:T(8,128)(2,1)S(1)} collective-permute-done((bf16[272,128]{1,0:T(8,128)(2,1)S(1)}, bf16[272,128]{1,0:T(8,128)(2,1)S(1)}, u32[]{:S(2)}, u32[]{:S(2)}) %collective-permute-start.11) | collective-permute-done | bytes 69664 | tf_op jit(solution)/shard_map/ppermute | solution.py:41
  39.7 0.8 %collective-permute-done.9.refs_1_ = bf16[528,128]{1,0:T(8,128)(2,1)S(1)} collective-permute-done((bf16[528,128]{1,0:T(8,128)(2,1)S(1)}, bf16[528,128]{1,0:T(8,128)(2,1)S(1)}, u32[]{:S(2)}, u32[]{:S(2)}) %collective-permute-start.9) | collective-permute-done | bytes 135200 | tf_op jit(solution)/shard_map/ppermute | solution.py:41
  40.5 1.1 %shard_map.104 = (f32[32,1024]{1,0:T(8,128)}, f32[32,1024]{1,0:T(8,128)}, f32[1,1024]{1,0:T(1,128)}) custom-call(bf16[528,128]{1,0:T(8,128)(2,1)S(1)} %get-tuple-element.31.refs_0_, bf16[528,128]{1,0:T(8,128)(2,1)S(1)} %collective-permute-done.9.refs_1_, bf16[528,128]{1,0:T(8,128)(2,1)S(1)} %collective-permute-done.10.refs_2_, ...), custom_call_target="tpu_custom_call" | custom-call | flops 67108864 | bytes 2312192 | tf_op jit(solution)/shard_map/pallas_call | solution.py:51
  (29 shorter events, 0.5 us)
Async XLA Ops:
  0.6 2.4 %collective-permute-start.1 = (bf16[128,1024]{1,0:T(8,128)(2,1)}, bf16[128,1024]{1,0:T(8,128)(2,1)S(1)}, u32[]{:S(2)}, u32[]{:S(2)}) collective-permute-start(bf16[128,1024]{1,0:T(8,128)(2,1)} %bitcast.11), channel_id=1, source_target_pairs={{0,16},{16,0},{1,17},{17,1},{2,18},{18,2},{3,19},{19,3},{4,20},{20... | collective-permute-start | bytes 786440 | tf_op jit(solution)/shard_map/ppermute | solution.py:41
  1.2 1.0 %copy-start = (bf16[2,128,1024]{2,1,0:T(8,128)(2,1)S(1)}, bf16[2,128,1024]{2,1,0:T(8,128)(2,1)}, u32[]{:S(2)}) copy-start(bf16[2,128,1024]{2,1,0:T(8,128)(2,1)} %param.7) | copy-start | bytes 1572868
  1.2 1.1 %copy-start.1 = (bf16[1,128,1024]{2,1,0:T(8,128)(2,1)S(1)}, bf16[1,128,1024]{2,1,0:T(8,128)(2,1)}, u32[]{:S(2)}) copy-start(bf16[1,128,1024]{2,1,0:T(8,128)(2,1)} %param.9) | copy-start | bytes 786436
  1.2 1.2 %copy-start.2 = (bf16[1,1024,128]{2,1,0:T(8,128)(2,1)S(1)}, bf16[1,1024,128]{2,1,0:T(8,128)(2,1)}, u32[]{:S(2)}) copy-start(bf16[1,1024,128]{2,1,0:T(8,128)(2,1)} %param.8) | copy-start | bytes 786436
  1.2 1.3 %copy-start.3 = (bf16[1024,128]{1,0:T(8,128)(2,1)S(1)}, bf16[1024,128]{1,0:T(8,128)(2,1)}, u32[]{:S(2)}) copy-start(bf16[1024,128]{1,0:T(8,128)(2,1)} %head_ref.3) | copy-start | bytes 786436
  1.2 1.3 %copy-start.4 = (bf16[1,1024]{1,0:T(2,128)(2,1)S(1)}, bf16[1,1024]{1,0:T(2,128)(2,1)}, u32[]{:S(2)}) copy-start(bf16[1,1024]{1,0:T(2,128)(2,1)} %refs_7_.3) | copy-start | bytes 6148
  1.2 1.8 %collective-permute-start = (bf16[1024,128]{1,0:T(8,128)(2,1)}, bf16[1024,128]{1,0:T(8,128)(2,1)S(1)}, u32[]{:S(2)}, u32[]{:S(2)}) collective-permute-start(bf16[1024,128]{1,0:T(8,128)(2,1)} %bitcast.15), channel_id=1, source_target_pairs={{0,16},{16,0},{1,17},{17,1},{2,18},{18,2},{3,19},{19,3},{4,20},{20... | collective-permute-start | bytes 786440 | tf_op jit(solution)/shard_map/ppermute | solution.py:41
  1.3 1.7 %collective-permute-start.2 = (bf16[1,1024]{1,0:T(2,128)(2,1)}, bf16[1,1024]{1,0:T(2,128)(2,1)S(1)}, u32[]{:S(2)}, u32[]{:S(2)}) collective-permute-start(bf16[1,1024]{1,0:T(2,128)(2,1)} %refs_7_.3), channel_id=1, source_target_pairs={{0,16},{16,0},{1,17},{17,1},{2,18},{18,2},{3,19},{19,3},{4,20},{20... | collective-permute-start | bytes 6152 | tf_op jit(solution)/shard_map/ppermute | solution.py:41
  3.0 16.9 %copy-start.5 = (s32[2,128]{1,0:T(2,128)S(1)}, s32[2,128]{1,0:T(2,128)}, u32[]{:S(2)}) copy-start(s32[2,128]{1,0:T(2,128)} %valid_ref.1) | copy-start | bytes 3076
  3.0 16.9 %copy-start.6 = (s32[2,128]{1,0:T(2,128)S(1)}, s32[2,128]{1,0:T(2,128)}, u32[]{:S(2)}) copy-start(s32[2,128]{1,0:T(2,128)} %refs_6_.1) | copy-start | bytes 3076
  3.6 6.8 %collective-permute-start.3 = (bf16[528,128]{1,0:T(8,128)(2,1)S(1)}, bf16[528,128]{1,0:T(8,128)(2,1)S(1)}, u32[]{:S(2)}, u32[]{:S(2)}) collective-permute-start(bf16[528,128]{1,0:T(8,128)(2,1)S(1)} %get-tuple-element.22.refs_0_), channel_id=1, source_target_pairs={{0,1},{1,0},{2,3},{3,2},{4,5},{5,4},{6,7},{7,6},{8,9},{9,8},{10,11... | collective-permute-start | bytes 405512 | tf_op jit(solution)/shard_map/ppermute | solution.py:41
  6.4 8.5 %collective-permute-start.5 = (bf16[512,128]{1,0:T(8,128)(2,1)S(1)}, bf16[512,128]{1,0:T(8,128)(2,1)S(1)}, u32[]{:S(2)}, u32[]{:S(2)}) collective-permute-start(bf16[512,128]{1,0:T(8,128)(2,1)S(1)} %get-tuple-element.23.refs_0_), channel_id=1, source_target_pairs={{0,2},{1,3},{2,0},{3,1},{4,6},{5,7},{6,4},{7,5},{8,10},{9,11},{10,... | collective-permute-start | bytes 393224 | tf_op jit(solution)/shard_map/ppermute | solution.py:41
  10.4 6.0 %collective-permute-start.4 = (bf16[528,128]{1,0:T(8,128)(2,1)S(1)}, bf16[528,128]{1,0:T(8,128)(2,1)S(1)}, u32[]{:S(2)}, u32[]{:S(2)}) collective-permute-start(bf16[528,128]{1,0:T(8,128)(2,1)S(1)} %shard_map.97.refs_0_), channel_id=1, source_target_pairs={{0,2},{1,3},{2,0},{3,1},{4,6},{5,7},{6,4},{7,5},{8,10},{9,11},{10,... | collective-permute-start | bytes 405512 | tf_op jit(solution)/shard_map/ppermute | solution.py:41
  12.2 13.8 %collective-permute-start.12 = (bf16[128,1024]{1,0:T(8,128)(2,1)S(1)}, bf16[128,1024]{1,0:T(8,128)(2,1)S(1)}, u32[]{:S(2)}, u32[]{:S(2)}) collective-permute-start(bf16[128,1024]{1,0:T(8,128)(2,1)S(1)} %get-tuple-element.35), channel_id=1, source_target_pairs={{0,8},{4,12},{8,0},{12,4},{1,9},{5,13},{9,1},{13,5},{2,10},{6,14},... | collective-permute-start | bytes 786440 | tf_op jit(solution)/shard_map/ppermute | solution.py:41
  14.9 5.0 %collective-permute-start.6 = (bf16[512,128]{1,0:T(8,128)(2,1)S(1)}, bf16[512,128]{1,0:T(8,128)(2,1)S(1)}, u32[]{:S(2)}, u32[]{:S(2)}) collective-permute-start(bf16[512,128]{1,0:T(8,128)(2,1)S(1)} %shard_map.98.refs_2_), channel_id=1, source_target_pairs={{0,1},{1,0},{2,3},{3,2},{4,5},{5,4},{6,7},{7,6},{8,9},{9,8},{10,11... | collective-permute-start | bytes 393224 | tf_op jit(solution)/shard_map/ppermute | solution.py:41
  16.5 3.4 %collective-permute-start.7 = (bf16[384,128]{1,0:T(8,128)(2,1)S(1)}, bf16[384,128]{1,0:T(8,128)(2,1)S(1)}, u32[]{:S(2)}, u32[]{:S(2)}) collective-permute-start(bf16[384,128]{1,0:T(8,128)(2,1)S(1)} %shard_map.99.refs_4_), channel_id=1, source_target_pairs={{0,16},{16,0},{1,17},{17,1},{2,18},{18,2},{3,19},{19,3},{4,20},{20... | collective-permute-start | bytes 294920 | tf_op jit(solution)/shard_map/ppermute | solution.py:41
  21.0 5.9 %collective-permute-start.8 = (bf16[768,128]{1,0:T(8,128)(2,1)S(1)}, bf16[768,128]{1,0:T(8,128)(2,1)S(1)}, u32[]{:S(2)}, u32[]{:S(2)}) collective-permute-start(bf16[768,128]{1,0:T(8,128)(2,1)S(1)} %get-tuple-element.24), channel_id=1, source_target_pairs={{0,16},{16,0},{1,17},{17,1},{2,18},{18,2},{3,19},{19,3},{4,20},{20... | collective-permute-start | bytes 589832 | tf_op jit(solution)/shard_map/ppermute | solution.py:41
  26.1 6.6 %collective-permute-start.13 = (bf16[128,1024]{1,0:T(8,128)(2,1)S(1)}, bf16[128,1024]{1,0:T(8,128)(2,1)S(1)}, u32[]{:S(2)}, u32[]{:S(2)}) collective-permute-start(bf16[128,1024]{1,0:T(8,128)(2,1)S(1)} %collective-permute-done.12.refs_4_), channel_id=1, source_target_pairs={{0,16},{16,0},{1,17},{17,1},{2,18},{18,2},{3,19},{19,3},{4,20},{20... | collective-permute-start | bytes 786440 | tf_op jit(solution)/shard_map/ppermute | solution.py:41
  28.3 11.4 %collective-permute-start.10 = (bf16[528,128]{1,0:T(8,128)(2,1)S(1)}, bf16[528,128]{1,0:T(8,128)(2,1)S(1)}, u32[]{:S(2)}, u32[]{:S(2)}) collective-permute-start(bf16[528,128]{1,0:T(8,128)(2,1)S(1)} %get-tuple-element.33), channel_id=1, source_target_pairs={{0,12},{4,8},{8,4},{12,0},{1,13},{5,9},{9,5},{13,1},{2,14},{6,10},... | collective-permute-start | bytes 405512 | tf_op jit(solution)/shard_map/ppermute | solution.py:41
  31.8 8.7 %collective-permute-start.9 = (bf16[528,128]{1,0:T(8,128)(2,1)S(1)}, bf16[528,128]{1,0:T(8,128)(2,1)S(1)}, u32[]{:S(2)}, u32[]{:S(2)}) collective-permute-start(bf16[528,128]{1,0:T(8,128)(2,1)S(1)} %get-tuple-element.32), channel_id=1, source_target_pairs={{0,4},{4,0},{8,12},{12,8},{1,5},{5,1},{9,13},{13,9},{2,6},{6,2},{1... | collective-permute-start | bytes 405512 | tf_op jit(solution)/shard_map/ppermute | solution.py:41
  31.8 7.9 %collective-permute-start.11 = (bf16[272,128]{1,0:T(8,128)(2,1)S(1)}, bf16[272,128]{1,0:T(8,128)(2,1)S(1)}, u32[]{:S(2)}, u32[]{:S(2)}) collective-permute-start(bf16[272,128]{1,0:T(8,128)(2,1)S(1)} %get-tuple-element.34), channel_id=1, source_target_pairs={{0,8},{4,12},{8,0},{12,4},{1,9},{5,13},{9,1},{13,5},{2,10},{6,14},... | collective-permute-start | bytes 208904 | tf_op jit(solution)/shard_map/ppermute | solution.py:41

commit v12 on v11

--- a/solution.py
+++ b/solution.py
@@ -225,12 +225,13 @@
         acc_ref[rank + i * slim : rank + (i + 1) * slim, :] = dot(rows, x)
 
 
-def grad_kernel(
-    replicas, near, made_ref, mix_ref, acc_ref, left_ref, stack_ref, down_t_ref, gain_ref, valid_ref, *refs
+def down_kernel(
+    replicas, far, made_ref, mix_ref, acc_ref, left_ref, stack_ref, down_t_ref, gain_ref, valid_ref,
+    far_ref, grad_ref, wide_ref, tail_ref, tall_ref
 ):
-    out_refs, (all_ref, tall_ref, wide_ref) = refs[:replicas], refs[replicas:]
     rank, features = down_t_ref.shape
     slim = rank // replicas
+    lines = features // rank
     section = lax.axis_index("section")
     first = section == 0
     mixes, weighted_t, scaled_t = products(made_ref[...])
@@ -241,67 +242,72 @@
     tall_ref[rows_of((5 - section) * rank, rank), :] = weighted_t
     tall_ref[rows_of((6 + section) * rank, rank), :] = left_ref[rank:, :]
     tall_ref[rows_of((7 - section) * rank, rank), :] = scaled_t
-    head_mix, own_mix, oth_mix, mix = mixes
-    none = jnp.zeros_like(mix)
-    left = jnp.concatenate([jnp.where(first, none, mix), weighted_t], axis=1)
+    none = jnp.zeros_like(mixes[3])
+    left = jnp.concatenate([jnp.where(first, none, mixes[3]), weighted_t], axis=1)
     grad = acc_ref[:rank, :] + dot(left, stack_ref[3 * rank :, :])
     gain = jnp.sum(grad * down_t_ref[...].astype(F32), axis=0, keepdims=True)
-    grad = (grad * gain_ref[...].astype(F32)).astype(BF16)
-    all_ref[...] = grad
-    for i, value in enumerate((head_mix, own_mix, oth_mix, jnp.where(first, mix, none), scaled_t)):
+    grad_ref[...] = (grad * gain_ref[...].astype(F32)).astype(BF16)
+    for i, value in enumerate((*mixes[:3], jnp.where(first, mixes[3], none), scaled_t)):
         wide_ref[:, i * rank : (i + 1) * rank] = value
-    place = lax.axis_index("dp")
-    targets = [partner(place, step, replicas) for step in range(replicas)]
-    left = jnp.concatenate([wide_ref[rows_of(t * slim, slim), :] for t in (targets[i] for i in near)], axis=0)
-    rest = (acc_ref[rank:, :] + dot(left, stack_ref[...])).astype(BF16)
     count = jnp.sum(valid_ref[...].astype(F32), keepdims=True)
-    lines = features // rank
     tail = jnp.concatenate(
         [gain[:, i * rank : (i + 1) * rank] for i in range(lines)] + [jnp.broadcast_to(count, (PACK - lines, rank))],
         axis=0,
     ).astype(BF16)
-    for step, out_ref in enumerate(out_refs):
-        if step in near:
-            at = near.index(step) * slim
-            block = all_ref[rows_of(targets[step] * slim, slim), :]
-            for i in range(lines):
-                lanes = slice(i * rank, (i + 1) * rank)
-                out_ref[i * 2 * slim : (2 * i + 1) * slim, :] = block[:, lanes]
-                out_ref[(2 * i + 1) * slim : (i + 1) * 2 * slim, :] = rest[at : at + slim, lanes]
-        else:
-            for i in range(8):
-                out_ref[i * slim : (i + 1) * slim, :] = tall_ref[rows_of(i * rank + targets[step] * slim, slim), :]
-        out_ref[-PACK:, :] = tail
-
-
-def last_kernel(count, *refs):
-    near, refs = refs[:count], refs[count:]
-    far_ref, sent_ref, cross_ref, stack_ref, gain_ref, down_out, up_out, gain_out = refs
+    tail_ref[...] = tail
+    target = partner(lax.axis_index("dp"), far, replicas)
+    for i in range(8):
+        far_ref[i * slim : (i + 1) * slim, :] = tall_ref[rows_of(i * rank + target * slim, slim), :]
+    far_ref[-PACK:, :] = tail
+
+
+def up_kernel(replicas, near, acc_ref, grad_ref, wide_ref, tail_ref, stack_ref, *out_refs):
+    rank, features = grad_ref.shape
+    slim = rank // replicas
+    place = lax.axis_index("dp")
+    targets = [partner(place, step, replicas) for step in near]
+    left = jnp.concatenate([wide_ref[rows_of(t * slim, slim), :] for t in targets], axis=0)
+    rest = (acc_ref[rank:, :] + dot(left, stack_ref[...])).astype(BF16)
+    for at, (target, out_ref) in enumerate(zip(targets, out_refs)):
+        block = grad_ref[rows_of(target * slim, slim), :]
+        for i in range(features // rank):
+            lanes = slice(i * rank, (i + 1) * rank)
+            out_ref[i * 2 * slim : (2 * i + 1) * slim, :] = block[:, lanes]
+            out_ref[(2 * i + 1) * slim : (i + 1) * 2 * slim, :] = rest[at * slim : (at + 1) * slim, lanes]
+        out_ref[-PACK:, :] = tail_ref[...]
+
+
+def far_kernel(far_ref, sent_ref, cross_ref, stack_ref, gain_ref, out_ref):
     rank = far_ref.shape[1]
-    slim, features = down_out.shape
-    lines = features // rank
+    slim = out_ref.shape[0] // 2
     first = lax.axis_index("section") == 0
-
-    def total(start, size):
-        return sum(p[start : start + size, :].astype(F32) for p in near)
-
-    def left(i):
-        return jnp.concatenate([far_ref[j * slim : (j + 1) * slim, :] for j in (4 + i, 6 + i)], axis=0)
-
-    tail = sum(p[-PACK:, :].astype(F32) for p in (*near, far_ref))
-    scale = 1.0 / tail[lines : lines + 1, :1]
-    one, two = left(0), left(1)
+    one, two = (
+        jnp.concatenate([far_ref[j * slim : (j + 1) * slim, :] for j in (4 + i, 6 + i)], axis=0) for i in range(2)
+    )
     moved = dot(jnp.where(first, one, two), sent_ref[...]) + dot(jnp.where(first, two, one), cross_ref[...])
     mixes = [far_ref[i * slim : (i + 1) * slim, :] for i in range(4)]
     none = jnp.zeros_like(mixes[3])
     down = moved[:slim] + dot(jnp.where(first, none, mixes[3]), stack_ref[3 * rank : 4 * rank, :])
-    down = down * gain_ref[...].astype(F32)
+    out_ref[:slim, :] = down * gain_ref[...].astype(F32)
     mixes = jnp.concatenate(mixes[:3] + [jnp.where(first, mixes[3], none)], axis=1)
-    up = moved[slim:] + dot(mixes, stack_ref[: 4 * rank, :])
+    out_ref[slim:, :] = moved[slim:] + dot(mixes, stack_ref[: 4 * rank, :])
+
+
+def last_kernel(*refs):
+    near, (far_ref, moved_ref, down_out, up_out, gain_out) = refs[:-5], refs[-5:]
+    rank = far_ref.shape[1]
+    slim, features = down_out.shape
+    lines = features // rank
+
+    def total(start, size):
+        return sum(p[start : start + size, :].astype(F32) for p in near)
+
+    tail = sum(p[-PACK:, :].astype(F32) for p in (*near, far_ref))
+    scale = 1.0 / tail[lines : lines + 1, :1]
     for i in range(lines):
         lanes = slice(i * rank, (i + 1) * rank)
-        down_out[:, lanes] = (total(i * 2 * slim, slim) + down[:, lanes]) * scale
-        up_out[:, lanes] = (total((2 * i + 1) * slim, slim) + up[:, lanes]) * scale
+        down_out[:, lanes] = (total(i * 2 * slim, slim) + moved_ref[:slim, lanes]) * scale
+        up_out[:, lanes] = (total((2 * i + 1) * slim, slim) + moved_ref[slim:, lanes]) * scale
         gain_out[:, lanes] = tail[i : i + 1, :] * scale
 
 
@@ -375,21 +381,37 @@
         4 * small,
         made, states,
     )
-    *parts, _, _, _ = call(
-        functools.partial(grad_kernel, replicas, near),
-        [shape(((lines * 2 if i in near else 8) * slim + PACK, rank), BF16) for i in range(replicas)]
-        + [shape((rank, features), BF16), shape((8 * rank, rank), BF16), shape((rank, 5 * rank), BF16)],
-        16 * small,
+    away, grad, wide, tail, _ = call(
+        functools.partial(down_kernel, replicas, far),
+        [
+            shape((8 * slim + PACK, rank), BF16),
+            shape((rank, features), BF16),
+            shape((rank, 5 * rank), BF16),
+            shape((PACK, rank), BF16),
+            shape((8 * rank, rank), BF16),
+        ],
+        8 * small,
         met, mixes, acc, left, stack, down_t, gains, valid,
     )
-    for step in range(1, replicas):
-        parts[step] = from_partner(parts[step], "dp", step)
+    away = from_partner(away, "dp", far)
+    *parts, = call(
+        functools.partial(up_kernel, replicas, near),
+        [shape((lines * 2 * slim + PACK, rank), BF16)] * len(near),
+        8 * small,
+        acc, grad, wide, tail, stack,
+    )
+    for i, step in enumerate(near):
+        if step > 0:
+            parts[i] = from_partner(parts[i], "dp", step)
     cross = from_partner(sent, "section", 1)
+    moved = call(
+        far_kernel, shape((2 * slim, features), F32), 2 * small, away, sent, cross, stack, gains
+    )
     down_grad, up_grad, gain_grad = call(
-        functools.partial(last_kernel, len(near)),
+        last_kernel,
         [shape((slim, features), F32), shape((slim, features), F32), shape((1, features), F32)],
-        2 * small,
-        *(parts[i] for i in near), parts[far], sent, cross, stack, gains,
+        small,
+        *parts, away, moved,
     )
     return down_grad.T[None], up_grad[None], gain_grad
 

time: 41.7 us -> 41.4 us (level)
    pallas_call x11 -> x13, Pallas kernels: 5.47 us -> 5.49 us  [call(): pl.pallas_call(kernel, out_shape=out, cost_estimate=pl.CostEstimate(flops...]
  transfers between devices with their start and end apart: 14 -> 14, of which waited for: 6 -> 6; matrix products, arithmetic and copies ran while one was open for 0% -> 0% of each run, Pallas kernels for 9% -> 10%
where the time goes in v12:
time: 41.4 us; the launch traced here: 41.3 us
  waiting for transfers between devices  18.3 us (44%)
  starting transfers between devices  16.1 us (39%)
  Pallas kernels  5.49 us (13%)
  between operations  0.74 us (2%)
  local copies, waits for them, and re-layouts  0.68 us (2%)
    ppermute x14, waiting for transfers between devices, from_partner(): lax.ppermute(value, axis, [(i, partner(i, step, size)) for i in range(siz...  18.3 us
    ppermute x14, starting transfers between devices, from_partner(): lax.ppermute(value, axis, [(i, partner(i, step, size)) for i in range(siz...  16.1 us
    pallas_call x13, Pallas kernels, call(): pl.pallas_call(kernel, out_shape=out, cost_estimate=pl.CostEstimate(flops...  5.49 us
  transfers between devices with their start and end apart: 14, of which 6 were waited for; matrix products, arithmetic and copies ran while one was open for 0% of the time, Pallas kernels for 10%

profile of v12, /device:TPU:0, one launch (start us, length us, event | category | flops | bytes accessed | tf_op | source)
XLA Modules:
  0.0 41.3 jit_solution(8851380966643820555)
XLA Ops:
  0.6 0.6 %collective-permute-start.1 = (bf16[128,1024]{1,0:T(8,128)(2,1)}, bf16[128,1024]{1,0:T(8,128)(2,1)S(1)}, u32[]{:S(2)}, u32[]{:S(2)}) collective-permute-start(bf16[128,1024]{1,0:T(8,128)(2,1)} %bitcast.11), channel_id=1, source_target_pairs={{0,16},{16,0},{1,17},{17,1},{2,18},{18,2},{3,19},{19,3},{4,20},{20... | collective-permute-start | bytes 786440 | tf_op jit(solution)/shard_map/ppermute | solution.py:41
  1.3 0.5 %collective-permute-start.2 = (bf16[1,1024]{1,0:T(2,128)(2,1)}, bf16[1,1024]{1,0:T(2,128)(2,1)S(1)}, u32[]{:S(2)}, u32[]{:S(2)}) collective-permute-start(bf16[1,1024]{1,0:T(2,128)(2,1)} %gain_ref.5), channel_id=1, source_target_pairs={{0,16},{16,0},{1,17},{17,1},{2,18},{18,2},{3,19},{19,3},{4,20},{20... | collective-permute-start | bytes 6152 | tf_op jit(solution)/shard_map/ppermute | solution.py:41
  1.8 0.4 %copy-done = bf16[2,128,1024]{2,1,0:T(8,128)(2,1)S(1)} copy-done((bf16[2,128,1024]{2,1,0:T(8,128)(2,1)S(1)}, bf16[2,128,1024]{2,1,0:T(8,128)(2,1)}, u32[]{:S(2)}) %copy-start) | copy-done | bytes 524312
  2.5 0.5 %shard_map.95 = (bf16[656,128]{1,0:T(8,128)(2,1)S(1)}, bf16[128,1024]{1,0:T(8,128)(2,1)S(1)}) custom-call(bf16[256,1024]{1,0:T(8,128)(2,1)S(1)} %bitcast.7, bf16[1024,128]{1,0:T(8,128)(2,1)S(1)} %bitcast.16, bf16[128,1024]{1,0:T(8,128)(2,1)S(1)} %bitcast.12, bf16[1024,128]{1,0:T(8,128)(2,1)S(1)} %copy-done.3, bf16[1,1024]{1,0:T(2,128)(2,1)S(1)} %copy-done.4, ...), custom_call_target="tpu_custom_call" | custom-call | flops 167772160 | bytes 1316864 | tf_op jit(solution)/shard_map/pallas_call | solution.py:51
  3.1 0.5 %shard_map.96 = (bf16[528,128]{1,0:T(8,128)(2,1)S(1)}, bf16[512,128]{1,0:T(8,128)(2,1)S(1)}) custom-call(bf16[256,1024]{1,0:T(8,128)(2,1)S(1)} %bitcast.8, bf16[128,1024]{1,0:T(8,128)(2,1)S(1)} %bitcast.13, bf16[656,128]{1,0:T(8,128)(2,1)S(1)} %get-tuple-element.24.own_ref, bf16[1024,128]{1,0:T(8,128)(2,1)S(1)} %collective-permute-done.down2_ref, ...), custom_call_target="tpu_custom_call" | custom-call | flops 100663296 | bytes 1480704 | tf_op jit(solution)/shard_map/pallas_call | solution.py:51
  3.6 2.8 %collective-permute-start.3 = (bf16[528,128]{1,0:T(8,128)(2,1)S(1)}, bf16[528,128]{1,0:T(8,128)(2,1)S(1)}, u32[]{:S(2)}, u32[]{:S(2)}) collective-permute-start(bf16[528,128]{1,0:T(8,128)(2,1)S(1)} %get-tuple-element.25.refs_0_), channel_id=1, source_target_pairs={{0,1},{1,0},{2,3},{3,2},{4,5},{5,4},{6,7},{7,6},{8,9},{9,8},{10,11... | collective-permute-start | bytes 405512 | tf_op jit(solution)/shard_map/ppermute | solution.py:41
  6.4 1.5 %collective-permute-start.5 = (bf16[512,128]{1,0:T(8,128)(2,1)S(1)}, bf16[512,128]{1,0:T(8,128)(2,1)S(1)}, u32[]{:S(2)}, u32[]{:S(2)}) collective-permute-start(bf16[512,128]{1,0:T(8,128)(2,1)S(1)} %get-tuple-element.26.refs_0_), channel_id=1, source_target_pairs={{0,2},{1,3},{2,0},{3,1},{4,6},{5,7},{6,4},{7,5},{8,10},{9,11},{10,... | collective-permute-start | bytes 393224 | tf_op jit(solution)/shard_map/ppermute | solution.py:41
  7.9 2.5 %collective-permute-done.3.refs_1_ = bf16[528,128]{1,0:T(8,128)(2,1)S(1)} collective-permute-done((bf16[528,128]{1,0:T(8,128)(2,1)S(1)}, bf16[528,128]{1,0:T(8,128)(2,1)S(1)}, u32[]{:S(2)}, u32[]{:S(2)}) %collective-permute-start.3) | collective-permute-done | bytes 135200 | tf_op jit(solution)/shard_map/ppermute | solution.py:41
  10.4 1.8 %collective-permute-start.4 = (bf16[528,128]{1,0:T(8,128)(2,1)S(1)}, bf16[528,128]{1,0:T(8,128)(2,1)S(1)}, u32[]{:S(2)}, u32[]{:S(2)}) collective-permute-start(bf16[528,128]{1,0:T(8,128)(2,1)S(1)} %shard_map.97.refs_0_), channel_id=1, source_target_pairs={{0,2},{1,3},{2,0},{3,1},{4,6},{5,7},{6,4},{7,5},{8,10},{9,11},{10,... | collective-permute-start | bytes 405512 | tf_op jit(solution)/shard_map/ppermute | solution.py:41
  12.3 2.6 %collective-permute-start.12 = (bf16[128,1024]{1,0:T(8,128)(2,1)S(1)}, bf16[128,1024]{1,0:T(8,128)(2,1)S(1)}, u32[]{:S(2)}, u32[]{:S(2)}) collective-permute-start(bf16[128,1024]{1,0:T(8,128)(2,1)S(1)} %get-tuple-element.41), channel_id=1, source_target_pairs={{0,8},{4,12},{8,0},{12,4},{1,9},{5,13},{9,1},{13,5},{2,10},{6,14},... | collective-permute-start | bytes 786440 | tf_op jit(solution)/shard_map/ppermute | solution.py:41
  14.9 1.6 %collective-permute-start.6 = (bf16[512,128]{1,0:T(8,128)(2,1)S(1)}, bf16[512,128]{1,0:T(8,128)(2,1)S(1)}, u32[]{:S(2)}, u32[]{:S(2)}) collective-permute-start(bf16[512,128]{1,0:T(8,128)(2,1)S(1)} %shard_map.98.refs_2_), channel_id=1, source_target_pairs={{0,1},{1,0},{2,3},{3,2},{4,5},{5,4},{6,7},{7,6},{8,9},{9,8},{10,11... | collective-permute-start | bytes 393224 | tf_op jit(solution)/shard_map/ppermute | solution.py:41
  16.6 3.4 %collective-permute-done.6.refs_3_ = bf16[512,128]{1,0:T(8,128)(2,1)S(1)} collective-permute-done((bf16[512,128]{1,0:T(8,128)(2,1)S(1)}, bf16[512,128]{1,0:T(8,128)(2,1)S(1)}, u32[]{:S(2)}, u32[]{:S(2)}) %collective-permute-start.6) | collective-permute-done | bytes 131104 | tf_op jit(solution)/shard_map/ppermute | solution.py:41
  19.9 1.1 %shard_map.100 = (bf16[768,128]{1,0:T(8,128)(2,1)S(1)}, bf16[768,128]{1,0:T(8,128)(2,1)S(1)}) custom-call(bf16[528,128]{1,0:T(8,128)(2,1)S(1)} %shard_map.97.refs_0_, bf16[528,128]{1,0:T(8,128)(2,1)S(1)} %collective-permute-done.4.refs_1_, bf16[512,128]{1,0:T(8,128)(2,1)S(1)} %shard_map.98.refs_2_, bf16[512,128]{1,0:T(8,128)(2,1)S(1)} %collective-permute-done.6.refs_3_, ...), custom_call_target="tpu_custom_call" | custom-call | flops 67108864 | bytes 731136 | tf_op jit(solution)/shard_map/pallas_call | solution.py:51
  21.1 5.0 %collective-permute-done.12.sent_ref = bf16[128,1024]{1,0:T(8,128)(2,1)S(1)} collective-permute-done((bf16[128,1024]{1,0:T(8,128)(2,1)S(1)}, bf16[128,1024]{1,0:T(8,128)(2,1)S(1)}, u32[]{:S(2)}, u32[]{:S(2)}) %collective-permute-start.12) | collective-permute-done | bytes 262176 | tf_op jit(solution)/shard_map/ppermute | solution.py:41
  26.1 0.4 shard_map.102
  26.5 0.4 %shard_map.101 = (f32[512,128]{1,0:T(8,128)S(1)}, f32[224,1024]{1,0:T(8,128)S(1)}, bf16[256,128]{1,0:T(8,128)(2,1)S(1)}) custom-call(bf16[768,128]{1,0:T(8,128)(2,1)S(1)} %get-tuple-element.27.made_ref, bf16[256,1024]{1,0:T(8,128)(2,1)S(1)} %bitcast.10), custom_call_target="tpu_custom_call" | custom-call | flops 134217728 | bytes 720896 | tf_op jit(solution)/shard_map/pallas_call | solution.py:51
  26.9 1.0 %shard_map.103 = (bf16[272,128]{1,0:T(8,128)(2,1)S(1)}, bf16[128,1024]{1,0:T(8,128)(2,1)S(1)}, bf16[128,640]{1,0:T(8,128)(2,1)S(1)}, bf16[16,128]{1,0:T(8,128)(2,1)S(1)}, bf16[1024,128]{1,0:T(8,128)(2,1)}) custom-call(bf16[768,128]{1,0:T(8,128)(2,1)S(1)} %collective-permute-done.8.made_ref, f32[512,128]{1,0:T(8,128)S(1)} %get-tuple-element.30.mix_ref, ...), custom_call_target="tpu_custom_call" | custom-call | flops 268435456 | bytes 3017728 | tf_op jit(solution)/shard_map/pallas_call | solution.py:51
  27.9 0.4 shard_map.104
  28.3 3.6 %collective-permute-start.10 = (bf16[528,128]{1,0:T(8,128)(2,1)S(1)}, bf16[528,128]{1,0:T(8,128)(2,1)S(1)}, u32[]{:S(2)}, u32[]{:S(2)}) collective-permute-start(bf16[528,128]{1,0:T(8,128)(2,1)S(1)} %get-tuple-element.39), channel_id=1, source_target_pairs={{0,12},{4,8},{8,4},{12,0},{1,13},{5,9},{9,5},{13,1},{2,14},{6,10},... | collective-permute-start | bytes 405512 | tf_op jit(solution)/shard_map/ppermute | solution.py:41
  31.9 0.9 %collective-permute-start.11 = (bf16[272,128]{1,0:T(8,128)(2,1)S(1)}, bf16[272,128]{1,0:T(8,128)(2,1)S(1)}, u32[]{:S(2)}, u32[]{:S(2)}) collective-permute-start(bf16[272,128]{1,0:T(8,128)(2,1)S(1)} %get-tuple-element.40), channel_id=1, source_target_pairs={{0,8},{4,12},{8,0},{12,4},{1,9},{5,13},{9,1},{13,5},{2,10},{6,14},... | collective-permute-start | bytes 208904 | tf_op jit(solution)/shard_map/ppermute | solution.py:41
  32.7 7.0 %collective-permute-done.11.far_ref.refs_3_ = bf16[272,128]{1,0:T(8,128)(2,1)S(1)} collective-permute-done((bf16[272,128]{1,0:T(8,128)(2,1)S(1)}, bf16[272,128]{1,0:T(8,128)(2,1)S(1)}, u32[]{:S(2)}, u32[]{:S(2)}) %collective-permute-start.11) | collective-permute-done | bytes 69664 | tf_op jit(solution)/shard_map/ppermute | solution.py:41
  39.7 0.4 shard_map.105.refs_4_
  40.1 0.4 collective-permute-done.9.refs_1_
  40.5 0.8 %shard_map.106 = (f32[32,1024]{1,0:T(8,128)}, f32[32,1024]{1,0:T(8,128)}, f32[1,1024]{1,0:T(1,128)}) custom-call(bf16[528,128]{1,0:T(8,128)(2,1)S(1)} %get-tuple-element.37.refs_0_, bf16[528,128]{1,0:T(8,128)(2,1)S(1)} %collective-permute-done.9.refs_1_, bf16[528,128]{1,0:T(8,128)(2,1)S(1)} %collective-permute-done.10.refs_2_, ...), custom_call_target="tpu_custom_call" | custom-call | flops 33554432 | bytes 737280 | tf_op jit(solution)/shard_map/pallas_call | solution.py:51
  (31 shorter events, 0.7 us)
Async XLA Ops:
  0.6 2.4 %collective-permute-start.1 = (bf16[128,1024]{1,0:T(8,128)(2,1)}, bf16[128,1024]{1,0:T(8,128)(2,1)S(1)}, u32[]{:S(2)}, u32[]{:S(2)}) collective-permute-start(bf16[128,1024]{1,0:T(8,128)(2,1)} %bitcast.11), channel_id=1, source_target_pairs={{0,16},{16,0},{1,17},{17,1},{2,18},{18,2},{3,19},{19,3},{4,20},{20... | collective-permute-start | bytes 786440 | tf_op jit(solution)/shard_map/ppermute | solution.py:41
  1.2 1.0 %copy-start = (bf16[2,128,1024]{2,1,0:T(8,128)(2,1)S(1)}, bf16[2,128,1024]{2,1,0:T(8,128)(2,1)}, u32[]{:S(2)}) copy-start(bf16[2,128,1024]{2,1,0:T(8,128)(2,1)} %param.7) | copy-start | bytes 1572868
  1.2 1.1 %copy-start.1 = (bf16[1,128,1024]{2,1,0:T(8,128)(2,1)S(1)}, bf16[1,128,1024]{2,1,0:T(8,128)(2,1)}, u32[]{:S(2)}) copy-start(bf16[1,128,1024]{2,1,0:T(8,128)(2,1)} %param.9) | copy-start | bytes 786436
  1.2 1.2 %copy-start.2 = (bf16[1,1024,128]{2,1,0:T(8,128)(2,1)S(1)}, bf16[1,1024,128]{2,1,0:T(8,128)(2,1)}, u32[]{:S(2)}) copy-start(bf16[1,1024,128]{2,1,0:T(8,128)(2,1)} %param.8) | copy-start | bytes 786436
  1.2 1.3 %copy-start.3 = (bf16[1024,128]{1,0:T(8,128)(2,1)S(1)}, bf16[1024,128]{1,0:T(8,128)(2,1)}, u32[]{:S(2)}) copy-start(bf16[1024,128]{1,0:T(8,128)(2,1)} %head_ref.3) | copy-start | bytes 786436
  1.2 1.3 %copy-start.4 = (bf16[1,1024]{1,0:T(2,128)(2,1)S(1)}, bf16[1,1024]{1,0:T(2,128)(2,1)}, u32[]{:S(2)}) copy-start(bf16[1,1024]{1,0:T(2,128)(2,1)} %gain_ref.5) | copy-start | bytes 6148
  1.2 1.8 %collective-permute-start = (bf16[1024,128]{1,0:T(8,128)(2,1)}, bf16[1024,128]{1,0:T(8,128)(2,1)S(1)}, u32[]{:S(2)}, u32[]{:S(2)}) collective-permute-start(bf16[1024,128]{1,0:T(8,128)(2,1)} %bitcast.15), channel_id=1, source_target_pairs={{0,16},{16,0},{1,17},{17,1},{2,18},{18,2},{3,19},{19,3},{4,20},{20... | collective-permute-start | bytes 786440 | tf_op jit(solution)/shard_map/ppermute | solution.py:41
  1.3 1.7 %collective-permute-start.2 = (bf16[1,1024]{1,0:T(2,128)(2,1)}, bf16[1,1024]{1,0:T(2,128)(2,1)S(1)}, u32[]{:S(2)}, u32[]{:S(2)}) collective-permute-start(bf16[1,1024]{1,0:T(2,128)(2,1)} %gain_ref.5), channel_id=1, source_target_pairs={{0,16},{16,0},{1,17},{17,1},{2,18},{18,2},{3,19},{19,3},{4,20},{20... | collective-permute-start | bytes 6152 | tf_op jit(solution)/shard_map/ppermute | solution.py:41
  3.0 16.9 %copy-start.5 = (s32[2,128]{1,0:T(2,128)S(1)}, s32[2,128]{1,0:T(2,128)}, u32[]{:S(2)}) copy-start(s32[2,128]{1,0:T(2,128)} %valid_ref.1) | copy-start | bytes 3076
  3.0 16.9 %copy-start.6 = (s32[2,128]{1,0:T(2,128)S(1)}, s32[2,128]{1,0:T(2,128)}, u32[]{:S(2)}) copy-start(s32[2,128]{1,0:T(2,128)} %refs_6_.1) | copy-start | bytes 3076
  3.6 6.8 %collective-permute-start.3 = (bf16[528,128]{1,0:T(8,128)(2,1)S(1)}, bf16[528,128]{1,0:T(8,128)(2,1)S(1)}, u32[]{:S(2)}, u32[]{:S(2)}) collective-permute-start(bf16[528,128]{1,0:T(8,128)(2,1)S(1)} %get-tuple-element.25.refs_0_), channel_id=1, source_target_pairs={{0,1},{1,0},{2,3},{3,2},{4,5},{5,4},{6,7},{7,6},{8,9},{9,8},{10,11... | collective-permute-start | bytes 405512 | tf_op jit(solution)/shard_map/ppermute | solution.py:41
  6.4 8.5 %collective-permute-start.5 = (bf16[512,128]{1,0:T(8,128)(2,1)S(1)}, bf16[512,128]{1,0:T(8,128)(2,1)S(1)}, u32[]{:S(2)}, u32[]{:S(2)}) collective-permute-start(bf16[512,128]{1,0:T(8,128)(2,1)S(1)} %get-tuple-element.26.refs_0_), channel_id=1, source_target_pairs={{0,2},{1,3},{2,0},{3,1},{4,6},{5,7},{6,4},{7,5},{8,10},{9,11},{10,... | collective-permute-start | bytes 393224 | tf_op jit(solution)/shard_map/ppermute | solution.py:41
  10.4 6.0 %collective-permute-start.4 = (bf16[528,128]{1,0:T(8,128)(2,1)S(1)}, bf16[528,128]{1,0:T(8,128)(2,1)S(1)}, u32[]{:S(2)}, u32[]{:S(2)}) collective-permute-start(bf16[528,128]{1,0:T(8,128)(2,1)S(1)} %shard_map.97.refs_0_), channel_id=1, source_target_pairs={{0,2},{1,3},{2,0},{3,1},{4,6},{5,7},{6,4},{7,5},{8,10},{9,11},{10,... | collective-permute-start | bytes 405512 | tf_op jit(solution)/shard_map/ppermute | solution.py:41
  12.3 13.8 %collective-permute-start.12 = (bf16[128,1024]{1,0:T(8,128)(2,1)S(1)}, bf16[128,1024]{1,0:T(8,128)(2,1)S(1)}, u32[]{:S(2)}, u32[]{:S(2)}) collective-permute-start(bf16[128,1024]{1,0:T(8,128)(2,1)S(1)} %get-tuple-element.41), channel_id=1, source_target_pairs={{0,8},{4,12},{8,0},{12,4},{1,9},{5,13},{9,1},{13,5},{2,10},{6,14},... | collective-permute-start | bytes 786440 | tf_op jit(solution)/shard_map/ppermute | solution.py:41
  14.9 5.0 %collective-permute-start.6 = (bf16[512,128]{1,0:T(8,128)(2,1)S(1)}, bf16[512,128]{1,0:T(8,128)(2,1)S(1)}, u32[]{:S(2)}, u32[]{:S(2)}) collective-permute-start(bf16[512,128]{1,0:T(8,128)(2,1)S(1)} %shard_map.98.refs_2_), channel_id=1, source_target_pairs={{0,1},{1,0},{2,3},{3,2},{4,5},{5,4},{6,7},{7,6},{8,9},{9,8},{10,11... | collective-permute-start | bytes 393224 | tf_op jit(solution)/shard_map/ppermute | solution.py:41
  16.5 3.4 %collective-permute-start.7 = (bf16[384,128]{1,0:T(8,128)(2,1)S(1)}, bf16[384,128]{1,0:T(8,128)(2,1)S(1)}, u32[]{:S(2)}, u32[]{:S(2)}) collective-permute-start(bf16[384,128]{1,0:T(8,128)(2,1)S(1)} %shard_map.99.refs_4_), channel_id=1, source_target_pairs={{0,16},{16,0},{1,17},{17,1},{2,18},{18,2},{3,19},{19,3},{4,20},{20... | collective-permute-start | bytes 294920 | tf_op jit(solution)/shard_map/ppermute | solution.py:41
  21.0 5.9 %collective-permute-start.8 = (bf16[768,128]{1,0:T(8,128)(2,1)S(1)}, bf16[768,128]{1,0:T(8,128)(2,1)S(1)}, u32[]{:S(2)}, u32[]{:S(2)}) collective-permute-start(bf16[768,128]{1,0:T(8,128)(2,1)S(1)} %get-tuple-element.29), channel_id=1, source_target_pairs={{0,16},{16,0},{1,17},{17,1},{2,18},{18,2},{3,19},{19,3},{4,20},{20... | collective-permute-start | bytes 589832 | tf_op jit(solution)/shard_map/ppermute | solution.py:41
  26.1 6.6 %collective-permute-start.13 = (bf16[128,1024]{1,0:T(8,128)(2,1)S(1)}, bf16[128,1024]{1,0:T(8,128)(2,1)S(1)}, u32[]{:S(2)}, u32[]{:S(2)}) collective-permute-start(bf16[128,1024]{1,0:T(8,128)(2,1)S(1)} %collective-permute-done.12.sent_ref), channel_id=1, source_target_pairs={{0,16},{16,0},{1,17},{17,1},{2,18},{18,2},{3,19},{19,3},{4,20},{20... | collective-permute-start | bytes 786440 | tf_op jit(solution)/shard_map/ppermute | solution.py:41
  28.3 11.9 %collective-permute-start.10 = (bf16[528,128]{1,0:T(8,128)(2,1)S(1)}, bf16[528,128]{1,0:T(8,128)(2,1)S(1)}, u32[]{:S(2)}, u32[]{:S(2)}) collective-permute-start(bf16[528,128]{1,0:T(8,128)(2,1)S(1)} %get-tuple-element.39), channel_id=1, source_target_pairs={{0,12},{4,8},{8,4},{12,0},{1,13},{5,9},{9,5},{13,1},{2,14},{6,10},... | collective-permute-start | bytes 405512 | tf_op jit(solution)/shard_map/ppermute | solution.py:41
  31.9 8.6 %collective-permute-start.9 = (bf16[528,128]{1,0:T(8,128)(2,1)S(1)}, bf16[528,128]{1,0:T(8,128)(2,1)S(1)}, u32[]{:S(2)}, u32[]{:S(2)}) collective-permute-start(bf16[528,128]{1,0:T(8,128)(2,1)S(1)} %get-tuple-element.38), channel_id=1, source_target_pairs={{0,4},{4,0},{8,12},{12,8},{1,5},{5,1},{9,13},{13,9},{2,6},{6,2},{1... | collective-permute-start | bytes 405512 | tf_op jit(solution)/shard_map/ppermute | solution.py:41
  31.9 7.9 %collective-permute-start.11 = (bf16[272,128]{1,0:T(8,128)(2,1)S(1)}, bf16[272,128]{1,0:T(8,128)(2,1)S(1)}, u32[]{:S(2)}, u32[]{:S(2)}) collective-permute-start(bf16[272,128]{1,0:T(8,128)(2,1)S(1)} %get-tuple-element.40), channel_id=1, source_target_pairs={{0,8},{4,12},{8,0},{12,4},{1,9},{5,13},{9,1},{13,5},{2,10},{6,14},... | collective-permute-start | bytes 208904 | tf_op jit(solution)/shard_map/ppermute | solution.py:41

commit v13 on v12

--- a/solution.py
+++ b/solution.py
@@ -158,6 +158,7 @@
     cross0 = total(b_refs, 2 * half, half)
     one_b0 = cross0 + dot(hidden0, b0b0)
     squares1 = squares0 + jnp.sum(hid0 * (cross0 + one_b0), axis=1, keepdims=True)
+    squares1 = jnp.maximum(squares1, 0.0)
     inv1 = lax.rsqrt(squares1 / width + epsilon)
     pre1 = inv1 * proj1
     sig1 = jax.nn.sigmoid(pre1)
@@ -167,6 +168,7 @@
     two_b0 = one_b0 + dot(hidden1, b1b0)
     two_b1 = one_b1 + dot(hidden1, b1b1)
     squares2 = squares1 + jnp.sum(hid1 * (one_b1 + two_b1), axis=1, keepdims=True)
+    squares2 = jnp.maximum(squares2, 0.0)
     inv2 = lax.rsqrt(squares2 / width + epsilon)
     base = total(a_refs, 3 * rank, half) + dot(hidden0, b0h) + dot(hidden1, b1h)
     logits = inv2 * base
@@ -249,11 +251,10 @@
     grad_ref[...] = (grad * gain_ref[...].astype(F32)).astype(BF16)
     for i, value in enumerate((*mixes[:3], jnp.where(first, mixes[3], none), scaled_t)):
         wide_ref[:, i * rank : (i + 1) * rank] = value
-    count = jnp.sum(valid_ref[...].astype(F32), keepdims=True)
-    tail = jnp.concatenate(
-        [gain[:, i * rank : (i + 1) * rank] for i in range(lines)] + [jnp.broadcast_to(count, (PACK - lines, rank))],
-        axis=0,
-    ).astype(BF16)
+    count = jnp.broadcast_to(jnp.sum(valid_ref[...].astype(F32), keepdims=True), (PACK - lines, rank))
+    high = count.astype(BF16).astype(F32)
+    count = jnp.where(lax.broadcasted_iota(jnp.int32, count.shape, 0) == 0, high, count - high)
+    tail = jnp.concatenate([gain[:, i * rank : (i + 1) * rank] for i in range(lines)] + [count], axis=0).astype(BF16)
     tail_ref[...] = tail
     target = partner(lax.axis_index("dp"), far, replicas)
     for i in range(8):
@@ -303,7 +304,7 @@
         return sum(p[start : start + size, :].astype(F32) for p in near)
 
     tail = sum(p[-PACK:, :].astype(F32) for p in (*near, far_ref))
-    scale = 1.0 / tail[lines : lines + 1, :1]
+    scale = 1.0 / (tail[lines : lines + 1, :1] + tail[lines + 1 : lines + 2, :1])
     for i in range(lines):
         lanes = slice(i * rank, (i + 1) * rank)
         down_out[:, lanes] = (total(i * 2 * slim, slim) + moved_ref[:slim, lanes]) * scale
@@ -318,7 +319,8 @@
     rank = adapter_down.shape[2]
     states = inputs.reshape(-1, features)
     half = states.shape[0] // sections
-    assert sections == 2 and half == rank and head.shape[1] == rank and features % rank == 0
+    assert sections == 2 and half == rank and head.shape[1] == rank
+    assert features % rank == 0 and features // rank < PACK - 1
     slim = rank // replicas
     lines = features // rank
     down, up = adapter_down[0], adapter_up[0]

time: 41.4 us -> 41.4 us (level)
  no operation moved by 1% of the time
where the time goes in v13:
time: 41.4 us; the launch traced here: 41.3 us
  waiting for transfers between devices  18.3 us (44%)
  starting transfers between devices  16.1 us (39%)
  Pallas kernels  5.49 us (13%)
  between operations  0.74 us (2%)
  local copies, waits for them, and re-layouts  0.68 us (2%)
    ppermute x14, waiting for transfers between devices, from_partner(): lax.ppermute(value, axis, [(i, partner(i, step, size)) for i in range(siz...  18.3 us
    ppermute x14, starting transfers between devices, from_partner(): lax.ppermute(value, axis, [(i, partner(i, step, size)) for i in range(siz...  16.1 us
    pallas_call x13, Pallas kernels, call(): pl.pallas_call(kernel, out_shape=out, cost_estimate=pl.CostEstimate(flops...  5.49 us
  transfers between devices with their start and end apart: 14, of which 6 were waited for; matrix products, arithmetic and copies ran while one was open for 0% of the time, Pallas kernels for 10%

profile of v13, /device:TPU:0, one launch (start us, length us, event | category | flops | bytes accessed | tf_op | source)
XLA Modules:
  0.0 41.3 jit_solution(11122749333589118694)
XLA Ops:
  0.6 0.6 %collective-permute-start.1 = (bf16[128,1024]{1,0:T(8,128)(2,1)}, bf16[128,1024]{1,0:T(8,128)(2,1)S(1)}, u32[]{:S(2)}, u32[]{:S(2)}) collective-permute-start(bf16[128,1024]{1,0:T(8,128)(2,1)} %bitcast.11), channel_id=1, source_target_pairs={{0,16},{16,0},{1,17},{17,1},{2,18},{18,2},{3,19},{19,3},{4,20},{20... | collective-permute-start | bytes 786440 | tf_op jit(solution)/shard_map/ppermute | solution.py:41
  1.3 0.5 %collective-permute-start.2 = (bf16[1,1024]{1,0:T(2,128)(2,1)}, bf16[1,1024]{1,0:T(2,128)(2,1)S(1)}, u32[]{:S(2)}, u32[]{:S(2)}) collective-permute-start(bf16[1,1024]{1,0:T(2,128)(2,1)} %gain_ref.5), channel_id=1, source_target_pairs={{0,16},{16,0},{1,17},{17,1},{2,18},{18,2},{3,19},{19,3},{4,20},{20... | collective-permute-start | bytes 6152 | tf_op jit(solution)/shard_map/ppermute | solution.py:41
  1.8 0.4 %copy-done = bf16[2,128,1024]{2,1,0:T(8,128)(2,1)S(1)} copy-done((bf16[2,128,1024]{2,1,0:T(8,128)(2,1)S(1)}, bf16[2,128,1024]{2,1,0:T(8,128)(2,1)}, u32[]{:S(2)}) %copy-start) | copy-done | bytes 524312
  2.5 0.5 %shard_map.95 = (bf16[656,128]{1,0:T(8,128)(2,1)S(1)}, bf16[128,1024]{1,0:T(8,128)(2,1)S(1)}) custom-call(bf16[256,1024]{1,0:T(8,128)(2,1)S(1)} %bitcast.7, bf16[1024,128]{1,0:T(8,128)(2,1)S(1)} %bitcast.16, bf16[128,1024]{1,0:T(8,128)(2,1)S(1)} %bitcast.12, bf16[1024,128]{1,0:T(8,128)(2,1)S(1)} %copy-done.3, bf16[1,1024]{1,0:T(2,128)(2,1)S(1)} %copy-done.4, ...), custom_call_target="tpu_custom_call" | custom-call | flops 167772160 | bytes 1316864 | tf_op jit(solution)/shard_map/pallas_call | solution.py:51
  3.1 0.5 %shard_map.96 = (bf16[528,128]{1,0:T(8,128)(2,1)S(1)}, bf16[512,128]{1,0:T(8,128)(2,1)S(1)}) custom-call(bf16[256,1024]{1,0:T(8,128)(2,1)S(1)} %bitcast.8, bf16[128,1024]{1,0:T(8,128)(2,1)S(1)} %bitcast.13, bf16[656,128]{1,0:T(8,128)(2,1)S(1)} %get-tuple-element.24.own_ref, bf16[1024,128]{1,0:T(8,128)(2,1)S(1)} %collective-permute-done.down2_ref, ...), custom_call_target="tpu_custom_call" | custom-call | flops 100663296 | bytes 1480704 | tf_op jit(solution)/shard_map/pallas_call | solution.py:51
  3.6 2.8 %collective-permute-start.3 = (bf16[528,128]{1,0:T(8,128)(2,1)S(1)}, bf16[528,128]{1,0:T(8,128)(2,1)S(1)}, u32[]{:S(2)}, u32[]{:S(2)}) collective-permute-start(bf16[528,128]{1,0:T(8,128)(2,1)S(1)} %get-tuple-element.25.refs_0_), channel_id=1, source_target_pairs={{0,1},{1,0},{2,3},{3,2},{4,5},{5,4},{6,7},{7,6},{8,9},{9,8},{10,11... | collective-permute-start | bytes 405512 | tf_op jit(solution)/shard_map/ppermute | solution.py:41
  6.4 1.5 %collective-permute-start.5 = (bf16[512,128]{1,0:T(8,128)(2,1)S(1)}, bf16[512,128]{1,0:T(8,128)(2,1)S(1)}, u32[]{:S(2)}, u32[]{:S(2)}) collective-permute-start(bf16[512,128]{1,0:T(8,128)(2,1)S(1)} %get-tuple-element.26.refs_0_), channel_id=1, source_target_pairs={{0,2},{1,3},{2,0},{3,1},{4,6},{5,7},{6,4},{7,5},{8,10},{9,11},{10,... | collective-permute-start | bytes 393224 | tf_op jit(solution)/shard_map/ppermute | solution.py:41
  7.9 2.5 %collective-permute-done.3.refs_1_ = bf16[528,128]{1,0:T(8,128)(2,1)S(1)} collective-permute-done((bf16[528,128]{1,0:T(8,128)(2,1)S(1)}, bf16[528,128]{1,0:T(8,128)(2,1)S(1)}, u32[]{:S(2)}, u32[]{:S(2)}) %collective-permute-start.3) | collective-permute-done | bytes 135200 | tf_op jit(solution)/shard_map/ppermute | solution.py:41
  10.4 1.8 %collective-permute-start.4 = (bf16[528,128]{1,0:T(8,128)(2,1)S(1)}, bf16[528,128]{1,0:T(8,128)(2,1)S(1)}, u32[]{:S(2)}, u32[]{:S(2)}) collective-permute-start(bf16[528,128]{1,0:T(8,128)(2,1)S(1)} %shard_map.97.refs_0_), channel_id=1, source_target_pairs={{0,2},{1,3},{2,0},{3,1},{4,6},{5,7},{6,4},{7,5},{8,10},{9,11},{10,... | collective-permute-start | bytes 405512 | tf_op jit(solution)/shard_map/ppermute | solution.py:41
  12.3 2.6 %collective-permute-start.12 = (bf16[128,1024]{1,0:T(8,128)(2,1)S(1)}, bf16[128,1024]{1,0:T(8,128)(2,1)S(1)}, u32[]{:S(2)}, u32[]{:S(2)}) collective-permute-start(bf16[128,1024]{1,0:T(8,128)(2,1)S(1)} %get-tuple-element.41), channel_id=1, source_target_pairs={{0,8},{4,12},{8,0},{12,4},{1,9},{5,13},{9,1},{13,5},{2,10},{6,14},... | collective-permute-start | bytes 786440 | tf_op jit(solution)/shard_map/ppermute | solution.py:41
  14.9 1.6 %collective-permute-start.6 = (bf16[512,128]{1,0:T(8,128)(2,1)S(1)}, bf16[512,128]{1,0:T(8,128)(2,1)S(1)}, u32[]{:S(2)}, u32[]{:S(2)}) collective-permute-start(bf16[512,128]{1,0:T(8,128)(2,1)S(1)} %shard_map.98.refs_2_), channel_id=1, source_target_pairs={{0,1},{1,0},{2,3},{3,2},{4,5},{5,4},{6,7},{7,6},{8,9},{9,8},{10,11... | collective-permute-start | bytes 393224 | tf_op jit(solution)/shard_map/ppermute | solution.py:41
  16.6 3.4 %collective-permute-done.6.refs_3_ = bf16[512,128]{1,0:T(8,128)(2,1)S(1)} collective-permute-done((bf16[512,128]{1,0:T(8,128)(2,1)S(1)}, bf16[512,128]{1,0:T(8,128)(2,1)S(1)}, u32[]{:S(2)}, u32[]{:S(2)}) %collective-permute-start.6) | collective-permute-done | bytes 131104 | tf_op jit(solution)/shard_map/ppermute | solution.py:41
  19.9 1.1 %shard_map.100 = (bf16[768,128]{1,0:T(8,128)(2,1)S(1)}, bf16[768,128]{1,0:T(8,128)(2,1)S(1)}) custom-call(bf16[528,128]{1,0:T(8,128)(2,1)S(1)} %shard_map.97.refs_0_, bf16[528,128]{1,0:T(8,128)(2,1)S(1)} %collective-permute-done.4.refs_1_, bf16[512,128]{1,0:T(8,128)(2,1)S(1)} %shard_map.98.refs_2_, bf16[512,128]{1,0:T(8,128)(2,1)S(1)} %collective-permute-done.6.refs_3_, ...), custom_call_target="tpu_custom_call" | custom-call | flops 67108864 | bytes 731136 | tf_op jit(solution)/shard_map/pallas_call | solution.py:51
  21.1 5.0 %collective-permute-done.12.sent_ref = bf16[128,1024]{1,0:T(8,128)(2,1)S(1)} collective-permute-done((bf16[128,1024]{1,0:T(8,128)(2,1)S(1)}, bf16[128,1024]{1,0:T(8,128)(2,1)S(1)}, u32[]{:S(2)}, u32[]{:S(2)}) %collective-permute-start.12) | collective-permute-done | bytes 262176 | tf_op jit(solution)/shard_map/ppermute | solution.py:41
  26.1 0.4 shard_map.102
  26.5 0.4 %shard_map.101 = (f32[512,128]{1,0:T(8,128)S(1)}, f32[224,1024]{1,0:T(8,128)S(1)}, bf16[256,128]{1,0:T(8,128)(2,1)S(1)}) custom-call(bf16[768,128]{1,0:T(8,128)(2,1)S(1)} %get-tuple-element.27.made_ref, bf16[256,1024]{1,0:T(8,128)(2,1)S(1)} %bitcast.10), custom_call_target="tpu_custom_call" | custom-call | flops 134217728 | bytes 720896 | tf_op jit(solution)/shard_map/pallas_call | solution.py:51
  26.9 1.0 %shard_map.103 = (bf16[272,128]{1,0:T(8,128)(2,1)S(1)}, bf16[128,1024]{1,0:T(8,128)(2,1)S(1)}, bf16[128,640]{1,0:T(8,128)(2,1)S(1)}, bf16[16,128]{1,0:T(8,128)(2,1)S(1)}, bf16[1024,128]{1,0:T(8,128)(2,1)}) custom-call(bf16[768,128]{1,0:T(8,128)(2,1)S(1)} %collective-permute-done.8.made_ref, f32[512,128]{1,0:T(8,128)S(1)} %get-tuple-element.30.mix_ref, ...), custom_call_target="tpu_custom_call" | custom-call | flops 268435456 | bytes 3017728 | tf_op jit(solution)/shard_map/pallas_call | solution.py:51
  27.9 0.4 shard_map.104
  28.3 3.6 %collective-permute-start.10 = (bf16[528,128]{1,0:T(8,128)(2,1)S(1)}, bf16[528,128]{1,0:T(8,128)(2,1)S(1)}, u32[]{:S(2)}, u32[]{:S(2)}) collective-permute-start(bf16[528,128]{1,0:T(8,128)(2,1)S(1)} %get-tuple-element.39), channel_id=1, source_target_pairs={{0,12},{4,8},{8,4},{12,0},{1,13},{5,9},{9,5},{13,1},{2,14},{6,10},... | collective-permute-start | bytes 405512 | tf_op jit(solution)/shard_map/ppermute | solution.py:41
  31.9 0.9 %collective-permute-start.11 = (bf16[272,128]{1,0:T(8,128)(2,1)S(1)}, bf16[272,128]{1,0:T(8,128)(2,1)S(1)}, u32[]{:S(2)}, u32[]{:S(2)}) collective-permute-start(bf16[272,128]{1,0:T(8,128)(2,1)S(1)} %get-tuple-element.40), channel_id=1, source_target_pairs={{0,8},{4,12},{8,0},{12,4},{1,9},{5,13},{9,1},{13,5},{2,10},{6,14},... | collective-permute-start | bytes 208904 | tf_op jit(solution)/shard_map/ppermute | solution.py:41
  32.7 7.0 %collective-permute-done.11.far_ref.refs_3_ = bf16[272,128]{1,0:T(8,128)(2,1)S(1)} collective-permute-done((bf16[272,128]{1,0:T(8,128)(2,1)S(1)}, bf16[272,128]{1,0:T(8,128)(2,1)S(1)}, u32[]{:S(2)}, u32[]{:S(2)}) %collective-permute-start.11) | collective-permute-done | bytes 69664 | tf_op jit(solution)/shard_map/ppermute | solution.py:41
  39.7 0.4 shard_map.105.refs_4_
  40.1 0.4 collective-permute-done.9.refs_1_
  40.5 0.8 %shard_map.106 = (f32[32,1024]{1,0:T(8,128)}, f32[32,1024]{1,0:T(8,128)}, f32[1,1024]{1,0:T(1,128)}) custom-call(bf16[528,128]{1,0:T(8,128)(2,1)S(1)} %get-tuple-element.37.refs_0_, bf16[528,128]{1,0:T(8,128)(2,1)S(1)} %collective-permute-done.9.refs_1_, bf16[528,128]{1,0:T(8,128)(2,1)S(1)} %collective-permute-done.10.refs_2_, ...), custom_call_target="tpu_custom_call" | custom-call | flops 33554432 | bytes 737280 | tf_op jit(solution)/shard_map/pallas_call | solution.py:51
  (31 shorter events, 0.7 us)
Async XLA Ops:
  0.6 2.4 %collective-permute-start.1 = (bf16[128,1024]{1,0:T(8,128)(2,1)}, bf16[128,1024]{1,0:T(8,128)(2,1)S(1)}, u32[]{:S(2)}, u32[]{:S(2)}) collective-permute-start(bf16[128,1024]{1,0:T(8,128)(2,1)} %bitcast.11), channel_id=1, source_target_pairs={{0,16},{16,0},{1,17},{17,1},{2,18},{18,2},{3,19},{19,3},{4,20},{20... | collective-permute-start | bytes 786440 | tf_op jit(solution)/shard_map/ppermute | solution.py:41
  1.2 1.0 %copy-start = (bf16[2,128,1024]{2,1,0:T(8,128)(2,1)S(1)}, bf16[2,128,1024]{2,1,0:T(8,128)(2,1)}, u32[]{:S(2)}) copy-start(bf16[2,128,1024]{2,1,0:T(8,128)(2,1)} %param.7) | copy-start | bytes 1572868
  1.2 1.1 %copy-start.1 = (bf16[1,128,1024]{2,1,0:T(8,128)(2,1)S(1)}, bf16[1,128,1024]{2,1,0:T(8,128)(2,1)}, u32[]{:S(2)}) copy-start(bf16[1,128,1024]{2,1,0:T(8,128)(2,1)} %param.9) | copy-start | bytes 786436
  1.2 1.2 %copy-start.2 = (bf16[1,1024,128]{2,1,0:T(8,128)(2,1)S(1)}, bf16[1,1024,128]{2,1,0:T(8,128)(2,1)}, u32[]{:S(2)}) copy-start(bf16[1,1024,128]{2,1,0:T(8,128)(2,1)} %param.8) | copy-start | bytes 786436
  1.2 1.3 %copy-start.3 = (bf16[1024,128]{1,0:T(8,128)(2,1)S(1)}, bf16[1024,128]{1,0:T(8,128)(2,1)}, u32[]{:S(2)}) copy-start(bf16[1024,128]{1,0:T(8,128)(2,1)} %head_ref.3) | copy-start | bytes 786436
  1.2 1.3 %copy-start.4 = (bf16[1,1024]{1,0:T(2,128)(2,1)S(1)}, bf16[1,1024]{1,0:T(2,128)(2,1)}, u32[]{:S(2)}) copy-start(bf16[1,1024]{1,0:T(2,128)(2,1)} %gain_ref.5) | copy-start | bytes 6148
  1.2 1.8 %collective-permute-start = (bf16[1024,128]{1,0:T(8,128)(2,1)}, bf16[1024,128]{1,0:T(8,128)(2,1)S(1)}, u32[]{:S(2)}, u32[]{:S(2)}) collective-permute-start(bf16[1024,128]{1,0:T(8,128)(2,1)} %bitcast.15), channel_id=1, source_target_pairs={{0,16},{16,0},{1,17},{17,1},{2,18},{18,2},{3,19},{19,3},{4,20},{20... | collective-permute-start | bytes 786440 | tf_op jit(solution)/shard_map/ppermute | solution.py:41
  1.3 1.7 %collective-permute-start.2 = (bf16[1,1024]{1,0:T(2,128)(2,1)}, bf16[1,1024]{1,0:T(2,128)(2,1)S(1)}, u32[]{:S(2)}, u32[]{:S(2)}) collective-permute-start(bf16[1,1024]{1,0:T(2,128)(2,1)} %gain_ref.5), channel_id=1, source_target_pairs={{0,16},{16,0},{1,17},{17,1},{2,18},{18,2},{3,19},{19,3},{4,20},{20... | collective-permute-start | bytes 6152 | tf_op jit(solution)/shard_map/ppermute | solution.py:41
  3.0 16.9 %copy-start.5 = (s32[2,128]{1,0:T(2,128)S(1)}, s32[2,128]{1,0:T(2,128)}, u32[]{:S(2)}) copy-start(s32[2,128]{1,0:T(2,128)} %valid_ref.1) | copy-start | bytes 3076
  3.0 16.9 %copy-start.6 = (s32[2,128]{1,0:T(2,128)S(1)}, s32[2,128]{1,0:T(2,128)}, u32[]{:S(2)}) copy-start(s32[2,128]{1,0:T(2,128)} %refs_6_.1) | copy-start | bytes 3076
  3.6 6.8 %collective-permute-start.3 = (bf16[528,128]{1,0:T(8,128)(2,1)S(1)}, bf16[528,128]{1,0:T(8,128)(2,1)S(1)}, u32[]{:S(2)}, u32[]{:S(2)}) collective-permute-start(bf16[528,128]{1,0:T(8,128)(2,1)S(1)} %get-tuple-element.25.refs_0_), channel_id=1, source_target_pairs={{0,1},{1,0},{2,3},{3,2},{4,5},{5,4},{6,7},{7,6},{8,9},{9,8},{10,11... | collective-permute-start | bytes 405512 | tf_op jit(solution)/shard_map/ppermute | solution.py:41
  6.4 8.5 %collective-permute-start.5 = (bf16[512,128]{1,0:T(8,128)(2,1)S(1)}, bf16[512,128]{1,0:T(8,128)(2,1)S(1)}, u32[]{:S(2)}, u32[]{:S(2)}) collective-permute-start(bf16[512,128]{1,0:T(8,128)(2,1)S(1)} %get-tuple-element.26.refs_0_), channel_id=1, source_target_pairs={{0,2},{1,3},{2,0},{3,1},{4,6},{5,7},{6,4},{7,5},{8,10},{9,11},{10,... | collective-permute-start | bytes 393224 | tf_op jit(solution)/shard_map/ppermute | solution.py:41
  10.4 6.0 %collective-permute-start.4 = (bf16[528,128]{1,0:T(8,128)(2,1)S(1)}, bf16[528,128]{1,0:T(8,128)(2,1)S(1)}, u32[]{:S(2)}, u32[]{:S(2)}) collective-permute-start(bf16[528,128]{1,0:T(8,128)(2,1)S(1)} %shard_map.97.refs_0_), channel_id=1, source_target_pairs={{0,2},{1,3},{2,0},{3,1},{4,6},{5,7},{6,4},{7,5},{8,10},{9,11},{10,... | collective-permute-start | bytes 405512 | tf_op jit(solution)/shard_map/ppermute | solution.py:41
  12.3 13.8 %collective-permute-start.12 = (bf16[128,1024]{1,0:T(8,128)(2,1)S(1)}, bf16[128,1024]{1,0:T(8,128)(2,1)S(1)}, u32[]{:S(2)}, u32[]{:S(2)}) collective-permute-start(bf16[128,1024]{1,0:T(8,128)(2,1)S(1)} %get-tuple-element.41), channel_id=1, source_target_pairs={{0,8},{4,12},{8,0},{12,4},{1,9},{5,13},{9,1},{13,5},{2,10},{6,14},... | collective-permute-start | bytes 786440 | tf_op jit(solution)/shard_map/ppermute | solution.py:41
  14.9 5.0 %collective-permute-start.6 = (bf16[512,128]{1,0:T(8,128)(2,1)S(1)}, bf16[512,128]{1,0:T(8,128)(2,1)S(1)}, u32[]{:S(2)}, u32[]{:S(2)}) collective-permute-start(bf16[512,128]{1,0:T(8,128)(2,1)S(1)} %shard_map.98.refs_2_), channel_id=1, source_target_pairs={{0,1},{1,0},{2,3},{3,2},{4,5},{5,4},{6,7},{7,6},{8,9},{9,8},{10,11... | collective-permute-start | bytes 393224 | tf_op jit(solution)/shard_map/ppermute | solution.py:41
  16.5 3.4 %collective-permute-start.7 = (bf16[384,128]{1,0:T(8,128)(2,1)S(1)}, bf16[384,128]{1,0:T(8,128)(2,1)S(1)}, u32[]{:S(2)}, u32[]{:S(2)}) collective-permute-start(bf16[384,128]{1,0:T(8,128)(2,1)S(1)} %shard_map.99.refs_4_), channel_id=1, source_target_pairs={{0,16},{16,0},{1,17},{17,1},{2,18},{18,2},{3,19},{19,3},{4,20},{20... | collective-permute-start | bytes 294920 | tf_op jit(solution)/shard_map/ppermute | solution.py:41
  21.0 5.9 %collective-permute-start.8 = (bf16[768,128]{1,0:T(8,128)(2,1)S(1)}, bf16[768,128]{1,0:T(8,128)(2,1)S(1)}, u32[]{:S(2)}, u32[]{:S(2)}) collective-permute-start(bf16[768,128]{1,0:T(8,128)(2,1)S(1)} %get-tuple-element.29), channel_id=1, source_target_pairs={{0,16},{16,0},{1,17},{17,1},{2,18},{18,2},{3,19},{19,3},{4,20},{20... | collective-permute-start | bytes 589832 | tf_op jit(solution)/shard_map/ppermute | solution.py:41
  26.1 6.6 %collective-permute-start.13 = (bf16[128,1024]{1,0:T(8,128)(2,1)S(1)}, bf16[128,1024]{1,0:T(8,128)(2,1)S(1)}, u32[]{:S(2)}, u32[]{:S(2)}) collective-permute-start(bf16[128,1024]{1,0:T(8,128)(2,1)S(1)} %collective-permute-done.12.sent_ref), channel_id=1, source_target_pairs={{0,16},{16,0},{1,17},{17,1},{2,18},{18,2},{3,19},{19,3},{4,20},{20... | collective-permute-start | bytes 786440 | tf_op jit(solution)/shard_map/ppermute | solution.py:41
  28.3 11.9 %collective-permute-start.10 = (bf16[528,128]{1,0:T(8,128)(2,1)S(1)}, bf16[528,128]{1,0:T(8,128)(2,1)S(1)}, u32[]{:S(2)}, u32[]{:S(2)}) collective-permute-start(bf16[528,128]{1,0:T(8,128)(2,1)S(1)} %get-tuple-element.39), channel_id=1, source_target_pairs={{0,12},{4,8},{8,4},{12,0},{1,13},{5,9},{9,5},{13,1},{2,14},{6,10},... | collective-permute-start | bytes 405512 | tf_op jit(solution)/shard_map/ppermute | solution.py:41
  31.9 8.7 %collective-permute-start.9 = (bf16[528,128]{1,0:T(8,128)(2,1)S(1)}, bf16[528,128]{1,0:T(8,128)(2,1)S(1)}, u32[]{:S(2)}, u32[]{:S(2)}) collective-permute-start(bf16[528,128]{1,0:T(8,128)(2,1)S(1)} %get-tuple-element.38), channel_id=1, source_target_pairs={{0,4},{4,0},{8,12},{12,8},{1,5},{5,1},{9,13},{13,9},{2,6},{6,2},{1... | collective-permute-start | bytes 405512 | tf_op jit(solution)/shard_map/ppermute | solution.py:41
  31.9 7.9 %collective-permute-start.11 = (bf16[272,128]{1,0:T(8,128)(2,1)S(1)}, bf16[272,128]{1,0:T(8,128)(2,1)S(1)}, u32[]{:S(2)}, u32[]{:S(2)}) collective-permute-start(bf16[272,128]{1,0:T(8,128)(2,1)S(1)} %get-tuple-element.40), channel_id=1, source_target_pairs={{0,8},{4,12},{8,0},{12,4},{1,9},{5,13},{9,1},{13,5},{2,10},{6,14},... | collective-permute-start | bytes 208904 | tf_op jit(solution)/shard_map/ppermute | solution.py:41
